TPU v7x, 32 devices: a whole 2x2x4 slice. The times are simulated.
32 devices in a mesh: row: 4 (over y, x), col: 4 (over z), head: 2 (over core).
Axes of the slice: x: 2, y: 2, z: 4, core: 2. Of those that a mesh axis runs over, the one named last changes fastest.
Arguments:
- queries: bfloat16 [256, 64, 256], P('row', 'col'), may hold values from -1000 to 1000
- level_zero: bfloat16 [256, 64, 256], P('row', 'col', 'head'), may hold values from -6 to 6
- level_one: bfloat16 [128, 32, 256], P('row', 'col', 'head'), may hold values from -6 to 6
- level_two: bfloat16 [64, 16, 256], P('row', 'col', 'head'), may hold values from -6 to 6
- level_three: bfloat16 [32, 8, 256], P('row', 'col', 'head'), may hold values from -6 to 6
- tile_lists: int32 [16, 4, 4, 8], P('row', 'col'), may hold values from 0 to 63, as said below
- samples: int32 [256, 64, 128], P('row', 'col', 'head'), may hold values from 0 to 133168895, as said below
- logit_weight: bfloat16 [256, 128], P(None, 'head'), may hold values from -1 to 1
- logit_bias: float32 [128], P('head'), may hold values from -3 to 3
- output_weight: bfloat16 [256, 256], replicated, may hold values from -0.375 to 0.375
- output_bias: float32 [256], replicated, may hold values from -3 to 3
- norm_gain: float32 [256], P('head'), may hold values from 0.5 to 1.5
- norm_shift: float32 [256], P('head'), may hold values from -3 to 3
Outputs:
- updated_queries: bfloat16 [256, 64, 256], P('row', 'col', 'head')
Inputs may be any that keep to these rules, and one draw needn't show every extreme that they name: `tile_lists`: entries are tile numbers r * 4 + c. Over all lists of the query blocks that one device holds, at one level, at most 2 entries name tiles that one device holds; at each level some device is named exactly 2 times by the lists of every device. A tile may be listed more than once. `samples`: slot is below 8; at level l, pos_row and pos_col are below (16 / 2^l - 1) * 256.
All inputs are finite; a program needn't handle non-finite values.
Results may differ from a plain program's by a relative error of at most 0.004.
Values may be sent and summed in bfloat16 or wider, within the bound.
No kernel may reach another device: no remote copies, remote signals or barrier semaphores. Data moves between devices by JAX's collectives and lax.ppermute only.
A program may use at most 128 MiB of HBM per device.

v0:
```python
import jax
import jax.numpy as jnp
from jax import lax
from jax.sharding import PartitionSpec as P

LEVELS = 4
POINTS = 4


def as_sent(array):

    def short(part):
        return part.astype(jnp.bfloat16) if part.dtype == jnp.float32 else part

    return jax.tree.map(short, array)


def to_blocks(source, tile_rows, tile_cols, tile_side):
    channels = source.shape[2]
    shaped = source.reshape(tile_rows, tile_side, tile_cols, tile_side, channels)
    return shaped.transpose(0, 2, 1, 3, 4).reshape(
        tile_rows * tile_cols, tile_side * tile_side, channels
    )


def pixel_weights(attend, packed, tile_side, width_total):
    slot_index = packed // 16777216
    pos_row = packed // 4096 % 4096
    pos_col = packed % 4096
    frac_row = (pos_row % 256).astype(jnp.float32) / 256.0
    frac_col = (pos_col % 256).astype(jnp.float32) / 256.0
    base_index = slot_index * tile_side * tile_side + pos_row // 256 * tile_side + pos_col // 256
    column = jnp.arange(width_total, dtype=jnp.int32)
    combined = jnp.zeros((attend.shape[1], attend.shape[0], width_total), jnp.float32)
    corners = (
        (0, 1.0 - frac_row, 1.0 - frac_col),
        (1, 1.0 - frac_row, frac_col),
        (tile_side, frac_row, 1.0 - frac_col),
        (tile_side + 1, frac_row, frac_col),
    )
    for point_num in range(attend.shape[2]):
        for offset, weight_row, weight_col in corners:
            corner_weight = (
                attend[:, :, point_num] * weight_row[:, :, point_num] * weight_col[:, :, point_num]
            ).T
            target = (base_index[:, :, point_num] + offset).T
            combined = combined + jnp.where(
                column[None, None, :] == target[:, :, None], corner_weight[:, :, None], 0.0
            )
    return combined.astype(jnp.bfloat16)


def on_device(
    queries,
    level_zero,
    level_one,
    level_two,
    level_three,
    tile_lists,
    samples,
    logit_weight,
    logit_bias,
    output_weight,
    output_bias,
    norm_gain,
    norm_shift,
):
    level_blocks = (level_zero, level_one, level_two, level_three)
    row_count = lax.axis_size("row")
    col_count = lax.axis_size("col")
    peer_count = row_count * col_count
    tile_rows, tile_cols, level_count, per_block = tile_lists.shape
    local_tiles = tile_rows * tile_cols
    requests = local_tiles * per_block
    capacity = max(2, (requests + peer_count - 1) // peer_count)
    grid_cols = tile_cols * col_count
    channels = level_zero.shape[2]
    width_all = queries.shape[2]
    head_count = samples.shape[2] // (LEVELS * POINTS)
    head_dim = channels // head_count
    tile_side = level_zero.shape[0] // tile_rows
    pixels = tile_side * tile_side
    tile_sides = [level_blocks[level_num].shape[0] // tile_rows for level_num in range(level_count)]
    tiles_local = []
    send_ids = []
    positions = []
    request_order = jnp.arange(requests, dtype=jnp.int32)
    for level_num in range(level_count):
        side_here = tile_sides[level_num]
        shaped = level_blocks[level_num].reshape(
            tile_rows, side_here, tile_cols, side_here, channels
        )
        tiles_local.append(
            shaped.transpose(0, 2, 1, 3, 4).reshape(local_tiles, side_here, side_here, channels)
        )
        wanted = tile_lists[:, :, level_num, :].reshape(requests)
        grid_row = wanted // grid_cols
        grid_col = wanted % grid_cols
        owner_dev = grid_row // tile_rows * col_count + grid_col // tile_cols
        local_index = grid_row % tile_rows * tile_cols + grid_col % tile_cols
        same_owner = (owner_dev[:, None] == owner_dev[None, :]) & (
            request_order[None, :] < request_order[:, None]
        )
        pair_rank = jnp.sum(same_owner.astype(jnp.int32), axis=1)
        slot_place = owner_dev * capacity + pair_rank
        slot_table = (
            jnp.full((peer_count * capacity,), -1, jnp.int32).at[slot_place].set(local_index)
        )
        send_ids.append(slot_table.reshape(peer_count, capacity))
        positions.append(slot_place)
    received = lax.all_to_all(
        tuple(send_ids), ("row", "col"), split_axis=0, concat_axis=0, tiled=True
    )
    replies = []
    for serve_level_num in range(level_count):
        asked_ids = received[serve_level_num]
        is_valid = asked_ids >= 0
        picked = jnp.take(tiles_local[serve_level_num], jnp.maximum(asked_ids, 0), axis=0)
        replies.append(jnp.where(is_valid[:, :, None, None, None], picked, jnp.zeros_like(picked)))
    fetched = lax.all_to_all(
        as_sent(tuple(replies)), ("row", "col"), split_axis=0, concat_axis=0, tiled=True
    )
    gathered = []
    for level_num in range(level_count):
        side_here = tile_sides[level_num]
        flat_tiles = fetched[level_num].reshape(
            (peer_count * capacity, side_here, side_here, channels)
        )
        chosen = jnp.take(flat_tiles, positions[level_num], axis=0)
        gathered.append(chosen.reshape(local_tiles, per_block * side_here * side_here, channels))
    queries_blocked = to_blocks(queries, tile_rows, tile_cols, tile_side).reshape(
        local_tiles * pixels, width_all
    )
    logits = jnp.dot(queries_blocked, logit_weight, preferred_element_type=jnp.float32) + logit_bias
    attend = jax.nn.softmax(
        logits.reshape(local_tiles * pixels, head_count, LEVELS * POINTS), axis=-1
    )
    attend = attend.reshape(local_tiles, pixels, head_count, LEVELS, POINTS)
    packed = to_blocks(samples, tile_rows, tile_cols, tile_side).reshape(
        local_tiles, pixels, head_count, LEVELS, POINTS
    )

    def block_output(operands):
        attend_blk = operands[0]
        packed_blk = operands[1]
        running = jnp.zeros((pixels, head_count, head_dim), jnp.float32)
        for level_num in range(level_count):
            tile_values = operands[2 + level_num]
            width_total = tile_values.shape[0]
            weights_px = pixel_weights(
                attend_blk[:, :, level_num, :],
                packed_blk[:, :, level_num, :],
                tile_sides[level_num],
                width_total,
            )
            running = running + jnp.einsum(
                "hqn,nhd->qhd",
                weights_px,
                tile_values.reshape(width_total, head_count, head_dim),
                preferred_element_type=jnp.float32,
            )
        return running.reshape(pixels, channels).astype(jnp.bfloat16)

    attn_out = lax.map(
        block_output, (attend, packed, gathered[0], gathered[1], gathered[2], gathered[3])
    )
    attn_out = attn_out.reshape(local_tiles * pixels, channels)
    head_index = lax.axis_index("head")
    full_attn = lax.all_gather(attn_out, "head", axis=1, tiled=True)
    pre_norm = (
        queries_blocked.astype(jnp.float32)
        + jnp.dot(full_attn, output_weight, preferred_element_type=jnp.float32)
        + output_bias
    )
    row_mean = jnp.mean(pre_norm, axis=1, keepdims=True)
    centered = pre_norm - row_mean
    variance = jnp.mean(centered * centered, axis=1, keepdims=True)
    own_part = lax.dynamic_slice_in_dim(centered, head_index * channels, channels, 1)
    normalized = own_part * lax.rsqrt(variance + 1e-05)
    updated = (normalized * norm_gain + norm_shift).astype(jnp.bfloat16)
    updated = updated.reshape(tile_rows, tile_cols, tile_side, tile_side, channels).transpose(
        0, 2, 1, 3, 4
    )
    return updated.reshape(tile_rows * tile_side, tile_cols * tile_side, channels)


def solution(mesh):
    in_specs = (
        P("row", "col", None),
        P("row", "col", "head"),
        P("row", "col", "head"),
        P("row", "col", "head"),
        P("row", "col", "head"),
        P("row", "col", None, None),
        P("row", "col", "head"),
        P(None, "head"),
        P("head"),
        P(),
        P(),
        P("head"),
        P("head"),
    )
    out_specs = P("row", "col", "head")
    return jax.shard_map(
        on_device, mesh=mesh, in_specs=in_specs, out_specs=out_specs, check_vma=False
    )
```

profile of v0, /device:TPU:0, one launch (start us, length us, event | category | flops | bytes accessed | tf_op | source)
XLA Modules:
  0.0 335.1 jit_solution(9578026117994345754)
XLA Ops:
  3.0 8.3 %all-to-all-start.2 = ((s32[16,1,2]{2,1,0:T(1,128)}), s32[16,1,2]{2,1,0:T(1,128)S(1)}, u32[]{:S(2)}, u32[]{:S(2)}) async-start(s32[16,1,2]{2,1,0:T(1,128)} %bitcast.239), calls=%async_computation.2 | async-start | bytes 16384 | tf_op jit(solution)/shard_map/all_to_all | solution.py:111
  17.2 1.3 all-to-all-done.2
  18.5 5.6 %all-to-all-start.4 = ((s32[16,1,2]{2,1,0:T(1,128)}), s32[16,1,2]{2,1,0:T(1,128)S(1)}, u32[]{:S(2)}, u32[]{:S(2)}) async-start(s32[16,1,2]{2,1,0:T(1,128)} %bitcast.248), calls=%async_computation.4 | async-start | bytes 16384 | tf_op jit(solution)/shard_map/all_to_all | solution.py:111
  24.3 7.2 %all-to-all-done.4 = s32[16,1,2]{2,1,0:T(1,128)S(1)} async-done(((s32[16,1,2]{2,1,0:T(1,128)}), s32[16,1,2]{2,1,0:T(1,128)S(1)}, u32[]{:S(2)}, u32[]{:S(2)}) %all-to-all-start.4) | async-done | bytes 160 | tf_op jit(solution)/shard_map/all_to_all | solution.py:111
  31.4 3.4 %all-to-all-start.6 = ((s32[16,1,2]{2,1,0:T(1,128)}), s32[16,1,2]{2,1,0:T(1,128)S(1)}, u32[]{:S(2)}, u32[]{:S(2)}) async-start(s32[16,1,2]{2,1,0:T(1,128)} %bitcast.257), calls=%async_computation.6 | async-start | bytes 16384 | tf_op jit(solution)/shard_map/all_to_all | solution.py:111
  35.0 7.2 %all-to-all-done.6 = s32[16,1,2]{2,1,0:T(1,128)S(1)} async-done(((s32[16,1,2]{2,1,0:T(1,128)}), s32[16,1,2]{2,1,0:T(1,128)S(1)}, u32[]{:S(2)}, u32[]{:S(2)}) %all-to-all-start.6) | async-done | bytes 160 | tf_op jit(solution)/shard_map/all_to_all | solution.py:111
  42.2 3.5 %all-to-all-start = ((s32[16,1,2]{2,1,0:T(1,128)}), s32[16,1,2]{2,1,0:T(1,128)S(1)}, u32[]{:S(2)}, u32[]{:S(2)}) async-start(s32[16,1,2]{2,1,0:T(1,128)} %bitcast.227), calls=%async_computation | async-start | bytes 16384 | tf_op jit(solution)/shard_map/all_to_all | solution.py:111
  46.7 1.4 gather_fusion.4
  48.0 1.3 gather_fusion.6
  51.1 1.7 all-to-all-done
  52.9 5.1 %all-to-all-start.7 = ((bf16[16,2,2,2,128]{4,3,2,1,0:T(2,128)(2,1)}), bf16[16,2,2,2,128]{4,3,2,1,0:T(2,128)(2,1)S(1)}, u32[]{:S(2)}, u32[]{:S(2)}) async-start(bf16[16,2,2,2,128]{4,3,2,1,0:T(2,128)(2,1)} %broadcast_select_fusion.4), calls=%async_computation.7 | async-start | bytes 65536 | tf_op jit(solution)/shard_map/all_to_all | solution.py:120
  58.0 1.5 gather_fusion.2
  59.5 5.8 %all-to-all-done.7 = bf16[16,2,2,2,128]{4,3,2,1,0:T(2,128)(2,1)S(1)} async-done(((bf16[16,2,2,2,128]{4,3,2,1,0:T(2,128)(2,1)}), bf16[16,2,2,2,128]{4,3,2,1,0:T(2,128)(2,1)S(1)}, u32[]{:S(2)}, u32[]{:S(2)}) %all-to-all-start.7) | async-done | bytes 32800 | tf_op jit(solution)/shard_map/all_to_all | solution.py:120
  65.4 3.5 %all-to-all-start.5 = ((bf16[16,2,4,4,128]{4,3,2,1,0:T(4,128)(2,1)}), bf16[16,2,4,4,128]{4,3,2,1,0:T(4,128)(2,1)S(1)}, u32[]{:S(2)}, u32[]{:S(2)}) async-start(bf16[16,2,4,4,128]{4,3,2,1,0:T(4,128)(2,1)} %select_select_fusion.2), calls=%async_computation.5 | async-start | bytes 262144 | tf_op jit(solution)/shard_map/all_to_all | solution.py:120
  68.9 1.0 select_select_fusion.1
  69.9 6.6 %all-to-all-done.5 = bf16[16,2,4,4,128]{4,3,2,1,0:T(4,128)(2,1)S(1)} async-done(((bf16[16,2,4,4,128]{4,3,2,1,0:T(4,128)(2,1)}), bf16[16,2,4,4,128]{4,3,2,1,0:T(4,128)(2,1)S(1)}, u32[]{:S(2)}, u32[]{:S(2)}) %all-to-all-start.5) | async-done | bytes 131104 | tf_op jit(solution)/shard_map/all_to_all | solution.py:120
  76.5 3.6 %all-to-all-start.3 = ((bf16[16,2,8,8,128]{4,3,2,1,0:T(8,128)(2,1)}), bf16[16,2,8,8,128]{4,3,2,1,0:T(8,128)(2,1)S(1)}, u32[]{:S(2)}, u32[]{:S(2)}) async-start(bf16[16,2,8,8,128]{4,3,2,1,0:T(8,128)(2,1)} %select_select_fusion.1), calls=%async_computation.3 | async-start | bytes 1048576 | tf_op jit(solution)/shard_map/all_to_all | solution.py:120
  80.6 1.0 gather_fusion
  81.5 1.7 select_select_fusion
  83.2 8.9 %all-to-all-done.3 = bf16[16,2,8,8,128]{4,3,2,1,0:T(8,128)(2,1)S(1)} async-done(((bf16[16,2,8,8,128]{4,3,2,1,0:T(8,128)(2,1)}), bf16[16,2,8,8,128]{4,3,2,1,0:T(8,128)(2,1)S(1)}, u32[]{:S(2)}, u32[]{:S(2)}) %all-to-all-start.3) | async-done | bytes 524320 | tf_op jit(solution)/shard_map/all_to_all | solution.py:120
  92.0 4.6 %all-to-all-start.1 = ((bf16[16,2,16,16,128]{4,3,2,1,0:T(8,128)(2,1)}), bf16[16,2,16,16,128]{4,3,2,1,0:T(8,128)(2,1)}, u32[]{:S(2)}, u32[]{:S(2)}) async-start(bf16[16,2,16,16,128]{4,3,2,1,0:T(8,128)(2,1)} %select_select_fusion), calls=%async_computation.1 | async-start | bytes 4194304 | tf_op jit(solution)/shard_map/all_to_all | solution.py:120
  97.0 2.9 copy.117
  99.9 1.6 reshape_reshape_transpose_reshape.7
  101.5 1.1 bitcast_reduce_fusion
  106.7 0.9 fusion.183
  111.1 1.2 broadcast_select_fusion.1
  112.3 27.3 %all-to-all-done.1 = bf16[16,2,16,16,128]{4,3,2,1,0:T(8,128)(2,1)} async-done(((bf16[16,2,16,16,128]{4,3,2,1,0:T(8,128)(2,1)}), bf16[16,2,16,16,128]{4,3,2,1,0:T(8,128)(2,1)}, u32[]{:S(2)}, u32[]{:S(2)}) %all-to-all-start.1) | async-done | bytes 2097184 | tf_op jit(solution)/shard_map/all_to_all | solution.py:120
  139.6 3.7 %gather_fusion.1 = bf16[32,16,16,128]{3,2,1,0:T(8,128)(2,1)} fusion(bf16[32,16,16,128]{3,2,1,0:T(8,128)(2,1)} %bitcast.232, s32[1024]{0:T(1024)S(1)} %pad_clamp_fusion.6), kind=kCustom, calls=%fused_computation.1 | custom fusion | bytes 4194432 | tf_op jit(solution)/shard_map/jit(_take)/gather | solution.py:129
  143.3 4.4 %broadcast_select_fusion = bf16[4,2048,128]{2,1,0:T(8,128)(2,1)S(1)} fusion(bf16[4,2048,128]{2,1,0:T(8,128)(2,1)} %bitcast.874, pred[4,2048]{1,0:T(4,128)(4,1)S(1)} %broadcast_in_dim.1051), kind=kLoop, calls=%fused_computation.549 | loop fusion | flops 1048576 | bytes 4202496 | tf_op jit(solution)/shard_map/jit(_take)/select_n | solution.py:129
  147.7 182.1 %while.13 = (s32[]{:T(128)}, bf16[4,256,128]{2,1,0:T(8,128)(2,1)}, bf16[4,2048,128]{2,1,0:T(8,128)(2,1)S(1)}, s32[4,256,4,4,4]{1,0,4,3,2:T(4,128)}, f32[4,256,4,...) while((s32[]{:T(128)}, bf16[4,256,128]{2,1,0:T(8,128)(2,1)}, ...), condition=%wide.region_11.12_spmd, body=%wide.region_10.11_spmd.sunk | while | flops 314474496 | bytes 19226808 | solution.py:164
  148.5 1.0 constant_dynamic-slice_fusion.11
  151.4 0.9 fusion.254
  152.5 1.1 fusion.256
  154.5 6.5 %fusion.258 = f32[4,32,256]{2,1,0:T(8,128)} fusion(bf16[128,4,32]{0,2,1:T(8,128)(2,1)S(1)} %bitcast.884, f32[4,256]{1,0:T(4,128)S(1)} %get-tuple-element.695, s32[4,256]{1,0:T(4,128)S(1)} %get-tuple-element.696, f32[4,256]{1,0:T(4,128)S(1)} %get-tuple-element.698, s32[4,256]{1,0:T(4,128)S(1)} %get-tuple-element.699, ...), kind=kOutput, calls=%fused_computation.100.clone.1 | convolution fusion | flops 14680064 | bytes 294912 | tf_op jit(solution)/shard_map/while/body/eval_jaxpr/hqn,nhd->qhd/dot_general | solution.py:156
  165.6 18.8 %add_convert_fusion.21 = bf16[4,256,2048]{2,1,0:T(8,128)(2,1)S(1)} fusion(f32[4,256]{1,0:T(4,128)S(1)} %get-tuple-element.732, s32[4,256]{1,0:T(4,128)S(1)} %get-tuple-element.734, f32[4,256]{1,0:T(4,128)S(1)} %get-tuple-element.736, s32[4,256]{1,0:T(4,128)S(1)} %get-tuple-element.737, f32[4,256]{1,0:T(4,128)S(1)} %get-tuple-element.739, ...), kind=kLoop, calls=%fused_computation.12.clone.clone.1.clone.1 | loop fusion | flops 100663296 | bytes 4325376 | tf_op jit(solution)/shard_map/while/body/eval_jaxpr/hqn,nhd->qhd/dot_general | solution.py:156
  184.4 1.3 fusion.260
  185.7 1.0 constant_dynamic-slice_fusion.14
  186.9 5.1 %add_convert_fusion.22 = bf16[4,256,512]{2,1,0:T(8,128)(2,1)S(1)} fusion(f32[4,256]{1,0:T(4,128)S(1)} %get-tuple-element.771, s32[4,256]{1,0:T(4,128)S(1)} %get-tuple-element.772, f32[4,256]{1,0:T(4,128)S(1)} %get-tuple-element.774, s32[4,256]{1,0:T(4,128)S(1)} %get-tuple-element.775, f32[4,256]{1,0:T(4,128)S(1)} %get-tuple-element.777, ...), kind=kLoop, calls=%fused_computation.30.clone.clone.1.clone.1 | loop fusion | flops 25165824 | bytes 1179648 | tf_op jit(solution)/shard_map/while/body/eval_jaxpr/hqn,nhd->qhd/dot_general | solution.py:156
  194.0 1.0 constant_dynamic-slice_fusion.11
  197.0 0.9 fusion.254
  198.0 1.1 fusion.256
  200.1 6.5 %fusion.258 = f32[4,32,256]{2,1,0:T(8,128)} fusion(bf16[128,4,32]{0,2,1:T(8,128)(2,1)S(1)} %bitcast.884, f32[4,256]{1,0:T(4,128)S(1)} %get-tuple-element.695, s32[4,256]{1,0:T(4,128)S(1)} %get-tuple-element.696, f32[4,256]{1,0:T(4,128)S(1)} %get-tuple-element.698, s32[4,256]{1,0:T(4,128)S(1)} %get-tuple-element.699, ...), kind=kOutput, calls=%fused_computation.100.clone.1 | convolution fusion | flops 14680064 | bytes 294912 | tf_op jit(solution)/shard_map/while/body/eval_jaxpr/hqn,nhd->qhd/dot_general | solution.py:156
  211.1 18.8 %add_convert_fusion.21 = bf16[4,256,2048]{2,1,0:T(8,128)(2,1)S(1)} fusion(f32[4,256]{1,0:T(4,128)S(1)} %get-tuple-element.732, s32[4,256]{1,0:T(4,128)S(1)} %get-tuple-element.734, f32[4,256]{1,0:T(4,128)S(1)} %get-tuple-element.736, s32[4,256]{1,0:T(4,128)S(1)} %get-tuple-element.737, f32[4,256]{1,0:T(4,128)S(1)} %get-tuple-element.739, ...), kind=kLoop, calls=%fused_computation.12.clone.clone.1.clone.1 | loop fusion | flops 100663296 | bytes 4325376 | tf_op jit(solution)/shard_map/while/body/eval_jaxpr/hqn,nhd->qhd/dot_general | solution.py:156
  229.9 1.3 fusion.260
  231.3 1.0 constant_dynamic-slice_fusion.14
  232.4 5.1 %add_convert_fusion.22 = bf16[4,256,512]{2,1,0:T(8,128)(2,1)S(1)} fusion(f32[4,256]{1,0:T(4,128)S(1)} %get-tuple-element.771, s32[4,256]{1,0:T(4,128)S(1)} %get-tuple-element.772, f32[4,256]{1,0:T(4,128)S(1)} %get-tuple-element.774, s32[4,256]{1,0:T(4,128)S(1)} %get-tuple-element.775, f32[4,256]{1,0:T(4,128)S(1)} %get-tuple-element.777, ...), kind=kLoop, calls=%fused_computation.30.clone.clone.1.clone.1 | loop fusion | flops 25165824 | bytes 1179648 | tf_op jit(solution)/shard_map/while/body/eval_jaxpr/hqn,nhd->qhd/dot_general | solution.py:156
  239.6 1.0 constant_dynamic-slice_fusion.11
  242.5 0.9 fusion.254
  243.5 1.1 fusion.256
  245.6 6.5 %fusion.258 = f32[4,32,256]{2,1,0:T(8,128)} fusion(bf16[128,4,32]{0,2,1:T(8,128)(2,1)S(1)} %bitcast.884, f32[4,256]{1,0:T(4,128)S(1)} %get-tuple-element.695, s32[4,256]{1,0:T(4,128)S(1)} %get-tuple-element.696, f32[4,256]{1,0:T(4,128)S(1)} %get-tuple-element.698, s32[4,256]{1,0:T(4,128)S(1)} %get-tuple-element.699, ...), kind=kOutput, calls=%fused_computation.100.clone.1 | convolution fusion | flops 14680064 | bytes 294912 | tf_op jit(solution)/shard_map/while/body/eval_jaxpr/hqn,nhd->qhd/dot_general | solution.py:156
  256.6 18.8 %add_convert_fusion.21 = bf16[4,256,2048]{2,1,0:T(8,128)(2,1)S(1)} fusion(f32[4,256]{1,0:T(4,128)S(1)} %get-tuple-element.732, s32[4,256]{1,0:T(4,128)S(1)} %get-tuple-element.734, f32[4,256]{1,0:T(4,128)S(1)} %get-tuple-element.736, s32[4,256]{1,0:T(4,128)S(1)} %get-tuple-element.737, f32[4,256]{1,0:T(4,128)S(1)} %get-tuple-element.739, ...), kind=kLoop, calls=%fused_computation.12.clone.clone.1.clone.1 | loop fusion | flops 100663296 | bytes 4325376 | tf_op jit(solution)/shard_map/while/body/eval_jaxpr/hqn,nhd->qhd/dot_general | solution.py:156
  275.4 1.3 fusion.260
  276.8 1.0 constant_dynamic-slice_fusion.14
  278.0 5.1 %add_convert_fusion.22 = bf16[4,256,512]{2,1,0:T(8,128)(2,1)S(1)} fusion(f32[4,256]{1,0:T(4,128)S(1)} %get-tuple-element.771, s32[4,256]{1,0:T(4,128)S(1)} %get-tuple-element.772, f32[4,256]{1,0:T(4,128)S(1)} %get-tuple-element.774, s32[4,256]{1,0:T(4,128)S(1)} %get-tuple-element.775, f32[4,256]{1,0:T(4,128)S(1)} %get-tuple-element.777, ...), kind=kLoop, calls=%fused_computation.30.clone.clone.1.clone.1 | loop fusion | flops 25165824 | bytes 1179648 | tf_op jit(solution)/shard_map/while/body/eval_jaxpr/hqn,nhd->qhd/dot_general | solution.py:156
  285.1 1.0 constant_dynamic-slice_fusion.11
  288.0 0.9 fusion.254
  289.0 1.1 fusion.256
  291.1 6.5 %fusion.258 = f32[4,32,256]{2,1,0:T(8,128)} fusion(bf16[128,4,32]{0,2,1:T(8,128)(2,1)S(1)} %bitcast.884, f32[4,256]{1,0:T(4,128)S(1)} %get-tuple-element.695, s32[4,256]{1,0:T(4,128)S(1)} %get-tuple-element.696, f32[4,256]{1,0:T(4,128)S(1)} %get-tuple-element.698, s32[4,256]{1,0:T(4,128)S(1)} %get-tuple-element.699, ...), kind=kOutput, calls=%fused_computation.100.clone.1 | convolution fusion | flops 14680064 | bytes 294912 | tf_op jit(solution)/shard_map/while/body/eval_jaxpr/hqn,nhd->qhd/dot_general | solution.py:156
  302.1 18.8 %add_convert_fusion.21 = bf16[4,256,2048]{2,1,0:T(8,128)(2,1)S(1)} fusion(f32[4,256]{1,0:T(4,128)S(1)} %get-tuple-element.732, s32[4,256]{1,0:T(4,128)S(1)} %get-tuple-element.734, f32[4,256]{1,0:T(4,128)S(1)} %get-tuple-element.736, s32[4,256]{1,0:T(4,128)S(1)} %get-tuple-element.737, f32[4,256]{1,0:T(4,128)S(1)} %get-tuple-element.739, ...), kind=kLoop, calls=%fused_computation.12.clone.clone.1.clone.1 | loop fusion | flops 100663296 | bytes 4325376 | tf_op jit(solution)/shard_map/while/body/eval_jaxpr/hqn,nhd->qhd/dot_general | solution.py:156
  320.9 1.3 fusion.260
  322.3 1.0 constant_dynamic-slice_fusion.14
  323.5 5.1 %add_convert_fusion.22 = bf16[4,256,512]{2,1,0:T(8,128)(2,1)S(1)} fusion(f32[4,256]{1,0:T(4,128)S(1)} %get-tuple-element.771, s32[4,256]{1,0:T(4,128)S(1)} %get-tuple-element.772, f32[4,256]{1,0:T(4,128)S(1)} %get-tuple-element.774, s32[4,256]{1,0:T(4,128)S(1)} %get-tuple-element.775, f32[4,256]{1,0:T(4,128)S(1)} %get-tuple-element.777, ...), kind=kLoop, calls=%fused_computation.30.clone.clone.1.clone.1 | loop fusion | flops 25165824 | bytes 1179648 | tf_op jit(solution)/shard_map/while/body/eval_jaxpr/hqn,nhd->qhd/dot_general | solution.py:156
  329.8 2.4 all_gather.3
  332.2 1.6 fusion.220
  (291 shorter events, 59.3 us)
Async XLA Ops:
  0.0 80.6 %copy-start = (bf16[64,16,128]{2,1,0:T(8,128)(2,1)S(1)}, bf16[64,16,128]{2,1,0:T(8,128)(2,1)}, u32[]{:S(2)}) copy-start(bf16[64,16,128]{2,1,0:T(8,128)(2,1)} %param.16) | copy-start | bytes 786436
  1.0 0.5 copy-start.10
  1.2 10.1 %copy-start.11 = (s32[32]{0:T(128)}, s32[32]{0:T(128)S(1)}, u32[]{:S(2)}) copy-start(s32[32]{0:T(128)S(1)} %convert_reduce_fusion.2) | copy-start | bytes 388
  3.0 15.6 %all-to-all-start.2 = ((s32[16,1,2]{2,1,0:T(1,128)}), s32[16,1,2]{2,1,0:T(1,128)S(1)}, u32[]{:S(2)}, u32[]{:S(2)}) async-start(s32[16,1,2]{2,1,0:T(1,128)} %bitcast.239), calls=%async_computation.2 | async-start | bytes 16384 | tf_op jit(solution)/shard_map/all_to_all | solution.py:111
  13.2 0.5 copy-start.12
  13.4 33.2 %copy-start.13 = (s32[32]{0:T(128)}, s32[32]{0:T(128)S(1)}, u32[]{:S(2)}) copy-start(s32[32]{0:T(128)S(1)} %convert_reduce_fusion.1) | copy-start | bytes 388
  13.9 0.5 copy-start.14
  14.1 32.5 %copy-start.15 = (s32[32]{0:T(128)}, s32[32]{0:T(128)S(1)}, u32[]{:S(2)}) copy-start(s32[32]{0:T(128)S(1)} %convert_reduce_fusion) | copy-start | bytes 388
  14.2 4.3 %copy-start.6 = (s32[32]{0:T(128)}, s32[32]{0:T(128)S(1)}, u32[]{:S(2)}) copy-start(s32[32]{0:T(128)S(1)} %fusion.198) | copy-start | bytes 388
  15.2 3.4 %copy-start.7 = (s32[32]{0:T(128)}, s32[32]{0:T(128)S(1)}, u32[]{:S(2)}) copy-start(s32[32]{0:T(128)S(1)} %fusion.199) | copy-start | bytes 388
  18.5 12.9 %all-to-all-start.4 = ((s32[16,1,2]{2,1,0:T(1,128)}), s32[16,1,2]{2,1,0:T(1,128)S(1)}, u32[]{:S(2)}, u32[]{:S(2)}) async-start(s32[16,1,2]{2,1,0:T(1,128)} %bitcast.248), calls=%async_computation.4 | async-start | bytes 16384 | tf_op jit(solution)/shard_map/all_to_all | solution.py:111
  31.4 10.7 %all-to-all-start.6 = ((s32[16,1,2]{2,1,0:T(1,128)}), s32[16,1,2]{2,1,0:T(1,128)S(1)}, u32[]{:S(2)}, u32[]{:S(2)}) async-start(s32[16,1,2]{2,1,0:T(1,128)} %bitcast.257), calls=%async_computation.6 | async-start | bytes 16384 | tf_op jit(solution)/shard_map/all_to_all | solution.py:111
  42.2 10.7 %all-to-all-start = ((s32[16,1,2]{2,1,0:T(1,128)}), s32[16,1,2]{2,1,0:T(1,128)S(1)}, u32[]{:S(2)}, u32[]{:S(2)}) async-start(s32[16,1,2]{2,1,0:T(1,128)} %bitcast.227), calls=%async_computation | async-start | bytes 16384 | tf_op jit(solution)/shard_map/all_to_all | solution.py:111
  52.9 12.5 %all-to-all-start.7 = ((bf16[16,2,2,2,128]{4,3,2,1,0:T(2,128)(2,1)}), bf16[16,2,2,2,128]{4,3,2,1,0:T(2,128)(2,1)S(1)}, u32[]{:S(2)}, u32[]{:S(2)}) async-start(bf16[16,2,2,2,128]{4,3,2,1,0:T(2,128)(2,1)} %broadcast_select_fusion.4), calls=%async_computation.7 | async-start | bytes 65536 | tf_op jit(solution)/shard_map/all_to_all | solution.py:120
  65.4 15.2 %copy-start.4 = (bf16[16,2,2,2,128]{4,3,2,1,0:T(2,128)(2,1)}, bf16[16,2,2,2,128]{4,3,2,1,0:T(2,128)(2,1)S(1)}, u32[]{:S(2)}) copy-start(bf16[16,2,2,2,128]{4,3,2,1,0:T(2,128)(2,1)S(1)} %all-to-all-done.7) | copy-start | bytes 98308
  65.4 11.1 %all-to-all-start.5 = ((bf16[16,2,4,4,128]{4,3,2,1,0:T(4,128)(2,1)}), bf16[16,2,4,4,128]{4,3,2,1,0:T(4,128)(2,1)S(1)}, u32[]{:S(2)}, u32[]{:S(2)}) async-start(bf16[16,2,4,4,128]{4,3,2,1,0:T(4,128)(2,1)} %select_select_fusion.2), calls=%async_computation.5 | async-start | bytes 262144 | tf_op jit(solution)/shard_map/all_to_all | solution.py:120
  76.5 15.6 %all-to-all-start.3 = ((bf16[16,2,8,8,128]{4,3,2,1,0:T(8,128)(2,1)}), bf16[16,2,8,8,128]{4,3,2,1,0:T(8,128)(2,1)S(1)}, u32[]{:S(2)}, u32[]{:S(2)}) async-start(bf16[16,2,8,8,128]{4,3,2,1,0:T(8,128)(2,1)} %select_select_fusion.1), calls=%async_computation.3 | async-start | bytes 1048576 | tf_op jit(solution)/shard_map/all_to_all | solution.py:120
  92.0 47.6 %all-to-all-start.1 = ((bf16[16,2,16,16,128]{4,3,2,1,0:T(8,128)(2,1)}), bf16[16,2,16,16,128]{4,3,2,1,0:T(8,128)(2,1)}, u32[]{:S(2)}, u32[]{:S(2)}) async-start(bf16[16,2,16,16,128]{4,3,2,1,0:T(8,128)(2,1)} %select_select_fusion), calls=%async_computation.1 | async-start | bytes 4194304 | tf_op jit(solution)/shard_map/all_to_all | solution.py:120
  97.0 4.5 %copy-start.3 = (bf16[64,16,256]{2,1,0:T(8,128)(2,1)S(1)}, bf16[64,16,256]{2,1,0:T(8,128)(2,1)}, u32[]{:S(2)}) copy-start(bf16[64,16,256]{2,1,0:T(8,128)(2,1)} %param.15) | copy-start | bytes 1572868
  101.5 6.2 %copy-start.5 = (bf16[16,2,2,2,128]{4,3,2,1,0:T(2,128)(2,1)S(1)}, bf16[16,2,2,2,128]{4,3,2,1,0:T(2,128)(2,1)}, u32[]{:S(2)}) copy-start(bf16[16,2,2,2,128]{4,3,2,1,0:T(2,128)(2,1)} %copy-done.4) | copy-start | bytes 98308
  185.7 6.3 %copy-start.1 = (f32[4,32,256]{2,1,0:T(8,128)S(1)}, f32[4,32,256]{2,1,0:T(8,128)}, u32[]{:S(2)}) copy-start(f32[4,32,256]{2,1,0:T(8,128)} %fusion.256) | copy-start | bytes 393220 | tf_op jit(solution)/shard_map/while
  185.7 6.3 %copy-start.2 = (f32[4,32,256]{2,1,0:T(8,128)S(1)}, f32[4,32,256]{2,1,0:T(8,128)}, u32[]{:S(2)}) copy-start(f32[4,32,256]{2,1,0:T(8,128)} %fusion.258) | copy-start | bytes 393220 | tf_op jit(solution)/shard_map/while
  231.2 6.3 %copy-start.1 = (f32[4,32,256]{2,1,0:T(8,128)S(1)}, f32[4,32,256]{2,1,0:T(8,128)}, u32[]{:S(2)}) copy-start(f32[4,32,256]{2,1,0:T(8,128)} %fusion.256) | copy-start | bytes 393220 | tf_op jit(solution)/shard_map/while
  231.3 6.3 %copy-start.2 = (f32[4,32,256]{2,1,0:T(8,128)S(1)}, f32[4,32,256]{2,1,0:T(8,128)}, u32[]{:S(2)}) copy-start(f32[4,32,256]{2,1,0:T(8,128)} %fusion.258) | copy-start | bytes 393220 | tf_op jit(solution)/shard_map/while
  276.8 6.3 %copy-start.1 = (f32[4,32,256]{2,1,0:T(8,128)S(1)}, f32[4,32,256]{2,1,0:T(8,128)}, u32[]{:S(2)}) copy-start(f32[4,32,256]{2,1,0:T(8,128)} %fusion.256) | copy-start | bytes 393220 | tf_op jit(solution)/shard_map/while
  276.8 6.3 %copy-start.2 = (f32[4,32,256]{2,1,0:T(8,128)S(1)}, f32[4,32,256]{2,1,0:T(8,128)}, u32[]{:S(2)}) copy-start(f32[4,32,256]{2,1,0:T(8,128)} %fusion.258) | copy-start | bytes 393220 | tf_op jit(solution)/shard_map/while
  322.3 6.3 %copy-start.1 = (f32[4,32,256]{2,1,0:T(8,128)S(1)}, f32[4,32,256]{2,1,0:T(8,128)}, u32[]{:S(2)}) copy-start(f32[4,32,256]{2,1,0:T(8,128)} %fusion.256) | copy-start | bytes 393220 | tf_op jit(solution)/shard_map/while
  322.3 6.3 %copy-start.2 = (f32[4,32,256]{2,1,0:T(8,128)S(1)}, f32[4,32,256]{2,1,0:T(8,128)}, u32[]{:S(2)}) copy-start(f32[4,32,256]{2,1,0:T(8,128)} %fusion.258) | copy-start | bytes 393220 | tf_op jit(solution)/shard_map/while
  332.2 2.0 copy-start.8
  332.2 2.0 copy-start.9
where the time goes:
time: 338 us; the launch traced here: 335 us
  other arithmetic  136 us (40%)
  waiting for transfers between devices  66.1 us (20%)
  local copies, waits for them, and re-layouts  51.6 us (15%)
  matrix products  40.2 us (12%)
  starting transfers between devices  37.7 us (11%)
    dot_general x8, other arithmetic, block_output(): jnp.einsum('hqn,nhd->qhd', weights_px, tile_values.reshape(width_total, h...  95.6 us
    all_to_all x4, waiting for transfers between devices, on_device(): lax.all_to_all(as_sent(tuple(replies)), ('row', 'col'), split_axis=0, con...  48.7 us
    dot_general x16, matrix products, block_output(): jnp.einsum('hqn,nhd->qhd', weights_px, tile_values.reshape(width_total, h...  37.6 us
    all_to_all x4, starting transfers between devices, on_device(): lax.all_to_all(tuple(send_ids), ('row', 'col'), split_axis=0, concat_axis...  20.8 us
    all_to_all x4, waiting for transfers between devices, on_device(): lax.all_to_all(tuple(send_ids), ('row', 'col'), split_axis=0, concat_axis...  17.4 us
    all_to_all x4, starting transfers between devices, on_device(): lax.all_to_all(as_sent(tuple(replies)), ('row', 'col'), split_axis=0, con...  16.9 us
    dynamic_slice x40, local copies, waits for them, and re-layouts, on_device(): lax.map(block_output, (attend, packed, gathered[0], gathered[1], gathered...  16.3 us
    transpose x64, other arithmetic, pixel_weights(): corner_weight = (attend[:, :, point_num] * weight_row[:, :, point_num] *...  11.8 us
  transfers between devices with their start and end apart: 8, of which 8 were waited for; matrix products, arithmetic and copies ran while one was open for 9% of the time, Pallas kernels for 0%

commit v1 on v0

v1 whole, which is shorter than its diff:
```python
import functools
import jax
import jax.numpy as jnp
from jax import lax
from jax.experimental import pallas as pl
from jax.experimental.pallas import tpu as pltpu
from jax.sharding import PartitionSpec as P

LEVELS = 4
POINTS = 4
ANY = pl.ANY
SMEM = pltpu.SMEM
VMEM = pltpu.VMEM


def to_blocks(source, tile_rows, tile_cols, tile_side):
    channels = source.shape[2]
    shaped = source.reshape(tile_rows, tile_side, tile_cols, tile_side, channels)
    return shaped.transpose(0, 2, 1, 3, 4).reshape(
        tile_rows * tile_cols, tile_side * tile_side, channels
    )


def hat(position, center):
    return jnp.maximum(1.0 - jnp.abs(position - center), 0.0)


def iota(shape, dim):
    return lax.broadcasted_iota(jnp.int32, shape, dim)


def prep_kernel(heads, query_ref, weight_ref, bias_ref, out_ref):
    logits = lax.dot_general(
        weight_ref[...], query_ref[...], (((1,), (1,)), ((), ())), preferred_element_type=jnp.float32
    )
    logits = logits + bias_ref[...]
    lanes = LEVELS * POINTS
    for head in range(heads):
        part = logits[head * lanes : (head + 1) * lanes, :]
        part = jnp.exp(part - jnp.max(part, axis=0, keepdims=True))
        out_ref[head * lanes : (head + 1) * lanes, :] = part / jnp.sum(part, axis=0, keepdims=True)


def select_kernel(dims, ids_ref, zero_ref, one_ref, two_ref, three_ref, out_ref, sem):
    peers, capacity, sizes = dims
    refs = (zero_ref, one_ref, two_ref)

    def copies(peer, make):
        base = 0
        for level in range(LEVELS - 1):
            size = sizes[level]
            for slot in range(capacity):
                index = jnp.maximum(ids_ref[peer, level * capacity + slot], 0)
                make(refs[level].at[index], out_ref.at[peer, base : base + size, :])
                base += size
        make(three_ref, out_ref.at[peer, base : base + three_ref.shape[0], :])

    def start(peer, carry):
        copies(peer, lambda src, dst: pltpu.make_async_copy(src, dst, sem).start())
        return carry

    def finish(peer, carry):
        copies(peer, lambda src, dst: pltpu.make_async_copy(src, dst, sem).wait())
        return carry

    lax.fori_loop(0, peers, start, 0)
    lax.fori_loop(0, peers, finish, 0)


def attend_kernel(
    dims,
    request_ref,
    fetched_ref,
    attend_ref,
    sample_ref,
    rowid_ref,
    out_ref,
    tile0,
    tile1,
    tile2,
    tile3,
    left0,
    left1,
    left2,
    weight0,
    weight1,
    weight2,
    code_ref,
    row_ref,
    col_ref,
    sem,
):
    peers, capacity, sizes, sides, per_block, heads, head_dim, blocks = dims
    block = pl.program_id(0)
    pixels = out_ref.shape[0]
    channels = heads * head_dim
    tiles = (tile0, tile1, tile2)
    small = tile3.shape[1]
    base3 = capacity * sum(sizes[:3])

    @pl.when(block == 0)
    def _():
        def start(peer, carry):
            base = 0
            for level in range(LEVELS - 1):
                size = sizes[level]
                for slot in range(capacity):
                    request = request_ref[peer, level * capacity + slot]

                    @pl.when(request >= 0)
                    def _(level=level, base=base, size=size, request=request):
                        here = request // per_block
                        pltpu.make_async_copy(
                            fetched_ref.at[peer, base : base + size, :],
                            tiles[level].at[here, request % per_block],
                            sem.at[level, here],
                        ).start()

                    base += size
            return carry

        pltpu.make_async_copy(
            fetched_ref.at[:, base3 : base3 + small, :], tile3, sem.at[LEVELS - 1, 0]
        ).start()
        lax.fori_loop(0, peers, start, 0)
        left0[...] = jnp.zeros_like(left0)
        weight2[...] = jnp.zeros_like(weight2)
        pltpu.make_async_copy(
            fetched_ref.at[:, base3 : base3 + small, :], tile3, sem.at[LEVELS - 1, 0]
        ).wait()
        flat = tile3[...].reshape(peers * small, channels)
        chosen = (rowid_ref[...] == iota((rowid_ref.shape[0], peers * small), 1)).astype(jnp.bfloat16)
        picked = jnp.dot(chosen, flat, preferred_element_type=jnp.float32)
        left2[:, 128:] = picked.T.astype(jnp.bfloat16)

    packed = sample_ref[...]
    level_of = iota(packed.shape, 0) // POINTS % LEVELS
    slot = packed >> 24
    pos_row = (packed >> 12) & 4095
    pos_col = packed & 4095
    half = lax.shift_right_logical(jnp.full_like(packed, sides[0] * 128), level_of)
    upper = (pos_row >= half) & (level_of < 2)
    code_ref[...] = slot + jnp.where(upper, per_block, 0)
    row_ref[...] = (pos_row - jnp.where(upper, half, 0)).astype(jnp.float32) * (1.0 / 256.0)
    col_ref[...] = pos_col.astype(jnp.float32) * (1.0 / 256.0)

    for level in range(LEVELS - 1):
        pltpu.make_async_copy(tiles[level].at[block], tiles[level].at[block], sem.at[level, block]).wait()

    side0, side1 = sides[0], sides[1]
    half0, half1 = side0 // 2, side1 // 2
    for line in range(side0):
        piece = tile0[block, :, line * side0 : (line + 1) * side0, :]
        turned = piece.reshape(per_block * side0, channels).T
        for group in range(2):
            offset = line - group * half0
            if 0 <= offset <= half0:
                for head in range(heads):
                    left0[
                        head,
                        offset * head_dim : (offset + 1) * head_dim,
                        group * per_block * side0 : (group + 1) * per_block * side0,
                    ] = turned[head * head_dim : (head + 1) * head_dim, :]
    wide1 = tile1[block].astype(jnp.float32)
    for offset in range(half1 + 1):
        first = wide1[:, offset * side1 : (offset + 1) * side1, :]
        other = min(half1 + offset, side1 - 1)
        second = wide1[:, other * side1 : (other + 1) * side1, :]
        both = jnp.concatenate(
            [first.reshape(per_block * side1, channels), second.reshape(per_block * side1, channels)], axis=0
        )
        turned = both.T.astype(jnp.bfloat16)
        for head in range(heads):
            left1[head, offset * head_dim : (offset + 1) * head_dim, :] = turned[
                head * head_dim : (head + 1) * head_dim, :
            ]
    left2[:, :128] = tile2[block].reshape(per_block * sizes[2], channels).T
    weight2[128:, :] = jnp.zeros_like(weight2[128:, :])

    for head in range(heads):
        total = jnp.zeros((head_dim, pixels), jnp.float32)
        for level in range(2):
            side = sides[level]
            left = (left0, left1)[level]
            weight = (weight0, weight1)[level]
            reach = side // 2 + 1
            for point in range(POINTS):
                row = (head * LEVELS + level) * POINTS + point
                line = slice(row, row + 1)
                code = code_ref[line, :]
                across = attend_ref[line, :] * hat(
                    col_ref[line, :], (iota((16, pixels), 0) % side).astype(jnp.float32)
                )
                step = 16 // side
                for index in range(0, 2 * per_block, step):
                    wanted = index + iota((16, pixels), 0) // side
                    weight[point, index * side : (index + step) * side, :] = jnp.where(
                        code == wanted, across, 0.0
                    ).astype(jnp.bfloat16)
                product = jnp.dot(left[head], weight[point], preferred_element_type=jnp.float32)
                down = row_ref[line, :]
                for offset in range(reach):
                    total = total + product[offset * head_dim : (offset + 1) * head_dim, :] * hat(
                        down, float(offset)
                    )
        side = sides[2]
        size = sizes[2]
        place = iota((size, pixels), 0)
        parts = []
        codes = []
        for point in range(POINTS):
            row = (head * LEVELS + 2) * POINTS + point
            line = slice(row, row + 1)
            parts.append(
                attend_ref[line, :]
                * hat(row_ref[line, :], (place // side).astype(jnp.float32))
                * hat(col_ref[line, :], (place % side).astype(jnp.float32))
            )
            codes.append(code_ref[line, :])
        for index in range(per_block):
            mixed = jnp.zeros((size, pixels), jnp.float32)
            for point in range(POINTS):
                mixed = mixed + jnp.where(codes[point] == index, parts[point], 0.0)
            weight2[index * size : (index + 1) * size, :] = mixed.astype(jnp.bfloat16)
        side = sides[3]
        size = sizes[3]
        deep = per_block * size
        place = iota((deep, pixels), 0)
        mixed = jnp.zeros((deep, pixels), jnp.float32)
        for point in range(POINTS):
            row = (head * LEVELS + 3) * POINTS + point
            line = slice(row, row + 1)
            value = (
                attend_ref[line, :]
                * hat(row_ref[line, :], (place % size // side).astype(jnp.float32))
                * hat(col_ref[line, :], (place % side).astype(jnp.float32))
            )
            mixed = mixed + jnp.where(code_ref[line, :] == place // size, value, 0.0)
        weight2[pl.ds(pl.multiple_of(128 + block * deep, deep), deep), :] = mixed.astype(jnp.bfloat16)
        total = total + jnp.dot(
            left2[head * head_dim : (head + 1) * head_dim, :], weight2[...], preferred_element_type=jnp.float32
        )
        out_ref[:, head * head_dim : (head + 1) * head_dim] = total.T.astype(jnp.bfloat16)


def norm_kernel(
    count, head_ref, query_ref, own_ref, other_ref, weight_ref, bias_ref, gain_ref, shift_ref, out_ref
):
    own_head = head_ref[0]
    channels = out_ref.shape[1]
    own_rows = weight_ref[pl.ds(pl.multiple_of(own_head * channels, channels), channels), :]
    other_rows = weight_ref[pl.ds(pl.multiple_of((1 - own_head) * channels, channels), channels), :]
    pre = query_ref[...].astype(jnp.float32) + bias_ref[...]
    pre = pre + jnp.dot(own_ref[...], own_rows, preferred_element_type=jnp.float32)
    pre = pre + jnp.dot(other_ref[...], other_rows, preferred_element_type=jnp.float32)
    centered = pre - jnp.mean(pre, axis=1, keepdims=True)
    variance = jnp.mean(centered * centered, axis=1, keepdims=True)
    own = jnp.where(own_head == 0, centered[:, :channels], centered[:, channels:])
    out_ref[...] = (own * lax.rsqrt(variance + 1e-05) * gain_ref[...] + shift_ref[...]).astype(jnp.bfloat16)


def on_device(
    queries,
    level_zero,
    level_one,
    level_two,
    level_three,
    tile_lists,
    samples,
    logit_weight,
    logit_bias,
    output_weight,
    output_bias,
    norm_gain,
    norm_shift,
):
    level_blocks = (level_zero, level_one, level_two, level_three)
    row_count = lax.axis_size("row")
    col_count = lax.axis_size("col")
    peers = row_count * col_count
    tile_rows, tile_cols, level_count, per_block = tile_lists.shape
    blocks = tile_rows * tile_cols
    requests = blocks * per_block
    capacity = max(2, (requests + peers - 1) // peers)
    grid_cols = tile_cols * col_count
    channels = level_zero.shape[2]
    width_all = queries.shape[2]
    lanes = samples.shape[2]
    heads = lanes // (LEVELS * POINTS)
    head_dim = channels // heads
    sides = tuple(block.shape[0] // tile_rows for block in level_blocks)
    sizes = tuple(side * side for side in sides)
    pixels = sizes[0]
    tile_sets = [
        to_blocks(level_blocks[level], tile_rows, tile_cols, sides[level]) for level in range(level_count)
    ]

    wanted = tile_lists.reshape(blocks, level_count, per_block).transpose(1, 0, 2).reshape(level_count, requests)
    grid_row = wanted // grid_cols
    grid_col = wanted % grid_cols
    owner = grid_row // tile_rows * col_count + grid_col // tile_cols
    local = grid_row % tile_rows * tile_cols + grid_col % tile_cols
    order = jnp.arange(requests, dtype=jnp.int32)
    earlier = (owner[:, :, None] == owner[:, None, :]) & (order[None, None, :] < order[None, :, None])
    rank = jnp.sum(earlier.astype(jnp.int32), axis=2)
    device = jnp.arange(peers, dtype=jnp.int32)
    slot = jnp.arange(capacity, dtype=jnp.int32)
    hit = (owner[None, :, None, :] == device[:, None, None, None]) & (
        rank[None, :, None, :] == slot[None, None, :, None]
    )
    table = jnp.sum(jnp.where(hit, 1 + order * blocks + local[:, None, :], 0), axis=3) - 1
    table = table.reshape(peers, level_count * capacity)
    asked = jnp.where(table >= 0, table % blocks, -1)
    request = jnp.where(table >= 0, table // blocks, -1)
    received = lax.all_to_all(asked, ("row", "col"), split_axis=0, concat_axis=0, tiled=True)

    small = blocks * sizes[3]
    pack = capacity * sum(sizes[:3]) + small
    packs = pl.pallas_call(
        functools.partial(select_kernel, (peers, capacity, sizes)),
        out_shape=jax.ShapeDtypeStruct((peers, pack, channels), jnp.bfloat16),
        in_specs=[pl.BlockSpec(memory_space=SMEM)] + [pl.BlockSpec(memory_space=VMEM)] * 4,
        out_specs=pl.BlockSpec(memory_space=ANY),
        scratch_shapes=[pltpu.SemaphoreType.DMA],
        name="select",
    )(received, tile_sets[0], tile_sets[1], tile_sets[2], tile_sets[3].reshape(small, channels))
    fetched = lax.all_to_all(packs, ("row", "col"), split_axis=0, concat_axis=0, tiled=True)

    queries_blocked = to_blocks(queries, tile_rows, tile_cols, sides[0]).reshape(blocks * pixels, width_all)
    samples_turned = to_blocks(samples, tile_rows, tile_cols, sides[0]).reshape(blocks * pixels, lanes).T
    attend = pl.pallas_call(
        functools.partial(prep_kernel, heads),
        out_shape=jax.ShapeDtypeStruct((lanes, blocks * pixels), jnp.float32),
        grid=(blocks,),
        in_specs=[
            pl.BlockSpec((pixels, width_all), lambda i: (i, 0)),
            pl.BlockSpec((lanes, width_all), lambda i: (0, 0)),
            pl.BlockSpec((lanes, 1), lambda i: (0, 0)),
        ],
        out_specs=pl.BlockSpec((lanes, pixels), lambda i: (0, i)),
        name="prep",
    )(queries_blocked, logit_weight.T, logit_bias.reshape(lanes, 1))

    rowid = (owner[3] * small + local[3] * sizes[3])[:, None] + jnp.arange(sizes[3], dtype=jnp.int32)
    rowid = rowid.reshape(requests * sizes[3], 1)
    depth0 = 2 * per_block * sides[0]
    depth1 = 2 * per_block * sides[1]
    dims = (peers, capacity, sizes, sides, per_block, heads, head_dim, blocks)
    attn = pl.pallas_call(
        functools.partial(attend_kernel, dims),
        out_shape=jax.ShapeDtypeStruct((blocks * pixels, channels), jnp.bfloat16),
        grid=(blocks,),
        in_specs=[
            pl.BlockSpec(memory_space=SMEM),
            pl.BlockSpec(memory_space=ANY),
            pl.BlockSpec((lanes, pixels), lambda i: (0, i)),
            pl.BlockSpec((lanes, pixels), lambda i: (0, i)),
            pl.BlockSpec((requests * sizes[3], 1), lambda i: (0, 0)),
        ],
        out_specs=pl.BlockSpec((pixels, channels), lambda i: (i, 0)),
        scratch_shapes=[
            VMEM((blocks, per_block, sizes[0], channels), jnp.bfloat16),
            VMEM((blocks, per_block, sizes[1], channels), jnp.bfloat16),
            VMEM((blocks, per_block, sizes[2], channels), jnp.bfloat16),
            VMEM((peers, small, channels), jnp.bfloat16),
            VMEM((heads, (sides[0] // 2 + 1) * head_dim, depth0), jnp.bfloat16),
            VMEM((heads, (sides[1] // 2 + 1) * head_dim, depth1), jnp.bfloat16),
            VMEM((channels, per_block * sizes[2] + requests * sizes[3]), jnp.bfloat16),
            VMEM((POINTS, depth0, pixels), jnp.bfloat16),
            VMEM((POINTS, depth1, pixels), jnp.bfloat16),
            VMEM((per_block * sizes[2] + requests * sizes[3], pixels), jnp.bfloat16),
            VMEM((lanes, pixels), jnp.int32),
            VMEM((lanes, pixels), jnp.float32),
            VMEM((lanes, pixels), jnp.float32),
            pltpu.SemaphoreType.DMA((LEVELS, blocks)),
        ],
        name="attend",
    )(request, fetched, attend, samples_turned, rowid)

    own_head = lax.axis_index("head")
    other = lax.ppermute(attn, "head", [(0, 1), (1, 0)])
    updated = pl.pallas_call(
        functools.partial(norm_kernel, blocks),
        out_shape=jax.ShapeDtypeStruct((blocks * pixels, channels), jnp.bfloat16),
        grid=(blocks,),
        in_specs=[
            pl.BlockSpec(memory_space=SMEM),
            pl.BlockSpec((pixels, width_all), lambda i: (i, 0)),
            pl.BlockSpec((pixels, channels), lambda i: (i, 0)),
            pl.BlockSpec((pixels, channels), lambda i: (i, 0)),
            pl.BlockSpec((width_all, width_all), lambda i: (0, 0)),
            pl.BlockSpec((1, width_all), lambda i: (0, 0)),
            pl.BlockSpec((1, channels), lambda i: (0, 0)),
            pl.BlockSpec((1, channels), lambda i: (0, 0)),
        ],
        out_specs=pl.BlockSpec((pixels, channels), lambda i: (i, 0)),
        name="norm",
    )(
        own_head.reshape(1).astype(jnp.int32),
        queries_blocked,
        attn,
        other,
        output_weight,
        output_bias.reshape(1, width_all),
        norm_gain.reshape(1, channels),
        norm_shift.reshape(1, channels),
    )
    side = sides[0]
    updated = updated.reshape(tile_rows, tile_cols, side, side, channels).transpose(0, 2, 1, 3, 4)
    return updated.reshape(tile_rows * side, tile_cols * side, channels)


def solution(mesh):
    in_specs = (
        P("row", "col", None),
        P("row", "col", "head"),
        P("row", "col", "head"),
        P("row", "col", "head"),
        P("row", "col", "head"),
        P("row", "col", None, None),
        P("row", "col", "head"),
        P(None, "head"),
        P("head"),
        P(),
        P(),
        P("head"),
        P("head"),
    )
    out_specs = P("row", "col", "head")
    return jax.shard_map(
        on_device, mesh=mesh, in_specs=in_specs, out_specs=out_specs, check_vma=False
    )
```

time: 338 us -> 109 us (0.32)
  other arithmetic: 136 us -> 1.2 us
  local copies, waits for them, and re-layouts: 51.6 us -> 5.49 us
  matrix products: 40.2 us -> 0 us
  starting transfers between devices: 37.7 us -> 3.95 us
  Pallas kernels: 0 us -> 23.5 us
  blocking collectives: 2.41 us -> 15.5 us
  waiting for transfers between devices: 66.1 us -> 59.2 us
    dot_general x8 -> x0, other arithmetic: 95.6 us -> none  [block_output(): jnp.einsum('hqn,nhd->qhd', weights_px, tile_values.reshape(width_total, h...]
    dot_general x18 -> x0, matrix products: 40.2 us -> none  [the longest x16 37.6 us: block_output(): jnp.einsum('hqn,nhd->qhd', weights_px, tile_values.reshape(width_total, h...]
    all_to_all x8 -> x1, starting transfers between devices: 37.7 us -> 3.88 us  [on_device(): lax.all_to_all(packs, ('row', 'col'), split_axis=0, concat_axis=0, tiled=...]
    pallas_call x0 -> x4, Pallas kernels: none -> 23.5 us  [the longest x1 13.2 us: on_device(): pl.pallas_call(functools.partial(attend_kernel, dims), out_shape=jax.Shap...]
    dynamic_slice x40 -> x0, local copies, waits for them, and re-layouts: 16.3 us -> none  [on_device(): lax.map(block_output, (attend, packed, gathered[0], gathered[1], gathered...]
    all_to_all x0 -> x1, blocking collectives: none -> 15.5 us  [on_device(): lax.all_to_all(asked, ('row', 'col'), split_axis=0, concat_axis=0, tiled=...]
    transpose x80 -> x0, other arithmetic: 14.7 us -> none  [the longest x64 11.8 us: pixel_weights(): corner_weight = (attend[:, :, point_num] * weight_row[:, :, point_num] *...]
    gather x8 -> x0, local copies, waits for them, and re-layouts: 10.8 us -> none  [the longest x4 5.66 us: on_device(): chosen = jnp.take(flat_tiles, positions[level_num], axis=0)]
  transfers between devices with their start and end apart: 8 -> 2, of which waited for: 8 -> 2; matrix products, arithmetic and copies ran while one was open for 9% -> 3% of each run, Pallas kernels for 0% -> 3%
where the time goes in v1:
time: 109 us
  waiting for transfers between devices  59.2 us (54%)
  Pallas kernels  23.5 us (22%)
  blocking collectives  15.5 us (14%)
  local copies, waits for them, and re-layouts  5.49 us (5%)
  starting transfers between devices  3.95 us (4%)
  other arithmetic  1.2 us (1%)
    all_to_all x1, waiting for transfers between devices, on_device(): lax.all_to_all(packs, ('row', 'col'), split_axis=0, concat_axis=0, tiled=...  57.5 us
    all_to_all x1, blocking collectives, on_device(): lax.all_to_all(asked, ('row', 'col'), split_axis=0, concat_axis=0, tiled=...  15.5 us
    pallas_call x1, Pallas kernels, on_device(): pl.pallas_call(functools.partial(attend_kernel, dims), out_shape=jax.Shap...  13.2 us
    pallas_call x1, Pallas kernels, on_device(): pl.pallas_call(functools.partial(norm_kernel, blocks), out_shape=jax.Shap...  4.12 us
    all_to_all x1, starting transfers between devices, on_device(): lax.all_to_all(packs, ('row', 'col'), split_axis=0, concat_axis=0, tiled=...  3.88 us
    pallas_call x1, Pallas kernels, on_device(): pl.pallas_call(functools.partial(prep_kernel, heads), out_shape=jax.Shape...  3.53 us
    pallas_call x1, Pallas kernels, on_device(): pl.pallas_call(functools.partial(select_kernel, (peers, capacity, sizes))...  2.61 us
    unnamed x8, local copies, waits for them, and re-layouts  2.26 us
  transfers between devices with their start and end apart: 2, of which 2 were waited for; matrix products, arithmetic and copies ran while one was open for 3% of the time, Pallas kernels for 3%

profile of v1, /device:TPU:0, one launch (start us, length us, event | category | flops | bytes accessed | tf_op | source)
XLA Modules:
  0.0 108.9 jit_solution(7995322273200667853)
XLA Ops:
  0.0 0.7 copy.46
  0.7 0.1 reshape.361
  0.8 0.2 convert_reduce_fusion
  1.1 0.2 select_reduce_fusion
  1.3 0.1 copy.52
  1.4 15.5 %all_to_all.13 = s32[16,1,8]{2,1,0:T(1,128)} all-to-all(s32[16,1,8]{2,1,0:T(1,128)S(1)} %copy.52), channel_id=1, replica_groups=mesh['row'=4,'col'=4,'head'=2] {'row','col'}, dimensions={0} | all-to-all | bytes 1024 | tf_op jit(solution)/shard_map/all_to_all | solution.py:315
  16.9 2.6 %select.153 = bf16[16,688,128]{2,1,0:T(8,128)(2,1)} custom-call(s32[16,8]{1,0:T(8,128)} %bitcast.41, bf16[4,256,128]{2,1,0:T(8,128)(2,1)} %bitcast.37, bf16[4,64,128]{2,1,0:T(8,128)(2,1)} %bitcast.38, bf16[4,16,128]{2,1,0:T(8,128)(2,1)} %bitcast.43, bf16[16,128]{1,0:T(8,128)(2,1)} %bitcast.45), custom_call_target="tpu_custom_call" | custom-call | tf_op jit(solution)/shard_map/select/pallas_call | solution.py:319
  19.5 0.0 copy-start.3
  19.6 0.0 copy-start.1
  19.6 3.9 %all-to-all-start.1 = ((bf16[16,688,128]{2,1,0:T(8,128)(2,1)}), bf16[16,688,128]{2,1,0:T(8,128)(2,1)S(1)}, u32[]{:S(2)}, u32[]{:S(2)}) async-start(bf16[16,688,128]{2,1,0:T(8,128)(2,1)} %select.153), calls=%async_computation.1 | async-start | bytes 5636096 | tf_op jit(solution)/shard_map/all_to_all | solution.py:327
  23.5 0.1 copy.47
  23.5 0.1 iota_add_fusion
  23.6 0.7 add.173.rowid_ref
  24.3 0.0 copy-done.3
  24.3 0.7 copy.55.bias_ref
  25.0 0.0 copy-done.1
  25.0 0.9 copy.56
  25.9 3.5 %prep.1.attend_ref = f32[64,1024]{1,0:T(8,128)} custom-call(bf16[1024,256]{1,0:T(8,128)(2,1)} %bitcast.33, bf16[64,256]{1,0:T(8,128)(2,1)} %bitcast.42, f32[64,1]{1,0:T(8,128)} %copy.55.bias_ref), custom_call_target="tpu_custom_call" | custom-call | tf_op jit(solution)/shard_map/prep/pallas_call | solution.py:331
  29.5 0.6 fusion.1.request_ref
  30.1 57.5 %all-to-all-done.1.fetched_ref = bf16[16,688,128]{2,1,0:T(8,128)(2,1)S(1)} async-done(((bf16[16,688,128]{2,1,0:T(8,128)(2,1)}), bf16[16,688,128]{2,1,0:T(8,128)(2,1)S(1)}, u32[]{:S(2)}, u32[]{:S(2)}) %all-to-all-start.1) | async-done | bytes 2818080 | tf_op jit(solution)/shard_map/all_to_all | solution.py:327
  87.5 0.0 copy-start
  87.5 1.6 %copy-done = bf16[16,688,128]{2,1,0:T(8,128)(2,1)} copy-done((bf16[16,688,128]{2,1,0:T(8,128)(2,1)}, bf16[16,688,128]{2,1,0:T(8,128)(2,1)S(1)}, u32[]{:S(2)}) %copy-start) | copy-done | bytes 2818072
  89.1 13.2 %attend.1.own_ref = bf16[1024,128]{1,0:T(8,128)(2,1)} custom-call(s32[16,8]{1,0:T(8,128)} %fusion.1.request_ref, bf16[16,688,128]{2,1,0:T(8,128)(2,1)} %copy-done, f32[64,1024]{1,0:T(8,128)} %prep.1.attend_ref, s32[64,1024]{1,0:T(8,128)} %bitcast.35, s32[128,1]{1,0:T(8,128)} %add.173.rowid_ref), custom_call_target="tpu_custom_call" | custom-call | tf_op jit(solution)/shard_map/attend/pallas_call | solution.py:349
  102.3 0.1 collective-permute-start
  102.4 1.7 %collective-permute-done.other_ref = bf16[1024,128]{1,0:T(8,128)(2,1)S(1)} collective-permute-done((bf16[1024,128]{1,0:T(8,128)(2,1)}, bf16[1024,128]{1,0:T(8,128)(2,1)S(1)}, u32[]{:S(2)}, u32[]{:S(2)}) %collective-permute-start) | collective-permute-done | bytes 262176 | tf_op jit(solution)/shard_map/ppermute | solution.py:381
  104.1 0.0 copy-start.2
  104.1 0.7 copy-done.2
  104.8 4.1 %norm.1 = bf16[1024,128]{1,0:T(8,128)(2,1)} custom-call(s32[1]{0:T(128)} %bitcast.head_ref, bf16[1024,256]{1,0:T(8,128)(2,1)} %bitcast.34, bf16[1024,128]{1,0:T(8,128)(2,1)} %attend.1.own_ref, bf16[1024,128]{1,0:T(8,128)(2,1)} %copy-done.2, bf16[256,256]{1,0:T(8,128)(2,1)} %weight_ref.1, f32[1,256]{1,0:T(1,128)} %bitcast.46, f32[1,128]{1,0:T(1,128)} %bitcast.48, ...), custom_call_target="tpu_custom_call" | custom-call | tf_op jit(solution)/shard_map/norm/pallas_call | solution.py:382
  (8 shorter events, 0.1 us)
Async XLA Ops:
  19.5 4.8 %copy-start.3 = (f32[64]{0:T(128)S(1)}, f32[64]{0:T(128)}, u32[]{:S(2)}) copy-start(f32[64]{0:T(128)} %param.21) | copy-start | bytes 772
  19.6 5.5 %copy-start.1 = (s32[64,16,64]{2,1,0:T(8,128)S(1)}, s32[64,16,64]{2,1,0:T(8,128)}, u32[]{:S(2)}) copy-start(s32[64,16,64]{2,1,0:T(8,128)} %param.19) | copy-start | bytes 786436
  19.6 67.9 %all-to-all-start.1 = ((bf16[16,688,128]{2,1,0:T(8,128)(2,1)}), bf16[16,688,128]{2,1,0:T(8,128)(2,1)S(1)}, u32[]{:S(2)}, u32[]{:S(2)}) async-start(bf16[16,688,128]{2,1,0:T(8,128)(2,1)} %select.153), calls=%async_computation.1 | async-start | bytes 5636096 | tf_op jit(solution)/shard_map/all_to_all | solution.py:327
  87.5 1.6 %copy-start = (bf16[16,688,128]{2,1,0:T(8,128)(2,1)}, bf16[16,688,128]{2,1,0:T(8,128)(2,1)S(1)}, u32[]{:S(2)}) copy-start(bf16[16,688,128]{2,1,0:T(8,128)(2,1)S(1)} %all-to-all-done.1.fetched_ref) | copy-start | bytes 8454148
  102.3 1.8 %collective-permute-start = (bf16[1024,128]{1,0:T(8,128)(2,1)}, bf16[1024,128]{1,0:T(8,128)(2,1)S(1)}, u32[]{:S(2)}, u32[]{:S(2)}) collective-permute-start(bf16[1024,128]{1,0:T(8,128)(2,1)} %attend.1.own_ref), channel_id=1, source_target_pairs={{0,1},{1,0},{2,3},{3,2},{4,5},{5,4},{6,7},{7,6},{8,9},{9,8},{10,11... | collective-permute-start | bytes 786440 | tf_op jit(solution)/shard_map/ppermute | solution.py:381
  104.1 0.7 copy-start.2

commit v2 on v1

--- a/solution.py
+++ b/solution.py
@@ -1,6 +1,7 @@
 import functools
 import jax
 import jax.numpy as jnp
+import numpy as np
 from jax import lax
 from jax.experimental import pallas as pl
 from jax.experimental.pallas import tpu as pltpu
@@ -11,6 +12,8 @@
 ANY = pl.ANY
 SMEM = pltpu.SMEM
 VMEM = pltpu.VMEM
+SELECT_VMEM = 8 * 1024 * 1024
+ATTEND_VMEM = 24 * 1024 * 1024
 
 
 def to_blocks(source, tile_rows, tile_cols, tile_side):
@@ -67,71 +70,156 @@
     lax.fori_loop(0, peers, finish, 0)
 
 
-def attend_kernel(
-    dims,
-    request_ref,
-    fetched_ref,
-    attend_ref,
-    sample_ref,
-    rowid_ref,
-    out_ref,
-    tile0,
-    tile1,
-    tile2,
-    tile3,
-    left0,
-    left1,
-    left2,
-    weight0,
-    weight1,
-    weight2,
-    code_ref,
-    row_ref,
-    col_ref,
-    sem,
-):
-    peers, capacity, sizes, sides, per_block, heads, head_dim, blocks = dims
+def relay_select_kernel(dims, slot, plan_ref, *refs):
+    partners, candidates, capacity, sizes, blocks = dims
+    ids = refs[:partners]
+    sources = refs[partners : partners + candidates]
+    outs = refs[partners + candidates :]
+    column = plan_ref[slot, 0]
+    for number, source in enumerate(sources):
+
+        @pl.when(plan_ref[slot, 1] == number)
+        def _(source=source):
+            for partner in range(partners):
+                base = 0
+                start = 0
+                for level in range(LEVELS - 1):
+                    size = sizes[level]
+                    for rank in range(capacity):
+                        index = jnp.maximum(ids[partner][column, level * capacity + rank], 0)
+                        outs[partner][base : base + size, :] = source[
+                            pl.ds(pl.multiple_of(start + index * size, size), size), :
+                        ]
+                        base += size
+                    start += blocks * size
+                small = blocks * sizes[3]
+                outs[partner][base : base + small, :] = source[start : start + small, :]
+
+
+def gather_direct(dims, request_ref, fetched_ref, tiles, tile3, sem):
+    peers, capacity, sizes, _, per_block, _, _, _ = dims
+    small = tile3.shape[1]
+    base3 = capacity * sum(sizes[:3])
+    pltpu.make_async_copy(fetched_ref.at[:, base3 : base3 + small, :], tile3, sem.at[LEVELS - 1, 0]).start()
+
+    def start(peer, carry):
+        base = 0
+        for level in range(LEVELS - 1):
+            size = sizes[level]
+            for rank in range(capacity):
+                fetch_one(
+                    request_ref[peer, level * capacity + rank],
+                    fetched_ref.at[peer, base : base + size, :],
+                    tiles[level],
+                    per_block,
+                    sem,
+                    level,
+                )
+                base += size
+        return carry
+
+    lax.fori_loop(0, peers, start, 0)
+
+
+def fetch_one(request, source, tile, per_block, sem, level):
+    @pl.when(request >= 0)
+    def _():
+        here = request // per_block
+        pltpu.make_async_copy(source, tile.at[here, request % per_block], sem.at[level, here]).start()
+
+
+def gather_relay(dims, relay, request_ref, plan_ref, asked_ref, blocks_refs, packs_refs, tiles, tile3, sem):
+    _, capacity, sizes, _, per_block, _, _, blocks = dims
+    rows, columns, partner_of = relay
+    small = tile3.shape[1]
+    my_row = plan_ref[columns, 0]
+    my_column = plan_ref[columns, 1]
+
+    def take_small(owner, source):
+        pltpu.make_async_copy(source, tile3.at[owner], sem.at[LEVELS - 1, 0]).start()
+
+    for number, source in enumerate(blocks_refs):
+        shift = (number + 1) // 2 * (-1 if number % 2 else 1)
+        column = my_column + shift
+
+        @pl.when((column >= 0) & (column < columns))
+        def _(source=source, column=column):
+            owner = my_row * columns + column
+            start = 0
+            for level in range(LEVELS - 1):
+                size = sizes[level]
+                for rank in range(capacity):
+                    index = jnp.maximum(asked_ref[owner, level * capacity + rank], 0)
+                    fetch_one(
+                        request_ref[owner, level * capacity + rank],
+                        source.at[pl.ds(pl.multiple_of(start + index * size, size), size), :],
+                        tiles[level],
+                        per_block,
+                        sem,
+                        level,
+                    )
+                start += blocks * size
+            take_small(owner, source.at[start : start + small, :])
+
+    for number, source in enumerate(packs_refs):
+        slot, partner = divmod(number, rows - 1)
+        owner = partner_of(my_row, partner + 1) * columns + plan_ref[slot, 0]
+        base = 0
+        for level in range(LEVELS - 1):
+            size = sizes[level]
+            for rank in range(capacity):
+                fetch_one(
+                    request_ref[owner, level * capacity + rank],
+                    source.at[base : base + size, :],
+                    tiles[level],
+                    per_block,
+                    sem,
+                    level,
+                )
+                base += size
+        take_small(owner, source.at[base : base + small, :])
+
+
+def attend_kernel(dims, gather, count, *refs):
+    sources = refs[:count]
+    (
+        attend_ref,
+        sample_ref,
+        rowid_ref,
+        out_ref,
+        tile0,
+        tile1,
+        tile2,
+        tile3,
+        left0,
+        left1,
+        left2,
+        weight0,
+        weight1,
+        weight2,
+        code_ref,
+        row_ref,
+        col_ref,
+        sem,
+    ) = refs[count:]
+    peers, _, sizes, sides, per_block, heads, head_dim, _ = dims
     block = pl.program_id(0)
     pixels = out_ref.shape[0]
     channels = heads * head_dim
     tiles = (tile0, tile1, tile2)
     small = tile3.shape[1]
-    base3 = capacity * sum(sizes[:3])
+    base2 = per_block * sizes[2]
 
     @pl.when(block == 0)
     def _():
-        def start(peer, carry):
-            base = 0
-            for level in range(LEVELS - 1):
-                size = sizes[level]
-                for slot in range(capacity):
-                    request = request_ref[peer, level * capacity + slot]
-
-                    @pl.when(request >= 0)
-                    def _(level=level, base=base, size=size, request=request):
-                        here = request // per_block
-                        pltpu.make_async_copy(
-                            fetched_ref.at[peer, base : base + size, :],
-                            tiles[level].at[here, request % per_block],
-                            sem.at[level, here],
-                        ).start()
-
-                    base += size
-            return carry
-
-        pltpu.make_async_copy(
-            fetched_ref.at[:, base3 : base3 + small, :], tile3, sem.at[LEVELS - 1, 0]
-        ).start()
-        lax.fori_loop(0, peers, start, 0)
+        gather(sources, tiles, tile3, sem)
         left0[...] = jnp.zeros_like(left0)
         weight2[...] = jnp.zeros_like(weight2)
-        pltpu.make_async_copy(
-            fetched_ref.at[:, base3 : base3 + small, :], tile3, sem.at[LEVELS - 1, 0]
-        ).wait()
+        pltpu.make_async_copy(tile3, tile3, sem.at[LEVELS - 1, 0]).wait()
         flat = tile3[...].reshape(peers * small, channels)
         chosen = (rowid_ref[...] == iota((rowid_ref.shape[0], peers * small), 1)).astype(jnp.bfloat16)
         picked = jnp.dot(chosen, flat, preferred_element_type=jnp.float32)
-        left2[:, 128:] = picked.T.astype(jnp.bfloat16)
+        left2[:, base2:] = picked.T.astype(jnp.bfloat16)
 
     packed = sample_ref[...]
     level_of = iota(packed.shape, 0) // POINTS % LEVELS
@@ -174,8 +262,8 @@
             left1[head, offset * head_dim : (offset + 1) * head_dim, :] = turned[
                 head * head_dim : (head + 1) * head_dim, :
             ]
-    left2[:, :128] = tile2[block].reshape(per_block * sizes[2], channels).T
-    weight2[128:, :] = jnp.zeros_like(weight2[128:, :])
+    left2[:, :base2] = tile2[block].reshape(per_block * sizes[2], channels).T
+    weight2[base2:, :] = jnp.zeros_like(weight2[base2:, :])
 
     for head in range(heads):
         total = jnp.zeros((head_dim, pixels), jnp.float32)
@@ -236,16 +324,14 @@
                 * hat(col_ref[line, :], (place % side).astype(jnp.float32))
             )
             mixed = mixed + jnp.where(code_ref[line, :] == place // size, value, 0.0)
-        weight2[pl.ds(pl.multiple_of(128 + block * deep, deep), deep), :] = mixed.astype(jnp.bfloat16)
+        weight2[pl.ds(pl.multiple_of(base2 + block * deep, deep), deep), :] = mixed.astype(jnp.bfloat16)
         total = total + jnp.dot(
             left2[head * head_dim : (head + 1) * head_dim, :], weight2[...], preferred_element_type=jnp.float32
         )
         out_ref[:, head * head_dim : (head + 1) * head_dim] = total.T.astype(jnp.bfloat16)
 
 
-def norm_kernel(
-    count, head_ref, query_ref, own_ref, other_ref, weight_ref, bias_ref, gain_ref, shift_ref, out_ref
-):
+def norm_kernel(head_ref, query_ref, own_ref, other_ref, weight_ref, bias_ref, gain_ref, shift_ref, out_ref):
     own_head = head_ref[0]
     channels = out_ref.shape[1]
     own_rows = weight_ref[pl.ds(pl.multiple_of(own_head * channels, channels), channels), :]
@@ -257,6 +343,103 @@
     variance = jnp.mean(centered * centered, axis=1, keepdims=True)
     own = jnp.where(own_head == 0, centered[:, :channels], centered[:, channels:])
     out_ref[...] = (own * lax.rsqrt(variance + 1e-05) * gain_ref[...] + shift_ref[...]).astype(jnp.bfloat16)
+
+
+def column_order(column, columns):
+    found = []
+    for step in range(1, columns):
+        found += [(step, side) for side in (-1, 1) if 0 <= column + side * step < columns]
+    return found
+
+
+def relay_tiles(dims, row_count, col_count, pack, flat_sets, asked, request):
+    _, capacity, sizes, _, _, heads, head_dim, blocks = dims
+    channels = heads * head_dim
+    my_row = lax.axis_index("row")
+    my_column = lax.axis_index("col")
+    power = row_count & (row_count - 1) == 0
+
+    def partner_of(row, number):
+        return row ^ number if power else (row + number) % row_count
+
+    def source_of(row, number):
+        return row ^ number if power else (row + row_count - number) % row_count
+
+    block = jnp.concatenate(flat_sets, axis=0)
+    arrived = {}
+
+    def hop(step):
+        for side in (-1, 1):
+            pairs = []
+            for column in range(col_count):
+                if 0 <= column + side * step < col_count:
+                    pairs.append((column + side, column))
+            held = arrived.get((step - 1, side), block)
+            arrived[(step, side)] = lax.ppermute(held, "col", pairs)
+
+    hop(1)
+    grid = asked.reshape(row_count, col_count, asked.shape[1])
+    ids = []
+    for number in range(1, row_count):
+        mine = lax.dynamic_index_in_dim(grid, partner_of(my_row, number), 0, keepdims=False)
+        ids.append(
+            lax.ppermute(mine, "row", [(row, partner_of(row, number)) for row in range(row_count)])
+        )
+
+    orders = [[(0, 1)] + column_order(column, col_count) for column in range(col_count)]
+    candidates = [sorted({order[slot] for order in orders}) for slot in range(col_count)]
+    plan = np.zeros((col_count, col_count, 2), np.int32)
+    for column in range(col_count):
+        for slot in range(col_count):
+            step, side = orders[column][slot]
+            plan[column, slot] = (column + side * step, candidates[slot].index(orders[column][slot]))
+    plan = lax.dynamic_index_in_dim(jnp.asarray(plan), my_column, 0, keepdims=False)
+    place = jnp.stack([my_row, my_column]).astype(jnp.int32)
+    plan = jnp.concatenate([plan, place[None, :]], axis=0)
+
+    packs = []
+    for slot in range(col_count):
+        if slot > 1:
+            hop(slot)
+        held = [block if slot == 0 else arrived[candidate] for candidate in candidates[slot]]
+        sent = pl.pallas_call(
+            functools.partial(
+                relay_select_kernel, (row_count - 1, len(held), capacity, sizes, blocks), slot
+            ),
+            out_shape=[jax.ShapeDtypeStruct((pack, channels), jnp.bfloat16)] * (row_count - 1),
+            in_specs=[pl.BlockSpec(memory_space=SMEM)] * row_count
+            + [pl.BlockSpec(memory_space=VMEM)] * len(held),
+            out_specs=[pl.BlockSpec(memory_space=VMEM)] * (row_count - 1),
+            compiler_params=pltpu.CompilerParams(vmem_limit_bytes=SELECT_VMEM),
+        )(plan, *ids, *held)
+        for number in range(1, row_count):
+            packs.append(
+                lax.ppermute(
+                    sent[number - 1], "row", [(row, source_of(row, number)) for row in range(row_count)]
+                )
+            )
+
+    near = [block]
+    for step in range(1, col_count):
+        near += [arrived[(step, -1)], arrived[(step, 1)]]
+    sources = (request, plan, asked, *near, *packs)
+    spaces = (SMEM, SMEM, SMEM) + (ANY,) * (len(near) + len(packs))
+
+    def gather(refs, tiles, tile3, sem):
+        gather_relay(
+            dims,
+            (row_count, col_count, partner_of),
+            refs[0],
+            refs[1],
+            refs[2],
+            refs[3 : 3 + len(near)],
+            refs[3 + len(near) :],
+            tiles,
+            tile3,
+            sem,
+        )
+
+    return gather, sources, spaces
 
 
 def on_device(
@@ -312,19 +495,30 @@
     table = table.reshape(peers, level_count * capacity)
     asked = jnp.where(table >= 0, table % blocks, -1)
     request = jnp.where(table >= 0, table // blocks, -1)
-    received = lax.all_to_all(asked, ("row", "col"), split_axis=0, concat_axis=0, tiled=True)
-
     small = blocks * sizes[3]
     pack = capacity * sum(sizes[:3]) + small
-    packs = pl.pallas_call(
-        functools.partial(select_kernel, (peers, capacity, sizes)),
-        out_shape=jax.ShapeDtypeStruct((peers, pack, channels), jnp.bfloat16),
-        in_specs=[pl.BlockSpec(memory_space=SMEM)] + [pl.BlockSpec(memory_space=VMEM)] * 4,
-        out_specs=pl.BlockSpec(memory_space=ANY),
-        scratch_shapes=[pltpu.SemaphoreType.DMA],
-        name="select",
-    )(received, tile_sets[0], tile_sets[1], tile_sets[2], tile_sets[3].reshape(small, channels))
-    fetched = lax.all_to_all(packs, ("row", "col"), split_axis=0, concat_axis=0, tiled=True)
+    dims = (peers, capacity, sizes, sides, per_block, heads, head_dim, blocks)
+    flat_sets = [
+        tile_sets[level].reshape(blocks * sizes[level], channels) for level in range(level_count)
+    ]
+    if peers * capacity <= requests and col_count > 1:
+        gather, sources, spaces = relay_tiles(dims, row_count, col_count, pack, flat_sets, asked, request)
+    else:
+        received = lax.all_to_all(asked, ("row", "col"), split_axis=0, concat_axis=0, tiled=True)
+        packs = pl.pallas_call(
+            functools.partial(select_kernel, (peers, capacity, sizes)),
+            out_shape=jax.ShapeDtypeStruct((peers, pack, channels), jnp.bfloat16),
+            in_specs=[pl.BlockSpec(memory_space=SMEM)] + [pl.BlockSpec(memory_space=VMEM)] * 4,
+            out_specs=pl.BlockSpec(memory_space=ANY),
+            scratch_shapes=[pltpu.SemaphoreType.DMA],
+            name="select",
+        )(received, tile_sets[0], tile_sets[1], tile_sets[2], flat_sets[3])
+        fetched = lax.all_to_all(packs, ("row", "col"), split_axis=0, concat_axis=0, tiled=True)
+        sources = (request, fetched)
+        spaces = (SMEM, ANY)
+
+        def gather(refs, tiles, tile3, sem):
+            gather_direct(dims, refs[0], refs[1], tiles, tile3, sem)
 
     queries_blocked = to_blocks(queries, tile_rows, tile_cols, sides[0]).reshape(blocks * pixels, width_all)
     samples_turned = to_blocks(samples, tile_rows, tile_cols, sides[0]).reshape(blocks * pixels, lanes).T
@@ -338,6 +532,7 @@
             pl.BlockSpec((lanes, 1), lambda i: (0, 0)),
         ],
         out_specs=pl.BlockSpec((lanes, pixels), lambda i: (0, i)),
+        compiler_params=pltpu.CompilerParams(vmem_limit_bytes=SELECT_VMEM),
         name="prep",
     )(queries_blocked, logit_weight.T, logit_bias.reshape(lanes, 1))
 
@@ -345,14 +540,12 @@
     rowid = rowid.reshape(requests * sizes[3], 1)
     depth0 = 2 * per_block * sides[0]
     depth1 = 2 * per_block * sides[1]
-    dims = (peers, capacity, sizes, sides, per_block, heads, head_dim, blocks)
     attn = pl.pallas_call(
-        functools.partial(attend_kernel, dims),
+        functools.partial(attend_kernel, dims, gather, len(sources)),
         out_shape=jax.ShapeDtypeStruct((blocks * pixels, channels), jnp.bfloat16),
         grid=(blocks,),
-        in_specs=[
-            pl.BlockSpec(memory_space=SMEM),
-            pl.BlockSpec(memory_space=ANY),
+        in_specs=[pl.BlockSpec(memory_space=space) for space in spaces]
+        + [
             pl.BlockSpec((lanes, pixels), lambda i: (0, i)),
             pl.BlockSpec((lanes, pixels), lambda i: (0, i)),
             pl.BlockSpec((requests * sizes[3], 1), lambda i: (0, 0)),
@@ -374,13 +567,14 @@
             VMEM((lanes, pixels), jnp.float32),
             pltpu.SemaphoreType.DMA((LEVELS, blocks)),
         ],
+        compiler_params=pltpu.CompilerParams(vmem_limit_bytes=ATTEND_VMEM),
         name="attend",
-    )(request, fetched, attend, samples_turned, rowid)
+    )(*sources, attend, samples_turned, rowid)
 
     own_head = lax.axis_index("head")
     other = lax.ppermute(attn, "head", [(0, 1), (1, 0)])
     updated = pl.pallas_call(
-        functools.partial(norm_kernel, blocks),
+        norm_kernel,
         out_shape=jax.ShapeDtypeStruct((blocks * pixels, channels), jnp.bfloat16),
         grid=(blocks,),
         in_specs=[
@@ -394,6 +588,7 @@
             pl.BlockSpec((1, channels), lambda i: (0, 0)),
         ],
         out_specs=pl.BlockSpec((pixels, channels), lambda i: (i, 0)),
+        compiler_params=pltpu.CompilerParams(vmem_limit_bytes=SELECT_VMEM),
         name="norm",
     )(
         own_head.reshape(1).astype(jnp.int32),
@@ -427,6 +622,4 @@
         P("head"),
     )
     out_specs = P("row", "col", "head")
-    return jax.shard_map(
-        on_device, mesh=mesh, in_specs=in_specs, out_specs=out_specs, check_vma=False
-    )
+    return jax.shard_map(on_device, mesh=mesh, in_specs=in_specs, out_specs=out_specs, check_vma=False)

time: 109 us -> 88.9 us (0.82)
  the two profiles are of different devices: /device:TPU:0 before, /device:TPU:17 now
where the time goes in v2:
time: 88.9 us; the launch traced here: 88.5 us
  starting transfers between devices  31.2 us (35%)
  Pallas kernels  23.9 us (27%)
  waiting for transfers between devices  20.7 us (23%)
  local copies, waits for them, and re-layouts  10.5 us (12%)
  other arithmetic  1.74 us (2%)
    pallas_call x1, Pallas kernels, on_device(): pl.pallas_call(functools.partial(attend_kernel, dims, gather, len(sources...  15.3 us
    ppermute x6, starting transfers between devices, hop(): arrived[step, side] = lax.ppermute(held, 'col', pairs)  13.9 us
    ppermute x12, waiting for transfers between devices, relay_tiles(): lax.ppermute(sent[number - 1], 'row', [(row, source_of(row, number)) for...  12.1 us
    ppermute x12, starting transfers between devices, relay_tiles(): lax.ppermute(sent[number - 1], 'row', [(row, source_of(row, number)) for...  10.6 us
    unnamed x38, local copies, waits for them, and re-layouts  7.87 us
    ppermute x6, waiting for transfers between devices, hop(): arrived[step, side] = lax.ppermute(held, 'col', pairs)  7.44 us
    pallas_call x4, Pallas kernels, relay_tiles(): pl.pallas_call(functools.partial(relay_select_kernel, (row_count - 1, len...  5.19 us
    ppermute x1, starting transfers between devices, on_device(): other = lax.ppermute(attn, 'head', [(0, 1), (1, 0)])  4.14 us
  transfers between devices with their start and end apart: 22, of which 7 were waited for; matrix products, arithmetic and copies ran while one was open for 4% of the time, Pallas kernels for 7%

profile of v2, /device:TPU:17, one launch (start us, length us, event | category | flops | bytes accessed | tf_op | source)
XLA Modules:
  0.0 88.5 jit_solution(17812023381890869228)
XLA Ops:
  0.0 0.7 copy-done.17
  0.7 1.0 %pad_maximum_fusion.refs_3_ = bf16[1360,128]{1,0:T(8,128)(2,1)S(1)} fusion(bf16[16,128]{1,0:T(8,128)(2,1)S(1)} %bitcast.44, bf16[64,128]{1,0:T(8,128)(2,1)} %bitcast.42, bf16[256,128]{1,0:T(8,128)(2,1)} %bitcast.40, bf16[1024,128]{1,0:T(8,128)(2,1)} %bitcast.39), kind=kLoop, calls=%fused_computation | loop fusion | flops 1392640 | bytes 696320 | tf_op jit(solution)/shard_map/concatenate | solution.py:368
  1.7 2.1 %collective-permute-start.1 = (bf16[1360,128]{1,0:T(8,128)(2,1)S(1)}, bf16[1360,128]{1,0:T(8,128)(2,1)S(1)}, u32[]{:S(2)}, u32[]{:S(2)}) collective-permute-start(bf16[1360,128]{1,0:T(8,128)(2,1)S(1)} %pad_maximum_fusion.refs_3_), channel_id=1, source_target_pairs={{2,0},{4,2},{6,4},{3,1},{5,3},{7,5},{10,8},{12,10},{14,12},{11,9},... | collective-permute-start | bytes 1044488 | tf_op jit(solution)/shard_map/ppermute | solution.py:378
  3.8 3.2 %collective-permute-start = (bf16[1360,128]{1,0:T(8,128)(2,1)S(1)}, bf16[1360,128]{1,0:T(8,128)(2,1)S(1)}, u32[]{:S(2)}, u32[]{:S(2)}) collective-permute-start(bf16[1360,128]{1,0:T(8,128)(2,1)S(1)} %pad_maximum_fusion.refs_3_), channel_id=1, source_target_pairs={{0,2},{2,4},{4,6},{1,3},{3,5},{5,7},{8,10},{10,12},{12,14},{9,11},... | collective-permute-start | bytes 1044488 | tf_op jit(solution)/shard_map/ppermute | solution.py:378
  7.1 0.1 reshape.312
  7.2 0.2 convert_reduce_fusion
  7.5 0.2 select_reduce_fusion
  7.7 0.1 sub.31
  7.8 4.9 %collective-permute-done.1.refs_4_.refs_3_.refs_5_ = bf16[1360,128]{1,0:T(8,128)(2,1)S(1)} collective-permute-done((bf16[1360,128]{1,0:T(8,128)(2,1)S(1)}, bf16[1360,128]{1,0:T(8,128)(2,1)S(1)}, u32[]{:S(2)}, u32[]{:S(2)}) %collective-permute-start.1) | collective-permute-done | bytes 348192 | tf_op jit(solution)/shard_map/ppermute | solution.py:378
  12.7 2.1 %collective-permute-start.3 = (bf16[1360,128]{1,0:T(8,128)(2,1)S(1)}, bf16[1360,128]{1,0:T(8,128)(2,1)S(1)}, u32[]{:S(2)}, u32[]{:S(2)}) collective-permute-start(bf16[1360,128]{1,0:T(8,128)(2,1)S(1)} %collective-permute-done.1.refs_4_.refs_3_.refs_5_), channel_id=1, source_target_pairs={{2,0},{4,2},{3,1},{5,3},{10,8},{12,10},{11,9},{13,11},{18,16},{20,... | collective-permute-start | bytes 1044488 | tf_op jit(solution)/shard_map/ppermute | solution.py:378
  14.8 2.9 %collective-permute-start.2 = (bf16[1360,128]{1,0:T(8,128)(2,1)S(1)}, bf16[1360,128]{1,0:T(8,128)(2,1)S(1)}, u32[]{:S(2)}, u32[]{:S(2)}) collective-permute-start(bf16[1360,128]{1,0:T(8,128)(2,1)S(1)} %collective-permute-done.refs_3_.refs_4_), channel_id=1, source_target_pairs={{2,4},{4,6},{3,5},{5,7},{10,12},{12,14},{11,13},{13,15},{18,20},{2... | collective-permute-start | bytes 1044488 | tf_op jit(solution)/shard_map/ppermute | solution.py:378
  17.7 0.1 copy.66
  17.8 1.2 %collective-permute-start.6 = (s32[4,8]{1,0:T(4,128)S(1)}, s32[4,8]{1,0:T(4,128)S(1)}, u32[]{:S(2)}, u32[]{:S(2)}) collective-permute-start(s32[4,8]{1,0:T(4,128)S(1)} %bitcast.45), channel_id=1, source_target_pairs={{0,8},{8,0},{16,24},{24,16},{1,9},{9,1},{17,25},{25,17},{2,10},{10... | collective-permute-start | bytes 392 | tf_op jit(solution)/shard_map/ppermute | solution.py:386
  19.0 0.1 copy.67
  19.1 1.2 %collective-permute-start.7 = (s32[4,8]{1,0:T(4,128)S(1)}, s32[4,8]{1,0:T(4,128)S(1)}, u32[]{:S(2)}, u32[]{:S(2)}) collective-permute-start(s32[4,8]{1,0:T(4,128)S(1)} %bitcast.46), channel_id=1, source_target_pairs={{0,16},{8,24},{16,0},{24,8},{1,17},{9,25},{17,1},{25,9},{2,18},{10... | collective-permute-start | bytes 392 | tf_op jit(solution)/shard_map/ppermute | solution.py:386
  20.4 0.1 copy.68
  20.4 0.2 collective-permute-start.8
  20.6 0.7 dynamic-slice_bitcast_fusion
  21.3 0.7 collective-permute-start.5
  22.0 2.6 %collective-permute-done.2.refs_4_.refs_3_.refs_6_ = bf16[1360,128]{1,0:T(8,128)(2,1)S(1)} collective-permute-done((bf16[1360,128]{1,0:T(8,128)(2,1)S(1)}, bf16[1360,128]{1,0:T(8,128)(2,1)S(1)}, u32[]{:S(2)}, u32[]{:S(2)}) %collective-permute-start.2) | collective-permute-done | bytes 348192 | tf_op jit(solution)/shard_map/ppermute | solution.py:378
  24.6 2.9 %collective-permute-start.4 = (bf16[1360,128]{1,0:T(8,128)(2,1)S(1)}, bf16[1360,128]{1,0:T(8,128)(2,1)S(1)}, u32[]{:S(2)}, u32[]{:S(2)}) collective-permute-start(bf16[1360,128]{1,0:T(8,128)(2,1)S(1)} %collective-permute-done.2.refs_4_.refs_3_.refs_6_), channel_id=1, source_target_pairs={{4,6},{5,7},{12,14},{13,15},{20,22},{21,23},{28,30},{29,31}} | collective-permute-start | bytes 1044488 | tf_op jit(solution)/shard_map/ppermute | solution.py:378
  27.5 0.1 add_bitcast_fusion
  27.6 0.1 copy.65
  27.7 0.1 copy.60
  27.7 0.7 copy-done.18
  28.4 0.1 copy.69.bias_ref
  28.5 1.4 %shard_map.136 = (bf16[688,128]{1,0:T(8,128)(2,1)S(1)}, bf16[688,128]{1,0:T(8,128)(2,1)S(1)}, bf16[688,128]{1,0:T(8,128)(2,1)}) custom-call(s32[5,2]{1,0:T(8,128)S(1)} %pad_add_fusion.plan_ref.refs_1_, s32[4,8]{1,0:T(4,128)S(1)} %collective-permute-done.6.refs_0_, s32[4,8]{1,0:T(4,128)S(1)} %collective-permute-done.7.refs_1_, ...), custom_call_target="tpu_custom_call" | custom-call | tf_op jit(solution)/shard_map/pallas_call | solution.py:405
  29.9 1.2 %collective-permute-start.9 = (bf16[688,128]{1,0:T(8,128)(2,1)S(1)}, bf16[688,128]{1,0:T(8,128)(2,1)S(1)}, u32[]{:S(2)}, u32[]{:S(2)}) collective-permute-start(bf16[688,128]{1,0:T(8,128)(2,1)S(1)} %get-tuple-element.17), channel_id=1, source_target_pairs={{0,8},{8,0},{16,24},{24,16},{1,9},{9,1},{17,25},{25,17},{2,10},{10... | collective-permute-start | bytes 528392 | tf_op jit(solution)/shard_map/ppermute | solution.py:417
  31.1 1.2 %collective-permute-start.10 = (bf16[688,128]{1,0:T(8,128)(2,1)S(1)}, bf16[688,128]{1,0:T(8,128)(2,1)S(1)}, u32[]{:S(2)}, u32[]{:S(2)}) collective-permute-start(bf16[688,128]{1,0:T(8,128)(2,1)S(1)} %get-tuple-element.18), channel_id=1, source_target_pairs={{0,16},{8,24},{16,0},{24,8},{1,17},{9,25},{17,1},{25,9},{2,18},{10... | collective-permute-start | bytes 528392 | tf_op jit(solution)/shard_map/ppermute | solution.py:417
  32.4 0.2 collective-permute-start.11
  32.6 1.6 %shard_map.137 = (bf16[688,128]{1,0:T(8,128)(2,1)}, bf16[688,128]{1,0:T(8,128)(2,1)}, bf16[688,128]{1,0:T(8,128)(2,1)}) custom-call(s32[5,2]{1,0:T(8,128)S(1)} %pad_add_fusion.plan_ref.refs_1_, s32[4,8]{1,0:T(4,128)S(1)} %collective-permute-done.6.refs_0_, s32[4,8]{1,0:T(4,128)S(1)} %collective-permute-done.7.refs_1_, ...), custom_call_target="tpu_custom_call" | custom-call | tf_op jit(solution)/shard_map/pallas_call | solution.py:405
  34.2 1.4 %shard_map.138 = (bf16[688,128]{1,0:T(8,128)(2,1)}, bf16[688,128]{1,0:T(8,128)(2,1)S(1)}, bf16[688,128]{1,0:T(8,128)(2,1)S(1)}) custom-call(s32[5,2]{1,0:T(8,128)S(1)} %pad_add_fusion.plan_ref.refs_1_, s32[4,8]{1,0:T(4,128)S(1)} %collective-permute-done.6.refs_0_, s32[4,8]{1,0:T(4,128)S(1)} %collective-permute-done.7.refs_1_, ...), custom_call_target="tpu_custom_call" | custom-call | tf_op jit(solution)/shard_map/pallas_call | solution.py:405
  35.6 0.7 copy-done.12
  36.2 0.7 copy-done.14
  36.9 0.7 copy-done.1
  37.6 1.2 %collective-permute-start.12 = (bf16[688,128]{1,0:T(8,128)(2,1)}, bf16[688,128]{1,0:T(8,128)(2,1)}, u32[]{:S(2)}, u32[]{:S(2)}) collective-permute-start(bf16[688,128]{1,0:T(8,128)(2,1)} %get-tuple-element.20), channel_id=1, source_target_pairs={{0,8},{8,0},{16,24},{24,16},{1,9},{9,1},{17,25},{25,17},{2,10},{10... | collective-permute-start | bytes 528392 | tf_op jit(solution)/shard_map/ppermute | solution.py:417
  38.8 0.7 copy-done.3
  39.5 1.2 %collective-permute-start.13 = (bf16[688,128]{1,0:T(8,128)(2,1)}, bf16[688,128]{1,0:T(8,128)(2,1)}, u32[]{:S(2)}, u32[]{:S(2)}) collective-permute-start(bf16[688,128]{1,0:T(8,128)(2,1)} %get-tuple-element.21), channel_id=1, source_target_pairs={{0,16},{8,24},{16,0},{24,8},{1,17},{9,25},{17,1},{25,9},{2,18},{10... | collective-permute-start | bytes 528392 | tf_op jit(solution)/shard_map/ppermute | solution.py:417
  40.7 0.2 collective-permute-start.14
  40.9 1.2 %collective-permute-start.15 = (bf16[688,128]{1,0:T(8,128)(2,1)}, bf16[688,128]{1,0:T(8,128)(2,1)}, u32[]{:S(2)}, u32[]{:S(2)}) collective-permute-start(bf16[688,128]{1,0:T(8,128)(2,1)} %get-tuple-element.23), channel_id=1, source_target_pairs={{0,8},{8,0},{16,24},{24,16},{1,9},{9,1},{17,25},{25,17},{2,10},{10... | collective-permute-start | bytes 528392 | tf_op jit(solution)/shard_map/ppermute | solution.py:417
  42.1 0.1 iota_add_fusion
  42.2 0.1 add.182.refs_24_
  42.3 1.2 %copy.70 = s32[1024,64]{0,1:T(8,128)S(1)} copy(s32[1024,64]{1,0:T(8,128)} %bitcast.38) | data formatting | bytes 524288 | tf_op jit(solution)/shard_map/reshape;reshape;transpose;reshape | solution.py:524
  43.6 1.0 %prep.1.refs_22_ = f32[64,1024]{1,0:T(8,128)S(1)} custom-call(bf16[1024,256]{1,0:T(8,128)(2,1)S(1)} %bitcast.31, bf16[64,256]{1,0:T(8,128)(2,1)S(1)} %bitcast.34, f32[64,1]{1,0:T(8,128)S(1)} %copy.69.bias_ref), custom_call_target="tpu_custom_call" | custom-call | tf_op jit(solution)/shard_map/prep/pallas_call | solution.py:525
  44.6 0.8 shard_map.139
  45.4 0.0 copy-start.5
  45.4 0.7 copy-done.5
  46.1 1.2 %collective-permute-start.16 = (bf16[688,128]{1,0:T(8,128)(2,1)S(1)}, bf16[688,128]{1,0:T(8,128)(2,1)S(1)}, u32[]{:S(2)}, u32[]{:S(2)}) collective-permute-start(bf16[688,128]{1,0:T(8,128)(2,1)S(1)} %copy-done.15), channel_id=1, source_target_pairs={{0,16},{8,24},{16,0},{24,8},{1,17},{9,25},{17,1},{25,9},{2,18},{10... | collective-permute-start | bytes 528392 | tf_op jit(solution)/shard_map/ppermute | solution.py:417
  47.3 0.2 collective-permute-start.17
  47.5 1.2 %collective-permute-start.18 = (bf16[688,128]{1,0:T(8,128)(2,1)S(1)}, bf16[688,128]{1,0:T(8,128)(2,1)S(1)}, u32[]{:S(2)}, u32[]{:S(2)}) collective-permute-start(bf16[688,128]{1,0:T(8,128)(2,1)S(1)} %get-tuple-element.26), channel_id=1, source_target_pairs={{0,8},{8,0},{16,24},{24,16},{1,9},{9,1},{17,25},{25,17},{2,10},{10... | collective-permute-start | bytes 528392 | tf_op jit(solution)/shard_map/ppermute | solution.py:417
  48.7 1.2 %collective-permute-start.19 = (bf16[688,128]{1,0:T(8,128)(2,1)S(1)}, bf16[688,128]{1,0:T(8,128)(2,1)S(1)}, u32[]{:S(2)}, u32[]{:S(2)}) collective-permute-start(bf16[688,128]{1,0:T(8,128)(2,1)S(1)} %get-tuple-element.27), channel_id=1, source_target_pairs={{0,16},{8,24},{16,0},{24,8},{1,17},{9,25},{17,1},{25,9},{2,18},{10... | collective-permute-start | bytes 528392 | tf_op jit(solution)/shard_map/ppermute | solution.py:417
  50.0 0.2 collective-permute-done.15.refs_16_
  50.2 0.2 collective-permute-start.20
  50.3 4.5 %collective-permute-done.16.refs_17_ = bf16[688,128]{1,0:T(8,128)(2,1)S(1)} collective-permute-done((bf16[688,128]{1,0:T(8,128)(2,1)S(1)}, bf16[688,128]{1,0:T(8,128)(2,1)S(1)}, u32[]{:S(2)}, u32[]{:S(2)}) %collective-permute-start.16) | collective-permute-done | bytes 176160 | tf_op jit(solution)/shard_map/ppermute | solution.py:417
  54.8 2.8 %collective-permute-done.18.refs_19_ = bf16[688,128]{1,0:T(8,128)(2,1)S(1)} collective-permute-done((bf16[688,128]{1,0:T(8,128)(2,1)S(1)}, bf16[688,128]{1,0:T(8,128)(2,1)S(1)}, u32[]{:S(2)}, u32[]{:S(2)}) %collective-permute-start.18) | collective-permute-done | bytes 176160 | tf_op jit(solution)/shard_map/ppermute | solution.py:417
  57.6 4.6 %collective-permute-done.19.refs_20_ = bf16[688,128]{1,0:T(8,128)(2,1)S(1)} collective-permute-done((bf16[688,128]{1,0:T(8,128)(2,1)S(1)}, bf16[688,128]{1,0:T(8,128)(2,1)S(1)}, u32[]{:S(2)}, u32[]{:S(2)}) %collective-permute-start.19) | collective-permute-done | bytes 176160 | tf_op jit(solution)/shard_map/ppermute | solution.py:417
  62.3 0.9 %copy-done.6 = bf16[688,128]{1,0:T(8,128)(2,1)S(1)} copy-done((bf16[688,128]{1,0:T(8,128)(2,1)S(1)}, bf16[688,128]{1,0:T(8,128)(2,1)}, u32[]{:S(2)}) %copy-start.6) | copy-done | bytes 176152
  63.2 15.3 %attend.1.own_ref = bf16[1024,128]{1,0:T(8,128)(2,1)S(1)} custom-call(s32[16,8]{1,0:T(8,128)S(1)} %get-tuple-element.35.refs_0_, s32[5,2]{1,0:T(8,128)S(1)} %pad_add_fusion.plan_ref.refs_1_, s32[16,8]{1,0:T(8,128)S(1)} %get-tuple-element.34.refs_2_, bf16[1360,128]{1,0:T(8,128)(2,1)S(1)} %pad_maximum_fusion.refs_3_, ...), custom_call_target="tpu_custom_call" | custom-call | tf_op jit(solution)/shard_map/attend/pallas_call | solution.py:543
  78.5 4.1 %collective-permute-start.21 = (bf16[1024,128]{1,0:T(8,128)(2,1)S(1)}, bf16[1024,128]{1,0:T(8,128)(2,1)S(1)}, u32[]{:S(2)}, u32[]{:S(2)}) collective-permute-start(bf16[1024,128]{1,0:T(8,128)(2,1)S(1)} %attend.1.own_ref), channel_id=1, source_target_pairs={{0,1},{1,0},{2,3},{3,2},{4,5},{5,4},{6,7},{7,6},{8,9},{9,8},{10,11... | collective-permute-start | bytes 786440 | tf_op jit(solution)/shard_map/ppermute | solution.py:575
  82.7 1.2 %collective-permute-done.21.other_ref = bf16[1024,128]{1,0:T(8,128)(2,1)S(1)} collective-permute-done((bf16[1024,128]{1,0:T(8,128)(2,1)S(1)}, bf16[1024,128]{1,0:T(8,128)(2,1)S(1)}, u32[]{:S(2)}, u32[]{:S(2)}) %collective-permute-start.21) | collective-permute-done | bytes 262176 | tf_op jit(solution)/shard_map/ppermute | solution.py:575
  83.8 0.7 copy-done.9
  84.5 0.9 %copy-done.7 = bf16[256,256]{1,0:T(8,128)(2,1)S(1)} copy-done((bf16[256,256]{1,0:T(8,128)(2,1)S(1)}, bf16[256,256]{1,0:T(8,128)(2,1)}, u32[]{:S(2)}) %copy-start.7) | copy-done | bytes 131096
  85.4 0.7 copy-done.11
  86.1 2.4 %norm.1 = bf16[1024,128]{1,0:T(8,128)(2,1)} custom-call(s32[1]{0:T(128)} %bitcast.head_ref, bf16[1024,256]{1,0:T(8,128)(2,1)S(1)} %bitcast.32, bf16[1024,128]{1,0:T(8,128)(2,1)S(1)} %attend.1.own_ref, bf16[1024,128]{1,0:T(8,128)(2,1)S(1)} %collective-permute-done.21.other_ref, bf16[256,256]{1,0:T(8,128)(2,1)S(1)} %copy-done.7, f32[1,256]{1,0:T(1,128)S(1)} %bitcast.35, ...), custom_call_target="tpu_custom_call" | custom-call | tf_op jit(solution)/shard_map/norm/pallas_call | solution.py:576
  (53 shorter events, 0.2 us)
Async XLA Ops:
  0.0 0.7 copy-start.17
  0.7 6.4 %copy-start.16 = (s32[4,1,4,8]{3,2,1,0:T(4,128)S(1)}, s32[4,1,4,8]{3,2,1,0:T(4,128)}, u32[]{:S(2)}) copy-start(s32[4,1,4,8]{3,2,1,0:T(4,128)} %param.19) | copy-start | bytes 1540
  1.7 10.9 %collective-permute-start.1 = (bf16[1360,128]{1,0:T(8,128)(2,1)S(1)}, bf16[1360,128]{1,0:T(8,128)(2,1)S(1)}, u32[]{:S(2)}, u32[]{:S(2)}) collective-permute-start(bf16[1360,128]{1,0:T(8,128)(2,1)S(1)} %pad_maximum_fusion.refs_3_), channel_id=1, source_target_pairs={{2,0},{4,2},{6,4},{3,1},{5,3},{7,5},{10,8},{12,10},{14,12},{11,9},... | collective-permute-start | bytes 1044488 | tf_op jit(solution)/shard_map/ppermute | solution.py:378
  3.8 10.9 %collective-permute-start = (bf16[1360,128]{1,0:T(8,128)(2,1)S(1)}, bf16[1360,128]{1,0:T(8,128)(2,1)S(1)}, u32[]{:S(2)}, u32[]{:S(2)}) collective-permute-start(bf16[1360,128]{1,0:T(8,128)(2,1)S(1)} %pad_maximum_fusion.refs_3_), channel_id=1, source_target_pairs={{0,2},{2,4},{4,6},{1,3},{3,5},{5,7},{8,10},{10,12},{12,14},{9,11},... | collective-permute-start | bytes 1044488 | tf_op jit(solution)/shard_map/ppermute | solution.py:378
  12.7 8.7 %collective-permute-start.3 = (bf16[1360,128]{1,0:T(8,128)(2,1)S(1)}, bf16[1360,128]{1,0:T(8,128)(2,1)S(1)}, u32[]{:S(2)}, u32[]{:S(2)}) collective-permute-start(bf16[1360,128]{1,0:T(8,128)(2,1)S(1)} %collective-permute-done.1.refs_4_.refs_3_.refs_5_), channel_id=1, source_target_pairs={{2,0},{4,2},{3,1},{5,3},{10,8},{12,10},{11,9},{13,11},{18,16},{20,... | collective-permute-start | bytes 1044488 | tf_op jit(solution)/shard_map/ppermute | solution.py:378
  14.8 9.8 %collective-permute-start.2 = (bf16[1360,128]{1,0:T(8,128)(2,1)S(1)}, bf16[1360,128]{1,0:T(8,128)(2,1)S(1)}, u32[]{:S(2)}, u32[]{:S(2)}) collective-permute-start(bf16[1360,128]{1,0:T(8,128)(2,1)S(1)} %collective-permute-done.refs_3_.refs_4_), channel_id=1, source_target_pairs={{2,4},{4,6},{3,5},{5,7},{10,12},{12,14},{11,13},{13,15},{18,20},{2... | collective-permute-start | bytes 1044488 | tf_op jit(solution)/shard_map/ppermute | solution.py:378
  17.8 10.7 %collective-permute-start.6 = (s32[4,8]{1,0:T(4,128)S(1)}, s32[4,8]{1,0:T(4,128)S(1)}, u32[]{:S(2)}, u32[]{:S(2)}) collective-permute-start(s32[4,8]{1,0:T(4,128)S(1)} %bitcast.45), channel_id=1, source_target_pairs={{0,8},{8,0},{16,24},{24,16},{1,9},{9,1},{17,25},{25,17},{2,10},{10... | collective-permute-start | bytes 392 | tf_op jit(solution)/shard_map/ppermute | solution.py:386
  19.1 9.4 %collective-permute-start.7 = (s32[4,8]{1,0:T(4,128)S(1)}, s32[4,8]{1,0:T(4,128)S(1)}, u32[]{:S(2)}, u32[]{:S(2)}) collective-permute-start(s32[4,8]{1,0:T(4,128)S(1)} %bitcast.46), channel_id=1, source_target_pairs={{0,16},{8,24},{16,0},{24,8},{1,17},{9,25},{17,1},{25,9},{2,18},{10... | collective-permute-start | bytes 392 | tf_op jit(solution)/shard_map/ppermute | solution.py:386
  20.4 8.1 %collective-permute-start.8 = (s32[4,8]{1,0:T(4,128)S(1)}, s32[4,8]{1,0:T(4,128)S(1)}, u32[]{:S(2)}, u32[]{:S(2)}) collective-permute-start(s32[4,8]{1,0:T(4,128)S(1)} %bitcast.47), channel_id=1, source_target_pairs={{0,24},{8,16},{16,8},{24,0},{1,25},{9,17},{17,9},{25,1},{2,26},{10... | collective-permute-start | bytes 392 | tf_op jit(solution)/shard_map/ppermute | solution.py:386
  21.3 19.4 %collective-permute-start.5 = (bf16[1360,128]{1,0:T(8,128)(2,1)S(1)}, bf16[1360,128]{1,0:T(8,128)(2,1)S(1)}, u32[]{:S(2)}, u32[]{:S(2)}) collective-permute-start(bf16[1360,128]{1,0:T(8,128)(2,1)S(1)} %collective-permute-done.3.refs_5_.refs_4_.refs_7_), channel_id=1, source_target_pairs={{2,0},{3,1},{10,8},{11,9},{18,16},{19,17},{26,24},{27,25}} | collective-permute-start | bytes 1044488 | tf_op jit(solution)/shard_map/ppermute | solution.py:378
  24.6 16.4 %collective-permute-start.4 = (bf16[1360,128]{1,0:T(8,128)(2,1)S(1)}, bf16[1360,128]{1,0:T(8,128)(2,1)S(1)}, u32[]{:S(2)}, u32[]{:S(2)}) collective-permute-start(bf16[1360,128]{1,0:T(8,128)(2,1)S(1)} %collective-permute-done.2.refs_4_.refs_3_.refs_6_), channel_id=1, source_target_pairs={{4,6},{5,7},{12,14},{13,15},{20,22},{21,23},{28,30},{29,31}} | collective-permute-start | bytes 1044488 | tf_op jit(solution)/shard_map/ppermute | solution.py:378
  27.7 0.7 copy-start.18
  29.9 7.0 %collective-permute-start.9 = (bf16[688,128]{1,0:T(8,128)(2,1)S(1)}, bf16[688,128]{1,0:T(8,128)(2,1)S(1)}, u32[]{:S(2)}, u32[]{:S(2)}) collective-permute-start(bf16[688,128]{1,0:T(8,128)(2,1)S(1)} %get-tuple-element.17), channel_id=1, source_target_pairs={{0,8},{8,0},{16,24},{24,16},{1,9},{9,1},{17,25},{25,17},{2,10},{10... | collective-permute-start | bytes 528392 | tf_op jit(solution)/shard_map/ppermute | solution.py:417
  31.1 7.7 %collective-permute-start.10 = (bf16[688,128]{1,0:T(8,128)(2,1)S(1)}, bf16[688,128]{1,0:T(8,128)(2,1)S(1)}, u32[]{:S(2)}, u32[]{:S(2)}) collective-permute-start(bf16[688,128]{1,0:T(8,128)(2,1)S(1)} %get-tuple-element.18), channel_id=1, source_target_pairs={{0,16},{8,24},{16,0},{24,8},{1,17},{9,25},{17,1},{25,9},{2,18},{10... | collective-permute-start | bytes 528392 | tf_op jit(solution)/shard_map/ppermute | solution.py:417
  32.4 13.0 %collective-permute-start.11 = (bf16[688,128]{1,0:T(8,128)(2,1)}, bf16[688,128]{1,0:T(8,128)(2,1)S(1)}, u32[]{:S(2)}, u32[]{:S(2)}) collective-permute-start(bf16[688,128]{1,0:T(8,128)(2,1)} %get-tuple-element.19), channel_id=1, source_target_pairs={{0,24},{8,16},{16,8},{24,0},{1,25},{9,17},{17,9},{25,1},{2,26},{10... | collective-permute-start | bytes 528392 | tf_op jit(solution)/shard_map/ppermute | solution.py:417
  35.6 0.7 copy-start.12
  36.2 0.7 copy-start.14
  36.9 6.6 %copy-start = (bf16[64,16,256]{2,1,0:T(8,128)(2,1)S(1)}, bf16[64,16,256]{2,1,0:T(8,128)(2,1)}, u32[]{:S(2)}) copy-start(bf16[64,16,256]{2,1,0:T(8,128)(2,1)} %param.14) | copy-start | bytes 1572868
  36.9 0.7 copy-start.1
  37.6 9.7 %collective-permute-start.12 = (bf16[688,128]{1,0:T(8,128)(2,1)}, bf16[688,128]{1,0:T(8,128)(2,1)}, u32[]{:S(2)}, u32[]{:S(2)}) collective-permute-start(bf16[688,128]{1,0:T(8,128)(2,1)} %get-tuple-element.20), channel_id=1, source_target_pairs={{0,8},{8,0},{16,24},{24,16},{1,9},{9,1},{17,25},{25,17},{2,10},{10... | collective-permute-start | bytes 528392 | tf_op jit(solution)/shard_map/ppermute | solution.py:417
  38.8 0.7 copy-start.3
  39.5 8.0 %collective-permute-start.13 = (bf16[688,128]{1,0:T(8,128)(2,1)}, bf16[688,128]{1,0:T(8,128)(2,1)}, u32[]{:S(2)}, u32[]{:S(2)}) collective-permute-start(bf16[688,128]{1,0:T(8,128)(2,1)} %get-tuple-element.21), channel_id=1, source_target_pairs={{0,16},{8,24},{16,0},{24,8},{1,17},{9,25},{17,1},{25,9},{2,18},{10... | collective-permute-start | bytes 528392 | tf_op jit(solution)/shard_map/ppermute | solution.py:417
  40.7 8.0 %collective-permute-start.14 = (bf16[688,128]{1,0:T(8,128)(2,1)}, bf16[688,128]{1,0:T(8,128)(2,1)}, u32[]{:S(2)}, u32[]{:S(2)}) collective-permute-start(bf16[688,128]{1,0:T(8,128)(2,1)} %get-tuple-element.22), channel_id=1, source_target_pairs={{0,24},{8,16},{16,8},{24,0},{1,25},{9,17},{17,9},{25,1},{2,26},{10... | collective-permute-start | bytes 528392 | tf_op jit(solution)/shard_map/ppermute | solution.py:417
  40.9 9.2 %collective-permute-start.15 = (bf16[688,128]{1,0:T(8,128)(2,1)}, bf16[688,128]{1,0:T(8,128)(2,1)}, u32[]{:S(2)}, u32[]{:S(2)}) collective-permute-start(bf16[688,128]{1,0:T(8,128)(2,1)} %get-tuple-element.23), channel_id=1, source_target_pairs={{0,8},{8,0},{16,24},{24,16},{1,9},{9,1},{17,25},{25,17},{2,10},{10... | collective-permute-start | bytes 528392 | tf_op jit(solution)/shard_map/ppermute | solution.py:417
  42.3 1.3 %copy-start.8 = (bf16[256,64]{0,1:T(8,128)(2,1)S(1)}, bf16[256,64]{0,1:T(8,128)(2,1)}, u32[]{:S(2)}) copy-start(bf16[256,64]{0,1:T(8,128)(2,1)} %param.21) | copy-start | bytes 98308
  44.6 1.5 %copy-start.15 = (bf16[688,128]{1,0:T(8,128)(2,1)S(1)}, bf16[688,128]{1,0:T(8,128)(2,1)}, u32[]{:S(2)}) copy-start(bf16[688,128]{1,0:T(8,128)(2,1)} %copy-done.14) | copy-start | bytes 528388
  44.6 2.7 %copy-start.13 = (bf16[688,128]{1,0:T(8,128)(2,1)S(1)}, bf16[688,128]{1,0:T(8,128)(2,1)}, u32[]{:S(2)}) copy-start(bf16[688,128]{1,0:T(8,128)(2,1)} %copy-done.12) | copy-start | bytes 528388
  44.6 17.7 %copy-start.2 = (bf16[688,128]{1,0:T(8,128)(2,1)S(1)}, bf16[688,128]{1,0:T(8,128)(2,1)}, u32[]{:S(2)}) copy-start(bf16[688,128]{1,0:T(8,128)(2,1)} %copy-done.1) | copy-start | bytes 528388
  44.6 17.7 %copy-start.4 = (bf16[688,128]{1,0:T(8,128)(2,1)S(1)}, bf16[688,128]{1,0:T(8,128)(2,1)}, u32[]{:S(2)}) copy-start(bf16[688,128]{1,0:T(8,128)(2,1)} %copy-done.3) | copy-start | bytes 528388
  45.4 0.7 copy-start.5
  46.1 8.8 %collective-permute-start.16 = (bf16[688,128]{1,0:T(8,128)(2,1)S(1)}, bf16[688,128]{1,0:T(8,128)(2,1)S(1)}, u32[]{:S(2)}, u32[]{:S(2)}) collective-permute-start(bf16[688,128]{1,0:T(8,128)(2,1)S(1)} %copy-done.15), channel_id=1, source_target_pairs={{0,16},{8,24},{16,0},{24,8},{1,17},{9,25},{17,1},{25,9},{2,18},{10... | collective-permute-start | bytes 528392 | tf_op jit(solution)/shard_map/ppermute | solution.py:417
  47.3 7.5 %collective-permute-start.17 = (bf16[688,128]{1,0:T(8,128)(2,1)S(1)}, bf16[688,128]{1,0:T(8,128)(2,1)S(1)}, u32[]{:S(2)}, u32[]{:S(2)}) collective-permute-start(bf16[688,128]{1,0:T(8,128)(2,1)S(1)} %copy-done.13), channel_id=1, source_target_pairs={{0,24},{8,16},{16,8},{24,0},{1,25},{9,17},{17,9},{25,1},{2,26},{10... | collective-permute-start | bytes 528392 | tf_op jit(solution)/shard_map/ppermute | solution.py:417
  47.5 10.1 %collective-permute-start.18 = (bf16[688,128]{1,0:T(8,128)(2,1)S(1)}, bf16[688,128]{1,0:T(8,128)(2,1)S(1)}, u32[]{:S(2)}, u32[]{:S(2)}) collective-permute-start(bf16[688,128]{1,0:T(8,128)(2,1)S(1)} %get-tuple-element.26), channel_id=1, source_target_pairs={{0,8},{8,0},{16,24},{24,16},{1,9},{9,1},{17,25},{25,17},{2,10},{10... | collective-permute-start | bytes 528392 | tf_op jit(solution)/shard_map/ppermute | solution.py:417
  48.7 13.5 %collective-permute-start.19 = (bf16[688,128]{1,0:T(8,128)(2,1)S(1)}, bf16[688,128]{1,0:T(8,128)(2,1)S(1)}, u32[]{:S(2)}, u32[]{:S(2)}) collective-permute-start(bf16[688,128]{1,0:T(8,128)(2,1)S(1)} %get-tuple-element.27), channel_id=1, source_target_pairs={{0,16},{8,24},{16,0},{24,8},{1,17},{9,25},{17,1},{25,9},{2,18},{10... | collective-permute-start | bytes 528392 | tf_op jit(solution)/shard_map/ppermute | solution.py:417
  50.2 12.1 %collective-permute-start.20 = (bf16[688,128]{1,0:T(8,128)(2,1)S(1)}, bf16[688,128]{1,0:T(8,128)(2,1)S(1)}, u32[]{:S(2)}, u32[]{:S(2)}) collective-permute-start(bf16[688,128]{1,0:T(8,128)(2,1)S(1)} %get-tuple-element.28), channel_id=1, source_target_pairs={{0,24},{8,16},{16,8},{24,0},{1,25},{9,17},{17,9},{25,1},{2,26},{10... | collective-permute-start | bytes 528392 | tf_op jit(solution)/shard_map/ppermute | solution.py:417
  62.2 0.9 %copy-start.6 = (bf16[688,128]{1,0:T(8,128)(2,1)S(1)}, bf16[688,128]{1,0:T(8,128)(2,1)}, u32[]{:S(2)}) copy-start(bf16[688,128]{1,0:T(8,128)(2,1)} %copy-done.5) | copy-start | bytes 528388
  78.5 5.3 %collective-permute-start.21 = (bf16[1024,128]{1,0:T(8,128)(2,1)S(1)}, bf16[1024,128]{1,0:T(8,128)(2,1)S(1)}, u32[]{:S(2)}, u32[]{:S(2)}) collective-permute-start(bf16[1024,128]{1,0:T(8,128)(2,1)S(1)} %attend.1.own_ref), channel_id=1, source_target_pairs={{0,1},{1,0},{2,3},{3,2},{4,5},{5,4},{6,7},{7,6},{8,9},{9,8},{10,11... | collective-permute-start | bytes 786440 | tf_op jit(solution)/shard_map/ppermute | solution.py:575
  83.8 0.7 copy-start.9
  83.8 0.7 copy-start.10
  84.5 0.9 %copy-start.7 = (bf16[256,256]{1,0:T(8,128)(2,1)S(1)}, bf16[256,256]{1,0:T(8,128)(2,1)}, u32[]{:S(2)}) copy-start(bf16[256,256]{1,0:T(8,128)(2,1)} %weight_ref.1) | copy-start | bytes 393220
  85.4 0.7 copy-start.11

commit v3 on v2

v3 whole, which is shorter than its diff:
```python
import functools
import jax
import jax.numpy as jnp
import numpy as np
from jax import lax
from jax.experimental import pallas as pl
from jax.experimental.pallas import tpu as pltpu
from jax.sharding import PartitionSpec as P

LEVELS = 4
POINTS = 4
ANY = pl.ANY
SMEM = pltpu.SMEM
VMEM = pltpu.VMEM
SELECT_VMEM = 8 * 1024 * 1024
PREP_VMEM = 12 * 1024 * 1024
ATTEND_VMEM = 20 * 1024 * 1024


def to_blocks(source, tile_rows, tile_cols, tile_side):
    channels = source.shape[2]
    shaped = source.reshape(tile_rows, tile_side, tile_cols, tile_side, channels)
    return shaped.transpose(0, 2, 1, 3, 4).reshape(
        tile_rows * tile_cols, tile_side * tile_side, channels
    )


def hat(position, center):
    return jnp.maximum(1.0 - jnp.abs(position - center), 0.0)


def iota(shape, dim):
    return lax.broadcasted_iota(jnp.int32, shape, dim)


def prep_kernel(
    dims,
    query_ref,
    logit_ref,
    bias_ref,
    sample_ref,
    weight0,
    weight1,
    weight2,
    down_ref,
    attend_ref,
    code_ref,
    row_ref,
    col_ref,
):
    _, _, sizes, sides, per_block, heads, _, _ = dims
    block = pl.program_id(0)
    pixels = query_ref.shape[0]
    base2 = per_block * sizes[2]
    logits = lax.dot_general(
        logit_ref[...], query_ref[...], (((1,), (1,)), ((), ())), preferred_element_type=jnp.float32
    )
    logits = logits + bias_ref[...]
    lanes = LEVELS * POINTS
    for head in range(heads):
        part = logits[head * lanes : (head + 1) * lanes, :]
        part = jnp.exp(part - jnp.max(part, axis=0, keepdims=True))
        attend_ref[head * lanes : (head + 1) * lanes, :] = part / jnp.sum(part, axis=0, keepdims=True)

    packed = sample_ref[...]
    level_of = iota(packed.shape, 0) // POINTS % LEVELS
    slot = packed >> 24
    pos_row = (packed >> 12) & 4095
    pos_col = packed & 4095
    half = lax.shift_right_logical(jnp.full_like(packed, sides[0] * 128), level_of)
    upper = (pos_row >= half) & (level_of < 2)
    code_ref[...] = slot + jnp.where(upper, per_block, 0)
    down = (pos_row - jnp.where(upper, half, 0)).astype(jnp.float32) * (1.0 / 256.0)
    row_ref[...] = down
    down_ref[...] = down
    col_ref[...] = pos_col.astype(jnp.float32) * (1.0 / 256.0)

    for head in range(heads):
        for level in range(2):
            side = sides[level]
            weight = (weight0, weight1)[level]
            for point in range(POINTS):
                row = (head * LEVELS + level) * POINTS + point
                line = slice(row, row + 1)
                code = code_ref[line, :]
                across = attend_ref[line, :] * hat(
                    col_ref[line, :], (iota((16, pixels), 0) % side).astype(jnp.float32)
                )
                step = 16 // side
                for index in range(0, 2 * per_block, step):
                    wanted = index + iota((16, pixels), 0) // side
                    weight[0, head, point, index * side : (index + step) * side, :] = jnp.where(
                        code == wanted, across, 0.0
                    ).astype(jnp.bfloat16)
        side = sides[2]
        size = sizes[2]
        place = iota((size, pixels), 0)
        parts = []
        codes = []
        for point in range(POINTS):
            row = (head * LEVELS + 2) * POINTS + point
            line = slice(row, row + 1)
            parts.append(
                attend_ref[line, :]
                * hat(row_ref[line, :], (place // side).astype(jnp.float32))
                * hat(col_ref[line, :], (place % side).astype(jnp.float32))
            )
            codes.append(code_ref[line, :])
        for index in range(per_block):
            mixed = jnp.zeros((size, pixels), jnp.float32)
            for point in range(POINTS):
                mixed = mixed + jnp.where(codes[point] == index, parts[point], 0.0)
            weight2[0, head, index * size : (index + 1) * size, :] = mixed.astype(jnp.bfloat16)
        side = sides[3]
        size = sizes[3]
        deep = per_block * size
        place = iota((deep, pixels), 0)
        mixed = jnp.zeros((deep, pixels), jnp.float32)
        for point in range(POINTS):
            row = (head * LEVELS + 3) * POINTS + point
            line = slice(row, row + 1)
            value = (
                attend_ref[line, :]
                * hat(row_ref[line, :], (place % size // side).astype(jnp.float32))
                * hat(col_ref[line, :], (place % side).astype(jnp.float32))
            )
            mixed = mixed + jnp.where(code_ref[line, :] == place // size, value, 0.0)
        weight2[0, head, base2:, :] = jnp.zeros((weight2.shape[2] - base2, pixels), jnp.bfloat16)
        weight2[0, head, pl.ds(pl.multiple_of(base2 + block * deep, deep), deep), :] = mixed.astype(
            jnp.bfloat16
        )


def select_kernel(dims, ids_ref, zero_ref, one_ref, two_ref, three_ref, out_ref, sem):
    peers, capacity, sizes = dims
    refs = (zero_ref, one_ref, two_ref)

    def copies(peer, make):
        base = 0
        for level in range(LEVELS - 1):
            size = sizes[level]
            for slot in range(capacity):
                index = jnp.maximum(ids_ref[peer, level * capacity + slot], 0)
                make(refs[level].at[index], out_ref.at[peer, base : base + size, :])
                base += size
        make(three_ref, out_ref.at[peer, base : base + three_ref.shape[0], :])

    def start(peer, carry):
        copies(peer, lambda src, dst: pltpu.make_async_copy(src, dst, sem).start())
        return carry

    def finish(peer, carry):
        copies(peer, lambda src, dst: pltpu.make_async_copy(src, dst, sem).wait())
        return carry

    lax.fori_loop(0, peers, start, 0)
    lax.fori_loop(0, peers, finish, 0)


def relay_select_kernel(dims, slot, plan_ref, *refs):
    partners, candidates, capacity, sizes, blocks = dims
    ids = refs[:partners]
    sources = refs[partners : partners + candidates]
    outs = refs[partners + candidates :]
    column = plan_ref[slot, 0]
    for number, source in enumerate(sources):

        @pl.when(plan_ref[slot, 1] == number)
        def _(source=source):
            for partner in range(partners):
                base = 0
                start = 0
                for level in range(LEVELS - 1):
                    size = sizes[level]
                    for rank in range(capacity):
                        index = jnp.maximum(ids[partner][column, level * capacity + rank], 0)
                        outs[partner][base : base + size, :] = source[
                            pl.ds(pl.multiple_of(start + index * size, size), size), :
                        ]
                        base += size
                    start += blocks * size
                small = blocks * sizes[3]
                outs[partner][base : base + small, :] = source[start : start + small, :]


def gather_direct(dims, request_ref, fetched_ref, tiles, tile3, sem):
    peers, capacity, sizes, _, _, _, _, _ = dims
    small = tile3.shape[1]
    base3 = capacity * sum(sizes[:3])
    pltpu.make_async_copy(fetched_ref.at[:, base3 : base3 + small, :], tile3, sem.at[LEVELS - 1]).start()

    def start(peer, carry):
        base = 0
        for level in range(LEVELS - 1):
            size = sizes[level]
            for rank in range(capacity):
                fetch_one(
                    request_ref[peer, level * capacity + rank],
                    fetched_ref.at[peer, base : base + size, :],
                    tiles[level],
                    sem.at[level],
                )
                base += size
        return carry

    lax.fori_loop(0, peers, start, 0)
    for level in range(LEVELS - 1):
        pltpu.make_async_copy(tiles[level], tiles[level], sem.at[level]).wait()
    pltpu.make_async_copy(tile3, tile3, sem.at[LEVELS - 1]).wait()


def fetch_one(request, source, tile, sem):
    @pl.when(request >= 0)
    def _():
        pltpu.make_async_copy(source, tile.at[request], sem).start()


def gather_relay(dims, relay, request_ref, plan_ref, asked_ref, blocks_refs, packs_refs, tiles, tile3):
    _, capacity, sizes, _, _, _, _, blocks = dims
    rows, columns, partner_of = relay
    small = tile3.shape[1]
    my_row = plan_ref[columns, 0]
    my_column = plan_ref[columns, 1]

    def put(owner, level, rank, source, start):
        request = request_ref[owner, level * capacity + rank]
        size = sizes[level]
        tiles[level][jnp.maximum(request, 0)] = source[pl.ds(start, size), :]

    for number, source in enumerate(blocks_refs):
        shift = (number + 1) // 2 * (-1 if number % 2 else 1)
        column = my_column + shift

        @pl.when((column >= 0) & (column < columns))
        def _(source=source, column=column):
            owner = my_row * columns + column
            start = 0
            for level in range(LEVELS - 1):
                size = sizes[level]
                for rank in range(capacity):
                    index = jnp.maximum(asked_ref[owner, level * capacity + rank], 0)
                    put(owner, level, rank, source, pl.multiple_of(start + index * size, size))
                start += blocks * size
            tile3[owner] = source[start : start + small, :]

    for number, source in enumerate(packs_refs):
        slot, partner = divmod(number, rows - 1)
        owner = partner_of(my_row, partner + 1) * columns + plan_ref[slot, 0]
        base = 0
        for level in range(LEVELS - 1):
            for rank in range(capacity):
                put(owner, level, rank, source, base)
                base += sizes[level]
        tile3[owner] = source[base : base + small, :]


def attend_kernel(dims, gather, count, *refs):
    sources = refs[:count]
    (
        weight0,
        weight1,
        weight2,
        down_ref,
        rowid_ref,
        out_ref,
        tile0,
        tile1,
        tile2,
        tile3,
        left0,
        left1,
        left2,
        sem,
    ) = refs[count:]
    peers, _, sizes, sides, per_block, heads, head_dim, _ = dims
    block = pl.program_id(0)
    channels = heads * head_dim
    small = tile3.shape[1]
    base2 = per_block * sizes[2]

    @pl.when(block == 0)
    def _():
        gather(sources, (tile0, tile1, tile2), tile3, sem)
        left0[...] = jnp.zeros_like(left0)
        flat = tile3[...].reshape(peers * small, channels)
        chosen = (rowid_ref[...] == iota((rowid_ref.shape[0], peers * small), 1)).astype(jnp.bfloat16)
        picked = jnp.dot(chosen, flat, preferred_element_type=jnp.float32)
        left2[:, base2:] = picked.T.astype(jnp.bfloat16)

    mine = pl.ds(block * per_block, per_block)
    side0, side1 = sides[0], sides[1]
    half0, half1 = side0 // 2, side1 // 2
    for line in range(side0):
        piece = tile0[mine, line * side0 : (line + 1) * side0, :]
        turned = piece.reshape(per_block * side0, channels).T
        for group in range(2):
            offset = line - group * half0
            if 0 <= offset <= half0:
                for head in range(heads):
                    left0[
                        head,
                        offset * head_dim : (offset + 1) * head_dim,
                        group * per_block * side0 : (group + 1) * per_block * side0,
                    ] = turned[head * head_dim : (head + 1) * head_dim, :]
    wide1 = tile1[mine].astype(jnp.float32)
    for offset in range(half1 + 1):
        first = wide1[:, offset * side1 : (offset + 1) * side1, :]
        other = min(half1 + offset, side1 - 1)
        second = wide1[:, other * side1 : (other + 1) * side1, :]
        both = jnp.concatenate(
            [first.reshape(per_block * side1, channels), second.reshape(per_block * side1, channels)], axis=0
        )
        turned = both.T.astype(jnp.bfloat16)
        for head in range(heads):
            left1[head, offset * head_dim : (offset + 1) * head_dim, :] = turned[
                head * head_dim : (head + 1) * head_dim, :
            ]
    left2[:, :base2] = tile2[mine].reshape(per_block * sizes[2], channels).T

    for head in range(heads):
        total = jnp.dot(
            left2[head * head_dim : (head + 1) * head_dim, :],
            weight2[0, head],
            preferred_element_type=jnp.float32,
        )
        for level in range(2):
            left = (left0, left1)[level]
            weight = (weight0, weight1)[level]
            reach = sides[level] // 2 + 1
            for point in range(POINTS):
                row = (head * LEVELS + level) * POINTS + point
                product = jnp.dot(left[head], weight[0, head, point], preferred_element_type=jnp.float32)
                down = down_ref[row : row + 1, :]
                for offset in range(reach):
                    total = total + product[offset * head_dim : (offset + 1) * head_dim, :] * hat(
                        down, float(offset)
                    )
        out_ref[:, head * head_dim : (head + 1) * head_dim] = total.T.astype(jnp.bfloat16)


def own_kernel(head_ref, query_ref, own_ref, weight_ref, bias_ref, out_ref):
    channels = own_ref.shape[1]
    rows = weight_ref[pl.ds(pl.multiple_of(head_ref[0] * channels, channels), channels), :]
    pre = query_ref[...].astype(jnp.float32) + bias_ref[...]
    out_ref[...] = pre + jnp.dot(own_ref[...], rows, preferred_element_type=jnp.float32)


def norm_kernel(head_ref, pre_ref, other_ref, weight_ref, gain_ref, shift_ref, out_ref):
    own_head = head_ref[0]
    channels = out_ref.shape[1]
    rows = weight_ref[pl.ds(pl.multiple_of((1 - own_head) * channels, channels), channels), :]
    pre = pre_ref[...] + jnp.dot(other_ref[...], rows, preferred_element_type=jnp.float32)
    centered = pre - jnp.mean(pre, axis=1, keepdims=True)
    variance = jnp.mean(centered * centered, axis=1, keepdims=True)
    own = jnp.where(own_head == 0, centered[:, :channels], centered[:, channels:])
    out_ref[...] = (own * lax.rsqrt(variance + 1e-05) * gain_ref[...] + shift_ref[...]).astype(jnp.bfloat16)


def column_order(column, columns):
    found = []
    for step in range(1, columns):
        found += [(step, side) for side in (-1, 1) if 0 <= column + side * step < columns]
    return found


def relay_tiles(dims, row_count, col_count, pack, flat_sets, asked, request):
    _, capacity, sizes, _, _, heads, head_dim, blocks = dims
    channels = heads * head_dim
    my_row = lax.axis_index("row")
    my_column = lax.axis_index("col")
    power = row_count & (row_count - 1) == 0

    def partner_of(row, number):
        return row ^ number if power else (row + number) % row_count

    def source_of(row, number):
        return row ^ number if power else (row + row_count - number) % row_count

    block = jnp.concatenate(flat_sets, axis=0)
    arrived = {}

    def hop(step):
        for side in (-1, 1):
            pairs = []
            for column in range(col_count):
                if 0 <= column + side * step < col_count:
                    pairs.append((column + side, column))
            held = arrived.get((step - 1, side), block)
            arrived[(step, side)] = lax.ppermute(held, "col", pairs)

    grid = asked.reshape(row_count, col_count, asked.shape[1])
    ids = []
    for number in range(1, row_count):
        mine = lax.dynamic_index_in_dim(grid, partner_of(my_row, number), 0, keepdims=False)
        ids.append(
            lax.ppermute(mine, "row", [(row, partner_of(row, number)) for row in range(row_count)])
        )

    hop(1)

    orders = [[(0, 1)] + column_order(column, col_count) for column in range(col_count)]
    candidates = [sorted({order[slot] for order in orders}) for slot in range(col_count)]
    plan = np.zeros((col_count, col_count, 2), np.int32)
    for column in range(col_count):
        for slot in range(col_count):
            step, side = orders[column][slot]
            plan[column, slot] = (column + side * step, candidates[slot].index(orders[column][slot]))
    plan = lax.dynamic_index_in_dim(jnp.asarray(plan), my_column, 0, keepdims=False)
    place = jnp.stack([my_row, my_column]).astype(jnp.int32)
    plan = jnp.concatenate([plan, place[None, :]], axis=0)

    packs = []
    for slot in range(col_count):
        if slot > 1:
            hop(slot)
        held = [block if slot == 0 else arrived[candidate] for candidate in candidates[slot]]
        sent = pl.pallas_call(
            functools.partial(
                relay_select_kernel, (row_count - 1, len(held), capacity, sizes, blocks), slot
            ),
            out_shape=[jax.ShapeDtypeStruct((pack, channels), jnp.bfloat16)] * (row_count - 1),
            in_specs=[pl.BlockSpec(memory_space=SMEM)] * row_count
            + [pl.BlockSpec(memory_space=VMEM)] * len(held),
            out_specs=[pl.BlockSpec(memory_space=VMEM)] * (row_count - 1),
            compiler_params=pltpu.CompilerParams(vmem_limit_bytes=SELECT_VMEM),
        )(plan, *ids, *held)
        for number in range(1, row_count):
            packs.append(
                lax.ppermute(
                    sent[number - 1], "row", [(row, source_of(row, number)) for row in range(row_count)]
                )
            )

    near = [block]
    for step in range(1, col_count):
        near += [arrived[(step, -1)], arrived[(step, 1)]]
    sources = (request, plan, asked, *near, *packs)
    spaces = (SMEM, SMEM, SMEM) + (VMEM,) * (len(near) + len(packs))

    def gather(refs, tiles, tile3, sem):
        gather_relay(
            dims,
            (row_count, col_count, partner_of),
            refs[0],
            refs[1],
            refs[2],
            refs[3 : 3 + len(near)],
            refs[3 + len(near) :],
            tiles,
            tile3,
        )

    return gather, sources, spaces


def on_device(
    queries,
    level_zero,
    level_one,
    level_two,
    level_three,
    tile_lists,
    samples,
    logit_weight,
    logit_bias,
    output_weight,
    output_bias,
    norm_gain,
    norm_shift,
):
    level_blocks = (level_zero, level_one, level_two, level_three)
    row_count = lax.axis_size("row")
    col_count = lax.axis_size("col")
    peers = row_count * col_count
    tile_rows, tile_cols, level_count, per_block = tile_lists.shape
    blocks = tile_rows * tile_cols
    requests = blocks * per_block
    capacity = max(2, (requests + peers - 1) // peers)
    grid_cols = tile_cols * col_count
    channels = level_zero.shape[2]
    width_all = queries.shape[2]
    lanes = samples.shape[2]
    heads = lanes // (LEVELS * POINTS)
    head_dim = channels // heads
    sides = tuple(block.shape[0] // tile_rows for block in level_blocks)
    sizes = tuple(side * side for side in sides)
    pixels = sizes[0]
    tile_sets = [
        to_blocks(level_blocks[level], tile_rows, tile_cols, sides[level]) for level in range(level_count)
    ]

    wanted = tile_lists.reshape(blocks, level_count, per_block).transpose(1, 0, 2).reshape(level_count, requests)
    grid_row = wanted // grid_cols
    grid_col = wanted % grid_cols
    owner = grid_row // tile_rows * col_count + grid_col // tile_cols
    local = grid_row % tile_rows * tile_cols + grid_col % tile_cols
    order = jnp.arange(requests, dtype=jnp.int32)
    earlier = (owner[:, :, None] == owner[:, None, :]) & (order[None, None, :] < order[None, :, None])
    rank = jnp.sum(earlier.astype(jnp.int32), axis=2)
    device = jnp.arange(peers, dtype=jnp.int32)
    slot = jnp.arange(capacity, dtype=jnp.int32)
    hit = (owner[None, :, None, :] == device[:, None, None, None]) & (
        rank[None, :, None, :] == slot[None, None, :, None]
    )
    table = jnp.sum(jnp.where(hit, 1 + order * blocks + local[:, None, :], 0), axis=3) - 1
    table = table.reshape(peers, level_count * capacity)
    asked = jnp.where(table >= 0, table % blocks, -1)
    request = jnp.where(table >= 0, table // blocks, -1)
    small = blocks * sizes[3]
    pack = capacity * sum(sizes[:3]) + small
    dims = (peers, capacity, sizes, sides, per_block, heads, head_dim, blocks)
    flat_sets = [
        tile_sets[level].reshape(blocks * sizes[level], channels) for level in range(level_count)
    ]
    if peers * capacity <= requests and col_count > 1:
        gather, sources, spaces = relay_tiles(dims, row_count, col_count, pack, flat_sets, asked, request)
    else:
        received = lax.all_to_all(asked, ("row", "col"), split_axis=0, concat_axis=0, tiled=True)
        packs = pl.pallas_call(
            functools.partial(select_kernel, (peers, capacity, sizes)),
            out_shape=jax.ShapeDtypeStruct((peers, pack, channels), jnp.bfloat16),
            in_specs=[pl.BlockSpec(memory_space=SMEM)] + [pl.BlockSpec(memory_space=VMEM)] * 4,
            out_specs=pl.BlockSpec(memory_space=ANY),
            scratch_shapes=[pltpu.SemaphoreType.DMA],
            name="select",
        )(received, tile_sets[0], tile_sets[1], tile_sets[2], flat_sets[3])
        fetched = lax.all_to_all(packs, ("row", "col"), split_axis=0, concat_axis=0, tiled=True)
        sources = (request, fetched)
        spaces = (SMEM, ANY)

        def gather(refs, tiles, tile3, sem):
            gather_direct(dims, refs[0], refs[1], tiles, tile3, sem)

    queries_blocked = to_blocks(queries, tile_rows, tile_cols, sides[0]).reshape(blocks * pixels, width_all)
    samples_turned = to_blocks(samples, tile_rows, tile_cols, sides[0]).reshape(blocks * pixels, lanes).T
    depth0 = 2 * per_block * sides[0]
    depth1 = 2 * per_block * sides[1]
    depth2 = per_block * sizes[2] + requests * sizes[3]
    shape0 = (heads, POINTS, depth0, pixels)
    shape1 = (heads, POINTS, depth1, pixels)
    shape2 = (heads, depth2, pixels)
    weight_specs = [
        pl.BlockSpec((1, *shape0), lambda i: (i, 0, 0, 0, 0)),
        pl.BlockSpec((1, *shape1), lambda i: (i, 0, 0, 0, 0)),
        pl.BlockSpec((1, *shape2), lambda i: (i, 0, 0, 0)),
        pl.BlockSpec((lanes, pixels), lambda i: (0, i)),
    ]
    weights = pl.pallas_call(
        functools.partial(prep_kernel, dims),
        out_shape=[
            jax.ShapeDtypeStruct((blocks, *shape0), jnp.bfloat16),
            jax.ShapeDtypeStruct((blocks, *shape1), jnp.bfloat16),
            jax.ShapeDtypeStruct((blocks, *shape2), jnp.bfloat16),
            jax.ShapeDtypeStruct((lanes, blocks * pixels), jnp.float32),
        ],
        grid=(blocks,),
        in_specs=[
            pl.BlockSpec((pixels, width_all), lambda i: (i, 0)),
            pl.BlockSpec((lanes, width_all), lambda i: (0, 0)),
            pl.BlockSpec((lanes, 1), lambda i: (0, 0)),
            pl.BlockSpec((lanes, pixels), lambda i: (0, i)),
        ],
        out_specs=weight_specs,
        scratch_shapes=[
            VMEM((lanes, pixels), jnp.float32),
            VMEM((lanes, pixels), jnp.int32),
            VMEM((lanes, pixels), jnp.float32),
            VMEM((lanes, pixels), jnp.float32),
        ],
        compiler_params=pltpu.CompilerParams(vmem_limit_bytes=PREP_VMEM),
        name="prep",
    )(queries_blocked, logit_weight.T, logit_bias.reshape(lanes, 1), samples_turned)

    rowid = (owner[3] * small + local[3] * sizes[3])[:, None] + jnp.arange(sizes[3], dtype=jnp.int32)
    rowid = rowid.reshape(requests * sizes[3], 1)
    attn = pl.pallas_call(
        functools.partial(attend_kernel, dims, gather, len(sources)),
        out_shape=jax.ShapeDtypeStruct((blocks * pixels, channels), jnp.bfloat16),
        grid=(blocks,),
        in_specs=[pl.BlockSpec(memory_space=space) for space in spaces]
        + weight_specs
        + [pl.BlockSpec((requests * sizes[3], 1), lambda i: (0, 0))],
        out_specs=pl.BlockSpec((pixels, channels), lambda i: (i, 0)),
        scratch_shapes=[
            VMEM((requests, sizes[0], channels), jnp.bfloat16),
            VMEM((requests, sizes[1], channels), jnp.bfloat16),
            VMEM((requests, sizes[2], channels), jnp.bfloat16),
            VMEM((peers, small, channels), jnp.bfloat16),
            VMEM((heads, (sides[0] // 2 + 1) * head_dim, depth0), jnp.bfloat16),
            VMEM((heads, (sides[1] // 2 + 1) * head_dim, depth1), jnp.bfloat16),
            VMEM((channels, depth2), jnp.bfloat16),
            pltpu.SemaphoreType.DMA((LEVELS,)),
        ],
        compiler_params=pltpu.CompilerParams(vmem_limit_bytes=ATTEND_VMEM),
        name="attend",
    )(*sources, *weights, rowid)

    own_head = lax.axis_index("head").reshape(1).astype(jnp.int32)
    other = lax.ppermute(attn, "head", [(0, 1), (1, 0)])
    wide_spec = pl.BlockSpec((pixels, width_all), lambda i: (i, 0))
    slim_spec = pl.BlockSpec((pixels, channels), lambda i: (i, 0))
    matrix_spec = pl.BlockSpec((width_all, width_all), lambda i: (0, 0))
    pre = pl.pallas_call(
        own_kernel,
        out_shape=jax.ShapeDtypeStruct((blocks * pixels, width_all), jnp.float32),
        grid=(blocks,),
        in_specs=[
            pl.BlockSpec(memory_space=SMEM),
            wide_spec,
            slim_spec,
            matrix_spec,
            pl.BlockSpec((1, width_all), lambda i: (0, 0)),
        ],
        out_specs=wide_spec,
        compiler_params=pltpu.CompilerParams(vmem_limit_bytes=SELECT_VMEM),
        name="own",
    )(own_head, queries_blocked, attn, output_weight, output_bias.reshape(1, width_all))
    updated = pl.pallas_call(
        norm_kernel,
        out_shape=jax.ShapeDtypeStruct((blocks * pixels, channels), jnp.bfloat16),
        grid=(blocks,),
        in_specs=[
            pl.BlockSpec(memory_space=SMEM),
            wide_spec,
            slim_spec,
            matrix_spec,
            pl.BlockSpec((1, channels), lambda i: (0, 0)),
            pl.BlockSpec((1, channels), lambda i: (0, 0)),
        ],
        out_specs=slim_spec,
        compiler_params=pltpu.CompilerParams(vmem_limit_bytes=SELECT_VMEM),
        name="norm",
    )(
        own_head,
        pre,
        other,
        output_weight,
        norm_gain.reshape(1, channels),
        norm_shift.reshape(1, channels),
    )
    side = sides[0]
    updated = updated.reshape(tile_rows, tile_cols, side, side, channels).transpose(0, 2, 1, 3, 4)
    return updated.reshape(tile_rows * side, tile_cols * side, channels)


def solution(mesh):
    in_specs = (
        P("row", "col", None),
        P("row", "col", "head"),
        P("row", "col", "head"),
        P("row", "col", "head"),
        P("row", "col", "head"),
        P("row", "col", None, None),
        P("row", "col", "head"),
        P(None, "head"),
        P("head"),
        P(),
        P(),
        P("head"),
        P("head"),
    )
    out_specs = P("row", "col", "head")
    return jax.shard_map(on_device, mesh=mesh, in_specs=in_specs, out_specs=out_specs, check_vma=False)
```

time: 88.9 us -> 83.4 us (0.938)
  the two profiles are of different devices: /device:TPU:17 before, /device:TPU:0 now
where the time goes in v3:
time: 83.4 us; the launch traced here: 83 us
  starting transfers between devices  27.8 us (33%)
  Pallas kernels  22.9 us (27%)
  waiting for transfers between devices  21.6 us (26%)
  local copies, waits for them, and re-layouts  8.6 us (10%)
  other arithmetic  1.8 us (2%)
    ppermute x12, starting transfers between devices, relay_tiles(): lax.ppermute(sent[number - 1], 'row', [(row, source_of(row, number)) for...  14 us
    ppermute x6, waiting for transfers between devices, hop(): arrived[step, side] = lax.ppermute(held, 'col', pairs)  12.4 us
    ppermute x6, starting transfers between devices, hop(): arrived[step, side] = lax.ppermute(held, 'col', pairs)  10.2 us
    ppermute x12, waiting for transfers between devices, relay_tiles(): lax.ppermute(sent[number - 1], 'row', [(row, source_of(row, number)) for...  8.47 us
    pallas_call x1, Pallas kernels, on_device(): pl.pallas_call(functools.partial(attend_kernel, dims, gather, len(sources...  8.39 us
    pallas_call x1, Pallas kernels, on_device(): pl.pallas_call(functools.partial(prep_kernel, dims), out_shape=[jax.Shape...  6.24 us
    pallas_call x4, Pallas kernels, relay_tiles(): pl.pallas_call(functools.partial(relay_select_kernel, (row_count - 1, len...  5.19 us
    unnamed x22, local copies, waits for them, and re-layouts  4.58 us
  transfers between devices with their start and end apart: 22, of which 6 were waited for; matrix products, arithmetic and copies ran while one was open for 6% of the time, Pallas kernels for 15%

profile of v3, /device:TPU:0, one launch (start us, length us, event | category | flops | bytes accessed | tf_op | source)
XLA Modules:
  0.0 83.0 jit_solution(12671740414683010739)
XLA Ops:
  0.0 1.1 %pad_maximum_fusion.refs_3_ = bf16[1360,128]{1,0:T(8,128)(2,1)S(1)} fusion(bf16[16,128]{1,0:T(8,128)(2,1)} %bitcast.44, bf16[64,128]{1,0:T(8,128)(2,1)} %bitcast.42, bf16[256,128]{1,0:T(8,128)(2,1)} %bitcast.40, bf16[1024,128]{1,0:T(8,128)(2,1)} %bitcast.39), kind=kLoop, calls=%fused_computation | loop fusion | flops 1392640 | bytes 696320 | tf_op jit(solution)/shard_map/concatenate | solution.py:379
  1.1 5.0 %collective-permute-start = (bf16[1360,128]{1,0:T(8,128)(2,1)S(1)}, bf16[1360,128]{1,0:T(8,128)(2,1)S(1)}, u32[]{:S(2)}, u32[]{:S(2)}) collective-permute-start(bf16[1360,128]{1,0:T(8,128)(2,1)S(1)} %pad_maximum_fusion.refs_3_), channel_id=1, source_target_pairs={{0,2},{2,4},{4,6},{1,3},{3,5},{5,7},{8,10},{10,12},{12,14},{9,11},... | collective-permute-start | bytes 1044488 | tf_op jit(solution)/shard_map/ppermute | solution.py:389
  6.1 1.3 %collective-permute-start.1 = (bf16[1360,128]{1,0:T(8,128)(2,1)S(1)}, bf16[1360,128]{1,0:T(8,128)(2,1)S(1)}, u32[]{:S(2)}, u32[]{:S(2)}) collective-permute-start(bf16[1360,128]{1,0:T(8,128)(2,1)S(1)} %pad_maximum_fusion.refs_3_), channel_id=1, source_target_pairs={{2,0},{4,2},{6,4},{3,1},{5,3},{7,5},{10,8},{12,10},{14,12},{11,9},... | collective-permute-start | bytes 1044488 | tf_op jit(solution)/shard_map/ppermute | solution.py:389
  7.4 0.7 copy.59
  8.1 0.1 reshape.312
  8.2 0.2 convert_reduce_fusion
  8.5 0.2 select_reduce_fusion
  8.7 0.1 sub.31
  8.8 4.6 %collective-permute-done.refs_3_.refs_4_ = bf16[1360,128]{1,0:T(8,128)(2,1)S(1)} collective-permute-done((bf16[1360,128]{1,0:T(8,128)(2,1)S(1)}, bf16[1360,128]{1,0:T(8,128)(2,1)S(1)}, u32[]{:S(2)}, u32[]{:S(2)}) %collective-permute-start) | collective-permute-done | bytes 348192 | tf_op jit(solution)/shard_map/ppermute | solution.py:389
  13.5 0.7 collective-permute-start.2
  14.1 3.5 %collective-permute-done.1.refs_4_.refs_3_.refs_5_ = bf16[1360,128]{1,0:T(8,128)(2,1)S(1)} collective-permute-done((bf16[1360,128]{1,0:T(8,128)(2,1)S(1)}, bf16[1360,128]{1,0:T(8,128)(2,1)S(1)}, u32[]{:S(2)}, u32[]{:S(2)}) %collective-permute-start.1) | collective-permute-done | bytes 348192 | tf_op jit(solution)/shard_map/ppermute | solution.py:389
  17.6 1.3 %collective-permute-start.3 = (bf16[1360,128]{1,0:T(8,128)(2,1)S(1)}, bf16[1360,128]{1,0:T(8,128)(2,1)S(1)}, u32[]{:S(2)}, u32[]{:S(2)}) collective-permute-start(bf16[1360,128]{1,0:T(8,128)(2,1)S(1)} %collective-permute-done.1.refs_4_.refs_3_.refs_5_), channel_id=1, source_target_pairs={{2,0},{4,2},{3,1},{5,3},{10,8},{12,10},{11,9},{13,11},{18,16},{20,... | collective-permute-start | bytes 1044488 | tf_op jit(solution)/shard_map/ppermute | solution.py:389
  18.9 0.1 copy.66
  19.0 1.5 %collective-permute-start.6 = (s32[4,8]{1,0:T(4,128)S(1)}, s32[4,8]{1,0:T(4,128)S(1)}, u32[]{:S(2)}, u32[]{:S(2)}) collective-permute-start(s32[4,8]{1,0:T(4,128)S(1)} %bitcast.45), channel_id=1, source_target_pairs={{0,8},{8,0},{16,24},{24,16},{1,9},{9,1},{17,25},{25,17},{2,10},{10... | collective-permute-start | bytes 392 | tf_op jit(solution)/shard_map/ppermute | solution.py:396
  20.5 0.1 copy.67
  20.6 1.5 %collective-permute-start.7 = (s32[4,8]{1,0:T(4,128)S(1)}, s32[4,8]{1,0:T(4,128)S(1)}, u32[]{:S(2)}, u32[]{:S(2)}) collective-permute-start(s32[4,8]{1,0:T(4,128)S(1)} %bitcast.46), channel_id=1, source_target_pairs={{0,16},{8,24},{16,0},{24,8},{1,17},{9,25},{17,1},{25,9},{2,18},{10... | collective-permute-start | bytes 392 | tf_op jit(solution)/shard_map/ppermute | solution.py:396
  22.1 0.1 copy.68
  22.2 0.5 collective-permute-start.8
  22.7 0.7 dynamic-slice_bitcast_fusion
  23.4 0.7 collective-permute-start.4
  24.0 4.3 %collective-permute-done.3.refs_5_.refs_4_.refs_7_ = bf16[1360,128]{1,0:T(8,128)(2,1)S(1)} collective-permute-done((bf16[1360,128]{1,0:T(8,128)(2,1)S(1)}, bf16[1360,128]{1,0:T(8,128)(2,1)S(1)}, u32[]{:S(2)}, u32[]{:S(2)}) %collective-permute-start.3) | collective-permute-done | bytes 348192 | tf_op jit(solution)/shard_map/ppermute | solution.py:389
  28.4 1.3 %collective-permute-start.5 = (bf16[1360,128]{1,0:T(8,128)(2,1)S(1)}, bf16[1360,128]{1,0:T(8,128)(2,1)S(1)}, u32[]{:S(2)}, u32[]{:S(2)}) collective-permute-start(bf16[1360,128]{1,0:T(8,128)(2,1)S(1)} %collective-permute-done.3.refs_5_.refs_4_.refs_7_), channel_id=1, source_target_pairs={{2,0},{3,1},{10,8},{11,9},{18,16},{19,17},{26,24},{27,25}} | collective-permute-start | bytes 1044488 | tf_op jit(solution)/shard_map/ppermute | solution.py:389
  29.7 0.1 add_bitcast_fusion
  29.7 0.1 copy.60
  29.8 0.1 copy.65
  29.9 0.7 copy.70.bias_ref
  30.6 1.2 %copy.69 = s32[1024,64]{0,1:T(8,128)S(1)} copy(s32[1024,64]{1,0:T(8,128)} %bitcast.38) | data formatting | bytes 524288 | tf_op jit(solution)/shard_map/reshape;reshape;transpose;reshape | solution.py:535
  31.9 0.0 collective-permute-done.7.refs_1_
  31.9 0.0 collective-permute-done.8.refs_2_
  31.9 1.4 %shard_map.136 = (bf16[688,128]{1,0:T(8,128)(2,1)S(1)}, bf16[688,128]{1,0:T(8,128)(2,1)S(1)}, bf16[688,128]{1,0:T(8,128)(2,1)}) custom-call(s32[5,2]{1,0:T(8,128)S(1)} %pad_add_fusion.plan_ref.refs_1_, s32[4,8]{1,0:T(4,128)S(1)} %collective-permute-done.6.refs_0_, s32[4,8]{1,0:T(4,128)S(1)} %collective-permute-done.7.refs_1_, ...), custom_call_target="tpu_custom_call" | custom-call | tf_op jit(solution)/shard_map/pallas_call | solution.py:417
  33.3 1.5 %collective-permute-start.9 = (bf16[688,128]{1,0:T(8,128)(2,1)S(1)}, bf16[688,128]{1,0:T(8,128)(2,1)S(1)}, u32[]{:S(2)}, u32[]{:S(2)}) collective-permute-start(bf16[688,128]{1,0:T(8,128)(2,1)S(1)} %get-tuple-element.21), channel_id=1, source_target_pairs={{0,8},{8,0},{16,24},{24,16},{1,9},{9,1},{17,25},{25,17},{2,10},{10... | collective-permute-start | bytes 528392 | tf_op jit(solution)/shard_map/ppermute | solution.py:429
  34.8 1.5 %collective-permute-start.10 = (bf16[688,128]{1,0:T(8,128)(2,1)S(1)}, bf16[688,128]{1,0:T(8,128)(2,1)S(1)}, u32[]{:S(2)}, u32[]{:S(2)}) collective-permute-start(bf16[688,128]{1,0:T(8,128)(2,1)S(1)} %get-tuple-element.22), channel_id=1, source_target_pairs={{0,16},{8,24},{16,0},{24,8},{1,17},{9,25},{17,1},{25,9},{2,18},{10... | collective-permute-start | bytes 528392 | tf_op jit(solution)/shard_map/ppermute | solution.py:429
  36.3 0.5 collective-permute-start.11
  36.8 1.6 %shard_map.137 = (bf16[688,128]{1,0:T(8,128)(2,1)}, bf16[688,128]{1,0:T(8,128)(2,1)}, bf16[688,128]{1,0:T(8,128)(2,1)}) custom-call(s32[5,2]{1,0:T(8,128)S(1)} %pad_add_fusion.plan_ref.refs_1_, s32[4,8]{1,0:T(4,128)S(1)} %collective-permute-done.6.refs_0_, s32[4,8]{1,0:T(4,128)S(1)} %collective-permute-done.7.refs_1_, ...), custom_call_target="tpu_custom_call" | custom-call | tf_op jit(solution)/shard_map/pallas_call | solution.py:417
  38.4 1.4 %shard_map.138 = (bf16[688,128]{1,0:T(8,128)(2,1)}, bf16[688,128]{1,0:T(8,128)(2,1)S(1)}, bf16[688,128]{1,0:T(8,128)(2,1)S(1)}) custom-call(s32[5,2]{1,0:T(8,128)S(1)} %pad_add_fusion.plan_ref.refs_1_, s32[4,8]{1,0:T(4,128)S(1)} %collective-permute-done.6.refs_0_, s32[4,8]{1,0:T(4,128)S(1)} %collective-permute-done.7.refs_1_, ...), custom_call_target="tpu_custom_call" | custom-call | tf_op jit(solution)/shard_map/pallas_call | solution.py:417
  39.8 0.7 copy-done.10
  40.5 0.0 collective-permute-done.9.refs_10_
  40.5 0.7 copy-done.2
  41.1 1.5 %collective-permute-start.12 = (bf16[688,128]{1,0:T(8,128)(2,1)}, bf16[688,128]{1,0:T(8,128)(2,1)}, u32[]{:S(2)}, u32[]{:S(2)}) collective-permute-start(bf16[688,128]{1,0:T(8,128)(2,1)} %get-tuple-element.24), channel_id=1, source_target_pairs={{0,8},{8,0},{16,24},{24,16},{1,9},{9,1},{17,25},{25,17},{2,10},{10... | collective-permute-start | bytes 528392 | tf_op jit(solution)/shard_map/ppermute | solution.py:429
  42.6 0.7 copy-done.4
  43.3 1.5 %collective-permute-start.13 = (bf16[688,128]{1,0:T(8,128)(2,1)}, bf16[688,128]{1,0:T(8,128)(2,1)}, u32[]{:S(2)}, u32[]{:S(2)}) collective-permute-start(bf16[688,128]{1,0:T(8,128)(2,1)} %get-tuple-element.25), channel_id=1, source_target_pairs={{0,16},{8,24},{16,0},{24,8},{1,17},{9,25},{17,1},{25,9},{2,18},{10... | collective-permute-start | bytes 528392 | tf_op jit(solution)/shard_map/ppermute | solution.py:429
  44.8 0.0 collective-permute-done.4.refs_5_.refs_8_
  44.8 0.5 collective-permute-start.14
  45.3 1.5 %collective-permute-start.15 = (bf16[688,128]{1,0:T(8,128)(2,1)}, bf16[688,128]{1,0:T(8,128)(2,1)}, u32[]{:S(2)}, u32[]{:S(2)}) collective-permute-start(bf16[688,128]{1,0:T(8,128)(2,1)} %get-tuple-element.27), channel_id=1, source_target_pairs={{0,8},{8,0},{16,24},{24,16},{1,9},{9,1},{17,25},{25,17},{2,10},{10... | collective-permute-start | bytes 528392 | tf_op jit(solution)/shard_map/ppermute | solution.py:429
  46.8 0.1 iota_add_fusion
  46.9 0.1 add.182.refs_26_
  46.9 0.0 copy-start.6
  46.9 0.8 copy-done.6
  47.7 6.2 %prep.1 = (bf16[4,4,4,256,256]{4,3,2,1,0:T(8,128)(2,1)S(1)}, bf16[4,4,4,128,256]{4,3,2,1,0:T(8,128)(2,1)S(1)}, bf16[4,4,256,256]{3,2,1,0:T(8,128)(2,1)S(1)}, f32[64,1024]{1,0:T(8,128)S(1)}) custom-call(bf16[1024,256]{1,0:T(8,128)(2,1)S(1)} %bitcast.31, bf16[64,256]{1,0:T(8,128)(2,1)S(1)} %bitcast.34, f32[64,1]{1,0:T(8,128)S(1)} %copy.70.bias_ref, ...), custom_call_target="tpu_custom_call" | custom-call | tf_op jit(solution)/shard_map/prep/pallas_call | solution.py:548
  53.9 0.8 shard_map.139
  54.7 1.6 %collective-permute-start.16 = (bf16[688,128]{1,0:T(8,128)(2,1)}, bf16[688,128]{1,0:T(8,128)(2,1)S(1)}, u32[]{:S(2)}, u32[]{:S(2)}) collective-permute-start(bf16[688,128]{1,0:T(8,128)(2,1)} %copy-done.10), channel_id=1, source_target_pairs={{0,16},{8,24},{16,0},{24,8},{1,17},{9,25},{17,1},{25,9},{2,18},{10... | collective-permute-start | bytes 528392 | tf_op jit(solution)/shard_map/ppermute | solution.py:429
  56.3 0.5 collective-permute-start.17
  56.8 1.5 %collective-permute-start.18 = (bf16[688,128]{1,0:T(8,128)(2,1)S(1)}, bf16[688,128]{1,0:T(8,128)(2,1)S(1)}, u32[]{:S(2)}, u32[]{:S(2)}) collective-permute-start(bf16[688,128]{1,0:T(8,128)(2,1)S(1)} %get-tuple-element.30), channel_id=1, source_target_pairs={{0,8},{8,0},{16,24},{24,16},{1,9},{9,1},{17,25},{25,17},{2,10},{10... | collective-permute-start | bytes 528392 | tf_op jit(solution)/shard_map/ppermute | solution.py:429
  58.3 1.5 %collective-permute-start.19 = (bf16[688,128]{1,0:T(8,128)(2,1)S(1)}, bf16[688,128]{1,0:T(8,128)(2,1)S(1)}, u32[]{:S(2)}, u32[]{:S(2)}) collective-permute-start(bf16[688,128]{1,0:T(8,128)(2,1)S(1)} %get-tuple-element.31), channel_id=1, source_target_pairs={{0,16},{8,24},{16,0},{24,8},{1,17},{9,25},{17,1},{25,9},{2,18},{10... | collective-permute-start | bytes 528392 | tf_op jit(solution)/shard_map/ppermute | solution.py:429
  59.8 0.5 collective-permute-start.20
  60.3 5.7 %collective-permute-done.16.refs_17_ = bf16[688,128]{1,0:T(8,128)(2,1)S(1)} collective-permute-done((bf16[688,128]{1,0:T(8,128)(2,1)}, bf16[688,128]{1,0:T(8,128)(2,1)S(1)}, u32[]{:S(2)}, u32[]{:S(2)}) %collective-permute-start.16) | collective-permute-done | bytes 176160 | tf_op jit(solution)/shard_map/ppermute | solution.py:429
  66.0 2.8 %collective-permute-done.19.refs_20_ = bf16[688,128]{1,0:T(8,128)(2,1)S(1)} collective-permute-done((bf16[688,128]{1,0:T(8,128)(2,1)S(1)}, bf16[688,128]{1,0:T(8,128)(2,1)S(1)}, u32[]{:S(2)}, u32[]{:S(2)}) %collective-permute-start.19) | collective-permute-done | bytes 176160 | tf_op jit(solution)/shard_map/ppermute | solution.py:429
  68.8 0.9 %copy-done.3 = bf16[688,128]{1,0:T(8,128)(2,1)S(1)} copy-done((bf16[688,128]{1,0:T(8,128)(2,1)S(1)}, bf16[688,128]{1,0:T(8,128)(2,1)}, u32[]{:S(2)}) %copy-start.3) | copy-done | bytes 176152
  69.7 0.9 %copy-done.5 = bf16[688,128]{1,0:T(8,128)(2,1)S(1)} copy-done((bf16[688,128]{1,0:T(8,128)(2,1)S(1)}, bf16[688,128]{1,0:T(8,128)(2,1)}, u32[]{:S(2)}) %copy-start.5) | copy-done | bytes 176152
  70.6 8.4 %attend.1.own_ref = bf16[1024,128]{1,0:T(8,128)(2,1)S(1)} custom-call(s32[16,8]{1,0:T(8,128)S(1)} %get-tuple-element.43.refs_0_, s32[5,2]{1,0:T(8,128)S(1)} %pad_add_fusion.plan_ref.refs_1_, s32[16,8]{1,0:T(8,128)S(1)} %get-tuple-element.42.refs_2_, bf16[1360,128]{1,0:T(8,128)(2,1)S(1)} %pad_maximum_fusion.refs_3_, ...), custom_call_target="tpu_custom_call" | custom-call | tf_op jit(solution)/shard_map/attend/pallas_call | solution.py:576
  79.0 0.1 collective-permute-start.21
  79.1 0.8 own.1.pre_ref
  79.9 0.7 collective-permute-done.21.other_ref
  80.6 2.3 %norm.1 = bf16[1024,128]{1,0:T(8,128)(2,1)} custom-call(s32[1]{0:T(128)} %bitcast.head_ref, f32[1024,256]{1,0:T(8,128)S(1)} %own.1.pre_ref, bf16[1024,128]{1,0:T(8,128)(2,1)S(1)} %collective-permute-done.21.other_ref, bf16[256,256]{1,0:T(8,128)(2,1)S(1)} %copy-done.1, f32[1,128]{1,0:T(1,128)S(1)} %bitcast.36, f32[1,128]{1,0:T(1,128)S(1)} %bitcast.37), custom_call_target="tpu_custom_call" | custom-call | tf_op jit(solution)/shard_map/norm/pallas_call | solution.py:618
  (38 shorter events, 0.2 us)
Async XLA Ops:
  0.0 46.9 %copy-start = (bf16[64,16,256]{2,1,0:T(8,128)(2,1)S(1)}, bf16[64,16,256]{2,1,0:T(8,128)(2,1)}, u32[]{:S(2)}) copy-start(bf16[64,16,256]{2,1,0:T(8,128)(2,1)} %param.14) | copy-start | bytes 1572868
  1.1 12.4 %collective-permute-start = (bf16[1360,128]{1,0:T(8,128)(2,1)S(1)}, bf16[1360,128]{1,0:T(8,128)(2,1)S(1)}, u32[]{:S(2)}, u32[]{:S(2)}) collective-permute-start(bf16[1360,128]{1,0:T(8,128)(2,1)S(1)} %pad_maximum_fusion.refs_3_), channel_id=1, source_target_pairs={{0,2},{2,4},{4,6},{1,3},{3,5},{5,7},{8,10},{10,12},{12,14},{9,11},... | collective-permute-start | bytes 1044488 | tf_op jit(solution)/shard_map/ppermute | solution.py:389
  6.1 11.5 %collective-permute-start.1 = (bf16[1360,128]{1,0:T(8,128)(2,1)S(1)}, bf16[1360,128]{1,0:T(8,128)(2,1)S(1)}, u32[]{:S(2)}, u32[]{:S(2)}) collective-permute-start(bf16[1360,128]{1,0:T(8,128)(2,1)S(1)} %pad_maximum_fusion.refs_3_), channel_id=1, source_target_pairs={{2,0},{4,2},{6,4},{3,1},{5,3},{7,5},{10,8},{12,10},{14,12},{11,9},... | collective-permute-start | bytes 1044488 | tf_op jit(solution)/shard_map/ppermute | solution.py:389
  13.5 9.9 %collective-permute-start.2 = (bf16[1360,128]{1,0:T(8,128)(2,1)S(1)}, bf16[1360,128]{1,0:T(8,128)(2,1)S(1)}, u32[]{:S(2)}, u32[]{:S(2)}) collective-permute-start(bf16[1360,128]{1,0:T(8,128)(2,1)S(1)} %collective-permute-done.refs_3_.refs_4_), channel_id=1, source_target_pairs={{2,4},{4,6},{3,5},{5,7},{10,12},{12,14},{11,13},{13,15},{18,20},{2... | collective-permute-start | bytes 1044488 | tf_op jit(solution)/shard_map/ppermute | solution.py:389
  17.6 10.8 %collective-permute-start.3 = (bf16[1360,128]{1,0:T(8,128)(2,1)S(1)}, bf16[1360,128]{1,0:T(8,128)(2,1)S(1)}, u32[]{:S(2)}, u32[]{:S(2)}) collective-permute-start(bf16[1360,128]{1,0:T(8,128)(2,1)S(1)} %collective-permute-done.1.refs_4_.refs_3_.refs_5_), channel_id=1, source_target_pairs={{2,0},{4,2},{3,1},{5,3},{10,8},{12,10},{11,9},{13,11},{18,16},{20,... | collective-permute-start | bytes 1044488 | tf_op jit(solution)/shard_map/ppermute | solution.py:389
  19.0 12.9 %collective-permute-start.6 = (s32[4,8]{1,0:T(4,128)S(1)}, s32[4,8]{1,0:T(4,128)S(1)}, u32[]{:S(2)}, u32[]{:S(2)}) collective-permute-start(s32[4,8]{1,0:T(4,128)S(1)} %bitcast.45), channel_id=1, source_target_pairs={{0,8},{8,0},{16,24},{24,16},{1,9},{9,1},{17,25},{25,17},{2,10},{10... | collective-permute-start | bytes 392 | tf_op jit(solution)/shard_map/ppermute | solution.py:396
  20.6 11.3 %collective-permute-start.7 = (s32[4,8]{1,0:T(4,128)S(1)}, s32[4,8]{1,0:T(4,128)S(1)}, u32[]{:S(2)}, u32[]{:S(2)}) collective-permute-start(s32[4,8]{1,0:T(4,128)S(1)} %bitcast.46), channel_id=1, source_target_pairs={{0,16},{8,24},{16,0},{24,8},{1,17},{9,25},{17,1},{25,9},{2,18},{10... | collective-permute-start | bytes 392 | tf_op jit(solution)/shard_map/ppermute | solution.py:396
  22.2 9.7 %collective-permute-start.8 = (s32[4,8]{1,0:T(4,128)S(1)}, s32[4,8]{1,0:T(4,128)S(1)}, u32[]{:S(2)}, u32[]{:S(2)}) collective-permute-start(s32[4,8]{1,0:T(4,128)S(1)} %bitcast.47), channel_id=1, source_target_pairs={{0,24},{8,16},{16,8},{24,0},{1,25},{9,17},{17,9},{25,1},{2,26},{10... | collective-permute-start | bytes 392 | tf_op jit(solution)/shard_map/ppermute | solution.py:396
  23.4 21.5 %collective-permute-start.4 = (bf16[1360,128]{1,0:T(8,128)(2,1)S(1)}, bf16[1360,128]{1,0:T(8,128)(2,1)S(1)}, u32[]{:S(2)}, u32[]{:S(2)}) collective-permute-start(bf16[1360,128]{1,0:T(8,128)(2,1)S(1)} %collective-permute-done.2.refs_4_.refs_3_.refs_6_), channel_id=1, source_target_pairs={{4,6},{5,7},{12,14},{13,15},{20,22},{21,23},{28,30},{29,31}} | collective-permute-start | bytes 1044488 | tf_op jit(solution)/shard_map/ppermute | solution.py:389
  28.4 16.9 %collective-permute-start.5 = (bf16[1360,128]{1,0:T(8,128)(2,1)S(1)}, bf16[1360,128]{1,0:T(8,128)(2,1)S(1)}, u32[]{:S(2)}, u32[]{:S(2)}) collective-permute-start(bf16[1360,128]{1,0:T(8,128)(2,1)S(1)} %collective-permute-done.3.refs_5_.refs_4_.refs_7_), channel_id=1, source_target_pairs={{2,0},{3,1},{10,8},{11,9},{18,16},{19,17},{26,24},{27,25}} | collective-permute-start | bytes 1044488 | tf_op jit(solution)/shard_map/ppermute | solution.py:389
  33.3 7.2 %collective-permute-start.9 = (bf16[688,128]{1,0:T(8,128)(2,1)S(1)}, bf16[688,128]{1,0:T(8,128)(2,1)S(1)}, u32[]{:S(2)}, u32[]{:S(2)}) collective-permute-start(bf16[688,128]{1,0:T(8,128)(2,1)S(1)} %get-tuple-element.21), channel_id=1, source_target_pairs={{0,8},{8,0},{16,24},{24,16},{1,9},{9,1},{17,25},{25,17},{2,10},{10... | collective-permute-start | bytes 528392 | tf_op jit(solution)/shard_map/ppermute | solution.py:429
  34.8 7.8 %collective-permute-start.10 = (bf16[688,128]{1,0:T(8,128)(2,1)S(1)}, bf16[688,128]{1,0:T(8,128)(2,1)S(1)}, u32[]{:S(2)}, u32[]{:S(2)}) collective-permute-start(bf16[688,128]{1,0:T(8,128)(2,1)S(1)} %get-tuple-element.22), channel_id=1, source_target_pairs={{0,16},{8,24},{16,0},{24,8},{1,17},{9,25},{17,1},{25,9},{2,18},{10... | collective-permute-start | bytes 528392 | tf_op jit(solution)/shard_map/ppermute | solution.py:429
  36.3 18.4 %collective-permute-start.11 = (bf16[688,128]{1,0:T(8,128)(2,1)}, bf16[688,128]{1,0:T(8,128)(2,1)}, u32[]{:S(2)}, u32[]{:S(2)}) collective-permute-start(bf16[688,128]{1,0:T(8,128)(2,1)} %get-tuple-element.23), channel_id=1, source_target_pairs={{0,24},{8,16},{16,8},{24,0},{1,25},{9,17},{17,9},{25,1},{2,26},{10... | collective-permute-start | bytes 528392 | tf_op jit(solution)/shard_map/ppermute | solution.py:429
  39.8 0.7 copy-start.10
  40.5 0.7 copy-start.2
  41.1 15.2 %collective-permute-start.12 = (bf16[688,128]{1,0:T(8,128)(2,1)}, bf16[688,128]{1,0:T(8,128)(2,1)}, u32[]{:S(2)}, u32[]{:S(2)}) collective-permute-start(bf16[688,128]{1,0:T(8,128)(2,1)} %get-tuple-element.24), channel_id=1, source_target_pairs={{0,8},{8,0},{16,24},{24,16},{1,9},{9,1},{17,25},{25,17},{2,10},{10... | collective-permute-start | bytes 528392 | tf_op jit(solution)/shard_map/ppermute | solution.py:429
  42.6 0.7 copy-start.4
  43.3 13.5 %collective-permute-start.13 = (bf16[688,128]{1,0:T(8,128)(2,1)}, bf16[688,128]{1,0:T(8,128)(2,1)}, u32[]{:S(2)}, u32[]{:S(2)}) collective-permute-start(bf16[688,128]{1,0:T(8,128)(2,1)} %get-tuple-element.25), channel_id=1, source_target_pairs={{0,16},{8,24},{16,0},{24,8},{1,17},{9,25},{17,1},{25,9},{2,18},{10... | collective-permute-start | bytes 528392 | tf_op jit(solution)/shard_map/ppermute | solution.py:429
  44.8 13.5 %collective-permute-start.14 = (bf16[688,128]{1,0:T(8,128)(2,1)}, bf16[688,128]{1,0:T(8,128)(2,1)}, u32[]{:S(2)}, u32[]{:S(2)}) collective-permute-start(bf16[688,128]{1,0:T(8,128)(2,1)} %get-tuple-element.26), channel_id=1, source_target_pairs={{0,24},{8,16},{16,8},{24,0},{1,25},{9,17},{17,9},{25,1},{2,26},{10... | collective-permute-start | bytes 528392 | tf_op jit(solution)/shard_map/ppermute | solution.py:429
  45.3 14.5 %collective-permute-start.15 = (bf16[688,128]{1,0:T(8,128)(2,1)}, bf16[688,128]{1,0:T(8,128)(2,1)}, u32[]{:S(2)}, u32[]{:S(2)}) collective-permute-start(bf16[688,128]{1,0:T(8,128)(2,1)} %get-tuple-element.27), channel_id=1, source_target_pairs={{0,8},{8,0},{16,24},{24,16},{1,9},{9,1},{17,25},{25,17},{2,10},{10... | collective-permute-start | bytes 528392 | tf_op jit(solution)/shard_map/ppermute | solution.py:429
  46.9 0.8 copy-start.6
  54.7 11.2 %collective-permute-start.16 = (bf16[688,128]{1,0:T(8,128)(2,1)}, bf16[688,128]{1,0:T(8,128)(2,1)S(1)}, u32[]{:S(2)}, u32[]{:S(2)}) collective-permute-start(bf16[688,128]{1,0:T(8,128)(2,1)} %copy-done.10), channel_id=1, source_target_pairs={{0,16},{8,24},{16,0},{24,8},{1,17},{9,25},{17,1},{25,9},{2,18},{10... | collective-permute-start | bytes 528392 | tf_op jit(solution)/shard_map/ppermute | solution.py:429
  56.3 9.7 %collective-permute-start.17 = (bf16[688,128]{1,0:T(8,128)(2,1)S(1)}, bf16[688,128]{1,0:T(8,128)(2,1)S(1)}, u32[]{:S(2)}, u32[]{:S(2)}) collective-permute-start(bf16[688,128]{1,0:T(8,128)(2,1)S(1)} %get-tuple-element.29), channel_id=1, source_target_pairs={{0,24},{8,16},{16,8},{24,0},{1,25},{9,17},{17,9},{25,1},{2,26},{10... | collective-permute-start | bytes 528392 | tf_op jit(solution)/shard_map/ppermute | solution.py:429
  56.8 9.2 %collective-permute-start.18 = (bf16[688,128]{1,0:T(8,128)(2,1)S(1)}, bf16[688,128]{1,0:T(8,128)(2,1)S(1)}, u32[]{:S(2)}, u32[]{:S(2)}) collective-permute-start(bf16[688,128]{1,0:T(8,128)(2,1)S(1)} %get-tuple-element.30), channel_id=1, source_target_pairs={{0,8},{8,0},{16,24},{24,16},{1,9},{9,1},{17,25},{25,17},{2,10},{10... | collective-permute-start | bytes 528392 | tf_op jit(solution)/shard_map/ppermute | solution.py:429
  58.3 10.5 %collective-permute-start.19 = (bf16[688,128]{1,0:T(8,128)(2,1)S(1)}, bf16[688,128]{1,0:T(8,128)(2,1)S(1)}, u32[]{:S(2)}, u32[]{:S(2)}) collective-permute-start(bf16[688,128]{1,0:T(8,128)(2,1)S(1)} %get-tuple-element.31), channel_id=1, source_target_pairs={{0,16},{8,24},{16,0},{24,8},{1,17},{9,25},{17,1},{25,9},{2,18},{10... | collective-permute-start | bytes 528392 | tf_op jit(solution)/shard_map/ppermute | solution.py:429
  59.8 8.9 %collective-permute-start.20 = (bf16[688,128]{1,0:T(8,128)(2,1)S(1)}, bf16[688,128]{1,0:T(8,128)(2,1)S(1)}, u32[]{:S(2)}, u32[]{:S(2)}) collective-permute-start(bf16[688,128]{1,0:T(8,128)(2,1)S(1)} %get-tuple-element.32), channel_id=1, source_target_pairs={{0,24},{8,16},{16,8},{24,0},{1,25},{9,17},{17,9},{25,1},{2,26},{10... | collective-permute-start | bytes 528392 | tf_op jit(solution)/shard_map/ppermute | solution.py:429
  68.8 0.9 %copy-start.3 = (bf16[688,128]{1,0:T(8,128)(2,1)S(1)}, bf16[688,128]{1,0:T(8,128)(2,1)}, u32[]{:S(2)}) copy-start(bf16[688,128]{1,0:T(8,128)(2,1)} %copy-done.2) | copy-start | bytes 528388
  69.7 0.9 %copy-start.5 = (bf16[688,128]{1,0:T(8,128)(2,1)S(1)}, bf16[688,128]{1,0:T(8,128)(2,1)}, u32[]{:S(2)}) copy-start(bf16[688,128]{1,0:T(8,128)(2,1)} %copy-done.4) | copy-start | bytes 528388
  70.6 8.5 %copy-start.1 = (bf16[256,256]{1,0:T(8,128)(2,1)S(1)}, bf16[256,256]{1,0:T(8,128)(2,1)}, u32[]{:S(2)}) copy-start(bf16[256,256]{1,0:T(8,128)(2,1)} %weight_ref.3) | copy-start | bytes 393220
  70.6 8.5 %copy-start.7 = (f32[256]{0:T(256)S(1)}, f32[256]{0:T(256)}, u32[]{:S(2)}) copy-start(f32[256]{0:T(256)} %param.24) | copy-start | bytes 3076
  70.6 10.0 %copy-start.8 = (f32[128]{0:T(128)S(1)}, f32[128]{0:T(128)}, u32[]{:S(2)}) copy-start(f32[128]{0:T(128)} %param.25) | copy-start | bytes 1540
  70.6 10.0 %copy-start.9 = (f32[128]{0:T(128)S(1)}, f32[128]{0:T(128)}, u32[]{:S(2)}) copy-start(f32[128]{0:T(128)} %param.26) | copy-start | bytes 1540
  79.0 1.6 %collective-permute-start.21 = (bf16[1024,128]{1,0:T(8,128)(2,1)S(1)}, bf16[1024,128]{1,0:T(8,128)(2,1)S(1)}, u32[]{:S(2)}, u32[]{:S(2)}) collective-permute-start(bf16[1024,128]{1,0:T(8,128)(2,1)S(1)} %attend.1.own_ref), channel_id=1, source_target_pairs={{0,1},{1,0},{2,3},{3,2},{4,5},{5,4},{6,7},{7,6},{8,9},{9,8},{10,11... | collective-permute-start | bytes 786440 | tf_op jit(solution)/shard_map/ppermute | solution.py:599

commit v4 on v3

v4 whole, which is shorter than its diff:
```python
import functools
import jax
import jax.numpy as jnp
from jax import lax
from jax.experimental import pallas as pl
from jax.experimental.pallas import tpu as pltpu
from jax.sharding import PartitionSpec as P

LEVELS = 4
POINTS = 4
ANY = pl.ANY
SMEM = pltpu.SMEM
VMEM = pltpu.VMEM
SELECT_VMEM = 4 * 1024 * 1024
PREP_VMEM = 8 * 1024 * 1024
ATTEND_VMEM = 12 * 1024 * 1024
GROUPS = (2, 4)


def to_blocks(source, tile_rows, tile_cols, tile_side):
    channels = source.shape[2]
    shaped = source.reshape(tile_rows, tile_side, tile_cols, tile_side, channels)
    return shaped.transpose(0, 2, 1, 3, 4).reshape(
        tile_rows * tile_cols, tile_side * tile_side, channels
    )


def hat(position, center):
    return jnp.maximum(1.0 - jnp.abs(position - center), 0.0)


def iota(shape, dim):
    return lax.broadcasted_iota(jnp.int32, shape, dim)


def prep_kernel(
    dims,
    query_hbm,
    logit_hbm,
    bias_hbm,
    sample_hbm,
    weight1,
    weight2,
    attend_ref,
    code_ref,
    down_ref,
    col_ref,
    query_ref,
    logit_ref,
    bias_ref,
    sample_ref,
    sem,
):
    _, _, sizes, sides, per_block, heads, _, blocks = dims
    pixels = sizes[0]
    base2 = per_block * sizes[2]
    lanes = LEVELS * POINTS
    moves = [
        pltpu.make_async_copy(source, target, sem.at[number])
        for number, (source, target) in enumerate(
            (
                (query_hbm, query_ref),
                (logit_hbm, logit_ref),
                (bias_hbm, bias_ref),
                (sample_hbm, sample_ref),
            )
        )
    ]
    for move in moves:
        move.start()
    weight2[...] = jnp.zeros_like(weight2)
    for move in moves:
        move.wait()

    def one(block, carry):
        here = pl.ds(pl.multiple_of(block * pixels, pixels), pixels)
        logits = lax.dot_general(
            query_ref[here, :], logit_ref[...], (((1,), (1,)), ((), ())), preferred_element_type=jnp.float32
        )
        logits = (logits + bias_ref[...]).T
        for head in range(heads):
            part = logits[head * lanes : (head + 1) * lanes, :]
            part = jnp.exp(part - jnp.max(part, axis=0, keepdims=True))
            attend_ref[block, head * lanes : (head + 1) * lanes, :] = part / jnp.sum(
                part, axis=0, keepdims=True
            )
        packed = sample_ref[here, :].T
        level_of = iota(packed.shape, 0) // POINTS % LEVELS
        slot = packed >> 24
        pos_row = (packed >> 12) & 4095
        pos_col = packed & 4095
        deep = jnp.where(level_of == 0, sides[0] * 128, sides[1] * 256 // GROUPS[1])
        group = jnp.where(level_of < 2, pos_row // deep, 0)
        code_ref[block] = slot + group * per_block
        down_ref[block] = (pos_row - group * deep).astype(jnp.float32) * (1.0 / 256.0)
        col_ref[block] = pos_col.astype(jnp.float32) * (1.0 / 256.0)

        for head in range(heads):
            hot_rows(1, block, head, sides, per_block, attend_ref, code_ref, col_ref, weight1)
            side = sides[2]
            size = sizes[2]
            place = iota((size, pixels), 0)
            parts = []
            codes = []
            for point in range(POINTS):
                row = (head * LEVELS + 2) * POINTS + point
                line = slice(row, row + 1)
                parts.append(
                    attend_ref[block, line, :]
                    * hat(down_ref[block, line, :], (place // side).astype(jnp.float32))
                    * hat(col_ref[block, line, :], (place % side).astype(jnp.float32))
                )
                codes.append(code_ref[block, line, :])
            for index in range(per_block):
                mixed = jnp.zeros((size, pixels), jnp.float32)
                for point in range(POINTS):
                    mixed = mixed + jnp.where(codes[point] == index, parts[point], 0.0)
                weight2[block, head, index * size : (index + 1) * size, :] = mixed.astype(jnp.bfloat16)
            side = sides[3]
            size = sizes[3]
            depth = per_block * size
            place = iota((depth, pixels), 0)
            mixed = jnp.zeros((depth, pixels), jnp.float32)
            for point in range(POINTS):
                row = (head * LEVELS + 3) * POINTS + point
                line = slice(row, row + 1)
                value = (
                    attend_ref[block, line, :]
                    * hat(down_ref[block, line, :], (place % size // side).astype(jnp.float32))
                    * hat(col_ref[block, line, :], (place % side).astype(jnp.float32))
                )
                mixed = mixed + jnp.where(code_ref[block, line, :] == place // size, value, 0.0)
            weight2[block, head, pl.ds(pl.multiple_of(base2 + block * depth, depth), depth), :] = mixed.astype(
                jnp.bfloat16
            )
        return carry

    lax.fori_loop(0, blocks, one, 0)


def hot_rows(level, block, head, sides, per_block, attend_ref, code_ref, col_ref, weight):
    side = sides[level]
    pixels = attend_ref.shape[2]
    step = 16 // side
    for point in range(POINTS):
        row = (head * LEVELS + level) * POINTS + point
        line = slice(row, row + 1)
        code = code_ref[block, line, :]
        across = attend_ref[block, line, :] * hat(
            col_ref[block, line, :], (iota((16, pixels), 0) % side).astype(jnp.float32)
        )
        for index in range(0, GROUPS[level] * per_block, step):
            wanted = index + iota((16, pixels), 0) // side
            weight[block, head, point, index * side : (index + step) * side, :] = jnp.where(
                code == wanted, across, 0.0
            ).astype(jnp.bfloat16)


def hot_kernel(dims, attend_ref, code_ref, col_ref, weight0):
    _, _, _, sides, per_block, heads, _, blocks = dims

    def one(block, carry):
        for head in range(heads):
            hot_rows(0, block, head, sides, per_block, attend_ref, code_ref, col_ref, weight0)
        return carry

    lax.fori_loop(0, blocks, one, 0)


def select_kernel(dims, ids_ref, zero_ref, one_ref, two_ref, three_ref, out_ref, sem):
    peers, capacity, sizes = dims
    refs = (zero_ref, one_ref, two_ref)

    def copies(peer, make):
        base = 0
        for level in range(LEVELS - 1):
            size = sizes[level]
            for slot in range(capacity):
                index = jnp.maximum(ids_ref[peer, level * capacity + slot], 0)
                make(refs[level].at[index], out_ref.at[peer, base : base + size, :])
                base += size
        make(three_ref, out_ref.at[peer, base : base + three_ref.shape[0], :])

    def start(peer, carry):
        copies(peer, lambda src, dst: pltpu.make_async_copy(src, dst, sem).start())
        return carry

    def finish(peer, carry):
        copies(peer, lambda src, dst: pltpu.make_async_copy(src, dst, sem).wait())
        return carry

    lax.fori_loop(0, peers, start, 0)
    lax.fori_loop(0, peers, finish, 0)


def pick(values, my_column):
    chosen = jnp.int32(values[0])
    for column in range(1, len(values)):
        chosen = jnp.where(my_column == column, values[column], chosen)
    return chosen


def relay_select_kernel(dims, order, place_ref, ids_ref, request_ref, *refs):
    partners, candidates, capacity, sizes, blocks = dims
    sources = refs[:candidates]
    outs = refs[candidates:]
    columns, numbers = order
    column = pick(columns, place_ref[1])
    which = pick(numbers, place_ref[1])
    for number, source in enumerate(sources):

        @pl.when(which == number)
        def _(source=source):
            for partner in range(partners):
                base = 0
                start = 0
                for level in range(LEVELS - 1):
                    size = sizes[level]
                    for rank in range(capacity):
                        index = jnp.maximum(ids_ref[partner + 1, column, level * capacity + rank], 0)
                        outs[partner][base : base + size, :] = source[
                            pl.ds(pl.multiple_of(start + index * size, size), size), :
                        ]
                        base += size
                    start += blocks * size
                small = blocks * sizes[3]
                outs[partner][base : base + small, :] = source[start : start + small, :]


def gather_direct(dims, request_ref, fetched_ref, tiles, tile3, sem):
    peers, capacity, sizes, _, _, _, _, _ = dims
    small = tile3.shape[1]
    base3 = capacity * sum(sizes[:3])
    pltpu.make_async_copy(fetched_ref.at[:, base3 : base3 + small, :], tile3, sem.at[LEVELS - 1]).start()

    def start(peer, carry):
        base = 0
        for level in range(LEVELS - 1):
            size = sizes[level]
            for rank in range(capacity):
                fetch_one(
                    request_ref[peer, level * capacity + rank],
                    fetched_ref.at[peer, base : base + size, :],
                    tiles[level],
                    sem.at[level],
                )
                base += size
        return carry

    lax.fori_loop(0, peers, start, 0)
    for level in range(LEVELS - 1):
        pltpu.make_async_copy(tiles[level], tiles[level], sem.at[level]).wait()
    pltpu.make_async_copy(tile3, tile3, sem.at[LEVELS - 1]).wait()


def fetch_one(request, source, tile, sem):
    @pl.when(request >= 0)
    def _():
        pltpu.make_async_copy(source, tile.at[request], sem).start()


def gather_relay(dims, relay, request_ref, place_ref, ids_ref, blocks_refs, packs_refs, tiles, tile3):
    _, capacity, sizes, _, _, _, _, blocks = dims
    rows, columns, partner_of, met = relay
    small = tile3.shape[1]
    my_row = place_ref[0]
    my_column = place_ref[1]

    def put(owner, level, rank, source, start):
        request = request_ref[owner, level * capacity + rank]
        size = sizes[level]
        tiles[level][jnp.maximum(request, 0)] = source[pl.ds(start, size), :]

    for number, source in enumerate(blocks_refs):
        shift = (number + 1) // 2 * (-1 if number % 2 else 1)
        column = my_column + shift

        @pl.when((column >= 0) & (column < columns))
        def _(source=source, column=column):
            owner = my_row * columns + column
            start = 0
            for level in range(LEVELS - 1):
                size = sizes[level]
                for rank in range(capacity):
                    index = jnp.maximum(ids_ref[0, column, level * capacity + rank], 0)
                    put(owner, level, rank, source, pl.multiple_of(start + index * size, size))
                start += blocks * size
            tile3[owner] = source[start : start + small, :]

    for number, source in enumerate(packs_refs):
        slot, partner = divmod(number, rows - 1)
        owner = partner_of(my_row, partner + 1) * columns + pick(met[slot], my_column)
        base = 0
        for level in range(LEVELS - 1):
            for rank in range(capacity):
                put(owner, level, rank, source, base)
                base += sizes[level]
        tile3[owner] = source[base : base + small, :]


def attend_kernel(dims, grid, gather, count, *refs):
    sources = refs[:count]
    (
        weight0,
        weight1,
        weight2,
        down_ref,
        lists_ref,
        out_ref,
        tile0,
        tile1,
        tile2,
        tile3,
        left0,
        left1,
        left2,
        sem,
    ) = refs[count:]
    peers, capacity, sizes, sides, per_block, heads, head_dim, blocks = dims
    pixels = sizes[0]
    channels = heads * head_dim
    small = tile3.shape[1]
    base2 = per_block * sizes[2]
    side0, side1 = sides[0], sides[1]

    gather(sources, (tile0, tile1, tile2), tile3, sem)
    left0[...] = jnp.zeros_like(left0)
    flat = tile3[...].reshape(peers * small, channels)
    size3 = sizes[3]
    wide = blocks * per_block * size3
    lane = iota((1, wide), 1)
    target = lane % size3
    tile_rows, tile_cols, grid_cols, col_count, capacity = grid
    for request in range(blocks * per_block):
        block, entry = divmod(request, per_block)
        tile = lists_ref[block // tile_cols, block % tile_cols, LEVELS - 1, entry]
        tile_row = tile // grid_cols
        tile_col = tile % grid_cols
        owner = tile_row // tile_rows * col_count + tile_col // tile_cols
        first = owner * small + (tile_row % tile_rows * tile_cols + tile_col % tile_cols) * size3
        target = target + jnp.where(lane // size3 == request, first, 0)
    chosen = (iota((peers * small, wide), 0) == target).astype(jnp.bfloat16)
    picked = lax.dot_general(flat, chosen, (((0,), (0,)), ((), ())), preferred_element_type=jnp.float32)
    left2[:, base2:] = picked.astype(jnp.bfloat16)

    def one(block, carry):
        mine = pl.ds(block * per_block, per_block)
        reach0 = side0 // GROUPS[0]
        for line in range(side0):
            piece = tile0[mine, line * side0 : (line + 1) * side0, :]
            turned = piece.reshape(per_block * side0, channels).T
            for group in range(GROUPS[0]):
                offset = line - group * reach0
                if 0 <= offset <= reach0:
                    for head in range(heads):
                        left0[
                            head,
                            offset * head_dim : (offset + 1) * head_dim,
                            group * per_block * side0 : (group + 1) * per_block * side0,
                        ] = turned[head * head_dim : (head + 1) * head_dim, :]
        wide1 = tile1[mine].astype(jnp.float32)
        reach1 = side1 // GROUPS[1]
        for offset in range(reach1 + 1):
            stack = []
            for group in range(GROUPS[1]):
                line = min(group * reach1 + offset, side1 - 1)
                stack.append(
                    wide1[:, line * side1 : (line + 1) * side1, :].reshape(per_block * side1, channels)
                )
            turned = jnp.concatenate(stack, axis=0).astype(jnp.bfloat16).T
            for head in range(heads):
                left1[head, offset * head_dim : (offset + 1) * head_dim, :] = turned[
                    head * head_dim : (head + 1) * head_dim, :
                ]
        left2[:, :base2] = tile2[mine].reshape(per_block * sizes[2], channels).T

        for head in range(heads):
            total = jnp.dot(
                left2[head * head_dim : (head + 1) * head_dim, :],
                weight2[block, head],
                preferred_element_type=jnp.float32,
            )
            for level in range(2):
                left = (left0, left1)[level]
                weight = (weight0, weight1)[level]
                for point in range(POINTS):
                    row = (head * LEVELS + level) * POINTS + point
                    product = jnp.dot(left[head], weight[block, head, point], preferred_element_type=jnp.float32)
                    down = down_ref[block, row : row + 1, :]
                    for offset in range(sides[level] // GROUPS[level] + 1):
                        total = total + product[offset * head_dim : (offset + 1) * head_dim, :] * hat(
                            down, float(offset)
                        )
            out_ref[
                pl.ds(pl.multiple_of(block * pixels, pixels), pixels), head * head_dim : (head + 1) * head_dim
            ] = total.T.astype(jnp.bfloat16)
        return carry

    lax.fori_loop(0, blocks, one, 0)


def own_kernel(head_ref, query_ref, own_ref, weight_ref, bias_ref, out_ref):
    channels = own_ref.shape[1]
    rows = weight_ref[pl.ds(pl.multiple_of(head_ref[0] * channels, channels), channels), :]
    pre = query_ref[...].astype(jnp.float32) + bias_ref[...]
    out_ref[...] = pre + jnp.dot(own_ref[...], rows, preferred_element_type=jnp.float32)


def norm_kernel(head_ref, pre_ref, other_ref, weight_ref, gain_ref, shift_ref, out_ref):
    own_head = head_ref[0]
    channels = out_ref.shape[1]
    rows = weight_ref[pl.ds(pl.multiple_of((1 - own_head) * channels, channels), channels), :]
    pre = pre_ref[...] + jnp.dot(other_ref[...], rows, preferred_element_type=jnp.float32)
    centered = pre - jnp.mean(pre, axis=1, keepdims=True)
    variance = jnp.mean(centered * centered, axis=1, keepdims=True)
    own = jnp.where(own_head == 0, centered[:, :channels], centered[:, channels:])
    out_ref[...] = (own * lax.rsqrt(variance + 1e-05) * gain_ref[...] + shift_ref[...]).astype(jnp.bfloat16)


def column_order(column, columns):
    found = []
    for step in range(1, columns):
        found += [(step, side) for side in (-1, 1) if 0 <= column + side * step < columns]
    return found


def tables(lists, grid):
    tile_rows, tile_cols, grid_cols, col_count, _ = grid
    count, blocks, level_count, per_block = lists.shape
    requests = blocks * per_block
    wanted = lists.transpose(0, 2, 1, 3).reshape(count, level_count, requests)
    grid_row = wanted // grid_cols
    grid_col = wanted % grid_cols
    owner = grid_row // tile_rows * col_count + grid_col // tile_cols
    local = grid_row % tile_rows * tile_cols + grid_col % tile_cols
    order = jnp.arange(requests, dtype=jnp.int32)
    earlier = (owner[..., :, None] == owner[..., None, :]) & (order[None, :] < order[:, None])
    rank = jnp.sum(earlier.astype(jnp.int32), axis=3)
    return owner, local, rank


def entries(owner, rank, owners, capacity, value):
    slot = jnp.arange(capacity, dtype=jnp.int32)
    hit = (owner[:, None, :, None, :] == owners[None, :, None, None, None]) & (
        rank[:, None, :, None, :] == slot[None, None, None, :, None]
    )
    found = jnp.sum(jnp.where(hit, 1 + value[:, None, :, None, :], 0), axis=4) - 1
    return found.reshape(owner.shape[0], owners.shape[0], -1)


def relay_tiles(dims, row_count, col_count, pack, flat_sets, lists, grid):
    peers, capacity, sizes, _, per_block, heads, head_dim, blocks = dims
    channels = heads * head_dim
    my_row = lax.axis_index("row")
    my_column = lax.axis_index("col")
    power = row_count & (row_count - 1) == 0

    def partner_of(row, number):
        return row ^ number if power else (row + number) % row_count

    def source_of(row, number):
        return row ^ number if power else (row + row_count - number) % row_count

    gathered = [lists]
    for number in range(1, row_count):
        gathered.append(
            lax.ppermute(lists, "row", [(row, partner_of(row, number)) for row in range(row_count)])
        )
    block = jnp.concatenate(flat_sets, axis=0)
    arrived = {}

    def hop(step):
        for side in (-1, 1):
            pairs = []
            for column in range(col_count):
                if 0 <= column + side * step < col_count:
                    pairs.append((column + side, column))
            held = arrived.get((step - 1, side), block)
            arrived[(step, side)] = lax.ppermute(held, "col", pairs)

    hop(1)
    place = jnp.stack([my_row, my_column]).astype(jnp.int32)
    owner, local, rank = tables(jnp.stack(gathered).reshape(row_count, blocks, LEVELS, per_block), grid)
    row_owners = my_row * col_count + jnp.arange(col_count, dtype=jnp.int32)
    ids = entries(owner, rank, row_owners, capacity, local)
    order = jnp.broadcast_to(jnp.arange(blocks * per_block, dtype=jnp.int32), owner[:1].shape)
    request = entries(owner[:1], rank[:1], jnp.arange(peers, dtype=jnp.int32), capacity, order)[0]

    orders = [[(0, 1)] + column_order(column, col_count) for column in range(col_count)]
    candidates = [sorted({order[slot] for order in orders}) for slot in range(col_count)]
    met = []
    packs = []
    for slot in range(col_count):
        if slot > 1:
            hop(slot)
        columns = [column + order[slot][0] * order[slot][1] for column, order in enumerate(orders)]
        numbers = [candidates[slot].index(order[slot]) for order in orders]
        met.append(columns)
        held = [block if slot == 0 else arrived[candidate] for candidate in candidates[slot]]
        sent = pl.pallas_call(
            functools.partial(
                relay_select_kernel, (row_count - 1, len(held), capacity, sizes, blocks), (columns, numbers)
            ),
            out_shape=[jax.ShapeDtypeStruct((pack, channels), jnp.bfloat16)] * (row_count - 1),
            in_specs=[pl.BlockSpec(memory_space=SMEM)] * 3 + [pl.BlockSpec(memory_space=VMEM)] * len(held),
            out_specs=[pl.BlockSpec(memory_space=VMEM)] * (row_count - 1),
            compiler_params=pltpu.CompilerParams(vmem_limit_bytes=SELECT_VMEM),
        )(place, ids, request, *held)
        for number in range(1, row_count):
            packs.append(
                lax.ppermute(
                    sent[number - 1], "row", [(row, source_of(row, number)) for row in range(row_count)]
                )
            )

    near = [block]
    for step in range(1, col_count):
        near += [arrived[(step, -1)], arrived[(step, 1)]]
    sources = (request, place, ids, *near, *packs)
    spaces = (SMEM, SMEM, SMEM) + (VMEM,) * (len(near) + len(packs))

    def gather(refs, tiles, tile3, sem):
        gather_relay(
            dims,
            (row_count, col_count, partner_of, met),
            refs[0],
            refs[1],
            refs[2],
            refs[3 : 3 + len(near)],
            refs[3 + len(near) :],
            tiles,
            tile3,
        )

    return gather, sources, spaces


def direct_tiles(dims, pack, tile_sets, flat_sets, lists, grid):
    peers, capacity, sizes, _, per_block, heads, head_dim, blocks = dims
    channels = heads * head_dim
    owner, local, rank = tables(lists.reshape(1, blocks, LEVELS, per_block), grid)
    owners = jnp.arange(peers, dtype=jnp.int32)
    order = jnp.broadcast_to(jnp.arange(blocks * per_block, dtype=jnp.int32), owner.shape)
    asked = entries(owner, rank, owners, capacity, local)[0]
    request = entries(owner, rank, owners, capacity, order)[0]
    received = lax.all_to_all(asked, ("row", "col"), split_axis=0, concat_axis=0, tiled=True)
    packs = pl.pallas_call(
        functools.partial(select_kernel, (peers, capacity, sizes)),
        out_shape=jax.ShapeDtypeStruct((peers, pack, channels), jnp.bfloat16),
        in_specs=[pl.BlockSpec(memory_space=SMEM)] + [pl.BlockSpec(memory_space=VMEM)] * 4,
        out_specs=pl.BlockSpec(memory_space=ANY),
        scratch_shapes=[pltpu.SemaphoreType.DMA],
        name="select",
    )(received, tile_sets[0], tile_sets[1], tile_sets[2], flat_sets[3])
    fetched = lax.all_to_all(packs, ("row", "col"), split_axis=0, concat_axis=0, tiled=True)

    def gather(refs, tiles, tile3, sem):
        gather_direct(dims, refs[0], refs[1], tiles, tile3, sem)

    return gather, (request, fetched), (SMEM, ANY)


def on_device(
    queries,
    level_zero,
    level_one,
    level_two,
    level_three,
    tile_lists,
    samples,
    logit_weight,
    logit_bias,
    output_weight,
    output_bias,
    norm_gain,
    norm_shift,
):
    level_blocks = (level_zero, level_one, level_two, level_three)
    row_count = lax.axis_size("row")
    col_count = lax.axis_size("col")
    peers = row_count * col_count
    tile_rows, tile_cols, level_count, per_block = tile_lists.shape
    blocks = tile_rows * tile_cols
    requests = blocks * per_block
    capacity = max(2, (requests + peers - 1) // peers)
    grid_cols = tile_cols * col_count
    channels = level_zero.shape[2]
    width_all = queries.shape[2]
    lanes = samples.shape[2]
    heads = lanes // (LEVELS * POINTS)
    head_dim = channels // heads
    sides = tuple(block.shape[0] // tile_rows for block in level_blocks)
    sizes = tuple(side * side for side in sides)
    pixels = sizes[0]
    tile_sets = [
        to_blocks(level_blocks[level], tile_rows, tile_cols, sides[level]) for level in range(level_count)
    ]

    small = blocks * sizes[3]
    pack = capacity * sum(sizes[:3]) + small
    dims = (peers, capacity, sizes, sides, per_block, heads, head_dim, blocks)
    grid = (tile_rows, tile_cols, grid_cols, col_count, capacity)
    flat_sets = [
        tile_sets[level].reshape(blocks * sizes[level], channels) for level in range(level_count)
    ]
    if peers * capacity <= requests and col_count > 1:
        gather, sources, spaces = relay_tiles(
            dims, row_count, col_count, pack, flat_sets, tile_lists, grid
        )
    else:
        gather, sources, spaces = direct_tiles(
            dims, pack, tile_sets, flat_sets, tile_lists, grid
        )

    queries_blocked = to_blocks(queries, tile_rows, tile_cols, sides[0]).reshape(blocks * pixels, width_all)
    samples_blocked = to_blocks(samples, tile_rows, tile_cols, sides[0]).reshape(blocks * pixels, lanes)
    depth0 = GROUPS[0] * per_block * sides[0]
    depth1 = GROUPS[1] * per_block * sides[1]
    depth2 = per_block * sizes[2] + requests * sizes[3]
    whole = pl.BlockSpec(memory_space=VMEM)
    turned = (blocks, lanes, pixels)
    weight1, weight2, attend, code, down, col = pl.pallas_call(
        functools.partial(prep_kernel, dims),
        out_shape=[
            jax.ShapeDtypeStruct((blocks, heads, POINTS, depth1, pixels), jnp.bfloat16),
            jax.ShapeDtypeStruct((blocks, heads, depth2, pixels), jnp.bfloat16),
            jax.ShapeDtypeStruct(turned, jnp.float32),
            jax.ShapeDtypeStruct(turned, jnp.int32),
            jax.ShapeDtypeStruct(turned, jnp.float32),
            jax.ShapeDtypeStruct(turned, jnp.float32),
        ],
        in_specs=[pl.BlockSpec(memory_space=pltpu.HBM)] * 4,
        out_specs=[whole] * 6,
        scratch_shapes=[
            VMEM((blocks * pixels, width_all), jnp.bfloat16),
            VMEM((lanes, width_all), jnp.bfloat16),
            VMEM((1, lanes), jnp.float32),
            VMEM((blocks * pixels, lanes), jnp.int32),
            pltpu.SemaphoreType.DMA((4,)),
        ],
        compiler_params=pltpu.CompilerParams(vmem_limit_bytes=PREP_VMEM),
        name="prep",
    )(queries_blocked, logit_weight.T, logit_bias.reshape(1, lanes), samples_blocked)
    weight0 = pl.pallas_call(
        functools.partial(hot_kernel, dims),
        out_shape=jax.ShapeDtypeStruct((blocks, heads, POINTS, depth0, pixels), jnp.bfloat16),
        in_specs=[whole] * 3,
        out_specs=whole,
        compiler_params=pltpu.CompilerParams(vmem_limit_bytes=PREP_VMEM),
        name="hot",
    )(attend, code, col)

    attn = pl.pallas_call(
        functools.partial(attend_kernel, dims, grid, gather, len(sources)),
        out_shape=jax.ShapeDtypeStruct((blocks * pixels, channels), jnp.bfloat16),
        in_specs=[pl.BlockSpec(memory_space=space) for space in spaces]
        + [whole] * 4
        + [pl.BlockSpec(memory_space=SMEM)],
        out_specs=whole,
        scratch_shapes=[
            VMEM((requests, sizes[0], channels), jnp.bfloat16),
            VMEM((requests, sizes[1], channels), jnp.bfloat16),
            VMEM((requests, sizes[2], channels), jnp.bfloat16),
            VMEM((peers, small, channels), jnp.bfloat16),
            VMEM((heads, (sides[0] // GROUPS[0] + 1) * head_dim, depth0), jnp.bfloat16),
            VMEM((heads, (sides[1] // GROUPS[1] + 1) * head_dim, depth1), jnp.bfloat16),
            VMEM((channels, depth2), jnp.bfloat16),
            pltpu.SemaphoreType.DMA((LEVELS,)),
        ],
        compiler_params=pltpu.CompilerParams(vmem_limit_bytes=ATTEND_VMEM),
        name="attend",
    )(*sources, weight0, weight1, weight2, down, tile_lists)

    own_head = lax.axis_index("head").reshape(1).astype(jnp.int32)
    other = lax.ppermute(attn, "head", [(0, 1), (1, 0)])
    wide_spec = pl.BlockSpec((pixels, width_all), lambda i: (i, 0))
    slim_spec = pl.BlockSpec((pixels, channels), lambda i: (i, 0))
    matrix_spec = pl.BlockSpec((width_all, width_all), lambda i: (0, 0))
    pre = pl.pallas_call(
        own_kernel,
        out_shape=jax.ShapeDtypeStruct((blocks * pixels, width_all), jnp.float32),
        grid=(blocks,),
        in_specs=[
            pl.BlockSpec(memory_space=SMEM),
            wide_spec,
            slim_spec,
            matrix_spec,
            pl.BlockSpec((1, width_all), lambda i: (0, 0)),
        ],
        out_specs=wide_spec,
        compiler_params=pltpu.CompilerParams(vmem_limit_bytes=SELECT_VMEM),
        name="own",
    )(own_head, queries_blocked, attn, output_weight, output_bias.reshape(1, width_all))
    updated = pl.pallas_call(
        norm_kernel,
        out_shape=jax.ShapeDtypeStruct((blocks * pixels, channels), jnp.bfloat16),
        grid=(blocks,),
        in_specs=[
            pl.BlockSpec(memory_space=SMEM),
            wide_spec,
            slim_spec,
            matrix_spec,
            pl.BlockSpec((1, channels), lambda i: (0, 0)),
            pl.BlockSpec((1, channels), lambda i: (0, 0)),
        ],
        out_specs=slim_spec,
        compiler_params=pltpu.CompilerParams(vmem_limit_bytes=SELECT_VMEM),
        name="norm",
    )(
        own_head,
        pre,
        other,
        output_weight,
        norm_gain.reshape(1, channels),
        norm_shift.reshape(1, channels),
    )
    side = sides[0]
    updated = updated.reshape(tile_rows, tile_cols, side, side, channels).transpose(0, 2, 1, 3, 4)
    return updated.reshape(tile_rows * side, tile_cols * side, channels)


def solution(mesh):
    in_specs = (
        P("row", "col", None),
        P("row", "col", "head"),
        P("row", "col", "head"),
        P("row", "col", "head"),
        P("row", "col", "head"),
        P("row", "col", None, None),
        P("row", "col", "head"),
        P(None, "head"),
        P("head"),
        P(),
        P(),
        P("head"),
        P("head"),
    )
    out_specs = P("row", "col", "head")
    return jax.shard_map(on_device, mesh=mesh, in_specs=in_specs, out_specs=out_specs, check_vma=False)
```

time: 83.4 us -> 82.8 us (level)
  the two profiles are of different devices: /device:TPU:0 before, /device:TPU:17 now
where the time goes in v4:
time: 82.8 us; the launch traced here: 82.4 us
  starting transfers between devices  37.4 us (45%)
  Pallas kernels  24.4 us (29%)
  waiting for transfers between devices  12.9 us (16%)
  local copies, waits for them, and re-layouts  3.94 us (5%)
  other arithmetic  3.36 us (4%)
    ppermute x6, starting transfers between devices, hop(): arrived[step, side] = lax.ppermute(held, 'col', pairs)  13.9 us
    ppermute x12, starting transfers between devices, relay_tiles(): lax.ppermute(sent[number - 1], 'row', [(row, source_of(row, number)) for...  13 us
    pallas_call x1, Pallas kernels, on_device(): pl.pallas_call(functools.partial(attend_kernel, dims, grid, gather, len(s...  8.36 us
    ppermute x1, starting transfers between devices, on_device(): other = lax.ppermute(attn, 'head', [(0, 1), (1, 0)])  7.87 us
    pallas_call x1, Pallas kernels, on_device(): pl.pallas_call(functools.partial(prep_kernel, dims), out_shape=[jax.Shape...  7.72 us
    ppermute x6, waiting for transfers between devices, hop(): arrived[step, side] = lax.ppermute(held, 'col', pairs)  7.37 us
    ppermute x12, waiting for transfers between devices, relay_tiles(): lax.ppermute(sent[number - 1], 'row', [(row, source_of(row, number)) for...  5.13 us
    unnamed x20, local copies, waits for them, and re-layouts  3.53 us
  transfers between devices with their start and end apart: 22, of which 7 were waited for; matrix products, arithmetic and copies ran while one was open for 5% of the time, Pallas kernels for 17%

profile of v4, /device:TPU:17, one launch (start us, length us, event | category | flops | bytes accessed | tf_op | source)
XLA Modules:
  0.0 82.4 jit_solution(17713221702821644688)
XLA Ops:
  0.0 1.2 %collective-permute-start.1 = (s32[4,1,4,8]{3,2,1,0:T(4,128)}, s32[4,1,4,8]{3,2,1,0:T(4,128)S(1)}, u32[]{:S(2)}, u32[]{:S(2)}) collective-permute-start(s32[4,1,4,8]{3,2,1,0:T(4,128)} %refs_26_.1), channel_id=1, source_target_pairs={{0,16},{8,24},{16,0},{24,8},{1,17},{9,25},{17,1},{25,9},{2,18},{10... | collective-permute-start | bytes 1544 | tf_op jit(solution)/shard_map/ppermute | solution.py:467
  1.2 1.2 %collective-permute-start = (s32[4,1,4,8]{3,2,1,0:T(4,128)}, s32[4,1,4,8]{3,2,1,0:T(4,128)S(1)}, u32[]{:S(2)}, u32[]{:S(2)}) collective-permute-start(s32[4,1,4,8]{3,2,1,0:T(4,128)} %refs_26_.1), channel_id=1, source_target_pairs={{0,8},{8,0},{16,24},{24,16},{1,9},{9,1},{17,25},{25,17},{2,10},{10... | collective-permute-start | bytes 1544 | tf_op jit(solution)/shard_map/ppermute | solution.py:467
  2.5 0.2 collective-permute-start.2
  2.7 1.0 %pad_maximum_fusion.refs_0_.refs_3_ = bf16[1360,128]{1,0:T(8,128)(2,1)S(1)} fusion(bf16[16,128]{1,0:T(8,128)(2,1)} %bitcast.46, bf16[64,128]{1,0:T(8,128)(2,1)} %bitcast.41, bf16[256,128]{1,0:T(8,128)(2,1)} %bitcast.40, bf16[1024,128]{1,0:T(8,128)(2,1)} %bitcast.38), kind=kLoop, calls=%fused_computation | loop fusion | flops 1392640 | bytes 696320 | tf_op jit(solution)/shard_map/concatenate | solution.py:469
  3.7 2.1 %collective-permute-start.4 = (bf16[1360,128]{1,0:T(8,128)(2,1)S(1)}, bf16[1360,128]{1,0:T(8,128)(2,1)S(1)}, u32[]{:S(2)}, u32[]{:S(2)}) collective-permute-start(bf16[1360,128]{1,0:T(8,128)(2,1)S(1)} %pad_maximum_fusion.refs_0_.refs_3_), channel_id=1, source_target_pairs={{2,0},{4,2},{6,4},{3,1},{5,3},{7,5},{10,8},{12,10},{14,12},{11,9},... | collective-permute-start | bytes 1044488 | tf_op jit(solution)/shard_map/ppermute | solution.py:479
  5.8 3.2 %collective-permute-start.3 = (bf16[1360,128]{1,0:T(8,128)(2,1)S(1)}, bf16[1360,128]{1,0:T(8,128)(2,1)S(1)}, u32[]{:S(2)}, u32[]{:S(2)}) collective-permute-start(bf16[1360,128]{1,0:T(8,128)(2,1)S(1)} %pad_maximum_fusion.refs_0_.refs_3_), channel_id=1, source_target_pairs={{0,2},{2,4},{4,6},{1,3},{3,5},{5,7},{8,10},{10,12},{12,14},{9,11},... | collective-permute-start | bytes 1044488 | tf_op jit(solution)/shard_map/ppermute | solution.py:479
  9.1 0.1 pad_add_fusion.place_ref.refs_1_
  9.1 0.0 collective-permute-done.1
  9.1 0.0 collective-permute-done
  9.1 0.0 collective-permute-done.2
  9.2 0.7 add_bitcast_fusion
  9.9 0.1 reshape.312
  10.0 0.5 convert_reduce_fusion
  10.5 0.1 broadcast_compare_fusion
  10.6 0.6 select_reduce_fusion
  11.3 2.5 %collective-permute-done.4.refs_1_.refs_0_.refs_5_ = bf16[1360,128]{1,0:T(8,128)(2,1)S(1)} collective-permute-done((bf16[1360,128]{1,0:T(8,128)(2,1)S(1)}, bf16[1360,128]{1,0:T(8,128)(2,1)S(1)}, u32[]{:S(2)}, u32[]{:S(2)}) %collective-permute-start.4) | collective-permute-done | bytes 348192 | tf_op jit(solution)/shard_map/ppermute | solution.py:479
  13.8 2.1 %collective-permute-start.6 = (bf16[1360,128]{1,0:T(8,128)(2,1)S(1)}, bf16[1360,128]{1,0:T(8,128)(2,1)S(1)}, u32[]{:S(2)}, u32[]{:S(2)}) collective-permute-start(bf16[1360,128]{1,0:T(8,128)(2,1)S(1)} %collective-permute-done.4.refs_1_.refs_0_.refs_5_), channel_id=1, source_target_pairs={{2,0},{4,2},{3,1},{5,3},{10,8},{12,10},{11,9},{13,11},{18,16},{20,... | collective-permute-start | bytes 1044488 | tf_op jit(solution)/shard_map/ppermute | solution.py:479
  15.9 2.9 %collective-permute-start.5 = (bf16[1360,128]{1,0:T(8,128)(2,1)S(1)}, bf16[1360,128]{1,0:T(8,128)(2,1)S(1)}, u32[]{:S(2)}, u32[]{:S(2)}) collective-permute-start(bf16[1360,128]{1,0:T(8,128)(2,1)S(1)} %collective-permute-done.3.refs_0_.refs_4_), channel_id=1, source_target_pairs={{2,4},{4,6},{3,5},{5,7},{10,12},{12,14},{11,13},{13,15},{18,20},{2... | collective-permute-start | bytes 1044488 | tf_op jit(solution)/shard_map/ppermute | solution.py:479
  18.8 0.1 copy.49
  19.0 0.1 copy.59.ids_ref.refs_2_
  19.1 0.2 select_reduce_fusion.1
  19.3 1.7 %collective-permute-done.6.refs_2_.refs_1_.refs_7_ = bf16[1360,128]{1,0:T(8,128)(2,1)S(1)} collective-permute-done((bf16[1360,128]{1,0:T(8,128)(2,1)S(1)}, bf16[1360,128]{1,0:T(8,128)(2,1)S(1)}, u32[]{:S(2)}, u32[]{:S(2)}) %collective-permute-start.6) | collective-permute-done | bytes 348192 | tf_op jit(solution)/shard_map/ppermute | solution.py:479
  21.0 0.7 collective-permute-start.8
  21.6 3.2 %collective-permute-done.5.refs_1_.refs_0_.refs_6_ = bf16[1360,128]{1,0:T(8,128)(2,1)S(1)} collective-permute-done((bf16[1360,128]{1,0:T(8,128)(2,1)S(1)}, bf16[1360,128]{1,0:T(8,128)(2,1)S(1)}, u32[]{:S(2)}, u32[]{:S(2)}) %collective-permute-start.5) | collective-permute-done | bytes 348192 | tf_op jit(solution)/shard_map/ppermute | solution.py:479
  24.8 2.9 %collective-permute-start.7 = (bf16[1360,128]{1,0:T(8,128)(2,1)S(1)}, bf16[1360,128]{1,0:T(8,128)(2,1)S(1)}, u32[]{:S(2)}, u32[]{:S(2)}) collective-permute-start(bf16[1360,128]{1,0:T(8,128)(2,1)S(1)} %collective-permute-done.5.refs_1_.refs_0_.refs_6_), channel_id=1, source_target_pairs={{4,6},{5,7},{12,14},{13,15},{20,22},{21,23},{28,30},{29,31}} | collective-permute-start | bytes 1044488 | tf_op jit(solution)/shard_map/ppermute | solution.py:479
  27.8 0.1 copy.58.request_ref.refs_0_
  27.8 0.9 %shard_map.127 = (bf16[688,128]{1,0:T(8,128)(2,1)S(1)}, bf16[688,128]{1,0:T(8,128)(2,1)S(1)}, bf16[688,128]{1,0:T(8,128)(2,1)S(1)}) custom-call(s32[2]{0:T(128)S(1)} %pad_add_fusion.place_ref.refs_1_, s32[4,4,8]{2,1,0:T(4,128)S(1)} %copy.59.ids_ref.refs_2_, s32[16,8]{1,0:T(8,128)S(1)} %copy.58.request_ref.refs_0_, ...), custom_call_target="tpu_custom_call" | custom-call | tf_op jit(solution)/shard_map/pallas_call | solution.py:500
  28.7 1.3 %collective-permute-start.9 = (bf16[688,128]{1,0:T(8,128)(2,1)S(1)}, bf16[688,128]{1,0:T(8,128)(2,1)S(1)}, u32[]{:S(2)}, u32[]{:S(2)}) collective-permute-start(bf16[688,128]{1,0:T(8,128)(2,1)S(1)} %get-tuple-element.23), channel_id=1, source_target_pairs={{0,8},{8,0},{16,24},{24,16},{1,9},{9,1},{17,25},{25,17},{2,10},{10... | collective-permute-start | bytes 528392 | tf_op jit(solution)/shard_map/ppermute | solution.py:511
  30.0 1.2 %collective-permute-start.10 = (bf16[688,128]{1,0:T(8,128)(2,1)S(1)}, bf16[688,128]{1,0:T(8,128)(2,1)S(1)}, u32[]{:S(2)}, u32[]{:S(2)}) collective-permute-start(bf16[688,128]{1,0:T(8,128)(2,1)S(1)} %get-tuple-element.24), channel_id=1, source_target_pairs={{0,16},{8,24},{16,0},{24,8},{1,17},{9,25},{17,1},{25,9},{2,18},{10... | collective-permute-start | bytes 528392 | tf_op jit(solution)/shard_map/ppermute | solution.py:511
  31.2 0.2 collective-permute-start.11
  31.4 0.9 %shard_map.128 = (bf16[688,128]{1,0:T(8,128)(2,1)S(1)}, bf16[688,128]{1,0:T(8,128)(2,1)S(1)}, bf16[688,128]{1,0:T(8,128)(2,1)S(1)}) custom-call(s32[2]{0:T(128)S(1)} %pad_add_fusion.place_ref.refs_1_, s32[4,4,8]{2,1,0:T(4,128)S(1)} %copy.59.ids_ref.refs_2_, s32[16,8]{1,0:T(8,128)S(1)} %copy.58.request_ref.refs_0_, ...), custom_call_target="tpu_custom_call" | custom-call | tf_op jit(solution)/shard_map/pallas_call | solution.py:500
  32.3 0.9 %shard_map.129 = (bf16[688,128]{1,0:T(8,128)(2,1)S(1)}, bf16[688,128]{1,0:T(8,128)(2,1)S(1)}, bf16[688,128]{1,0:T(8,128)(2,1)S(1)}) custom-call(s32[2]{0:T(128)S(1)} %pad_add_fusion.place_ref.refs_1_, s32[4,4,8]{2,1,0:T(4,128)S(1)} %copy.59.ids_ref.refs_2_, s32[16,8]{1,0:T(8,128)S(1)} %copy.58.request_ref.refs_0_, ...), custom_call_target="tpu_custom_call" | custom-call | tf_op jit(solution)/shard_map/pallas_call | solution.py:500
  33.2 1.3 %collective-permute-start.12 = (bf16[688,128]{1,0:T(8,128)(2,1)S(1)}, bf16[688,128]{1,0:T(8,128)(2,1)S(1)}, u32[]{:S(2)}, u32[]{:S(2)}) collective-permute-start(bf16[688,128]{1,0:T(8,128)(2,1)S(1)} %get-tuple-element.26), channel_id=1, source_target_pairs={{0,8},{8,0},{16,24},{24,16},{1,9},{9,1},{17,25},{25,17},{2,10},{10... | collective-permute-start | bytes 528392 | tf_op jit(solution)/shard_map/ppermute | solution.py:511
  34.5 1.0 %collective-permute-done.10.refs_11_ = bf16[688,128]{1,0:T(8,128)(2,1)S(1)} collective-permute-done((bf16[688,128]{1,0:T(8,128)(2,1)S(1)}, bf16[688,128]{1,0:T(8,128)(2,1)S(1)}, u32[]{:S(2)}, u32[]{:S(2)}) %collective-permute-start.10) | collective-permute-done | bytes 176160 | tf_op jit(solution)/shard_map/ppermute | solution.py:511
  35.5 2.2 %collective-permute-start.13 = (bf16[688,128]{1,0:T(8,128)(2,1)S(1)}, bf16[688,128]{1,0:T(8,128)(2,1)S(1)}, u32[]{:S(2)}, u32[]{:S(2)}) collective-permute-start(bf16[688,128]{1,0:T(8,128)(2,1)S(1)} %get-tuple-element.27), channel_id=1, source_target_pairs={{0,16},{8,24},{16,0},{24,8},{1,17},{9,25},{17,1},{25,9},{2,18},{10... | collective-permute-start | bytes 528392 | tf_op jit(solution)/shard_map/ppermute | solution.py:511
  37.7 0.0 collective-permute-done.8.refs_3_.refs_9_
  37.7 0.0 collective-permute-start.14
  37.7 0.0 collective-permute-done.7.refs_2_.refs_8_
  37.7 1.2 %collective-permute-start.15 = (bf16[688,128]{1,0:T(8,128)(2,1)S(1)}, bf16[688,128]{1,0:T(8,128)(2,1)S(1)}, u32[]{:S(2)}, u32[]{:S(2)}) collective-permute-start(bf16[688,128]{1,0:T(8,128)(2,1)S(1)} %get-tuple-element.29), channel_id=1, source_target_pairs={{0,8},{8,0},{16,24},{24,16},{1,9},{9,1},{17,25},{25,17},{2,10},{10... | collective-permute-start | bytes 528392 | tf_op jit(solution)/shard_map/ppermute | solution.py:511
  38.9 0.9 %shard_map.130 = (bf16[688,128]{1,0:T(8,128)(2,1)S(1)}, bf16[688,128]{1,0:T(8,128)(2,1)S(1)}, bf16[688,128]{1,0:T(8,128)(2,1)S(1)}) custom-call(s32[2]{0:T(128)S(1)} %pad_add_fusion.place_ref.refs_1_, s32[4,4,8]{2,1,0:T(4,128)S(1)} %copy.59.ids_ref.refs_2_, s32[16,8]{1,0:T(8,128)S(1)} %copy.58.request_ref.refs_0_, ...), custom_call_target="tpu_custom_call" | custom-call | tf_op jit(solution)/shard_map/pallas_call | solution.py:500
  39.8 0.0 collective-permute-done.11.refs_12_
  39.8 1.5 %collective-permute-start.16 = (bf16[688,128]{1,0:T(8,128)(2,1)S(1)}, bf16[688,128]{1,0:T(8,128)(2,1)S(1)}, u32[]{:S(2)}, u32[]{:S(2)}) collective-permute-start(bf16[688,128]{1,0:T(8,128)(2,1)S(1)} %get-tuple-element.30), channel_id=1, source_target_pairs={{0,16},{8,24},{16,0},{24,8},{1,17},{9,25},{17,1},{25,9},{2,18},{10... | collective-permute-start | bytes 528392 | tf_op jit(solution)/shard_map/ppermute | solution.py:511
  41.3 0.6 collective-permute-start.17
  41.9 3.1 %collective-permute-done.13.refs_14_ = bf16[688,128]{1,0:T(8,128)(2,1)S(1)} collective-permute-done((bf16[688,128]{1,0:T(8,128)(2,1)S(1)}, bf16[688,128]{1,0:T(8,128)(2,1)S(1)}, u32[]{:S(2)}, u32[]{:S(2)}) %collective-permute-start.13) | collective-permute-done | bytes 176160 | tf_op jit(solution)/shard_map/ppermute | solution.py:511
  45.0 1.6 %collective-permute-start.19 = (bf16[688,128]{1,0:T(8,128)(2,1)S(1)}, bf16[688,128]{1,0:T(8,128)(2,1)S(1)}, u32[]{:S(2)}, u32[]{:S(2)}) collective-permute-start(bf16[688,128]{1,0:T(8,128)(2,1)S(1)} %get-tuple-element.33), channel_id=1, source_target_pairs={{0,16},{8,24},{16,0},{24,8},{1,17},{9,25},{17,1},{25,9},{2,18},{10... | collective-permute-start | bytes 528392 | tf_op jit(solution)/shard_map/ppermute | solution.py:511
  46.6 1.0 %collective-permute-done.15.refs_16_ = bf16[688,128]{1,0:T(8,128)(2,1)S(1)} collective-permute-done((bf16[688,128]{1,0:T(8,128)(2,1)S(1)}, bf16[688,128]{1,0:T(8,128)(2,1)S(1)}, u32[]{:S(2)}, u32[]{:S(2)}) %collective-permute-start.15) | collective-permute-done | bytes 176160 | tf_op jit(solution)/shard_map/ppermute | solution.py:511
  47.6 1.9 %collective-permute-start.20 = (bf16[688,128]{1,0:T(8,128)(2,1)S(1)}, bf16[688,128]{1,0:T(8,128)(2,1)S(1)}, u32[]{:S(2)}, u32[]{:S(2)}) collective-permute-start(bf16[688,128]{1,0:T(8,128)(2,1)S(1)} %get-tuple-element.34), channel_id=1, source_target_pairs={{0,24},{8,16},{16,8},{24,0},{1,25},{9,17},{17,9},{25,1},{2,26},{10... | collective-permute-start | bytes 528392 | tf_op jit(solution)/shard_map/ppermute | solution.py:511
  49.5 1.0 %copy-done = bf16[64,16,256]{2,1,0:T(8,128)(2,1)S(1)} copy-done((bf16[64,16,256]{2,1,0:T(8,128)(2,1)S(1)}, bf16[64,16,256]{2,1,0:T(8,128)(2,1)}, u32[]{:S(2)}) %copy-start) | copy-done | bytes 524312
  50.5 1.0 %copy-done.2 = s32[64,16,64]{2,1,0:T(8,128)S(1)} copy-done((s32[64,16,64]{2,1,0:T(8,128)S(1)}, s32[64,16,64]{2,1,0:T(8,128)}, u32[]{:S(2)}) %copy-start.2) | copy-done | bytes 262168
  51.6 0.8 copy-done.5
  52.3 0.7 copy-done.7
  53.0 7.7 %prep.1 = (bf16[4,4,4,256,256]{4,3,2,1,0:T(8,128)(2,1)S(1)}, bf16[4,4,256,256]{3,2,1,0:T(8,128)(2,1)S(1)}, f32[4,64,256]{2,1,0:T(8,128)S(1)}, s32[4,64,256]{2,1,...) custom-call(bf16[1024,256]{1,0:T(8,128)(2,1)S(1)} %bitcast.29, bf16[64,256]{1,0:T(8,128)(2,1)S(1)} %bitcast.33, ...), custom_call_target="tpu_custom_call" | custom-call | tf_op jit(solution)/shard_map/prep/pallas_call | solution.py:622
  60.7 1.8 %hot.1.refs_22_ = bf16[4,4,4,256,256]{4,3,2,1,0:T(8,128)(2,1)S(1)} custom-call(f32[4,64,256]{2,1,0:T(8,128)S(1)} %get-tuple-element.35.attend_ref, s32[4,64,256]{2,1,0:T(8,128)S(1)} %get-tuple-element.36.code_ref, f32[4,64,256]{2,1,0:T(8,128)S(1)} %get-tuple-element.37.col_ref), custom_call_target="tpu_custom_call" | custom-call | tf_op jit(solution)/shard_map/hot/pallas_call | solution.py:644
  62.5 0.0 collective-permute-done.16.refs_17_
  62.6 0.0 copy-start.1
  62.6 0.0 copy-start.3
  62.6 0.0 copy-start.6
  62.6 0.0 copy-start.8
  62.6 0.0 copy-start.9
  62.6 8.4 %attend.1.own_ref = bf16[1024,128]{1,0:T(8,128)(2,1)S(1)} custom-call(s32[16,8]{1,0:T(8,128)S(1)} %copy.58.request_ref.refs_0_, s32[2]{0:T(128)S(1)} %pad_add_fusion.place_ref.refs_1_, s32[4,4,8]{2,1,0:T(4,128)S(1)} %copy.59.ids_ref.refs_2_, bf16[1360,128]{1,0:T(8,128)(2,1)S(1)} %pad_maximum_fusion.refs_0_.refs_3_, ...), custom_call_target="tpu_custom_call" | custom-call | tf_op jit(solution)/shard_map/attend/pallas_call | solution.py:653
  71.0 7.9 %collective-permute-start.21 = (bf16[1024,128]{1,0:T(8,128)(2,1)S(1)}, bf16[1024,128]{1,0:T(8,128)(2,1)S(1)}, u32[]{:S(2)}, u32[]{:S(2)}) collective-permute-start(bf16[1024,128]{1,0:T(8,128)(2,1)S(1)} %attend.1.own_ref), channel_id=1, source_target_pairs={{0,1},{1,0},{2,3},{3,2},{4,5},{5,4},{6,7},{7,6},{8,9},{9,8},{10,11... | collective-permute-start | bytes 786440 | tf_op jit(solution)/shard_map/ppermute | solution.py:675
  78.9 0.7 own.1.pre_ref
  79.6 0.4 collective-permute-done.21.other_ref
  80.0 2.3 %norm.1 = bf16[1024,128]{1,0:T(8,128)(2,1)} custom-call(s32[1]{0:T(128)} %bitcast.head_ref, f32[1024,256]{1,0:T(8,128)S(1)} %own.1.pre_ref, bf16[1024,128]{1,0:T(8,128)(2,1)S(1)} %collective-permute-done.21.other_ref, bf16[256,256]{1,0:T(8,128)(2,1)S(1)} %copy-done.3, f32[1,128]{1,0:T(1,128)S(1)} %bitcast.36, f32[1,128]{1,0:T(1,128)S(1)} %bitcast.37), custom_call_target="tpu_custom_call" | custom-call | tf_op jit(solution)/shard_map/norm/pallas_call | solution.py:694
  (32 shorter events, 0.2 us)
Async XLA Ops:
  0.0 62.6 %copy-start.4 = (s32[4,1,4,8]{3,2,1,0:T(4,128)S(1)}, s32[4,1,4,8]{3,2,1,0:T(4,128)}, u32[]{:S(2)}) copy-start(s32[4,1,4,8]{3,2,1,0:T(4,128)} %refs_26_.1) | copy-start | bytes 1540
  0.0 9.1 %collective-permute-start.1 = (s32[4,1,4,8]{3,2,1,0:T(4,128)}, s32[4,1,4,8]{3,2,1,0:T(4,128)S(1)}, u32[]{:S(2)}, u32[]{:S(2)}) collective-permute-start(s32[4,1,4,8]{3,2,1,0:T(4,128)} %refs_26_.1), channel_id=1, source_target_pairs={{0,16},{8,24},{16,0},{24,8},{1,17},{9,25},{17,1},{25,9},{2,18},{10... | collective-permute-start | bytes 1544 | tf_op jit(solution)/shard_map/ppermute | solution.py:467
  1.2 7.9 %collective-permute-start = (s32[4,1,4,8]{3,2,1,0:T(4,128)}, s32[4,1,4,8]{3,2,1,0:T(4,128)S(1)}, u32[]{:S(2)}, u32[]{:S(2)}) collective-permute-start(s32[4,1,4,8]{3,2,1,0:T(4,128)} %refs_26_.1), channel_id=1, source_target_pairs={{0,8},{8,0},{16,24},{24,16},{1,9},{9,1},{17,25},{25,17},{2,10},{10... | collective-permute-start | bytes 1544 | tf_op jit(solution)/shard_map/ppermute | solution.py:467
  2.5 6.7 %collective-permute-start.2 = (s32[4,1,4,8]{3,2,1,0:T(4,128)}, s32[4,1,4,8]{3,2,1,0:T(4,128)S(1)}, u32[]{:S(2)}, u32[]{:S(2)}) collective-permute-start(s32[4,1,4,8]{3,2,1,0:T(4,128)} %refs_26_.1), channel_id=1, source_target_pairs={{0,24},{8,16},{16,8},{24,0},{1,25},{9,17},{17,9},{25,1},{2,26},{10... | collective-permute-start | bytes 1544 | tf_op jit(solution)/shard_map/ppermute | solution.py:467
  3.7 10.1 %collective-permute-start.4 = (bf16[1360,128]{1,0:T(8,128)(2,1)S(1)}, bf16[1360,128]{1,0:T(8,128)(2,1)S(1)}, u32[]{:S(2)}, u32[]{:S(2)}) collective-permute-start(bf16[1360,128]{1,0:T(8,128)(2,1)S(1)} %pad_maximum_fusion.refs_0_.refs_3_), channel_id=1, source_target_pairs={{2,0},{4,2},{6,4},{3,1},{5,3},{7,5},{10,8},{12,10},{14,12},{11,9},... | collective-permute-start | bytes 1044488 | tf_op jit(solution)/shard_map/ppermute | solution.py:479
  5.8 10.1 %collective-permute-start.3 = (bf16[1360,128]{1,0:T(8,128)(2,1)S(1)}, bf16[1360,128]{1,0:T(8,128)(2,1)S(1)}, u32[]{:S(2)}, u32[]{:S(2)}) collective-permute-start(bf16[1360,128]{1,0:T(8,128)(2,1)S(1)} %pad_maximum_fusion.refs_0_.refs_3_), channel_id=1, source_target_pairs={{0,2},{2,4},{4,6},{1,3},{3,5},{5,7},{8,10},{10,12},{12,14},{9,11},... | collective-permute-start | bytes 1044488 | tf_op jit(solution)/shard_map/ppermute | solution.py:479
  13.8 7.2 %collective-permute-start.6 = (bf16[1360,128]{1,0:T(8,128)(2,1)S(1)}, bf16[1360,128]{1,0:T(8,128)(2,1)S(1)}, u32[]{:S(2)}, u32[]{:S(2)}) collective-permute-start(bf16[1360,128]{1,0:T(8,128)(2,1)S(1)} %collective-permute-done.4.refs_1_.refs_0_.refs_5_), channel_id=1, source_target_pairs={{2,0},{4,2},{3,1},{5,3},{10,8},{12,10},{11,9},{13,11},{18,16},{20,... | collective-permute-start | bytes 1044488 | tf_op jit(solution)/shard_map/ppermute | solution.py:479
  15.9 8.9 %collective-permute-start.5 = (bf16[1360,128]{1,0:T(8,128)(2,1)S(1)}, bf16[1360,128]{1,0:T(8,128)(2,1)S(1)}, u32[]{:S(2)}, u32[]{:S(2)}) collective-permute-start(bf16[1360,128]{1,0:T(8,128)(2,1)S(1)} %collective-permute-done.3.refs_0_.refs_4_), channel_id=1, source_target_pairs={{2,4},{4,6},{3,5},{5,7},{10,12},{12,14},{11,13},{13,15},{18,20},{2... | collective-permute-start | bytes 1044488 | tf_op jit(solution)/shard_map/ppermute | solution.py:479
  21.0 16.7 %collective-permute-start.8 = (bf16[1360,128]{1,0:T(8,128)(2,1)S(1)}, bf16[1360,128]{1,0:T(8,128)(2,1)S(1)}, u32[]{:S(2)}, u32[]{:S(2)}) collective-permute-start(bf16[1360,128]{1,0:T(8,128)(2,1)S(1)} %collective-permute-done.6.refs_2_.refs_1_.refs_7_), channel_id=1, source_target_pairs={{2,0},{3,1},{10,8},{11,9},{18,16},{19,17},{26,24},{27,25}} | collective-permute-start | bytes 1044488 | tf_op jit(solution)/shard_map/ppermute | solution.py:479
  24.8 12.9 %collective-permute-start.7 = (bf16[1360,128]{1,0:T(8,128)(2,1)S(1)}, bf16[1360,128]{1,0:T(8,128)(2,1)S(1)}, u32[]{:S(2)}, u32[]{:S(2)}) collective-permute-start(bf16[1360,128]{1,0:T(8,128)(2,1)S(1)} %collective-permute-done.5.refs_1_.refs_0_.refs_6_), channel_id=1, source_target_pairs={{4,6},{5,7},{12,14},{13,15},{20,22},{21,23},{28,30},{29,31}} | collective-permute-start | bytes 1044488 | tf_op jit(solution)/shard_map/ppermute | solution.py:479
  28.7 4.5 %collective-permute-start.9 = (bf16[688,128]{1,0:T(8,128)(2,1)S(1)}, bf16[688,128]{1,0:T(8,128)(2,1)S(1)}, u32[]{:S(2)}, u32[]{:S(2)}) collective-permute-start(bf16[688,128]{1,0:T(8,128)(2,1)S(1)} %get-tuple-element.23), channel_id=1, source_target_pairs={{0,8},{8,0},{16,24},{24,16},{1,9},{9,1},{17,25},{25,17},{2,10},{10... | collective-permute-start | bytes 528392 | tf_op jit(solution)/shard_map/ppermute | solution.py:511
  30.0 5.5 %collective-permute-start.10 = (bf16[688,128]{1,0:T(8,128)(2,1)S(1)}, bf16[688,128]{1,0:T(8,128)(2,1)S(1)}, u32[]{:S(2)}, u32[]{:S(2)}) collective-permute-start(bf16[688,128]{1,0:T(8,128)(2,1)S(1)} %get-tuple-element.24), channel_id=1, source_target_pairs={{0,16},{8,24},{16,0},{24,8},{1,17},{9,25},{17,1},{25,9},{2,18},{10... | collective-permute-start | bytes 528392 | tf_op jit(solution)/shard_map/ppermute | solution.py:511
  31.2 8.6 %collective-permute-start.11 = (bf16[688,128]{1,0:T(8,128)(2,1)S(1)}, bf16[688,128]{1,0:T(8,128)(2,1)S(1)}, u32[]{:S(2)}, u32[]{:S(2)}) collective-permute-start(bf16[688,128]{1,0:T(8,128)(2,1)S(1)} %get-tuple-element.25), channel_id=1, source_target_pairs={{0,24},{8,16},{16,8},{24,0},{1,25},{9,17},{17,9},{25,1},{2,26},{10... | collective-permute-start | bytes 528392 | tf_op jit(solution)/shard_map/ppermute | solution.py:511
  33.2 8.1 %collective-permute-start.12 = (bf16[688,128]{1,0:T(8,128)(2,1)S(1)}, bf16[688,128]{1,0:T(8,128)(2,1)S(1)}, u32[]{:S(2)}, u32[]{:S(2)}) collective-permute-start(bf16[688,128]{1,0:T(8,128)(2,1)S(1)} %get-tuple-element.26), channel_id=1, source_target_pairs={{0,8},{8,0},{16,24},{24,16},{1,9},{9,1},{17,25},{25,17},{2,10},{10... | collective-permute-start | bytes 528392 | tf_op jit(solution)/shard_map/ppermute | solution.py:511
  35.5 9.5 %collective-permute-start.13 = (bf16[688,128]{1,0:T(8,128)(2,1)S(1)}, bf16[688,128]{1,0:T(8,128)(2,1)S(1)}, u32[]{:S(2)}, u32[]{:S(2)}) collective-permute-start(bf16[688,128]{1,0:T(8,128)(2,1)S(1)} %get-tuple-element.27), channel_id=1, source_target_pairs={{0,16},{8,24},{16,0},{24,8},{1,17},{9,25},{17,1},{25,9},{2,18},{10... | collective-permute-start | bytes 528392 | tf_op jit(solution)/shard_map/ppermute | solution.py:511
  37.7 7.3 %collective-permute-start.14 = (bf16[688,128]{1,0:T(8,128)(2,1)S(1)}, bf16[688,128]{1,0:T(8,128)(2,1)S(1)}, u32[]{:S(2)}, u32[]{:S(2)}) collective-permute-start(bf16[688,128]{1,0:T(8,128)(2,1)S(1)} %get-tuple-element.28), channel_id=1, source_target_pairs={{0,24},{8,16},{16,8},{24,0},{1,25},{9,17},{17,9},{25,1},{2,26},{10... | collective-permute-start | bytes 528392 | tf_op jit(solution)/shard_map/ppermute | solution.py:511
  37.7 9.9 %collective-permute-start.15 = (bf16[688,128]{1,0:T(8,128)(2,1)S(1)}, bf16[688,128]{1,0:T(8,128)(2,1)S(1)}, u32[]{:S(2)}, u32[]{:S(2)}) collective-permute-start(bf16[688,128]{1,0:T(8,128)(2,1)S(1)} %get-tuple-element.29), channel_id=1, source_target_pairs={{0,8},{8,0},{16,24},{24,16},{1,9},{9,1},{17,25},{25,17},{2,10},{10... | collective-permute-start | bytes 528392 | tf_op jit(solution)/shard_map/ppermute | solution.py:511
  39.8 22.7 %collective-permute-start.16 = (bf16[688,128]{1,0:T(8,128)(2,1)S(1)}, bf16[688,128]{1,0:T(8,128)(2,1)S(1)}, u32[]{:S(2)}, u32[]{:S(2)}) collective-permute-start(bf16[688,128]{1,0:T(8,128)(2,1)S(1)} %get-tuple-element.30), channel_id=1, source_target_pairs={{0,16},{8,24},{16,0},{24,8},{1,17},{9,25},{17,1},{25,9},{2,18},{10... | collective-permute-start | bytes 528392 | tf_op jit(solution)/shard_map/ppermute | solution.py:511
  41.3 21.2 %collective-permute-start.17 = (bf16[688,128]{1,0:T(8,128)(2,1)S(1)}, bf16[688,128]{1,0:T(8,128)(2,1)S(1)}, u32[]{:S(2)}, u32[]{:S(2)}) collective-permute-start(bf16[688,128]{1,0:T(8,128)(2,1)S(1)} %get-tuple-element.31), channel_id=1, source_target_pairs={{0,24},{8,16},{16,8},{24,0},{1,25},{9,17},{17,9},{25,1},{2,26},{10... | collective-permute-start | bytes 528392 | tf_op jit(solution)/shard_map/ppermute | solution.py:511
  45.0 17.6 %collective-permute-start.18 = (bf16[688,128]{1,0:T(8,128)(2,1)S(1)}, bf16[688,128]{1,0:T(8,128)(2,1)S(1)}, u32[]{:S(2)}, u32[]{:S(2)}) collective-permute-start(bf16[688,128]{1,0:T(8,128)(2,1)S(1)} %get-tuple-element.32), channel_id=1, source_target_pairs={{0,8},{8,0},{16,24},{24,16},{1,9},{9,1},{17,25},{25,17},{2,10},{10... | collective-permute-start | bytes 528392 | tf_op jit(solution)/shard_map/ppermute | solution.py:511
  45.0 17.6 %collective-permute-start.19 = (bf16[688,128]{1,0:T(8,128)(2,1)S(1)}, bf16[688,128]{1,0:T(8,128)(2,1)S(1)}, u32[]{:S(2)}, u32[]{:S(2)}) collective-permute-start(bf16[688,128]{1,0:T(8,128)(2,1)S(1)} %get-tuple-element.33), channel_id=1, source_target_pairs={{0,16},{8,24},{16,0},{24,8},{1,17},{9,25},{17,1},{25,9},{2,18},{10... | collective-permute-start | bytes 528392 | tf_op jit(solution)/shard_map/ppermute | solution.py:511
  47.6 15.0 %collective-permute-start.20 = (bf16[688,128]{1,0:T(8,128)(2,1)S(1)}, bf16[688,128]{1,0:T(8,128)(2,1)S(1)}, u32[]{:S(2)}, u32[]{:S(2)}) collective-permute-start(bf16[688,128]{1,0:T(8,128)(2,1)S(1)} %get-tuple-element.34), channel_id=1, source_target_pairs={{0,24},{8,16},{16,8},{24,0},{1,25},{9,17},{17,9},{25,1},{2,26},{10... | collective-permute-start | bytes 528392 | tf_op jit(solution)/shard_map/ppermute | solution.py:511
  49.5 1.0 %copy-start = (bf16[64,16,256]{2,1,0:T(8,128)(2,1)S(1)}, bf16[64,16,256]{2,1,0:T(8,128)(2,1)}, u32[]{:S(2)}) copy-start(bf16[64,16,256]{2,1,0:T(8,128)(2,1)} %param.13) | copy-start | bytes 1572868
  50.5 1.0 %copy-start.2 = (s32[64,16,64]{2,1,0:T(8,128)S(1)}, s32[64,16,64]{2,1,0:T(8,128)}, u32[]{:S(2)}) copy-start(s32[64,16,64]{2,1,0:T(8,128)} %param.19) | copy-start | bytes 786436
  51.6 0.8 copy-start.5
  52.3 0.7 copy-start.7
  62.6 16.3 %copy-start.1 = (bf16[64,16,256]{2,1,0:T(8,128)(2,1)S(1)}, bf16[64,16,256]{2,1,0:T(8,128)(2,1)}, u32[]{:S(2)}) copy-start(bf16[64,16,256]{2,1,0:T(8,128)(2,1)} %param.13) | copy-start | bytes 1572868
  62.6 16.3 %copy-start.3 = (bf16[256,256]{1,0:T(8,128)(2,1)S(1)}, bf16[256,256]{1,0:T(8,128)(2,1)}, u32[]{:S(2)}) copy-start(bf16[256,256]{1,0:T(8,128)(2,1)} %weight_ref.3) | copy-start | bytes 393220
  62.6 16.3 %copy-start.6 = (f32[256]{0:T(256)S(1)}, f32[256]{0:T(256)}, u32[]{:S(2)}) copy-start(f32[256]{0:T(256)} %param.23) | copy-start | bytes 3076
  62.6 17.4 %copy-start.8 = (f32[128]{0:T(128)S(1)}, f32[128]{0:T(128)}, u32[]{:S(2)}) copy-start(f32[128]{0:T(128)} %param.24) | copy-start | bytes 1540
  62.6 17.4 %copy-start.9 = (f32[128]{0:T(128)S(1)}, f32[128]{0:T(128)}, u32[]{:S(2)}) copy-start(f32[128]{0:T(128)} %param.25) | copy-start | bytes 1540
  71.0 9.0 %collective-permute-start.21 = (bf16[1024,128]{1,0:T(8,128)(2,1)S(1)}, bf16[1024,128]{1,0:T(8,128)(2,1)S(1)}, u32[]{:S(2)}, u32[]{:S(2)}) collective-permute-start(bf16[1024,128]{1,0:T(8,128)(2,1)S(1)} %attend.1.own_ref), channel_id=1, source_target_pairs={{0,1},{1,0},{2,3},{3,2},{4,5},{5,4},{6,7},{7,6},{8,9},{9,8},{10,11... | collective-permute-start | bytes 786440 | tf_op jit(solution)/shard_map/ppermute | solution.py:675

commit v5 on v4

--- a/solution.py
+++ b/solution.py
@@ -89,8 +89,11 @@
         slot = packed >> 24
         pos_row = (packed >> 12) & 4095
         pos_col = packed & 4095
-        deep = jnp.where(level_of == 0, sides[0] * 128, sides[1] * 256 // GROUPS[1])
-        group = jnp.where(level_of < 2, pos_row // deep, 0)
+        deep = jnp.where(level_of == 0, sides[0] * 256 // GROUPS[0], sides[1] * 256 // GROUPS[1])
+        group = jnp.zeros_like(packed)
+        for bound in range(1, max(GROUPS)):
+            group = group + jnp.where(pos_row >= bound * deep, 1, 0)
+        group = jnp.where(level_of < 2, group, 0)
         code_ref[block] = slot + group * per_block
         down_ref[block] = (pos_row - group * deep).astype(jnp.float32) * (1.0 / 256.0)
         col_ref[block] = pos_col.astype(jnp.float32) * (1.0 / 256.0)
@@ -119,17 +122,26 @@
             side = sides[3]
             size = sizes[3]
             depth = per_block * size
-            place = iota((depth, pixels), 0)
-            mixed = jnp.zeros((depth, pixels), jnp.float32)
+            step = 8 // size
+            place = iota((8, pixels), 0)
+            parts = []
+            codes = []
             for point in range(POINTS):
                 row = (head * LEVELS + 3) * POINTS + point
                 line = slice(row, row + 1)
-                value = (
+                parts.append(
                     attend_ref[block, line, :]
                     * hat(down_ref[block, line, :], (place % size // side).astype(jnp.float32))
                     * hat(col_ref[block, line, :], (place % side).astype(jnp.float32))
                 )
-                mixed = mixed + jnp.where(code_ref[block, line, :] == place // size, value, 0.0)
+                codes.append(code_ref[block, line, :] - place // size)
+            stack = []
+            for index in range(0, per_block, step):
+                mixed = jnp.zeros((8, pixels), jnp.float32)
+                for point in range(POINTS):
+                    mixed = mixed + jnp.where(codes[point] == index, parts[point], 0.0)
+                stack.append(mixed)
+            mixed = jnp.concatenate(stack, axis=0)
             weight2[block, head, pl.ds(pl.multiple_of(base2 + block * depth, depth), depth), :] = mixed.astype(
                 jnp.bfloat16
             )
@@ -200,10 +212,11 @@
     return chosen
 
 
-def relay_select_kernel(dims, order, place_ref, ids_ref, request_ref, *refs):
+def relay_select_kernel(dims, order, place_ref, request_ref, asked_ref, *refs):
     partners, candidates, capacity, sizes, blocks = dims
-    sources = refs[:candidates]
-    outs = refs[candidates:]
+    ids = refs[:partners]
+    sources = refs[partners : partners + candidates]
+    outs = refs[partners + candidates :]
     columns, numbers = order
     column = pick(columns, place_ref[1])
     which = pick(numbers, place_ref[1])
@@ -217,7 +230,7 @@
                 for level in range(LEVELS - 1):
                     size = sizes[level]
                     for rank in range(capacity):
-                        index = jnp.maximum(ids_ref[partner + 1, column, level * capacity + rank], 0)
+                        index = jnp.maximum(ids[partner][column, level * capacity + rank], 0)
                         outs[partner][base : base + size, :] = source[
                             pl.ds(pl.multiple_of(start + index * size, size), size), :
                         ]
@@ -259,9 +272,9 @@
         pltpu.make_async_copy(source, tile.at[request], sem).start()
 
 
-def gather_relay(dims, relay, request_ref, place_ref, ids_ref, blocks_refs, packs_refs, tiles, tile3):
+def gather_relay(dims, relay, request_ref, place_ref, asked_ref, near_refs, packs_refs, tiles, tile3):
     _, capacity, sizes, _, _, _, _, blocks = dims
-    rows, columns, partner_of, met = relay
+    rows, columns, partner_of = relay
     small = tile3.shape[1]
     my_row = place_ref[0]
     my_column = place_ref[1]
@@ -271,25 +284,29 @@
         size = sizes[level]
         tiles[level][jnp.maximum(request, 0)] = source[pl.ds(start, size), :]
 
-    for number, source in enumerate(blocks_refs):
-        shift = (number + 1) // 2 * (-1 if number % 2 else 1)
-        column = my_column + shift
-
-        @pl.when((column >= 0) & (column < columns))
+    for name, source in zip(NEAR, near_refs, strict=True):
+        held = [-1] * columns
+        for buffers, owners in SLOTS:
+            for column in range(columns):
+                if buffers[column] == name:
+                    held[column] = owners[column]
+        column = pick(held, my_column)
+
+        @pl.when(column >= 0)
         def _(source=source, column=column):
             owner = my_row * columns + column
             start = 0
             for level in range(LEVELS - 1):
                 size = sizes[level]
                 for rank in range(capacity):
-                    index = jnp.maximum(ids_ref[0, column, level * capacity + rank], 0)
+                    index = jnp.maximum(asked_ref[owner, level * capacity + rank], 0)
                     put(owner, level, rank, source, pl.multiple_of(start + index * size, size))
                 start += blocks * size
             tile3[owner] = source[start : start + small, :]
 
     for number, source in enumerate(packs_refs):
         slot, partner = divmod(number, rows - 1)
-        owner = partner_of(my_row, partner + 1) * columns + pick(met[slot], my_column)
+        owner = partner_of(my_row, partner + 1) * columns + pick(SLOTS[slot][1], my_column)
         base = 0
         for level in range(LEVELS - 1):
             for rank in range(capacity):
@@ -417,13 +434,6 @@
     out_ref[...] = (own * lax.rsqrt(variance + 1e-05) * gain_ref[...] + shift_ref[...]).astype(jnp.bfloat16)
 
 
-def column_order(column, columns):
-    found = []
-    for step in range(1, columns):
-        found += [(step, side) for side in (-1, 1) if 0 <= column + side * step < columns]
-    return found
-
-
 def tables(lists, grid):
     tile_rows, tile_cols, grid_cols, col_count, _ = grid
     count, blocks, level_count, per_block = lists.shape
@@ -448,6 +458,23 @@
     return found.reshape(owner.shape[0], owners.shape[0], -1)
 
 
+LINE = 4
+STEPS = (
+    ("first", None, ((0, 1), (1, 0), (2, 3), (3, 2))),
+    ("cross", None, ((1, 2), (2, 1))),
+    ("out", "cross", ((1, 0), (2, 3))),
+    ("over", "first", ((1, 2), (2, 1))),
+    ("last", "over", ((1, 0), (2, 3))),
+)
+NEAR = ("own", "first", "cross", "out", "over", "last")
+SLOTS = (
+    (("own",) * 4, (0, 1, 2, 3)),
+    (("first",) * 4, (1, 0, 3, 2)),
+    (("out", "cross", "cross", "out"), (2, 2, 1, 1)),
+    (("last", "over", "over", "last"), (3, 3, 0, 0)),
+)
+
+
 def relay_tiles(dims, row_count, col_count, pack, flat_sets, lists, grid):
     peers, capacity, sizes, _, per_block, heads, head_dim, blocks = dims
     channels = heads * head_dim
@@ -461,51 +488,52 @@
     def source_of(row, number):
         return row ^ number if power else (row + row_count - number) % row_count
 
-    gathered = [lists]
+    held = {"own": jnp.concatenate(flat_sets, axis=0)}
+
+    def move(name):
+        source, pairs = {step[0]: step[1:] for step in STEPS}[name]
+        held[name] = lax.ppermute(held[source or "own"], "col", pairs)
+
+    move("first")
+    move("cross")
+    place = jnp.stack([my_row, my_column]).astype(jnp.int32)
+    owner, local, rank = tables(lists.reshape(1, blocks, LEVELS, per_block), grid)
+    order = jnp.arange(blocks * per_block, dtype=jnp.int32)
+    code = entries(owner, rank, jnp.arange(peers, dtype=jnp.int32), capacity, order * blocks + local)[0]
+    asked = jnp.where(code >= 0, code % blocks, -1)
+    request = jnp.where(code >= 0, code // blocks, -1)
+    by_row = asked.reshape(row_count, col_count, asked.shape[1])
+    ids = []
     for number in range(1, row_count):
-        gathered.append(
-            lax.ppermute(lists, "row", [(row, partner_of(row, number)) for row in range(row_count)])
+        mine = jnp.sum(
+            jnp.where(
+                (jnp.arange(row_count) == partner_of(my_row, number))[:, None, None], by_row, 0
+            ),
+            axis=0,
         )
-    block = jnp.concatenate(flat_sets, axis=0)
-    arrived = {}
-
-    def hop(step):
-        for side in (-1, 1):
-            pairs = []
-            for column in range(col_count):
-                if 0 <= column + side * step < col_count:
-                    pairs.append((column + side, column))
-            held = arrived.get((step - 1, side), block)
-            arrived[(step, side)] = lax.ppermute(held, "col", pairs)
-
-    hop(1)
-    place = jnp.stack([my_row, my_column]).astype(jnp.int32)
-    owner, local, rank = tables(jnp.stack(gathered).reshape(row_count, blocks, LEVELS, per_block), grid)
-    row_owners = my_row * col_count + jnp.arange(col_count, dtype=jnp.int32)
-    ids = entries(owner, rank, row_owners, capacity, local)
-    order = jnp.broadcast_to(jnp.arange(blocks * per_block, dtype=jnp.int32), owner[:1].shape)
-    request = entries(owner[:1], rank[:1], jnp.arange(peers, dtype=jnp.int32), capacity, order)[0]
-
-    orders = [[(0, 1)] + column_order(column, col_count) for column in range(col_count)]
-    candidates = [sorted({order[slot] for order in orders}) for slot in range(col_count)]
-    met = []
+        ids.append(
+            lax.ppermute(mine, "row", [(row, partner_of(row, number)) for row in range(row_count)])
+        )
+
     packs = []
-    for slot in range(col_count):
-        if slot > 1:
-            hop(slot)
-        columns = [column + order[slot][0] * order[slot][1] for column, order in enumerate(orders)]
-        numbers = [candidates[slot].index(order[slot]) for order in orders]
-        met.append(columns)
-        held = [block if slot == 0 else arrived[candidate] for candidate in candidates[slot]]
+    for slot, (buffers, columns) in enumerate(SLOTS):
+        if slot == 1:
+            move("out")
+            move("over")
+        if slot == 2:
+            move("last")
+        names = sorted(set(buffers))
+        numbers = [names.index(name) for name in buffers]
         sent = pl.pallas_call(
             functools.partial(
-                relay_select_kernel, (row_count - 1, len(held), capacity, sizes, blocks), (columns, numbers)
+                relay_select_kernel, (row_count - 1, len(names), capacity, sizes, blocks), (columns, numbers)
             ),
             out_shape=[jax.ShapeDtypeStruct((pack, channels), jnp.bfloat16)] * (row_count - 1),
-            in_specs=[pl.BlockSpec(memory_space=SMEM)] * 3 + [pl.BlockSpec(memory_space=VMEM)] * len(held),
+            in_specs=[pl.BlockSpec(memory_space=SMEM)] * (row_count + 2)
+            + [pl.BlockSpec(memory_space=VMEM)] * len(names),
             out_specs=[pl.BlockSpec(memory_space=VMEM)] * (row_count - 1),
             compiler_params=pltpu.CompilerParams(vmem_limit_bytes=SELECT_VMEM),
-        )(place, ids, request, *held)
+        )(place, request, asked, *ids, *[held[name] for name in names])
         for number in range(1, row_count):
             packs.append(
                 lax.ppermute(
@@ -513,16 +541,14 @@
                 )
             )
 
-    near = [block]
-    for step in range(1, col_count):
-        near += [arrived[(step, -1)], arrived[(step, 1)]]
-    sources = (request, place, ids, *near, *packs)
+    near = [held[name] for name in NEAR]
+    sources = (request, place, asked, *near, *packs)
     spaces = (SMEM, SMEM, SMEM) + (VMEM,) * (len(near) + len(packs))
 
     def gather(refs, tiles, tile3, sem):
         gather_relay(
             dims,
-            (row_count, col_count, partner_of, met),
+            (row_count, col_count, partner_of),
             refs[0],
             refs[1],
             refs[2],
@@ -603,7 +629,7 @@
     flat_sets = [
         tile_sets[level].reshape(blocks * sizes[level], channels) for level in range(level_count)
     ]
-    if peers * capacity <= requests and col_count > 1:
+    if peers * capacity <= requests and col_count == LINE:
         gather, sources, spaces = relay_tiles(
             dims, row_count, col_count, pack, flat_sets, tile_lists, grid
         )

time: 82.8 us -> 75.9 us (0.917)
  the two profiles are of different devices: /device:TPU:17 before, /device:TPU:9 now
where the time goes in v5:
time: 75.9 us; the launch traced here: 75.5 us
  starting transfers between devices  28.4 us (37%)
  Pallas kernels  22.3 us (29%)
  waiting for transfers between devices  18.1 us (24%)
  local copies, waits for them, and re-layouts  4.71 us (6%)
  other arithmetic  1.77 us (2%)
    ppermute x12, starting transfers between devices, relay_tiles(): lax.ppermute(sent[number - 1], 'row', [(row, source_of(row, number)) for...  11.1 us
    ppermute x5, waiting for transfers between devices, move(): held[name] = lax.ppermute(held[source or 'own'], 'col', pairs)  10.6 us
    pallas_call x1, Pallas kernels, on_device(): pl.pallas_call(functools.partial(attend_kernel, dims, grid, gather, len(s...  8.42 us
    ppermute x5, starting transfers between devices, move(): held[name] = lax.ppermute(held[source or 'own'], 'col', pairs)  7.94 us
    ppermute x12, waiting for transfers between devices, relay_tiles(): lax.ppermute(sent[number - 1], 'row', [(row, source_of(row, number)) for...  7.11 us
    ppermute x1, starting transfers between devices, on_device(): other = lax.ppermute(attn, 'head', [(0, 1), (1, 0)])  6.67 us
    pallas_call x1, Pallas kernels, on_device(): pl.pallas_call(functools.partial(prep_kernel, dims), out_shape=[jax.Shape...  5.17 us
    pallas_call x4, Pallas kernels, relay_tiles(): pl.pallas_call(functools.partial(relay_select_kernel, (row_count - 1, len...  3.84 us
  transfers between devices with their start and end apart: 21, of which 8 were waited for; matrix products, arithmetic and copies ran while one was open for 3% of the time, Pallas kernels for 15%

profile of v5, /device:TPU:9, one launch (start us, length us, event | category | flops | bytes accessed | tf_op | source)
XLA Modules:
  0.0 75.5 jit_solution(16106475851606596709)
XLA Ops:
  0.0 1.1 %pad_maximum_fusion.refs_3_ = bf16[1360,128]{1,0:T(8,128)(2,1)S(1)} fusion(bf16[16,128]{1,0:T(8,128)(2,1)} %bitcast.34, bf16[64,128]{1,0:T(8,128)(2,1)} %bitcast.33, bf16[256,128]{1,0:T(8,128)(2,1)} %bitcast.31, bf16[1024,128]{1,0:T(8,128)(2,1)} %bitcast.30), kind=kLoop, calls=%fused_computation | loop fusion | flops 1392640 | bytes 696320 | tf_op jit(solution)/shard_map/concatenate | solution.py:491
  1.1 3.2 %collective-permute-start.1 = (bf16[1360,128]{1,0:T(8,128)(2,1)S(1)}, bf16[1360,128]{1,0:T(8,128)(2,1)S(1)}, u32[]{:S(2)}, u32[]{:S(2)}) collective-permute-start(bf16[1360,128]{1,0:T(8,128)(2,1)S(1)} %pad_maximum_fusion.refs_3_), channel_id=1, source_target_pairs={{2,4},{4,2},{3,5},{5,3},{10,12},{12,10},{11,13},{13,11},{18,20},{2... | collective-permute-start | bytes 1044488 | tf_op jit(solution)/shard_map/ppermute | solution.py:495
  4.3 0.1 collective-permute-start
  4.4 0.7 copy.35
  5.1 0.1 reshape.489
  5.2 0.2 convert_reduce_fusion
  5.4 0.2 select_reduce_fusion
  5.7 7.4 %collective-permute-done.refs_3_.refs_4_ = bf16[1360,128]{1,0:T(8,128)(2,1)S(1)} collective-permute-done((bf16[1360,128]{1,0:T(8,128)(2,1)S(1)}, bf16[1360,128]{1,0:T(8,128)(2,1)S(1)}, u32[]{:S(2)}, u32[]{:S(2)}) %collective-permute-start) | collective-permute-done | bytes 348192 | tf_op jit(solution)/shard_map/ppermute | solution.py:495
  13.1 2.1 %collective-permute-start.3 = (bf16[1360,128]{1,0:T(8,128)(2,1)S(1)}, bf16[1360,128]{1,0:T(8,128)(2,1)S(1)}, u32[]{:S(2)}, u32[]{:S(2)}) collective-permute-start(bf16[1360,128]{1,0:T(8,128)(2,1)S(1)} %collective-permute-done.refs_3_.refs_4_), channel_id=1, source_target_pairs={{2,4},{4,2},{3,5},{5,3},{10,12},{12,10},{11,13},{13,11},{18,20},{2... | collective-permute-start | bytes 1044488 | tf_op jit(solution)/shard_map/ppermute | solution.py:495
  15.2 0.1 sub.31
  15.3 0.1 select_reduce_fusion.1
  15.4 0.1 copy.41
  15.5 1.2 %collective-permute-start.5 = (s32[4,8]{1,0:T(4,128)S(1)}, s32[4,8]{1,0:T(4,128)S(1)}, u32[]{:S(2)}, u32[]{:S(2)}) collective-permute-start(s32[4,8]{1,0:T(4,128)S(1)} %copy.41), channel_id=1, source_target_pairs={{0,8},{8,0},{16,24},{24,16},{1,9},{9,1},{17,25},{25,17},{2,10},{10... | collective-permute-start | bytes 392 | tf_op jit(solution)/shard_map/ppermute | solution.py:515
  16.7 0.1 copy.42
  16.8 1.2 %collective-permute-start.6 = (s32[4,8]{1,0:T(4,128)S(1)}, s32[4,8]{1,0:T(4,128)S(1)}, u32[]{:S(2)}, u32[]{:S(2)}) collective-permute-start(s32[4,8]{1,0:T(4,128)S(1)} %copy.42), channel_id=1, source_target_pairs={{0,16},{8,24},{16,0},{24,8},{1,17},{9,25},{17,1},{25,9},{2,18},{10... | collective-permute-start | bytes 392 | tf_op jit(solution)/shard_map/ppermute | solution.py:515
  18.0 0.1 copy.43
  18.1 0.2 collective-permute-start.7
  18.3 0.1 copy.36
  18.4 0.0 collective-permute-done.1.refs_3_.refs_5_
  18.4 1.3 %collective-permute-start.2 = (bf16[1360,128]{1,0:T(8,128)(2,1)S(1)}, bf16[1360,128]{1,0:T(8,128)(2,1)S(1)}, u32[]{:S(2)}, u32[]{:S(2)}) collective-permute-start(bf16[1360,128]{1,0:T(8,128)(2,1)S(1)} %collective-permute-done.1.refs_3_.refs_5_), channel_id=1, source_target_pairs={{2,0},{4,6},{3,1},{5,7},{10,8},{12,14},{11,9},{13,15},{18,16},{20,... | collective-permute-start | bytes 1044488 | tf_op jit(solution)/shard_map/ppermute | solution.py:495
  19.7 3.2 %collective-permute-done.3.refs_4_.refs_7_ = bf16[1360,128]{1,0:T(8,128)(2,1)S(1)} collective-permute-done((bf16[1360,128]{1,0:T(8,128)(2,1)S(1)}, bf16[1360,128]{1,0:T(8,128)(2,1)S(1)}, u32[]{:S(2)}, u32[]{:S(2)}) %collective-permute-start.3) | collective-permute-done | bytes 348192 | tf_op jit(solution)/shard_map/ppermute | solution.py:495
  22.9 1.3 %collective-permute-start.4 = (bf16[1360,128]{1,0:T(8,128)(2,1)S(1)}, bf16[1360,128]{1,0:T(8,128)(2,1)S(1)}, u32[]{:S(2)}, u32[]{:S(2)}) collective-permute-start(bf16[1360,128]{1,0:T(8,128)(2,1)S(1)} %collective-permute-done.3.refs_4_.refs_7_), channel_id=1, source_target_pairs={{2,0},{4,6},{3,1},{5,7},{10,8},{12,14},{11,9},{13,15},{18,16},{20,... | collective-permute-start | bytes 1044488 | tf_op jit(solution)/shard_map/ppermute | solution.py:495
  24.2 0.1 pad_add_fusion.place_ref.refs_1_
  24.3 0.0 collective-permute-done.5.refs_0_
  24.3 0.0 collective-permute-done.6.refs_1_
  24.3 1.0 %shard_map.127 = (bf16[688,128]{1,0:T(8,128)(2,1)S(1)}, bf16[688,128]{1,0:T(8,128)(2,1)S(1)}, bf16[688,128]{1,0:T(8,128)(2,1)S(1)}) custom-call(s32[2]{0:T(128)S(1)} %pad_add_fusion.place_ref.refs_1_, s32[16,8]{1,0:T(8,128)S(1)} %get-tuple-element.45.request_ref.refs_0_, s32[16,8]{1,0:T(8,128)S(1)} %get-tuple-element.44.asked_ref.refs_2_, ...), custom_call_target="tpu_custom_call" | custom-call | tf_op jit(solution)/shard_map/pallas_call | solution.py:527
  25.3 1.3 %collective-permute-start.8 = (bf16[688,128]{1,0:T(8,128)(2,1)S(1)}, bf16[688,128]{1,0:T(8,128)(2,1)S(1)}, u32[]{:S(2)}, u32[]{:S(2)}) collective-permute-start(bf16[688,128]{1,0:T(8,128)(2,1)S(1)} %get-tuple-element.23), channel_id=1, source_target_pairs={{0,8},{8,0},{16,24},{24,16},{1,9},{9,1},{17,25},{25,17},{2,10},{10... | collective-permute-start | bytes 528392 | tf_op jit(solution)/shard_map/ppermute | solution.py:539
  26.5 1.2 %collective-permute-start.9 = (bf16[688,128]{1,0:T(8,128)(2,1)S(1)}, bf16[688,128]{1,0:T(8,128)(2,1)S(1)}, u32[]{:S(2)}, u32[]{:S(2)}) collective-permute-start(bf16[688,128]{1,0:T(8,128)(2,1)S(1)} %get-tuple-element.24), channel_id=1, source_target_pairs={{0,16},{8,24},{16,0},{24,8},{1,17},{9,25},{17,1},{25,9},{2,18},{10... | collective-permute-start | bytes 528392 | tf_op jit(solution)/shard_map/ppermute | solution.py:539
  27.8 0.2 collective-permute-start.10
  28.0 1.0 %shard_map.128 = (bf16[688,128]{1,0:T(8,128)(2,1)S(1)}, bf16[688,128]{1,0:T(8,128)(2,1)S(1)}, bf16[688,128]{1,0:T(8,128)(2,1)S(1)}) custom-call(s32[2]{0:T(128)S(1)} %pad_add_fusion.place_ref.refs_1_, s32[16,8]{1,0:T(8,128)S(1)} %get-tuple-element.45.request_ref.refs_0_, s32[16,8]{1,0:T(8,128)S(1)} %get-tuple-element.44.asked_ref.refs_2_, ...), custom_call_target="tpu_custom_call" | custom-call | tf_op jit(solution)/shard_map/pallas_call | solution.py:527
  29.0 1.3 %collective-permute-start.11 = (bf16[688,128]{1,0:T(8,128)(2,1)S(1)}, bf16[688,128]{1,0:T(8,128)(2,1)S(1)}, u32[]{:S(2)}, u32[]{:S(2)}) collective-permute-start(bf16[688,128]{1,0:T(8,128)(2,1)S(1)} %get-tuple-element.26), channel_id=1, source_target_pairs={{0,8},{8,0},{16,24},{24,16},{1,9},{9,1},{17,25},{25,17},{2,10},{10... | collective-permute-start | bytes 528392 | tf_op jit(solution)/shard_map/ppermute | solution.py:539
  30.2 1.0 %shard_map.129 = (bf16[688,128]{1,0:T(8,128)(2,1)S(1)}, bf16[688,128]{1,0:T(8,128)(2,1)S(1)}, bf16[688,128]{1,0:T(8,128)(2,1)S(1)}) custom-call(s32[2]{0:T(128)S(1)} %pad_add_fusion.place_ref.refs_1_, s32[16,8]{1,0:T(8,128)S(1)} %get-tuple-element.45.request_ref.refs_0_, s32[16,8]{1,0:T(8,128)S(1)} %get-tuple-element.44.asked_ref.refs_2_, ...), custom_call_target="tpu_custom_call" | custom-call | tf_op jit(solution)/shard_map/pallas_call | solution.py:527
  31.2 0.0 collective-permute-done.8.refs_9_
  31.2 1.3 %collective-permute-start.12 = (bf16[688,128]{1,0:T(8,128)(2,1)S(1)}, bf16[688,128]{1,0:T(8,128)(2,1)S(1)}, u32[]{:S(2)}, u32[]{:S(2)}) collective-permute-start(bf16[688,128]{1,0:T(8,128)(2,1)S(1)} %get-tuple-element.27), channel_id=1, source_target_pairs={{0,16},{8,24},{16,0},{24,8},{1,17},{9,25},{17,1},{25,9},{2,18},{10... | collective-permute-start | bytes 528392 | tf_op jit(solution)/shard_map/ppermute | solution.py:539
  32.5 0.0 collective-permute-done.9.refs_10_
  32.5 1.3 %collective-permute-start.13 = (bf16[688,128]{1,0:T(8,128)(2,1)S(1)}, bf16[688,128]{1,0:T(8,128)(2,1)S(1)}, u32[]{:S(2)}, u32[]{:S(2)}) collective-permute-start(bf16[688,128]{1,0:T(8,128)(2,1)S(1)} %get-tuple-element.28), channel_id=1, source_target_pairs={{0,24},{8,16},{16,8},{24,0},{1,25},{9,17},{17,9},{25,1},{2,26},{10... | collective-permute-start | bytes 528392 | tf_op jit(solution)/shard_map/ppermute | solution.py:539
  33.8 0.0 collective-permute-done.4.refs_3_.refs_8_
  33.8 1.2 %collective-permute-start.14 = (bf16[688,128]{1,0:T(8,128)(2,1)S(1)}, bf16[688,128]{1,0:T(8,128)(2,1)S(1)}, u32[]{:S(2)}, u32[]{:S(2)}) collective-permute-start(bf16[688,128]{1,0:T(8,128)(2,1)S(1)} %get-tuple-element.29), channel_id=1, source_target_pairs={{0,8},{8,0},{16,24},{24,16},{1,9},{9,1},{17,25},{25,17},{2,10},{10... | collective-permute-start | bytes 528392 | tf_op jit(solution)/shard_map/ppermute | solution.py:539
  35.1 1.0 %shard_map.130 = (bf16[688,128]{1,0:T(8,128)(2,1)S(1)}, bf16[688,128]{1,0:T(8,128)(2,1)S(1)}, bf16[688,128]{1,0:T(8,128)(2,1)S(1)}) custom-call(s32[2]{0:T(128)S(1)} %pad_add_fusion.place_ref.refs_1_, s32[16,8]{1,0:T(8,128)S(1)} %get-tuple-element.45.request_ref.refs_0_, s32[16,8]{1,0:T(8,128)S(1)} %get-tuple-element.44.asked_ref.refs_2_, ...), custom_call_target="tpu_custom_call" | custom-call | tf_op jit(solution)/shard_map/pallas_call | solution.py:527
  36.0 0.2 collective-permute-start.15
  36.2 1.0 %collective-permute-done.11.refs_12_ = bf16[688,128]{1,0:T(8,128)(2,1)S(1)} collective-permute-done((bf16[688,128]{1,0:T(8,128)(2,1)S(1)}, bf16[688,128]{1,0:T(8,128)(2,1)S(1)}, u32[]{:S(2)}, u32[]{:S(2)}) %collective-permute-start.11) | collective-permute-done | bytes 176160 | tf_op jit(solution)/shard_map/ppermute | solution.py:539
  37.2 1.2 %collective-permute-start.16 = (bf16[688,128]{1,0:T(8,128)(2,1)S(1)}, bf16[688,128]{1,0:T(8,128)(2,1)S(1)}, u32[]{:S(2)}, u32[]{:S(2)}) collective-permute-start(bf16[688,128]{1,0:T(8,128)(2,1)S(1)} %get-tuple-element.31), channel_id=1, source_target_pairs={{0,24},{8,16},{16,8},{24,0},{1,25},{9,17},{17,9},{25,1},{2,26},{10... | collective-permute-start | bytes 528392 | tf_op jit(solution)/shard_map/ppermute | solution.py:539
  38.4 2.1 %collective-permute-done.12.refs_13_ = bf16[688,128]{1,0:T(8,128)(2,1)S(1)} collective-permute-done((bf16[688,128]{1,0:T(8,128)(2,1)S(1)}, bf16[688,128]{1,0:T(8,128)(2,1)S(1)}, u32[]{:S(2)}, u32[]{:S(2)}) %collective-permute-start.12) | collective-permute-done | bytes 176160 | tf_op jit(solution)/shard_map/ppermute | solution.py:539
  40.5 0.0 collective-permute-start.17
  40.5 1.2 %collective-permute-done.13.refs_14_ = bf16[688,128]{1,0:T(8,128)(2,1)S(1)} collective-permute-done((bf16[688,128]{1,0:T(8,128)(2,1)S(1)}, bf16[688,128]{1,0:T(8,128)(2,1)S(1)}, u32[]{:S(2)}, u32[]{:S(2)}) %collective-permute-start.13) | collective-permute-done | bytes 176160 | tf_op jit(solution)/shard_map/ppermute | solution.py:539
  41.7 0.8 %collective-permute-start.18 = (bf16[688,128]{1,0:T(8,128)(2,1)S(1)}, bf16[688,128]{1,0:T(8,128)(2,1)S(1)}, u32[]{:S(2)}, u32[]{:S(2)}) collective-permute-start(bf16[688,128]{1,0:T(8,128)(2,1)S(1)} %get-tuple-element.33), channel_id=1, source_target_pairs={{0,16},{8,24},{16,0},{24,8},{1,17},{9,25},{17,1},{25,9},{2,18},{10... | collective-permute-start | bytes 528392 | tf_op jit(solution)/shard_map/ppermute | solution.py:539
  42.5 2.3 %collective-permute-done.14.refs_15_ = bf16[688,128]{1,0:T(8,128)(2,1)S(1)} collective-permute-done((bf16[688,128]{1,0:T(8,128)(2,1)S(1)}, bf16[688,128]{1,0:T(8,128)(2,1)S(1)}, u32[]{:S(2)}, u32[]{:S(2)}) %collective-permute-start.14) | collective-permute-done | bytes 176160 | tf_op jit(solution)/shard_map/ppermute | solution.py:539
  44.8 1.1 %collective-permute-start.19 = (bf16[688,128]{1,0:T(8,128)(2,1)S(1)}, bf16[688,128]{1,0:T(8,128)(2,1)S(1)}, u32[]{:S(2)}, u32[]{:S(2)}) collective-permute-start(bf16[688,128]{1,0:T(8,128)(2,1)S(1)} %get-tuple-element.34), channel_id=1, source_target_pairs={{0,24},{8,16},{16,8},{24,0},{1,25},{9,17},{17,9},{25,1},{2,26},{10... | collective-permute-start | bytes 528392 | tf_op jit(solution)/shard_map/ppermute | solution.py:539
  46.0 1.0 %copy-done = bf16[64,16,256]{2,1,0:T(8,128)(2,1)S(1)} copy-done((bf16[64,16,256]{2,1,0:T(8,128)(2,1)S(1)}, bf16[64,16,256]{2,1,0:T(8,128)(2,1)}, u32[]{:S(2)}) %copy-start) | copy-done | bytes 524312
  47.0 1.0 %copy-done.2 = s32[64,16,64]{2,1,0:T(8,128)S(1)} copy-done((s32[64,16,64]{2,1,0:T(8,128)S(1)}, s32[64,16,64]{2,1,0:T(8,128)}, u32[]{:S(2)}) %copy-start.2) | copy-done | bytes 262168
  48.1 0.8 %copy-done.5 = bf16[256,64]{0,1:T(8,128)(2,1)S(1)} copy-done((bf16[256,64]{0,1:T(8,128)(2,1)S(1)}, bf16[256,64]{0,1:T(8,128)(2,1)}, u32[]{:S(2)}) %copy-start.5) | copy-done | bytes 32792
  48.8 0.7 copy-done.7
  49.5 5.2 %prep.1 = (bf16[4,4,4,256,256]{4,3,2,1,0:T(8,128)(2,1)S(1)}, bf16[4,4,256,256]{3,2,1,0:T(8,128)(2,1)S(1)}, f32[4,64,256]{2,1,0:T(8,128)S(1)}, s32[4,64,256]{2,1,...) custom-call(bf16[1024,256]{1,0:T(8,128)(2,1)S(1)} %bitcast.21, bf16[64,256]{1,0:T(8,128)(2,1)S(1)} %bitcast.25, ...), custom_call_target="tpu_custom_call" | custom-call | tf_op jit(solution)/shard_map/prep/pallas_call | solution.py:648
  54.7 1.8 %hot.1.refs_21_ = bf16[4,4,4,256,256]{4,3,2,1,0:T(8,128)(2,1)S(1)} custom-call(f32[4,64,256]{2,1,0:T(8,128)S(1)} %get-tuple-element.35.attend_ref, s32[4,64,256]{2,1,0:T(8,128)S(1)} %get-tuple-element.36.code_ref, f32[4,64,256]{2,1,0:T(8,128)S(1)} %get-tuple-element.37.col_ref), custom_call_target="tpu_custom_call" | custom-call | tf_op jit(solution)/shard_map/hot/pallas_call | solution.py:670
  56.5 0.0 collective-permute-done.16.refs_17_
  56.5 0.0 collective-permute-done.17.refs_18_
  56.5 0.4 collective-permute-done.19.refs_20_
  56.9 0.0 copy-start.8
  56.9 0.0 copy-start.9
  57.0 8.4 %attend.1.own_ref = bf16[1024,128]{1,0:T(8,128)(2,1)S(1)} custom-call(s32[16,8]{1,0:T(8,128)S(1)} %get-tuple-element.45.request_ref.refs_0_, s32[2]{0:T(128)S(1)} %pad_add_fusion.place_ref.refs_1_, s32[16,8]{1,0:T(8,128)S(1)} %get-tuple-element.44.asked_ref.refs_2_, bf16[1360,128]{1,0:T(8,128)(2,1)S(1)} %pad_maximum_fusion.refs_3_, ...), custom_call_target="tpu_custom_call" | custom-call | tf_op jit(solution)/shard_map/attend/pallas_call | solution.py:679
  65.4 6.7 %collective-permute-start.20 = (bf16[1024,128]{1,0:T(8,128)(2,1)S(1)}, bf16[1024,128]{1,0:T(8,128)(2,1)S(1)}, u32[]{:S(2)}, u32[]{:S(2)}) collective-permute-start(bf16[1024,128]{1,0:T(8,128)(2,1)S(1)} %attend.1.own_ref), channel_id=1, source_target_pairs={{0,1},{1,0},{2,3},{3,2},{4,5},{5,4},{6,7},{7,6},{8,9},{9,8},{10,11... | collective-permute-start | bytes 786440 | tf_op jit(solution)/shard_map/ppermute | solution.py:701
  72.1 0.7 own.1.pre_ref
  72.8 0.4 collective-permute-done.20.other_ref
  73.2 2.3 %norm.1 = bf16[1024,128]{1,0:T(8,128)(2,1)} custom-call(s32[1]{0:T(128)} %bitcast.head_ref, f32[1024,256]{1,0:T(8,128)S(1)} %own.1.pre_ref, bf16[1024,128]{1,0:T(8,128)(2,1)S(1)} %collective-permute-done.20.other_ref, bf16[256,256]{1,0:T(8,128)(2,1)S(1)} %copy-done.3, f32[1,128]{1,0:T(1,128)S(1)} %bitcast.28, f32[1,128]{1,0:T(1,128)S(1)} %bitcast.29), custom_call_target="tpu_custom_call" | custom-call | tf_op jit(solution)/shard_map/norm/pallas_call | solution.py:720
  (28 shorter events, 0.1 us)
Async XLA Ops:
  0.0 56.9 %copy-start.4 = (s32[4,1,4,8]{3,2,1,0:T(4,128)S(1)}, s32[4,1,4,8]{3,2,1,0:T(4,128)}, u32[]{:S(2)}) copy-start(s32[4,1,4,8]{3,2,1,0:T(4,128)} %refs_25_.1) | copy-start | bytes 1540
  1.1 17.3 %collective-permute-start.1 = (bf16[1360,128]{1,0:T(8,128)(2,1)S(1)}, bf16[1360,128]{1,0:T(8,128)(2,1)S(1)}, u32[]{:S(2)}, u32[]{:S(2)}) collective-permute-start(bf16[1360,128]{1,0:T(8,128)(2,1)S(1)} %pad_maximum_fusion.refs_3_), channel_id=1, source_target_pairs={{2,4},{4,2},{3,5},{5,3},{10,12},{12,10},{11,13},{13,11},{18,20},{2... | collective-permute-start | bytes 1044488 | tf_op jit(solution)/shard_map/ppermute | solution.py:495
  4.3 8.8 %collective-permute-start = (bf16[1360,128]{1,0:T(8,128)(2,1)S(1)}, bf16[1360,128]{1,0:T(8,128)(2,1)S(1)}, u32[]{:S(2)}, u32[]{:S(2)}) collective-permute-start(bf16[1360,128]{1,0:T(8,128)(2,1)S(1)} %pad_maximum_fusion.refs_3_), channel_id=1, source_target_pairs={{0,2},{2,0},{4,6},{6,4},{1,3},{3,1},{5,7},{7,5},{8,10},{10,8},{12,... | collective-permute-start | bytes 1044488 | tf_op jit(solution)/shard_map/ppermute | solution.py:495
  13.1 9.8 %collective-permute-start.3 = (bf16[1360,128]{1,0:T(8,128)(2,1)S(1)}, bf16[1360,128]{1,0:T(8,128)(2,1)S(1)}, u32[]{:S(2)}, u32[]{:S(2)}) collective-permute-start(bf16[1360,128]{1,0:T(8,128)(2,1)S(1)} %collective-permute-done.refs_3_.refs_4_), channel_id=1, source_target_pairs={{2,4},{4,2},{3,5},{5,3},{10,12},{12,10},{11,13},{13,11},{18,20},{2... | collective-permute-start | bytes 1044488 | tf_op jit(solution)/shard_map/ppermute | solution.py:495
  15.5 8.8 %collective-permute-start.5 = (s32[4,8]{1,0:T(4,128)S(1)}, s32[4,8]{1,0:T(4,128)S(1)}, u32[]{:S(2)}, u32[]{:S(2)}) collective-permute-start(s32[4,8]{1,0:T(4,128)S(1)} %copy.41), channel_id=1, source_target_pairs={{0,8},{8,0},{16,24},{24,16},{1,9},{9,1},{17,25},{25,17},{2,10},{10... | collective-permute-start | bytes 392 | tf_op jit(solution)/shard_map/ppermute | solution.py:515
  16.8 7.5 %collective-permute-start.6 = (s32[4,8]{1,0:T(4,128)S(1)}, s32[4,8]{1,0:T(4,128)S(1)}, u32[]{:S(2)}, u32[]{:S(2)}) collective-permute-start(s32[4,8]{1,0:T(4,128)S(1)} %copy.42), channel_id=1, source_target_pairs={{0,16},{8,24},{16,0},{24,8},{1,17},{9,25},{17,1},{25,9},{2,18},{10... | collective-permute-start | bytes 392 | tf_op jit(solution)/shard_map/ppermute | solution.py:515
  18.1 6.2 %collective-permute-start.7 = (s32[4,8]{1,0:T(4,128)S(1)}, s32[4,8]{1,0:T(4,128)S(1)}, u32[]{:S(2)}, u32[]{:S(2)}) collective-permute-start(s32[4,8]{1,0:T(4,128)S(1)} %copy.43), channel_id=1, source_target_pairs={{0,24},{8,16},{16,8},{24,0},{1,25},{9,17},{17,9},{25,1},{2,26},{10... | collective-permute-start | bytes 392 | tf_op jit(solution)/shard_map/ppermute | solution.py:515
  18.4 10.6 %collective-permute-start.2 = (bf16[1360,128]{1,0:T(8,128)(2,1)S(1)}, bf16[1360,128]{1,0:T(8,128)(2,1)S(1)}, u32[]{:S(2)}, u32[]{:S(2)}) collective-permute-start(bf16[1360,128]{1,0:T(8,128)(2,1)S(1)} %collective-permute-done.1.refs_3_.refs_5_), channel_id=1, source_target_pairs={{2,0},{4,6},{3,1},{5,7},{10,8},{12,14},{11,9},{13,15},{18,16},{20,... | collective-permute-start | bytes 1044488 | tf_op jit(solution)/shard_map/ppermute | solution.py:495
  22.9 10.9 %collective-permute-start.4 = (bf16[1360,128]{1,0:T(8,128)(2,1)S(1)}, bf16[1360,128]{1,0:T(8,128)(2,1)S(1)}, u32[]{:S(2)}, u32[]{:S(2)}) collective-permute-start(bf16[1360,128]{1,0:T(8,128)(2,1)S(1)} %collective-permute-done.3.refs_4_.refs_7_), channel_id=1, source_target_pairs={{2,0},{4,6},{3,1},{5,7},{10,8},{12,14},{11,9},{13,15},{18,16},{20,... | collective-permute-start | bytes 1044488 | tf_op jit(solution)/shard_map/ppermute | solution.py:495
  25.3 5.9 %collective-permute-start.8 = (bf16[688,128]{1,0:T(8,128)(2,1)S(1)}, bf16[688,128]{1,0:T(8,128)(2,1)S(1)}, u32[]{:S(2)}, u32[]{:S(2)}) collective-permute-start(bf16[688,128]{1,0:T(8,128)(2,1)S(1)} %get-tuple-element.23), channel_id=1, source_target_pairs={{0,8},{8,0},{16,24},{24,16},{1,9},{9,1},{17,25},{25,17},{2,10},{10... | collective-permute-start | bytes 528392 | tf_op jit(solution)/shard_map/ppermute | solution.py:539
  26.5 6.0 %collective-permute-start.9 = (bf16[688,128]{1,0:T(8,128)(2,1)S(1)}, bf16[688,128]{1,0:T(8,128)(2,1)S(1)}, u32[]{:S(2)}, u32[]{:S(2)}) collective-permute-start(bf16[688,128]{1,0:T(8,128)(2,1)S(1)} %get-tuple-element.24), channel_id=1, source_target_pairs={{0,16},{8,24},{16,0},{24,8},{1,17},{9,25},{17,1},{25,9},{2,18},{10... | collective-permute-start | bytes 528392 | tf_op jit(solution)/shard_map/ppermute | solution.py:539
  27.8 8.2 %collective-permute-start.10 = (bf16[688,128]{1,0:T(8,128)(2,1)S(1)}, bf16[688,128]{1,0:T(8,128)(2,1)S(1)}, u32[]{:S(2)}, u32[]{:S(2)}) collective-permute-start(bf16[688,128]{1,0:T(8,128)(2,1)S(1)} %get-tuple-element.25), channel_id=1, source_target_pairs={{0,24},{8,16},{16,8},{24,0},{1,25},{9,17},{17,9},{25,1},{2,26},{10... | collective-permute-start | bytes 528392 | tf_op jit(solution)/shard_map/ppermute | solution.py:539
  29.0 8.3 %collective-permute-start.11 = (bf16[688,128]{1,0:T(8,128)(2,1)S(1)}, bf16[688,128]{1,0:T(8,128)(2,1)S(1)}, u32[]{:S(2)}, u32[]{:S(2)}) collective-permute-start(bf16[688,128]{1,0:T(8,128)(2,1)S(1)} %get-tuple-element.26), channel_id=1, source_target_pairs={{0,8},{8,0},{16,24},{24,16},{1,9},{9,1},{17,25},{25,17},{2,10},{10... | collective-permute-start | bytes 528392 | tf_op jit(solution)/shard_map/ppermute | solution.py:539
  31.2 9.3 %collective-permute-start.12 = (bf16[688,128]{1,0:T(8,128)(2,1)S(1)}, bf16[688,128]{1,0:T(8,128)(2,1)S(1)}, u32[]{:S(2)}, u32[]{:S(2)}) collective-permute-start(bf16[688,128]{1,0:T(8,128)(2,1)S(1)} %get-tuple-element.27), channel_id=1, source_target_pairs={{0,16},{8,24},{16,0},{24,8},{1,17},{9,25},{17,1},{25,9},{2,18},{10... | collective-permute-start | bytes 528392 | tf_op jit(solution)/shard_map/ppermute | solution.py:539
  32.5 9.2 %collective-permute-start.13 = (bf16[688,128]{1,0:T(8,128)(2,1)S(1)}, bf16[688,128]{1,0:T(8,128)(2,1)S(1)}, u32[]{:S(2)}, u32[]{:S(2)}) collective-permute-start(bf16[688,128]{1,0:T(8,128)(2,1)S(1)} %get-tuple-element.28), channel_id=1, source_target_pairs={{0,24},{8,16},{16,8},{24,0},{1,25},{9,17},{17,9},{25,1},{2,26},{10... | collective-permute-start | bytes 528392 | tf_op jit(solution)/shard_map/ppermute | solution.py:539
  33.8 11.0 %collective-permute-start.14 = (bf16[688,128]{1,0:T(8,128)(2,1)S(1)}, bf16[688,128]{1,0:T(8,128)(2,1)S(1)}, u32[]{:S(2)}, u32[]{:S(2)}) collective-permute-start(bf16[688,128]{1,0:T(8,128)(2,1)S(1)} %get-tuple-element.29), channel_id=1, source_target_pairs={{0,8},{8,0},{16,24},{24,16},{1,9},{9,1},{17,25},{25,17},{2,10},{10... | collective-permute-start | bytes 528392 | tf_op jit(solution)/shard_map/ppermute | solution.py:539
  36.0 20.4 %collective-permute-start.15 = (bf16[688,128]{1,0:T(8,128)(2,1)S(1)}, bf16[688,128]{1,0:T(8,128)(2,1)S(1)}, u32[]{:S(2)}, u32[]{:S(2)}) collective-permute-start(bf16[688,128]{1,0:T(8,128)(2,1)S(1)} %get-tuple-element.30), channel_id=1, source_target_pairs={{0,16},{8,24},{16,0},{24,8},{1,17},{9,25},{17,1},{25,9},{2,18},{10... | collective-permute-start | bytes 528392 | tf_op jit(solution)/shard_map/ppermute | solution.py:539
  37.2 19.2 %collective-permute-start.16 = (bf16[688,128]{1,0:T(8,128)(2,1)S(1)}, bf16[688,128]{1,0:T(8,128)(2,1)S(1)}, u32[]{:S(2)}, u32[]{:S(2)}) collective-permute-start(bf16[688,128]{1,0:T(8,128)(2,1)S(1)} %get-tuple-element.31), channel_id=1, source_target_pairs={{0,24},{8,16},{16,8},{24,0},{1,25},{9,17},{17,9},{25,1},{2,26},{10... | collective-permute-start | bytes 528392 | tf_op jit(solution)/shard_map/ppermute | solution.py:539
  40.5 16.0 %collective-permute-start.17 = (bf16[688,128]{1,0:T(8,128)(2,1)S(1)}, bf16[688,128]{1,0:T(8,128)(2,1)S(1)}, u32[]{:S(2)}, u32[]{:S(2)}) collective-permute-start(bf16[688,128]{1,0:T(8,128)(2,1)S(1)} %get-tuple-element.32), channel_id=1, source_target_pairs={{0,8},{8,0},{16,24},{24,16},{1,9},{9,1},{17,25},{25,17},{2,10},{10... | collective-permute-start | bytes 528392 | tf_op jit(solution)/shard_map/ppermute | solution.py:539
  41.7 14.8 %collective-permute-start.18 = (bf16[688,128]{1,0:T(8,128)(2,1)S(1)}, bf16[688,128]{1,0:T(8,128)(2,1)S(1)}, u32[]{:S(2)}, u32[]{:S(2)}) collective-permute-start(bf16[688,128]{1,0:T(8,128)(2,1)S(1)} %get-tuple-element.33), channel_id=1, source_target_pairs={{0,16},{8,24},{16,0},{24,8},{1,17},{9,25},{17,1},{25,9},{2,18},{10... | collective-permute-start | bytes 528392 | tf_op jit(solution)/shard_map/ppermute | solution.py:539
  44.8 12.1 %collective-permute-start.19 = (bf16[688,128]{1,0:T(8,128)(2,1)S(1)}, bf16[688,128]{1,0:T(8,128)(2,1)S(1)}, u32[]{:S(2)}, u32[]{:S(2)}) collective-permute-start(bf16[688,128]{1,0:T(8,128)(2,1)S(1)} %get-tuple-element.34), channel_id=1, source_target_pairs={{0,24},{8,16},{16,8},{24,0},{1,25},{9,17},{17,9},{25,1},{2,26},{10... | collective-permute-start | bytes 528392 | tf_op jit(solution)/shard_map/ppermute | solution.py:539
  46.0 1.0 %copy-start = (bf16[64,16,256]{2,1,0:T(8,128)(2,1)S(1)}, bf16[64,16,256]{2,1,0:T(8,128)(2,1)}, u32[]{:S(2)}) copy-start(bf16[64,16,256]{2,1,0:T(8,128)(2,1)} %param.13) | copy-start | bytes 1572868
  47.0 1.0 %copy-start.2 = (s32[64,16,64]{2,1,0:T(8,128)S(1)}, s32[64,16,64]{2,1,0:T(8,128)}, u32[]{:S(2)}) copy-start(s32[64,16,64]{2,1,0:T(8,128)} %param.19) | copy-start | bytes 786436
  48.1 0.8 %copy-start.5 = (bf16[256,64]{0,1:T(8,128)(2,1)S(1)}, bf16[256,64]{0,1:T(8,128)(2,1)}, u32[]{:S(2)}) copy-start(bf16[256,64]{0,1:T(8,128)(2,1)} %param.20) | copy-start | bytes 98308
  48.8 0.7 copy-start.7
  56.9 15.1 %copy-start.1 = (bf16[64,16,256]{2,1,0:T(8,128)(2,1)S(1)}, bf16[64,16,256]{2,1,0:T(8,128)(2,1)}, u32[]{:S(2)}) copy-start(bf16[64,16,256]{2,1,0:T(8,128)(2,1)} %param.13) | copy-start | bytes 1572868
  56.9 15.1 %copy-start.3 = (bf16[256,256]{1,0:T(8,128)(2,1)S(1)}, bf16[256,256]{1,0:T(8,128)(2,1)}, u32[]{:S(2)}) copy-start(bf16[256,256]{1,0:T(8,128)(2,1)} %weight_ref.3) | copy-start | bytes 393220
  56.9 15.1 %copy-start.6 = (f32[256]{0:T(256)S(1)}, f32[256]{0:T(256)}, u32[]{:S(2)}) copy-start(f32[256]{0:T(256)} %param.23) | copy-start | bytes 3076
  56.9 16.3 %copy-start.8 = (f32[128]{0:T(128)S(1)}, f32[128]{0:T(128)}, u32[]{:S(2)}) copy-start(f32[128]{0:T(128)} %param.24) | copy-start | bytes 1540
  56.9 16.3 %copy-start.9 = (f32[128]{0:T(128)S(1)}, f32[128]{0:T(128)}, u32[]{:S(2)}) copy-start(f32[128]{0:T(128)} %param.25) | copy-start | bytes 1540
  65.4 7.8 %collective-permute-start.20 = (bf16[1024,128]{1,0:T(8,128)(2,1)S(1)}, bf16[1024,128]{1,0:T(8,128)(2,1)S(1)}, u32[]{:S(2)}, u32[]{:S(2)}) collective-permute-start(bf16[1024,128]{1,0:T(8,128)(2,1)S(1)} %attend.1.own_ref), channel_id=1, source_target_pairs={{0,1},{1,0},{2,3},{3,2},{4,5},{5,4},{6,7},{7,6},{8,9},{9,8},{10,11... | collective-permute-start | bytes 786440 | tf_op jit(solution)/shard_map/ppermute | solution.py:701

commit v6 on v5

--- a/solution.py
+++ b/solution.py
@@ -35,148 +35,111 @@
 
 def prep_kernel(
     dims,
-    query_hbm,
-    logit_hbm,
-    bias_hbm,
-    sample_hbm,
-    weight1,
-    weight2,
-    attend_ref,
-    code_ref,
-    down_ref,
-    col_ref,
     query_ref,
     logit_ref,
     bias_ref,
     sample_ref,
-    sem,
+    weight0,
+    weight1,
+    weight2,
+    down_ref,
+    attend_ref,
+    code_ref,
+    col_ref,
+    hot_ref,
 ):
-    _, _, sizes, sides, per_block, heads, _, blocks = dims
+    _, _, sizes, sides, per_block, heads, _, _ = dims
+    block = pl.program_id(0)
     pixels = sizes[0]
     base2 = per_block * sizes[2]
     lanes = LEVELS * POINTS
-    moves = [
-        pltpu.make_async_copy(source, target, sem.at[number])
-        for number, (source, target) in enumerate(
-            (
-                (query_hbm, query_ref),
-                (logit_hbm, logit_ref),
-                (bias_hbm, bias_ref),
-                (sample_hbm, sample_ref),
-            )
-        )
-    ]
-    for move in moves:
-        move.start()
-    weight2[...] = jnp.zeros_like(weight2)
-    for move in moves:
-        move.wait()
-
-    def one(block, carry):
-        here = pl.ds(pl.multiple_of(block * pixels, pixels), pixels)
-        logits = lax.dot_general(
-            query_ref[here, :], logit_ref[...], (((1,), (1,)), ((), ())), preferred_element_type=jnp.float32
-        )
-        logits = (logits + bias_ref[...]).T
-        for head in range(heads):
-            part = logits[head * lanes : (head + 1) * lanes, :]
-            part = jnp.exp(part - jnp.max(part, axis=0, keepdims=True))
-            attend_ref[block, head * lanes : (head + 1) * lanes, :] = part / jnp.sum(
-                part, axis=0, keepdims=True
-            )
-        packed = sample_ref[here, :].T
-        level_of = iota(packed.shape, 0) // POINTS % LEVELS
-        slot = packed >> 24
-        pos_row = (packed >> 12) & 4095
-        pos_col = packed & 4095
-        deep = jnp.where(level_of == 0, sides[0] * 256 // GROUPS[0], sides[1] * 256 // GROUPS[1])
-        group = jnp.zeros_like(packed)
-        for bound in range(1, max(GROUPS)):
-            group = group + jnp.where(pos_row >= bound * deep, 1, 0)
-        group = jnp.where(level_of < 2, group, 0)
-        code_ref[block] = slot + group * per_block
-        down_ref[block] = (pos_row - group * deep).astype(jnp.float32) * (1.0 / 256.0)
-        col_ref[block] = pos_col.astype(jnp.float32) * (1.0 / 256.0)
-
-        for head in range(heads):
-            hot_rows(1, block, head, sides, per_block, attend_ref, code_ref, col_ref, weight1)
-            side = sides[2]
-            size = sizes[2]
-            place = iota((size, pixels), 0)
+    logits = lax.dot_general(
+        query_ref[...], logit_ref[...], (((1,), (1,)), ((), ())), preferred_element_type=jnp.float32
+    )
+    logits = (logits + bias_ref[...]).T
+    for head in range(heads):
+        part = logits[head * lanes : (head + 1) * lanes, :]
+        part = jnp.exp(part - jnp.max(part, axis=0, keepdims=True))
+        attend_ref[head * lanes : (head + 1) * lanes, :] = part / jnp.sum(part, axis=0, keepdims=True)
+    packed = sample_ref[...].T
+    level_of = iota(packed.shape, 0) // POINTS % LEVELS
+    slot = packed >> 24
+    pos_row = (packed >> 12) & 4095
+    pos_col = packed & 4095
+    deep = jnp.where(level_of == 0, sides[0] * 256 // GROUPS[0], sides[1] * 256 // GROUPS[1])
+    group = jnp.zeros_like(packed)
+    for bound in range(1, max(GROUPS)):
+        group = group + jnp.where(pos_row >= bound * deep, 1, 0)
+    group = jnp.where(level_of < 2, group, 0)
+    code_ref[...] = slot + group * per_block
+    down_ref[0] = (pos_row - group * deep).astype(jnp.float32) * (1.0 / 256.0)
+    col_ref[...] = pos_col.astype(jnp.float32) * (1.0 / 256.0)
+
+    def line_of(head, level, point):
+        row = (head * LEVELS + level) * POINTS + point
+        return slice(row, row + 1)
+
+    def hot_of(head, level, point, rows):
+        line = line_of(head, level, point)
+        return jnp.where(code_ref[line, :] == iota((rows, pixels), 0), attend_ref[line, :], 0.0)
+
+    weight2[0, :, base2:, :] = jnp.zeros((heads, weight2.shape[2] - base2, pixels), jnp.bfloat16)
+    for head in range(heads):
+        for level in range(2):
+            side = sides[level]
+            weight = (weight0, weight1)[level]
+            step = 16 // side
+            rows = GROUPS[level] * per_block
+            for point in range(POINTS):
+                hot_ref[point, :rows, :] = hot_of(head, level, point, rows)
+                across = hat(
+                    col_ref[line_of(head, level, point), :], iota((side, pixels), 0).astype(jnp.float32)
+                )
+                for index in range(0, rows, step):
+                    stack = [hot_ref[point, row : row + 1, :] * across for row in range(index, index + step)]
+                    piece = stack[0] if step == 1 else jnp.concatenate(stack, axis=0)
+                    weight[0, head, point, index * side : (index + step) * side, :] = piece.astype(
+                        jnp.bfloat16
+                    )
+        for level in (2, 3):
+            side = sides[level]
+            size = sizes[level]
+            step = max(1, 8 // size)
+            tall = size * step
+            place = iota((tall, pixels), 0)
             parts = []
-            codes = []
             for point in range(POINTS):
-                row = (head * LEVELS + 2) * POINTS + point
-                line = slice(row, row + 1)
+                line = line_of(head, level, point)
                 parts.append(
-                    attend_ref[block, line, :]
-                    * hat(down_ref[block, line, :], (place // side).astype(jnp.float32))
-                    * hat(col_ref[block, line, :], (place % side).astype(jnp.float32))
+                    hat(down_ref[0, line, :], (place % size // side).astype(jnp.float32))
+                    * hat(col_ref[line, :], (place % side).astype(jnp.float32))
                 )
-                codes.append(code_ref[block, line, :])
-            for index in range(per_block):
-                mixed = jnp.zeros((size, pixels), jnp.float32)
-                for point in range(POINTS):
-                    mixed = mixed + jnp.where(codes[point] == index, parts[point], 0.0)
-                weight2[block, head, index * size : (index + 1) * size, :] = mixed.astype(jnp.bfloat16)
-            side = sides[3]
-            size = sizes[3]
-            depth = per_block * size
-            step = 8 // size
-            place = iota((8, pixels), 0)
-            parts = []
-            codes = []
-            for point in range(POINTS):
-                row = (head * LEVELS + 3) * POINTS + point
-                line = slice(row, row + 1)
-                parts.append(
-                    attend_ref[block, line, :]
-                    * hat(down_ref[block, line, :], (place % size // side).astype(jnp.float32))
-                    * hat(col_ref[block, line, :], (place % side).astype(jnp.float32))
-                )
-                codes.append(code_ref[block, line, :] - place // size)
+                if step == 1:
+                    hot_ref[point, :per_block, :] = hot_of(head, level, point, per_block)
+                else:
+                    line = line_of(head, level, point)
+                    parts[-1] = parts[-1] * attend_ref[line, :]
+                    hot_ref[point, :tall, :] = jnp.broadcast_to(
+                        code_ref[line, :], (tall, pixels)
+                    ).astype(jnp.float32) - (place // size).astype(jnp.float32)
             stack = []
             for index in range(0, per_block, step):
-                mixed = jnp.zeros((8, pixels), jnp.float32)
+                mixed = jnp.zeros((tall, pixels), jnp.float32)
                 for point in range(POINTS):
-                    mixed = mixed + jnp.where(codes[point] == index, parts[point], 0.0)
+                    if step == 1:
+                        mixed = mixed + hot_ref[point, index : index + 1, :] * parts[point]
+                    else:
+                        mixed = mixed + jnp.where(hot_ref[point, :tall, :] == float(index), parts[point], 0.0)
                 stack.append(mixed)
-            mixed = jnp.concatenate(stack, axis=0)
-            weight2[block, head, pl.ds(pl.multiple_of(base2 + block * depth, depth), depth), :] = mixed.astype(
-                jnp.bfloat16
-            )
-        return carry
-
-    lax.fori_loop(0, blocks, one, 0)
-
-
-def hot_rows(level, block, head, sides, per_block, attend_ref, code_ref, col_ref, weight):
-    side = sides[level]
-    pixels = attend_ref.shape[2]
-    step = 16 // side
-    for point in range(POINTS):
-        row = (head * LEVELS + level) * POINTS + point
-        line = slice(row, row + 1)
-        code = code_ref[block, line, :]
-        across = attend_ref[block, line, :] * hat(
-            col_ref[block, line, :], (iota((16, pixels), 0) % side).astype(jnp.float32)
-        )
-        for index in range(0, GROUPS[level] * per_block, step):
-            wanted = index + iota((16, pixels), 0) // side
-            weight[block, head, point, index * side : (index + step) * side, :] = jnp.where(
-                code == wanted, across, 0.0
-            ).astype(jnp.bfloat16)
-
-
-def hot_kernel(dims, attend_ref, code_ref, col_ref, weight0):
-    _, _, _, sides, per_block, heads, _, blocks = dims
-
-    def one(block, carry):
-        for head in range(heads):
-            hot_rows(0, block, head, sides, per_block, attend_ref, code_ref, col_ref, weight0)
-        return carry
-
-    lax.fori_loop(0, blocks, one, 0)
+            if level == 2:
+                for index, mixed in enumerate(stack):
+                    weight2[0, head, index * tall : (index + 1) * tall, :] = mixed.astype(jnp.bfloat16)
+            else:
+                depth = per_block * size
+                first = pl.multiple_of(base2 + block * depth, depth)
+                weight2[0, head, pl.ds(first, depth), :] = jnp.concatenate(stack, axis=0).astype(
+                    jnp.bfloat16
+                )
 
 
 def select_kernel(dims, ids_ref, zero_ref, one_ref, two_ref, three_ref, out_ref, sem):
@@ -459,6 +422,8 @@
 
 
 LINE = 4
+SELECT_COST = pl.CostEstimate(flops=500_000_000, bytes_accessed=1_000_000, transcendentals=0)
+PREP_COST = pl.CostEstimate(flops=2_000_000_000, bytes_accessed=4_000_000, transcendentals=0)
 STEPS = (
     ("first", None, ((0, 1), (1, 0), (2, 3), (3, 2))),
     ("cross", None, ((1, 2), (2, 1))),
@@ -533,6 +498,7 @@
             + [pl.BlockSpec(memory_space=VMEM)] * len(names),
             out_specs=[pl.BlockSpec(memory_space=VMEM)] * (row_count - 1),
             compiler_params=pltpu.CompilerParams(vmem_limit_bytes=SELECT_VMEM),
+            cost_estimate=SELECT_COST,
         )(place, request, asked, *ids, *[held[name] for name in names])
         for number in range(1, row_count):
             packs.append(
@@ -644,37 +610,37 @@
     depth1 = GROUPS[1] * per_block * sides[1]
     depth2 = per_block * sizes[2] + requests * sizes[3]
     whole = pl.BlockSpec(memory_space=VMEM)
-    turned = (blocks, lanes, pixels)
-    weight1, weight2, attend, code, down, col = pl.pallas_call(
+    weights = pl.pallas_call(
         functools.partial(prep_kernel, dims),
         out_shape=[
+            jax.ShapeDtypeStruct((blocks, heads, POINTS, depth0, pixels), jnp.bfloat16),
             jax.ShapeDtypeStruct((blocks, heads, POINTS, depth1, pixels), jnp.bfloat16),
             jax.ShapeDtypeStruct((blocks, heads, depth2, pixels), jnp.bfloat16),
-            jax.ShapeDtypeStruct(turned, jnp.float32),
-            jax.ShapeDtypeStruct(turned, jnp.int32),
-            jax.ShapeDtypeStruct(turned, jnp.float32),
-            jax.ShapeDtypeStruct(turned, jnp.float32),
+            jax.ShapeDtypeStruct((blocks, lanes, pixels), jnp.float32),
         ],
-        in_specs=[pl.BlockSpec(memory_space=pltpu.HBM)] * 4,
-        out_specs=[whole] * 6,
+        grid=(blocks,),
+        in_specs=[
+            pl.BlockSpec((pixels, width_all), lambda i: (i, 0)),
+            pl.BlockSpec((lanes, width_all), lambda i: (0, 0)),
+            pl.BlockSpec((1, lanes), lambda i: (0, 0)),
+            pl.BlockSpec((pixels, lanes), lambda i: (i, 0)),
+        ],
+        out_specs=[
+            pl.BlockSpec((1, heads, POINTS, depth0, pixels), lambda i: (i, 0, 0, 0, 0)),
+            pl.BlockSpec((1, heads, POINTS, depth1, pixels), lambda i: (i, 0, 0, 0, 0)),
+            pl.BlockSpec((1, heads, depth2, pixels), lambda i: (i, 0, 0, 0)),
+            pl.BlockSpec((1, lanes, pixels), lambda i: (i, 0, 0)),
+        ],
         scratch_shapes=[
-            VMEM((blocks * pixels, width_all), jnp.bfloat16),
-            VMEM((lanes, width_all), jnp.bfloat16),
-            VMEM((1, lanes), jnp.float32),
-            VMEM((blocks * pixels, lanes), jnp.int32),
-            pltpu.SemaphoreType.DMA((4,)),
+            VMEM((lanes, pixels), jnp.float32),
+            VMEM((lanes, pixels), jnp.int32),
+            VMEM((lanes, pixels), jnp.float32),
+            VMEM((POINTS, max(GROUPS) * per_block, pixels), jnp.float32),
         ],
         compiler_params=pltpu.CompilerParams(vmem_limit_bytes=PREP_VMEM),
+        cost_estimate=PREP_COST,
         name="prep",
     )(queries_blocked, logit_weight.T, logit_bias.reshape(1, lanes), samples_blocked)
-    weight0 = pl.pallas_call(
-        functools.partial(hot_kernel, dims),
-        out_shape=jax.ShapeDtypeStruct((blocks, heads, POINTS, depth0, pixels), jnp.bfloat16),
-        in_specs=[whole] * 3,
-        out_specs=whole,
-        compiler_params=pltpu.CompilerParams(vmem_limit_bytes=PREP_VMEM),
-        name="hot",
-    )(attend, code, col)
 
     attn = pl.pallas_call(
         functools.partial(attend_kernel, dims, grid, gather, len(sources)),
@@ -694,8 +660,9 @@
             pltpu.SemaphoreType.DMA((LEVELS,)),
         ],
         compiler_params=pltpu.CompilerParams(vmem_limit_bytes=ATTEND_VMEM),
+        cost_estimate=PREP_COST,
         name="attend",
-    )(*sources, weight0, weight1, weight2, down, tile_lists)
+    )(*sources, *weights, tile_lists)
 
     own_head = lax.axis_index("head").reshape(1).astype(jnp.int32)
     other = lax.ppermute(attn, "head", [(0, 1), (1, 0)])

time: 75.9 us -> 73.9 us (0.974)
  Pallas kernels: 22.3 us -> 20.2 us
  starting transfers between devices: 28.4 us -> 26.3 us
  waiting for transfers between devices: 18.1 us -> 20.1 us
    ppermute x12, waiting for transfers between devices: 7.11 us -> 9.11 us  [relay_tiles(): lax.ppermute(sent[number - 1], 'row', [(row, source_of(row, number)) for...]
    ppermute x1, starting transfers between devices: 6.67 us -> 4.66 us  [on_device(): other = lax.ppermute(attn, 'head', [(0, 1), (1, 0)])]
    pallas_call x1 -> x0, Pallas kernels: 1.79 us -> none  [on_device(): pl.pallas_call(functools.partial(hot_kernel, dims), out_shape=jax.ShapeDt...]
  transfers between devices with their start and end apart: 21 -> 21, of which waited for: 8 -> 9; matrix products, arithmetic and copies ran while one was open for 3% -> 3% of each run, Pallas kernels for 15% -> 13%
where the time goes in v6:
time: 73.9 us; the launch traced here: 73.5 us
  starting transfers between devices  26.3 us (36%)
  Pallas kernels  20.2 us (27%)
  waiting for transfers between devices  20.1 us (27%)
  local copies, waits for them, and re-layouts  4.71 us (6%)
  other arithmetic  1.77 us (2%)
    ppermute x12, starting transfers between devices, relay_tiles(): lax.ppermute(sent[number - 1], 'row', [(row, source_of(row, number)) for...  11.1 us
    ppermute x5, waiting for transfers between devices, move(): held[name] = lax.ppermute(held[source or 'own'], 'col', pairs)  10.6 us
    ppermute x12, waiting for transfers between devices, relay_tiles(): lax.ppermute(sent[number - 1], 'row', [(row, source_of(row, number)) for...  9.11 us
    pallas_call x1, Pallas kernels, on_device(): pl.pallas_call(functools.partial(attend_kernel, dims, grid, gather, len(s...  8.35 us
    ppermute x5, starting transfers between devices, move(): held[name] = lax.ppermute(held[source or 'own'], 'col', pairs)  7.94 us
    pallas_call x1, Pallas kernels, on_device(): pl.pallas_call(functools.partial(prep_kernel, dims), out_shape=[jax.Shape...  4.97 us
    ppermute x1, starting transfers between devices, on_device(): other = lax.ppermute(attn, 'head', [(0, 1), (1, 0)])  4.66 us
    pallas_call x4, Pallas kernels, relay_tiles(): pl.pallas_call(functools.partial(relay_select_kernel, (row_count - 1, len...  3.84 us
  transfers between devices with their start and end apart: 21, of which 9 were waited for; matrix products, arithmetic and copies ran while one was open for 3% of the time, Pallas kernels for 13%

profile of v6, /device:TPU:9, one launch (start us, length us, event | category | flops | bytes accessed | tf_op | source)
XLA Modules:
  0.0 73.5 jit_solution(18383338257633649774)
XLA Ops:
  0.0 1.1 %pad_maximum_fusion.refs_3_ = bf16[1360,128]{1,0:T(8,128)(2,1)S(1)} fusion(bf16[16,128]{1,0:T(8,128)(2,1)} %bitcast.34, bf16[64,128]{1,0:T(8,128)(2,1)} %bitcast.33, bf16[256,128]{1,0:T(8,128)(2,1)} %bitcast.31, bf16[1024,128]{1,0:T(8,128)(2,1)} %bitcast.30), kind=kLoop, calls=%fused_computation | loop fusion | flops 1392640 | bytes 696320 | tf_op jit(solution)/shard_map/concatenate | solution.py:456
  1.1 3.2 %collective-permute-start.1 = (bf16[1360,128]{1,0:T(8,128)(2,1)S(1)}, bf16[1360,128]{1,0:T(8,128)(2,1)S(1)}, u32[]{:S(2)}, u32[]{:S(2)}) collective-permute-start(bf16[1360,128]{1,0:T(8,128)(2,1)S(1)} %pad_maximum_fusion.refs_3_), channel_id=1, source_target_pairs={{2,4},{4,2},{3,5},{5,3},{10,12},{12,10},{11,13},{13,11},{18,20},{2... | collective-permute-start | bytes 1044488 | tf_op jit(solution)/shard_map/ppermute | solution.py:460
  4.3 0.1 collective-permute-start
  4.4 0.7 copy.35
  5.1 0.1 reshape.489
  5.2 0.2 convert_reduce_fusion
  5.4 0.2 select_reduce_fusion
  5.7 7.4 %collective-permute-done.refs_3_.refs_4_ = bf16[1360,128]{1,0:T(8,128)(2,1)S(1)} collective-permute-done((bf16[1360,128]{1,0:T(8,128)(2,1)S(1)}, bf16[1360,128]{1,0:T(8,128)(2,1)S(1)}, u32[]{:S(2)}, u32[]{:S(2)}) %collective-permute-start) | collective-permute-done | bytes 348192 | tf_op jit(solution)/shard_map/ppermute | solution.py:460
  13.1 2.1 %collective-permute-start.3 = (bf16[1360,128]{1,0:T(8,128)(2,1)S(1)}, bf16[1360,128]{1,0:T(8,128)(2,1)S(1)}, u32[]{:S(2)}, u32[]{:S(2)}) collective-permute-start(bf16[1360,128]{1,0:T(8,128)(2,1)S(1)} %collective-permute-done.refs_3_.refs_4_), channel_id=1, source_target_pairs={{2,4},{4,2},{3,5},{5,3},{10,12},{12,10},{11,13},{13,11},{18,20},{2... | collective-permute-start | bytes 1044488 | tf_op jit(solution)/shard_map/ppermute | solution.py:460
  15.2 0.1 sub.31
  15.3 0.1 select_reduce_fusion.1
  15.4 0.1 copy.41
  15.5 1.2 %collective-permute-start.5 = (s32[4,8]{1,0:T(4,128)S(1)}, s32[4,8]{1,0:T(4,128)S(1)}, u32[]{:S(2)}, u32[]{:S(2)}) collective-permute-start(s32[4,8]{1,0:T(4,128)S(1)} %copy.41), channel_id=1, source_target_pairs={{0,8},{8,0},{16,24},{24,16},{1,9},{9,1},{17,25},{25,17},{2,10},{10... | collective-permute-start | bytes 392 | tf_op jit(solution)/shard_map/ppermute | solution.py:480
  16.7 0.1 copy.42
  16.8 1.2 %collective-permute-start.6 = (s32[4,8]{1,0:T(4,128)S(1)}, s32[4,8]{1,0:T(4,128)S(1)}, u32[]{:S(2)}, u32[]{:S(2)}) collective-permute-start(s32[4,8]{1,0:T(4,128)S(1)} %copy.42), channel_id=1, source_target_pairs={{0,16},{8,24},{16,0},{24,8},{1,17},{9,25},{17,1},{25,9},{2,18},{10... | collective-permute-start | bytes 392 | tf_op jit(solution)/shard_map/ppermute | solution.py:480
  18.0 0.1 copy.43
  18.1 0.2 collective-permute-start.7
  18.3 0.1 copy.36
  18.4 0.0 collective-permute-done.1.refs_3_.refs_5_
  18.4 1.3 %collective-permute-start.2 = (bf16[1360,128]{1,0:T(8,128)(2,1)S(1)}, bf16[1360,128]{1,0:T(8,128)(2,1)S(1)}, u32[]{:S(2)}, u32[]{:S(2)}) collective-permute-start(bf16[1360,128]{1,0:T(8,128)(2,1)S(1)} %collective-permute-done.1.refs_3_.refs_5_), channel_id=1, source_target_pairs={{2,0},{4,6},{3,1},{5,7},{10,8},{12,14},{11,9},{13,15},{18,16},{20,... | collective-permute-start | bytes 1044488 | tf_op jit(solution)/shard_map/ppermute | solution.py:460
  19.7 3.2 %collective-permute-done.3.refs_4_.refs_7_ = bf16[1360,128]{1,0:T(8,128)(2,1)S(1)} collective-permute-done((bf16[1360,128]{1,0:T(8,128)(2,1)S(1)}, bf16[1360,128]{1,0:T(8,128)(2,1)S(1)}, u32[]{:S(2)}, u32[]{:S(2)}) %collective-permute-start.3) | collective-permute-done | bytes 348192 | tf_op jit(solution)/shard_map/ppermute | solution.py:460
  22.9 1.3 %collective-permute-start.4 = (bf16[1360,128]{1,0:T(8,128)(2,1)S(1)}, bf16[1360,128]{1,0:T(8,128)(2,1)S(1)}, u32[]{:S(2)}, u32[]{:S(2)}) collective-permute-start(bf16[1360,128]{1,0:T(8,128)(2,1)S(1)} %collective-permute-done.3.refs_4_.refs_7_), channel_id=1, source_target_pairs={{2,0},{4,6},{3,1},{5,7},{10,8},{12,14},{11,9},{13,15},{18,16},{20,... | collective-permute-start | bytes 1044488 | tf_op jit(solution)/shard_map/ppermute | solution.py:460
  24.2 0.1 pad_add_fusion.place_ref.refs_1_
  24.3 0.0 collective-permute-done.5.refs_0_
  24.3 0.0 collective-permute-done.6.refs_1_
  24.3 1.0 %shard_map.127 = (bf16[688,128]{1,0:T(8,128)(2,1)S(1)}, bf16[688,128]{1,0:T(8,128)(2,1)S(1)}, bf16[688,128]{1,0:T(8,128)(2,1)S(1)}) custom-call(s32[2]{0:T(128)S(1)} %pad_add_fusion.place_ref.refs_1_, s32[16,8]{1,0:T(8,128)S(1)} %get-tuple-element.41.request_ref.refs_0_, s32[16,8]{1,0:T(8,128)S(1)} %get-tuple-element.40.asked_ref.refs_2_, ...), custom_call_target="tpu_custom_call" | custom-call | flops 500000000 | bytes 1000000 | tf_op jit(solution)/shard_map/pallas_call | solution.py:492
  25.3 1.3 %collective-permute-start.8 = (bf16[688,128]{1,0:T(8,128)(2,1)S(1)}, bf16[688,128]{1,0:T(8,128)(2,1)S(1)}, u32[]{:S(2)}, u32[]{:S(2)}) collective-permute-start(bf16[688,128]{1,0:T(8,128)(2,1)S(1)} %get-tuple-element.21), channel_id=1, source_target_pairs={{0,8},{8,0},{16,24},{24,16},{1,9},{9,1},{17,25},{25,17},{2,10},{10... | collective-permute-start | bytes 528392 | tf_op jit(solution)/shard_map/ppermute | solution.py:505
  26.5 1.2 %collective-permute-start.9 = (bf16[688,128]{1,0:T(8,128)(2,1)S(1)}, bf16[688,128]{1,0:T(8,128)(2,1)S(1)}, u32[]{:S(2)}, u32[]{:S(2)}) collective-permute-start(bf16[688,128]{1,0:T(8,128)(2,1)S(1)} %get-tuple-element.22), channel_id=1, source_target_pairs={{0,16},{8,24},{16,0},{24,8},{1,17},{9,25},{17,1},{25,9},{2,18},{10... | collective-permute-start | bytes 528392 | tf_op jit(solution)/shard_map/ppermute | solution.py:505
  27.8 0.2 collective-permute-start.10
  28.0 1.0 %shard_map.128 = (bf16[688,128]{1,0:T(8,128)(2,1)S(1)}, bf16[688,128]{1,0:T(8,128)(2,1)S(1)}, bf16[688,128]{1,0:T(8,128)(2,1)S(1)}) custom-call(s32[2]{0:T(128)S(1)} %pad_add_fusion.place_ref.refs_1_, s32[16,8]{1,0:T(8,128)S(1)} %get-tuple-element.41.request_ref.refs_0_, s32[16,8]{1,0:T(8,128)S(1)} %get-tuple-element.40.asked_ref.refs_2_, ...), custom_call_target="tpu_custom_call" | custom-call | flops 500000000 | bytes 1000000 | tf_op jit(solution)/shard_map/pallas_call | solution.py:492
  29.0 1.3 %collective-permute-start.11 = (bf16[688,128]{1,0:T(8,128)(2,1)S(1)}, bf16[688,128]{1,0:T(8,128)(2,1)S(1)}, u32[]{:S(2)}, u32[]{:S(2)}) collective-permute-start(bf16[688,128]{1,0:T(8,128)(2,1)S(1)} %get-tuple-element.24), channel_id=1, source_target_pairs={{0,8},{8,0},{16,24},{24,16},{1,9},{9,1},{17,25},{25,17},{2,10},{10... | collective-permute-start | bytes 528392 | tf_op jit(solution)/shard_map/ppermute | solution.py:505
  30.2 1.0 %shard_map.129 = (bf16[688,128]{1,0:T(8,128)(2,1)S(1)}, bf16[688,128]{1,0:T(8,128)(2,1)S(1)}, bf16[688,128]{1,0:T(8,128)(2,1)S(1)}) custom-call(s32[2]{0:T(128)S(1)} %pad_add_fusion.place_ref.refs_1_, s32[16,8]{1,0:T(8,128)S(1)} %get-tuple-element.41.request_ref.refs_0_, s32[16,8]{1,0:T(8,128)S(1)} %get-tuple-element.40.asked_ref.refs_2_, ...), custom_call_target="tpu_custom_call" | custom-call | flops 500000000 | bytes 1000000 | tf_op jit(solution)/shard_map/pallas_call | solution.py:492
  31.2 0.0 collective-permute-done.8.refs_9_
  31.2 1.3 %collective-permute-start.12 = (bf16[688,128]{1,0:T(8,128)(2,1)S(1)}, bf16[688,128]{1,0:T(8,128)(2,1)S(1)}, u32[]{:S(2)}, u32[]{:S(2)}) collective-permute-start(bf16[688,128]{1,0:T(8,128)(2,1)S(1)} %get-tuple-element.25), channel_id=1, source_target_pairs={{0,16},{8,24},{16,0},{24,8},{1,17},{9,25},{17,1},{25,9},{2,18},{10... | collective-permute-start | bytes 528392 | tf_op jit(solution)/shard_map/ppermute | solution.py:505
  32.5 0.0 collective-permute-done.9.refs_10_
  32.5 1.3 %collective-permute-start.13 = (bf16[688,128]{1,0:T(8,128)(2,1)S(1)}, bf16[688,128]{1,0:T(8,128)(2,1)S(1)}, u32[]{:S(2)}, u32[]{:S(2)}) collective-permute-start(bf16[688,128]{1,0:T(8,128)(2,1)S(1)} %get-tuple-element.26), channel_id=1, source_target_pairs={{0,24},{8,16},{16,8},{24,0},{1,25},{9,17},{17,9},{25,1},{2,26},{10... | collective-permute-start | bytes 528392 | tf_op jit(solution)/shard_map/ppermute | solution.py:505
  33.8 0.0 collective-permute-done.4.refs_3_.refs_8_
  33.8 1.2 %collective-permute-start.14 = (bf16[688,128]{1,0:T(8,128)(2,1)S(1)}, bf16[688,128]{1,0:T(8,128)(2,1)S(1)}, u32[]{:S(2)}, u32[]{:S(2)}) collective-permute-start(bf16[688,128]{1,0:T(8,128)(2,1)S(1)} %get-tuple-element.27), channel_id=1, source_target_pairs={{0,8},{8,0},{16,24},{24,16},{1,9},{9,1},{17,25},{25,17},{2,10},{10... | collective-permute-start | bytes 528392 | tf_op jit(solution)/shard_map/ppermute | solution.py:505
  35.1 1.0 %shard_map.130 = (bf16[688,128]{1,0:T(8,128)(2,1)S(1)}, bf16[688,128]{1,0:T(8,128)(2,1)S(1)}, bf16[688,128]{1,0:T(8,128)(2,1)S(1)}) custom-call(s32[2]{0:T(128)S(1)} %pad_add_fusion.place_ref.refs_1_, s32[16,8]{1,0:T(8,128)S(1)} %get-tuple-element.41.request_ref.refs_0_, s32[16,8]{1,0:T(8,128)S(1)} %get-tuple-element.40.asked_ref.refs_2_, ...), custom_call_target="tpu_custom_call" | custom-call | flops 500000000 | bytes 1000000 | tf_op jit(solution)/shard_map/pallas_call | solution.py:492
  36.0 0.2 collective-permute-start.15
  36.2 1.0 %collective-permute-done.11.refs_12_ = bf16[688,128]{1,0:T(8,128)(2,1)S(1)} collective-permute-done((bf16[688,128]{1,0:T(8,128)(2,1)S(1)}, bf16[688,128]{1,0:T(8,128)(2,1)S(1)}, u32[]{:S(2)}, u32[]{:S(2)}) %collective-permute-start.11) | collective-permute-done | bytes 176160 | tf_op jit(solution)/shard_map/ppermute | solution.py:505
  37.2 1.2 %collective-permute-start.16 = (bf16[688,128]{1,0:T(8,128)(2,1)S(1)}, bf16[688,128]{1,0:T(8,128)(2,1)S(1)}, u32[]{:S(2)}, u32[]{:S(2)}) collective-permute-start(bf16[688,128]{1,0:T(8,128)(2,1)S(1)} %get-tuple-element.29), channel_id=1, source_target_pairs={{0,24},{8,16},{16,8},{24,0},{1,25},{9,17},{17,9},{25,1},{2,26},{10... | collective-permute-start | bytes 528392 | tf_op jit(solution)/shard_map/ppermute | solution.py:505
  38.4 2.1 %collective-permute-done.12.refs_13_ = bf16[688,128]{1,0:T(8,128)(2,1)S(1)} collective-permute-done((bf16[688,128]{1,0:T(8,128)(2,1)S(1)}, bf16[688,128]{1,0:T(8,128)(2,1)S(1)}, u32[]{:S(2)}, u32[]{:S(2)}) %collective-permute-start.12) | collective-permute-done | bytes 176160 | tf_op jit(solution)/shard_map/ppermute | solution.py:505
  40.5 0.0 collective-permute-start.17
  40.5 1.2 %collective-permute-done.13.refs_14_ = bf16[688,128]{1,0:T(8,128)(2,1)S(1)} collective-permute-done((bf16[688,128]{1,0:T(8,128)(2,1)S(1)}, bf16[688,128]{1,0:T(8,128)(2,1)S(1)}, u32[]{:S(2)}, u32[]{:S(2)}) %collective-permute-start.13) | collective-permute-done | bytes 176160 | tf_op jit(solution)/shard_map/ppermute | solution.py:505
  41.7 0.8 %collective-permute-start.18 = (bf16[688,128]{1,0:T(8,128)(2,1)S(1)}, bf16[688,128]{1,0:T(8,128)(2,1)S(1)}, u32[]{:S(2)}, u32[]{:S(2)}) collective-permute-start(bf16[688,128]{1,0:T(8,128)(2,1)S(1)} %get-tuple-element.31), channel_id=1, source_target_pairs={{0,16},{8,24},{16,0},{24,8},{1,17},{9,25},{17,1},{25,9},{2,18},{10... | collective-permute-start | bytes 528392 | tf_op jit(solution)/shard_map/ppermute | solution.py:505
  42.5 2.3 %collective-permute-done.14.refs_15_ = bf16[688,128]{1,0:T(8,128)(2,1)S(1)} collective-permute-done((bf16[688,128]{1,0:T(8,128)(2,1)S(1)}, bf16[688,128]{1,0:T(8,128)(2,1)S(1)}, u32[]{:S(2)}, u32[]{:S(2)}) %collective-permute-start.14) | collective-permute-done | bytes 176160 | tf_op jit(solution)/shard_map/ppermute | solution.py:505
  44.8 1.1 %collective-permute-start.19 = (bf16[688,128]{1,0:T(8,128)(2,1)S(1)}, bf16[688,128]{1,0:T(8,128)(2,1)S(1)}, u32[]{:S(2)}, u32[]{:S(2)}) collective-permute-start(bf16[688,128]{1,0:T(8,128)(2,1)S(1)} %get-tuple-element.32), channel_id=1, source_target_pairs={{0,24},{8,16},{16,8},{24,0},{1,25},{9,17},{17,9},{25,1},{2,26},{10... | collective-permute-start | bytes 528392 | tf_op jit(solution)/shard_map/ppermute | solution.py:505
  46.0 1.0 %copy-done = bf16[64,16,256]{2,1,0:T(8,128)(2,1)S(1)} copy-done((bf16[64,16,256]{2,1,0:T(8,128)(2,1)S(1)}, bf16[64,16,256]{2,1,0:T(8,128)(2,1)}, u32[]{:S(2)}) %copy-start) | copy-done | bytes 524312
  47.0 1.0 %copy-done.7 = s32[64,16,64]{2,1,0:T(8,128)S(1)} copy-done((s32[64,16,64]{2,1,0:T(8,128)S(1)}, s32[64,16,64]{2,1,0:T(8,128)}, u32[]{:S(2)}) %copy-start.7) | copy-done | bytes 262168
  48.1 0.8 %copy-done.8 = bf16[256,64]{0,1:T(8,128)(2,1)S(1)} copy-done((bf16[256,64]{0,1:T(8,128)(2,1)S(1)}, bf16[256,64]{0,1:T(8,128)(2,1)}, u32[]{:S(2)}) %copy-start.8) | copy-done | bytes 32792
  48.8 0.7 copy-done.9
  49.5 5.0 %prep.1 = (bf16[4,4,4,256,256]{4,3,2,1,0:T(8,128)(2,1)S(1)}, bf16[4,4,4,256,256]{4,3,2,1,0:T(8,128)(2,1)S(1)}, bf16[4,4,256,256]{3,2,1,0:T(8,128)(2,1)S(1)}, f32[4,64,256]{2,1,0:T(8,128)S(1)}) custom-call(bf16[1024,256]{1,0:T(8,128)(2,1)S(1)} %bitcast.21, bf16[64,256]{1,0:T(8,128)(2,1)S(1)} %bitcast.28, f32[1,64]{1,0:T(1,128)S(1)} %bitcast.29, ...), custom_call_target="tpu_custom_call" | custom-call | flops 2000000000 | bytes 4000000 | tf_op jit(solution)/shard_map/prep/pallas_call | solution.py:613
  54.5 0.0 collective-permute-done.16.refs_17_
  54.5 0.0 collective-permute-done.17.refs_18_
  54.5 1.0 %collective-permute-done.18.refs_19_ = bf16[688,128]{1,0:T(8,128)(2,1)S(1)} collective-permute-done((bf16[688,128]{1,0:T(8,128)(2,1)S(1)}, bf16[688,128]{1,0:T(8,128)(2,1)S(1)}, u32[]{:S(2)}, u32[]{:S(2)}) %collective-permute-start.18) | collective-permute-done | bytes 176160 | tf_op jit(solution)/shard_map/ppermute | solution.py:505
  55.5 1.4 %collective-permute-done.19.refs_20_ = bf16[688,128]{1,0:T(8,128)(2,1)S(1)} collective-permute-done((bf16[688,128]{1,0:T(8,128)(2,1)S(1)}, bf16[688,128]{1,0:T(8,128)(2,1)S(1)}, u32[]{:S(2)}, u32[]{:S(2)}) %collective-permute-start.19) | collective-permute-done | bytes 176160 | tf_op jit(solution)/shard_map/ppermute | solution.py:505
  56.9 0.0 copy-start.5
  56.9 0.0 copy-start.6
  57.0 8.4 %attend.1.own_ref = bf16[1024,128]{1,0:T(8,128)(2,1)S(1)} custom-call(s32[16,8]{1,0:T(8,128)S(1)} %get-tuple-element.41.request_ref.refs_0_, s32[2]{0:T(128)S(1)} %pad_add_fusion.place_ref.refs_1_, s32[16,8]{1,0:T(8,128)S(1)} %get-tuple-element.40.asked_ref.refs_2_, bf16[1360,128]{1,0:T(8,128)(2,1)S(1)} %pad_maximum_fusion.refs_3_, ...), custom_call_target="tpu_custom_call" | custom-call | flops 2000000000 | bytes 4000000 | tf_op jit(solution)/shard_map/attend/pallas_call | solution.py:645
  65.3 4.7 %collective-permute-start.20 = (bf16[1024,128]{1,0:T(8,128)(2,1)S(1)}, bf16[1024,128]{1,0:T(8,128)(2,1)S(1)}, u32[]{:S(2)}, u32[]{:S(2)}) collective-permute-start(bf16[1024,128]{1,0:T(8,128)(2,1)S(1)} %attend.1.own_ref), channel_id=1, source_target_pairs={{0,1},{1,0},{2,3},{3,2},{4,5},{5,4},{6,7},{7,6},{8,9},{9,8},{10,11... | collective-permute-start | bytes 786440 | tf_op jit(solution)/shard_map/ppermute | solution.py:668
  70.0 0.7 %own.1.pre_ref = f32[1024,256]{1,0:T(8,128)S(1)} custom-call(s32[1]{0:T(128)} %bitcast.head_ref, bf16[1024,256]{1,0:T(8,128)(2,1)S(1)} %bitcast.22, bf16[1024,128]{1,0:T(8,128)(2,1)S(1)} %attend.1.own_ref, bf16[256,256]{1,0:T(8,128)(2,1)S(1)} %copy-done.2, f32[1,256]{1,0:T(1,128)S(1)} %bitcast.24), custom_call_target="tpu_custom_call" | custom-call | tf_op jit(solution)/shard_map/own/pallas_call | solution.py:672
  70.7 0.4 collective-permute-done.20.other_ref
  71.1 2.3 %norm.1 = bf16[1024,128]{1,0:T(8,128)(2,1)} custom-call(s32[1]{0:T(128)} %bitcast.head_ref, f32[1024,256]{1,0:T(8,128)S(1)} %own.1.pre_ref, bf16[1024,128]{1,0:T(8,128)(2,1)S(1)} %collective-permute-done.20.other_ref, bf16[256,256]{1,0:T(8,128)(2,1)S(1)} %copy-done.2, f32[1,128]{1,0:T(1,128)S(1)} %bitcast.25, f32[1,128]{1,0:T(1,128)S(1)} %bitcast.26), custom_call_target="tpu_custom_call" | custom-call | tf_op jit(solution)/shard_map/norm/pallas_call | solution.py:687
  (27 shorter events, 0.1 us)
Async XLA Ops:
  0.0 56.9 %copy-start.3 = (s32[4,1,4,8]{3,2,1,0:T(4,128)S(1)}, s32[4,1,4,8]{3,2,1,0:T(4,128)}, u32[]{:S(2)}) copy-start(s32[4,1,4,8]{3,2,1,0:T(4,128)} %refs_25_.1) | copy-start | bytes 1540
  1.1 17.3 %collective-permute-start.1 = (bf16[1360,128]{1,0:T(8,128)(2,1)S(1)}, bf16[1360,128]{1,0:T(8,128)(2,1)S(1)}, u32[]{:S(2)}, u32[]{:S(2)}) collective-permute-start(bf16[1360,128]{1,0:T(8,128)(2,1)S(1)} %pad_maximum_fusion.refs_3_), channel_id=1, source_target_pairs={{2,4},{4,2},{3,5},{5,3},{10,12},{12,10},{11,13},{13,11},{18,20},{2... | collective-permute-start | bytes 1044488 | tf_op jit(solution)/shard_map/ppermute | solution.py:460
  4.3 8.8 %collective-permute-start = (bf16[1360,128]{1,0:T(8,128)(2,1)S(1)}, bf16[1360,128]{1,0:T(8,128)(2,1)S(1)}, u32[]{:S(2)}, u32[]{:S(2)}) collective-permute-start(bf16[1360,128]{1,0:T(8,128)(2,1)S(1)} %pad_maximum_fusion.refs_3_), channel_id=1, source_target_pairs={{0,2},{2,0},{4,6},{6,4},{1,3},{3,1},{5,7},{7,5},{8,10},{10,8},{12,... | collective-permute-start | bytes 1044488 | tf_op jit(solution)/shard_map/ppermute | solution.py:460
  13.1 9.8 %collective-permute-start.3 = (bf16[1360,128]{1,0:T(8,128)(2,1)S(1)}, bf16[1360,128]{1,0:T(8,128)(2,1)S(1)}, u32[]{:S(2)}, u32[]{:S(2)}) collective-permute-start(bf16[1360,128]{1,0:T(8,128)(2,1)S(1)} %collective-permute-done.refs_3_.refs_4_), channel_id=1, source_target_pairs={{2,4},{4,2},{3,5},{5,3},{10,12},{12,10},{11,13},{13,11},{18,20},{2... | collective-permute-start | bytes 1044488 | tf_op jit(solution)/shard_map/ppermute | solution.py:460
  15.5 8.8 %collective-permute-start.5 = (s32[4,8]{1,0:T(4,128)S(1)}, s32[4,8]{1,0:T(4,128)S(1)}, u32[]{:S(2)}, u32[]{:S(2)}) collective-permute-start(s32[4,8]{1,0:T(4,128)S(1)} %copy.41), channel_id=1, source_target_pairs={{0,8},{8,0},{16,24},{24,16},{1,9},{9,1},{17,25},{25,17},{2,10},{10... | collective-permute-start | bytes 392 | tf_op jit(solution)/shard_map/ppermute | solution.py:480
  16.8 7.5 %collective-permute-start.6 = (s32[4,8]{1,0:T(4,128)S(1)}, s32[4,8]{1,0:T(4,128)S(1)}, u32[]{:S(2)}, u32[]{:S(2)}) collective-permute-start(s32[4,8]{1,0:T(4,128)S(1)} %copy.42), channel_id=1, source_target_pairs={{0,16},{8,24},{16,0},{24,8},{1,17},{9,25},{17,1},{25,9},{2,18},{10... | collective-permute-start | bytes 392 | tf_op jit(solution)/shard_map/ppermute | solution.py:480
  18.1 6.2 %collective-permute-start.7 = (s32[4,8]{1,0:T(4,128)S(1)}, s32[4,8]{1,0:T(4,128)S(1)}, u32[]{:S(2)}, u32[]{:S(2)}) collective-permute-start(s32[4,8]{1,0:T(4,128)S(1)} %copy.43), channel_id=1, source_target_pairs={{0,24},{8,16},{16,8},{24,0},{1,25},{9,17},{17,9},{25,1},{2,26},{10... | collective-permute-start | bytes 392 | tf_op jit(solution)/shard_map/ppermute | solution.py:480
  18.4 10.6 %collective-permute-start.2 = (bf16[1360,128]{1,0:T(8,128)(2,1)S(1)}, bf16[1360,128]{1,0:T(8,128)(2,1)S(1)}, u32[]{:S(2)}, u32[]{:S(2)}) collective-permute-start(bf16[1360,128]{1,0:T(8,128)(2,1)S(1)} %collective-permute-done.1.refs_3_.refs_5_), channel_id=1, source_target_pairs={{2,0},{4,6},{3,1},{5,7},{10,8},{12,14},{11,9},{13,15},{18,16},{20,... | collective-permute-start | bytes 1044488 | tf_op jit(solution)/shard_map/ppermute | solution.py:460
  22.9 10.9 %collective-permute-start.4 = (bf16[1360,128]{1,0:T(8,128)(2,1)S(1)}, bf16[1360,128]{1,0:T(8,128)(2,1)S(1)}, u32[]{:S(2)}, u32[]{:S(2)}) collective-permute-start(bf16[1360,128]{1,0:T(8,128)(2,1)S(1)} %collective-permute-done.3.refs_4_.refs_7_), channel_id=1, source_target_pairs={{2,0},{4,6},{3,1},{5,7},{10,8},{12,14},{11,9},{13,15},{18,16},{20,... | collective-permute-start | bytes 1044488 | tf_op jit(solution)/shard_map/ppermute | solution.py:460
  25.3 5.9 %collective-permute-start.8 = (bf16[688,128]{1,0:T(8,128)(2,1)S(1)}, bf16[688,128]{1,0:T(8,128)(2,1)S(1)}, u32[]{:S(2)}, u32[]{:S(2)}) collective-permute-start(bf16[688,128]{1,0:T(8,128)(2,1)S(1)} %get-tuple-element.21), channel_id=1, source_target_pairs={{0,8},{8,0},{16,24},{24,16},{1,9},{9,1},{17,25},{25,17},{2,10},{10... | collective-permute-start | bytes 528392 | tf_op jit(solution)/shard_map/ppermute | solution.py:505
  26.5 6.0 %collective-permute-start.9 = (bf16[688,128]{1,0:T(8,128)(2,1)S(1)}, bf16[688,128]{1,0:T(8,128)(2,1)S(1)}, u32[]{:S(2)}, u32[]{:S(2)}) collective-permute-start(bf16[688,128]{1,0:T(8,128)(2,1)S(1)} %get-tuple-element.22), channel_id=1, source_target_pairs={{0,16},{8,24},{16,0},{24,8},{1,17},{9,25},{17,1},{25,9},{2,18},{10... | collective-permute-start | bytes 528392 | tf_op jit(solution)/shard_map/ppermute | solution.py:505
  27.8 8.2 %collective-permute-start.10 = (bf16[688,128]{1,0:T(8,128)(2,1)S(1)}, bf16[688,128]{1,0:T(8,128)(2,1)S(1)}, u32[]{:S(2)}, u32[]{:S(2)}) collective-permute-start(bf16[688,128]{1,0:T(8,128)(2,1)S(1)} %get-tuple-element.23), channel_id=1, source_target_pairs={{0,24},{8,16},{16,8},{24,0},{1,25},{9,17},{17,9},{25,1},{2,26},{10... | collective-permute-start | bytes 528392 | tf_op jit(solution)/shard_map/ppermute | solution.py:505
  29.0 8.3 %collective-permute-start.11 = (bf16[688,128]{1,0:T(8,128)(2,1)S(1)}, bf16[688,128]{1,0:T(8,128)(2,1)S(1)}, u32[]{:S(2)}, u32[]{:S(2)}) collective-permute-start(bf16[688,128]{1,0:T(8,128)(2,1)S(1)} %get-tuple-element.24), channel_id=1, source_target_pairs={{0,8},{8,0},{16,24},{24,16},{1,9},{9,1},{17,25},{25,17},{2,10},{10... | collective-permute-start | bytes 528392 | tf_op jit(solution)/shard_map/ppermute | solution.py:505
  31.2 9.3 %collective-permute-start.12 = (bf16[688,128]{1,0:T(8,128)(2,1)S(1)}, bf16[688,128]{1,0:T(8,128)(2,1)S(1)}, u32[]{:S(2)}, u32[]{:S(2)}) collective-permute-start(bf16[688,128]{1,0:T(8,128)(2,1)S(1)} %get-tuple-element.25), channel_id=1, source_target_pairs={{0,16},{8,24},{16,0},{24,8},{1,17},{9,25},{17,1},{25,9},{2,18},{10... | collective-permute-start | bytes 528392 | tf_op jit(solution)/shard_map/ppermute | solution.py:505
  32.5 9.2 %collective-permute-start.13 = (bf16[688,128]{1,0:T(8,128)(2,1)S(1)}, bf16[688,128]{1,0:T(8,128)(2,1)S(1)}, u32[]{:S(2)}, u32[]{:S(2)}) collective-permute-start(bf16[688,128]{1,0:T(8,128)(2,1)S(1)} %get-tuple-element.26), channel_id=1, source_target_pairs={{0,24},{8,16},{16,8},{24,0},{1,25},{9,17},{17,9},{25,1},{2,26},{10... | collective-permute-start | bytes 528392 | tf_op jit(solution)/shard_map/ppermute | solution.py:505
  33.8 11.0 %collective-permute-start.14 = (bf16[688,128]{1,0:T(8,128)(2,1)S(1)}, bf16[688,128]{1,0:T(8,128)(2,1)S(1)}, u32[]{:S(2)}, u32[]{:S(2)}) collective-permute-start(bf16[688,128]{1,0:T(8,128)(2,1)S(1)} %get-tuple-element.27), channel_id=1, source_target_pairs={{0,8},{8,0},{16,24},{24,16},{1,9},{9,1},{17,25},{25,17},{2,10},{10... | collective-permute-start | bytes 528392 | tf_op jit(solution)/shard_map/ppermute | solution.py:505
  36.0 18.4 %collective-permute-start.15 = (bf16[688,128]{1,0:T(8,128)(2,1)S(1)}, bf16[688,128]{1,0:T(8,128)(2,1)S(1)}, u32[]{:S(2)}, u32[]{:S(2)}) collective-permute-start(bf16[688,128]{1,0:T(8,128)(2,1)S(1)} %get-tuple-element.28), channel_id=1, source_target_pairs={{0,16},{8,24},{16,0},{24,8},{1,17},{9,25},{17,1},{25,9},{2,18},{10... | collective-permute-start | bytes 528392 | tf_op jit(solution)/shard_map/ppermute | solution.py:505
  37.2 17.2 %collective-permute-start.16 = (bf16[688,128]{1,0:T(8,128)(2,1)S(1)}, bf16[688,128]{1,0:T(8,128)(2,1)S(1)}, u32[]{:S(2)}, u32[]{:S(2)}) collective-permute-start(bf16[688,128]{1,0:T(8,128)(2,1)S(1)} %get-tuple-element.29), channel_id=1, source_target_pairs={{0,24},{8,16},{16,8},{24,0},{1,25},{9,17},{17,9},{25,1},{2,26},{10... | collective-permute-start | bytes 528392 | tf_op jit(solution)/shard_map/ppermute | solution.py:505
  40.5 14.0 %collective-permute-start.17 = (bf16[688,128]{1,0:T(8,128)(2,1)S(1)}, bf16[688,128]{1,0:T(8,128)(2,1)S(1)}, u32[]{:S(2)}, u32[]{:S(2)}) collective-permute-start(bf16[688,128]{1,0:T(8,128)(2,1)S(1)} %get-tuple-element.30), channel_id=1, source_target_pairs={{0,8},{8,0},{16,24},{24,16},{1,9},{9,1},{17,25},{25,17},{2,10},{10... | collective-permute-start | bytes 528392 | tf_op jit(solution)/shard_map/ppermute | solution.py:505
  41.7 13.8 %collective-permute-start.18 = (bf16[688,128]{1,0:T(8,128)(2,1)S(1)}, bf16[688,128]{1,0:T(8,128)(2,1)S(1)}, u32[]{:S(2)}, u32[]{:S(2)}) collective-permute-start(bf16[688,128]{1,0:T(8,128)(2,1)S(1)} %get-tuple-element.31), channel_id=1, source_target_pairs={{0,16},{8,24},{16,0},{24,8},{1,17},{9,25},{17,1},{25,9},{2,18},{10... | collective-permute-start | bytes 528392 | tf_op jit(solution)/shard_map/ppermute | solution.py:505
  44.8 12.1 %collective-permute-start.19 = (bf16[688,128]{1,0:T(8,128)(2,1)S(1)}, bf16[688,128]{1,0:T(8,128)(2,1)S(1)}, u32[]{:S(2)}, u32[]{:S(2)}) collective-permute-start(bf16[688,128]{1,0:T(8,128)(2,1)S(1)} %get-tuple-element.32), channel_id=1, source_target_pairs={{0,24},{8,16},{16,8},{24,0},{1,25},{9,17},{17,9},{25,1},{2,26},{10... | collective-permute-start | bytes 528392 | tf_op jit(solution)/shard_map/ppermute | solution.py:505
  46.0 1.0 %copy-start = (bf16[64,16,256]{2,1,0:T(8,128)(2,1)S(1)}, bf16[64,16,256]{2,1,0:T(8,128)(2,1)}, u32[]{:S(2)}) copy-start(bf16[64,16,256]{2,1,0:T(8,128)(2,1)} %param.13) | copy-start | bytes 1572868
  47.0 1.0 %copy-start.7 = (s32[64,16,64]{2,1,0:T(8,128)S(1)}, s32[64,16,64]{2,1,0:T(8,128)}, u32[]{:S(2)}) copy-start(s32[64,16,64]{2,1,0:T(8,128)} %param.19) | copy-start | bytes 786436
  48.1 0.8 %copy-start.8 = (bf16[256,64]{0,1:T(8,128)(2,1)S(1)}, bf16[256,64]{0,1:T(8,128)(2,1)}, u32[]{:S(2)}) copy-start(bf16[256,64]{0,1:T(8,128)(2,1)} %param.20) | copy-start | bytes 98308
  48.8 0.7 copy-start.9
  56.9 13.1 %copy-start.1 = (bf16[64,16,256]{2,1,0:T(8,128)(2,1)S(1)}, bf16[64,16,256]{2,1,0:T(8,128)(2,1)}, u32[]{:S(2)}) copy-start(bf16[64,16,256]{2,1,0:T(8,128)(2,1)} %param.13) | copy-start | bytes 1572868
  56.9 13.1 %copy-start.2 = (bf16[256,256]{1,0:T(8,128)(2,1)S(1)}, bf16[256,256]{1,0:T(8,128)(2,1)}, u32[]{:S(2)}) copy-start(bf16[256,256]{1,0:T(8,128)(2,1)} %weight_ref.3) | copy-start | bytes 393220
  56.9 13.1 %copy-start.4 = (f32[256]{0:T(256)S(1)}, f32[256]{0:T(256)}, u32[]{:S(2)}) copy-start(f32[256]{0:T(256)} %param.23) | copy-start | bytes 3076
  56.9 14.2 %copy-start.5 = (f32[128]{0:T(128)S(1)}, f32[128]{0:T(128)}, u32[]{:S(2)}) copy-start(f32[128]{0:T(128)} %param.24) | copy-start | bytes 1540
  56.9 14.2 %copy-start.6 = (f32[128]{0:T(128)S(1)}, f32[128]{0:T(128)}, u32[]{:S(2)}) copy-start(f32[128]{0:T(128)} %param.25) | copy-start | bytes 1540
  65.3 5.8 %collective-permute-start.20 = (bf16[1024,128]{1,0:T(8,128)(2,1)S(1)}, bf16[1024,128]{1,0:T(8,128)(2,1)S(1)}, u32[]{:S(2)}, u32[]{:S(2)}) collective-permute-start(bf16[1024,128]{1,0:T(8,128)(2,1)S(1)} %attend.1.own_ref), channel_id=1, source_target_pairs={{0,1},{1,0},{2,3},{3,2},{4,5},{5,4},{6,7},{7,6},{8,9},{9,8},{10,11... | collective-permute-start | bytes 786440 | tf_op jit(solution)/shard_map/ppermute | solution.py:668

commit v7 on v6

--- a/solution.py
+++ b/solution.py
@@ -142,6 +142,18 @@
                 )
 
 
+def load_kernel(*refs):
+    count = len(refs) // 2
+    sem = refs[-1]
+    moves = [
+        pltpu.make_async_copy(refs[number], refs[count + number], sem.at[number]) for number in range(count)
+    ]
+    for move in moves:
+        move.start()
+    for move in moves:
+        move.wait()
+
+
 def select_kernel(dims, ids_ref, zero_ref, one_ref, two_ref, three_ref, out_ref, sem):
     peers, capacity, sizes = dims
     refs = (zero_ref, one_ref, two_ref)
@@ -610,6 +622,16 @@
     depth1 = GROUPS[1] * per_block * sides[1]
     depth2 = per_block * sizes[2] + requests * sizes[3]
     whole = pl.BlockSpec(memory_space=VMEM)
+    staged = (queries_blocked, samples_blocked, logit_weight.T)
+    queries_blocked, samples_blocked, logit_turned = pl.pallas_call(
+        load_kernel,
+        out_shape=[jax.ShapeDtypeStruct(array.shape, array.dtype) for array in staged],
+        in_specs=[pl.BlockSpec(memory_space=ANY)] * len(staged),
+        out_specs=[whole] * len(staged),
+        scratch_shapes=[pltpu.SemaphoreType.DMA((len(staged),))],
+        compiler_params=pltpu.CompilerParams(vmem_limit_bytes=SELECT_VMEM),
+        name="load",
+    )(*staged)
     weights = pl.pallas_call(
         functools.partial(prep_kernel, dims),
         out_shape=[
@@ -640,7 +662,7 @@
         compiler_params=pltpu.CompilerParams(vmem_limit_bytes=PREP_VMEM),
         cost_estimate=PREP_COST,
         name="prep",
-    )(queries_blocked, logit_weight.T, logit_bias.reshape(1, lanes), samples_blocked)
+    )(queries_blocked, logit_turned, logit_bias.reshape(1, lanes), samples_blocked)
 
     attn = pl.pallas_call(
         functools.partial(attend_kernel, dims, grid, gather, len(sources)),

time: 73.9 us -> 72.7 us (0.984)
  the two profiles are of different devices: /device:TPU:9 before, /device:TPU:0 now
where the time goes in v7:
time: 72.7 us; the launch traced here: 71.7 us
  starting transfers between devices  27.6 us (38%)
  Pallas kernels  20.4 us (28%)
  waiting for transfers between devices  17.6 us (24%)
  local copies, waits for them, and re-layouts  4.06 us (6%)
  other arithmetic  1.78 us (2%)
    ppermute x12, starting transfers between devices, relay_tiles(): lax.ppermute(sent[number - 1], 'row', [(row, source_of(row, number)) for...  14.2 us
    ppermute x5, waiting for transfers between devices, move(): held[name] = lax.ppermute(held[source or 'own'], 'col', pairs)  10.7 us
    ppermute x5, starting transfers between devices, move(): held[name] = lax.ppermute(held[source or 'own'], 'col', pairs)  9.85 us
    pallas_call x1, Pallas kernels, on_device(): pl.pallas_call(functools.partial(attend_kernel, dims, grid, gather, len(s...  8.35 us
    pallas_call x1, Pallas kernels, on_device(): pl.pallas_call(functools.partial(prep_kernel, dims), out_shape=[jax.Shape...  4.97 us
    ppermute x12, waiting for transfers between devices, relay_tiles(): lax.ppermute(sent[number - 1], 'row', [(row, source_of(row, number)) for...  4.97 us
    pallas_call x4, Pallas kernels, relay_tiles(): pl.pallas_call(functools.partial(relay_select_kernel, (row_count - 1, len...  3.85 us
    ppermute x3, starting transfers between devices, relay_tiles(): lax.ppermute(mine, 'row', [(row, partner_of(row, number)) for row in rang...  3.49 us
  transfers between devices with their start and end apart: 21, of which 6 were waited for; matrix products, arithmetic and copies ran while one was open for 3% of the time, Pallas kernels for 14%

profile of v7, /device:TPU:0, one launch (start us, length us, event | category | flops | bytes accessed | tf_op | source)
XLA Modules:
  0.0 71.7 jit_solution(1594679107778078683)
XLA Ops:
  0.0 1.1 %pad_maximum_fusion.refs_3_ = bf16[1360,128]{1,0:T(8,128)(2,1)S(1)} fusion(bf16[16,128]{1,0:T(8,128)(2,1)} %bitcast.33, bf16[64,128]{1,0:T(8,128)(2,1)} %bitcast.32, bf16[256,128]{1,0:T(8,128)(2,1)} %bitcast.30, bf16[1024,128]{1,0:T(8,128)(2,1)} %bitcast.29), kind=kLoop, calls=%fused_computation | loop fusion | flops 1392640 | bytes 696320 | tf_op jit(solution)/shard_map/concatenate | solution.py:468
  1.1 0.7 collective-permute-start.1
  1.8 5.9 %collective-permute-start = (bf16[1360,128]{1,0:T(8,128)(2,1)S(1)}, bf16[1360,128]{1,0:T(8,128)(2,1)S(1)}, u32[]{:S(2)}, u32[]{:S(2)}) collective-permute-start(bf16[1360,128]{1,0:T(8,128)(2,1)S(1)} %pad_maximum_fusion.refs_3_), channel_id=1, source_target_pairs={{0,2},{2,0},{4,6},{6,4},{1,3},{3,1},{5,7},{7,5},{8,10},{10,8},{12,... | collective-permute-start | bytes 1044488 | tf_op jit(solution)/shard_map/ppermute | solution.py:472
  7.7 0.7 copy.35
  8.4 0.1 reshape.489
  8.5 0.2 convert_reduce_fusion
  8.8 0.2 select_reduce_fusion
  9.0 6.6 %collective-permute-done.refs_3_.refs_4_ = bf16[1360,128]{1,0:T(8,128)(2,1)S(1)} collective-permute-done((bf16[1360,128]{1,0:T(8,128)(2,1)S(1)}, bf16[1360,128]{1,0:T(8,128)(2,1)S(1)}, u32[]{:S(2)}, u32[]{:S(2)}) %collective-permute-start) | collective-permute-done | bytes 348192 | tf_op jit(solution)/shard_map/ppermute | solution.py:472
  15.6 0.7 collective-permute-start.3
  16.3 0.1 sub.31
  16.4 0.1 select_reduce_fusion.1
  16.5 0.1 copy.41
  16.6 1.5 %collective-permute-start.5 = (s32[4,8]{1,0:T(4,128)S(1)}, s32[4,8]{1,0:T(4,128)S(1)}, u32[]{:S(2)}, u32[]{:S(2)}) collective-permute-start(s32[4,8]{1,0:T(4,128)S(1)} %copy.41), channel_id=1, source_target_pairs={{0,8},{8,0},{16,24},{24,16},{1,9},{9,1},{17,25},{25,17},{2,10},{10... | collective-permute-start | bytes 392 | tf_op jit(solution)/shard_map/ppermute | solution.py:492
  18.0 0.1 copy.42
  18.1 1.5 %collective-permute-start.6 = (s32[4,8]{1,0:T(4,128)S(1)}, s32[4,8]{1,0:T(4,128)S(1)}, u32[]{:S(2)}, u32[]{:S(2)}) collective-permute-start(s32[4,8]{1,0:T(4,128)S(1)} %copy.42), channel_id=1, source_target_pairs={{0,16},{8,24},{16,0},{24,8},{1,17},{9,25},{17,1},{25,9},{2,18},{10... | collective-permute-start | bytes 392 | tf_op jit(solution)/shard_map/ppermute | solution.py:492
  19.6 0.1 copy.43
  19.7 0.5 collective-permute-start.7
  20.2 0.1 copy.36
  20.3 0.0 collective-permute-done.1.refs_3_.refs_5_
  20.3 1.3 %collective-permute-start.2 = (bf16[1360,128]{1,0:T(8,128)(2,1)S(1)}, bf16[1360,128]{1,0:T(8,128)(2,1)S(1)}, u32[]{:S(2)}, u32[]{:S(2)}) collective-permute-start(bf16[1360,128]{1,0:T(8,128)(2,1)S(1)} %collective-permute-done.1.refs_3_.refs_5_), channel_id=1, source_target_pairs={{2,0},{4,6},{3,1},{5,7},{10,8},{12,14},{11,9},{13,15},{18,16},{20,... | collective-permute-start | bytes 1044488 | tf_op jit(solution)/shard_map/ppermute | solution.py:472
  21.6 0.0 collective-permute-done.3.refs_4_.refs_7_
  21.6 1.3 %collective-permute-start.4 = (bf16[1360,128]{1,0:T(8,128)(2,1)S(1)}, bf16[1360,128]{1,0:T(8,128)(2,1)S(1)}, u32[]{:S(2)}, u32[]{:S(2)}) collective-permute-start(bf16[1360,128]{1,0:T(8,128)(2,1)S(1)} %collective-permute-done.3.refs_4_.refs_7_), channel_id=1, source_target_pairs={{2,0},{4,6},{3,1},{5,7},{10,8},{12,14},{11,9},{13,15},{18,16},{20,... | collective-permute-start | bytes 1044488 | tf_op jit(solution)/shard_map/ppermute | solution.py:472
  22.9 0.1 pad_add_fusion.place_ref.refs_1_
  23.0 0.0 collective-permute-done.5.refs_0_
  23.0 0.0 collective-permute-done.6.refs_1_
  23.0 1.2 %collective-permute-done.7.refs_2_ = s32[4,8]{1,0:T(4,128)S(1)} collective-permute-done((s32[4,8]{1,0:T(4,128)S(1)}, s32[4,8]{1,0:T(4,128)S(1)}, u32[]{:S(2)}, u32[]{:S(2)}) %collective-permute-start.7) | collective-permute-done | bytes 160 | tf_op jit(solution)/shard_map/ppermute | solution.py:492
  24.2 1.0 %shard_map.127 = (bf16[688,128]{1,0:T(8,128)(2,1)S(1)}, bf16[688,128]{1,0:T(8,128)(2,1)S(1)}, bf16[688,128]{1,0:T(8,128)(2,1)S(1)}) custom-call(s32[2]{0:T(128)S(1)} %pad_add_fusion.place_ref.refs_1_, s32[16,8]{1,0:T(8,128)S(1)} %get-tuple-element.47.request_ref.refs_0_, s32[16,8]{1,0:T(8,128)S(1)} %get-tuple-element.46.asked_ref.refs_2_, ...), custom_call_target="tpu_custom_call" | custom-call | flops 500000000 | bytes 1000000 | tf_op jit(solution)/shard_map/pallas_call | solution.py:504
  25.2 0.6 collective-permute-start.8
  25.8 1.3 %collective-permute-start.9 = (bf16[688,128]{1,0:T(8,128)(2,1)S(1)}, bf16[688,128]{1,0:T(8,128)(2,1)S(1)}, u32[]{:S(2)}, u32[]{:S(2)}) collective-permute-start(bf16[688,128]{1,0:T(8,128)(2,1)S(1)} %get-tuple-element.26), channel_id=1, source_target_pairs={{0,16},{8,24},{16,0},{24,8},{1,17},{9,25},{17,1},{25,9},{2,18},{10... | collective-permute-start | bytes 528392 | tf_op jit(solution)/shard_map/ppermute | solution.py:517
  27.0 1.7 %collective-permute-start.10 = (bf16[688,128]{1,0:T(8,128)(2,1)S(1)}, bf16[688,128]{1,0:T(8,128)(2,1)S(1)}, u32[]{:S(2)}, u32[]{:S(2)}) collective-permute-start(bf16[688,128]{1,0:T(8,128)(2,1)S(1)} %get-tuple-element.27), channel_id=1, source_target_pairs={{0,24},{8,16},{16,8},{24,0},{1,25},{9,17},{17,9},{25,1},{2,26},{10... | collective-permute-start | bytes 528392 | tf_op jit(solution)/shard_map/ppermute | solution.py:517
  28.7 1.0 %shard_map.128 = (bf16[688,128]{1,0:T(8,128)(2,1)S(1)}, bf16[688,128]{1,0:T(8,128)(2,1)S(1)}, bf16[688,128]{1,0:T(8,128)(2,1)S(1)}) custom-call(s32[2]{0:T(128)S(1)} %pad_add_fusion.place_ref.refs_1_, s32[16,8]{1,0:T(8,128)S(1)} %get-tuple-element.47.request_ref.refs_0_, s32[16,8]{1,0:T(8,128)S(1)} %get-tuple-element.46.asked_ref.refs_2_, ...), custom_call_target="tpu_custom_call" | custom-call | flops 500000000 | bytes 1000000 | tf_op jit(solution)/shard_map/pallas_call | solution.py:504
  29.7 4.1 %collective-permute-done.2.refs_4_.refs_6_ = bf16[1360,128]{1,0:T(8,128)(2,1)S(1)} collective-permute-done((bf16[1360,128]{1,0:T(8,128)(2,1)S(1)}, bf16[1360,128]{1,0:T(8,128)(2,1)S(1)}, u32[]{:S(2)}, u32[]{:S(2)}) %collective-permute-start.2) | collective-permute-done | bytes 348192 | tf_op jit(solution)/shard_map/ppermute | solution.py:472
  33.8 1.5 %collective-permute-start.11 = (bf16[688,128]{1,0:T(8,128)(2,1)S(1)}, bf16[688,128]{1,0:T(8,128)(2,1)S(1)}, u32[]{:S(2)}, u32[]{:S(2)}) collective-permute-start(bf16[688,128]{1,0:T(8,128)(2,1)S(1)} %get-tuple-element.28), channel_id=1, source_target_pairs={{0,8},{8,0},{16,24},{24,16},{1,9},{9,1},{17,25},{25,17},{2,10},{10... | collective-permute-start | bytes 528392 | tf_op jit(solution)/shard_map/ppermute | solution.py:517
  35.3 1.0 %shard_map.129 = (bf16[688,128]{1,0:T(8,128)(2,1)S(1)}, bf16[688,128]{1,0:T(8,128)(2,1)S(1)}, bf16[688,128]{1,0:T(8,128)(2,1)S(1)}) custom-call(s32[2]{0:T(128)S(1)} %pad_add_fusion.place_ref.refs_1_, s32[16,8]{1,0:T(8,128)S(1)} %get-tuple-element.47.request_ref.refs_0_, s32[16,8]{1,0:T(8,128)S(1)} %get-tuple-element.46.asked_ref.refs_2_, ...), custom_call_target="tpu_custom_call" | custom-call | flops 500000000 | bytes 1000000 | tf_op jit(solution)/shard_map/pallas_call | solution.py:504
  36.3 0.0 collective-permute-done.8.refs_9_
  36.3 1.6 %collective-permute-start.12 = (bf16[688,128]{1,0:T(8,128)(2,1)S(1)}, bf16[688,128]{1,0:T(8,128)(2,1)S(1)}, u32[]{:S(2)}, u32[]{:S(2)}) collective-permute-start(bf16[688,128]{1,0:T(8,128)(2,1)S(1)} %get-tuple-element.29), channel_id=1, source_target_pairs={{0,16},{8,24},{16,0},{24,8},{1,17},{9,25},{17,1},{25,9},{2,18},{10... | collective-permute-start | bytes 528392 | tf_op jit(solution)/shard_map/ppermute | solution.py:517
  37.9 0.5 collective-permute-start.13
  38.3 0.0 collective-permute-done.4.refs_3_.refs_8_
  38.4 1.5 %collective-permute-start.14 = (bf16[688,128]{1,0:T(8,128)(2,1)S(1)}, bf16[688,128]{1,0:T(8,128)(2,1)S(1)}, u32[]{:S(2)}, u32[]{:S(2)}) collective-permute-start(bf16[688,128]{1,0:T(8,128)(2,1)S(1)} %get-tuple-element.31), channel_id=1, source_target_pairs={{0,8},{8,0},{16,24},{24,16},{1,9},{9,1},{17,25},{25,17},{2,10},{10... | collective-permute-start | bytes 528392 | tf_op jit(solution)/shard_map/ppermute | solution.py:517
  39.8 1.0 %copy-done = bf16[64,16,256]{2,1,0:T(8,128)(2,1)S(1)} copy-done((bf16[64,16,256]{2,1,0:T(8,128)(2,1)S(1)}, bf16[64,16,256]{2,1,0:T(8,128)(2,1)}, u32[]{:S(2)}) %copy-start) | copy-done | bytes 524312
  40.9 1.0 %copy-done.1 = s32[64,16,64]{2,1,0:T(8,128)S(1)} copy-done((s32[64,16,64]{2,1,0:T(8,128)S(1)}, s32[64,16,64]{2,1,0:T(8,128)}, u32[]{:S(2)}) %copy-start.1) | copy-done | bytes 262168
  41.9 0.8 %copy-done.4 = bf16[256,64]{0,1:T(8,128)(2,1)S(1)} copy-done((bf16[256,64]{0,1:T(8,128)(2,1)S(1)}, bf16[256,64]{0,1:T(8,128)(2,1)}, u32[]{:S(2)}) %copy-start.4) | copy-done | bytes 32792
  42.7 0.1 load.1
  42.8 1.0 %shard_map.130 = (bf16[688,128]{1,0:T(8,128)(2,1)S(1)}, bf16[688,128]{1,0:T(8,128)(2,1)S(1)}, bf16[688,128]{1,0:T(8,128)(2,1)S(1)}) custom-call(s32[2]{0:T(128)S(1)} %pad_add_fusion.place_ref.refs_1_, s32[16,8]{1,0:T(8,128)S(1)} %get-tuple-element.47.request_ref.refs_0_, s32[16,8]{1,0:T(8,128)S(1)} %get-tuple-element.46.asked_ref.refs_2_, ...), custom_call_target="tpu_custom_call" | custom-call | flops 500000000 | bytes 1000000 | tf_op jit(solution)/shard_map/pallas_call | solution.py:504
  43.8 0.0 collective-permute-done.10.refs_11_
  43.8 1.6 %collective-permute-start.15 = (bf16[688,128]{1,0:T(8,128)(2,1)S(1)}, bf16[688,128]{1,0:T(8,128)(2,1)S(1)}, u32[]{:S(2)}, u32[]{:S(2)}) collective-permute-start(bf16[688,128]{1,0:T(8,128)(2,1)S(1)} %get-tuple-element.32), channel_id=1, source_target_pairs={{0,16},{8,24},{16,0},{24,8},{1,17},{9,25},{17,1},{25,9},{2,18},{10... | collective-permute-start | bytes 528392 | tf_op jit(solution)/shard_map/ppermute | solution.py:517
  45.4 0.0 collective-permute-done.11.refs_12_
  45.4 0.5 collective-permute-start.16
  45.9 0.0 collective-permute-done.12.refs_13_
  45.9 1.5 %collective-permute-start.17 = (bf16[688,128]{1,0:T(8,128)(2,1)S(1)}, bf16[688,128]{1,0:T(8,128)(2,1)S(1)}, u32[]{:S(2)}, u32[]{:S(2)}) collective-permute-start(bf16[688,128]{1,0:T(8,128)(2,1)S(1)} %get-tuple-element.34), channel_id=1, source_target_pairs={{0,8},{8,0},{16,24},{24,16},{1,9},{9,1},{17,25},{25,17},{2,10},{10... | collective-permute-start | bytes 528392 | tf_op jit(solution)/shard_map/ppermute | solution.py:517
  47.4 0.0 collective-permute-done.13.refs_14_
  47.4 1.5 %collective-permute-start.18 = (bf16[688,128]{1,0:T(8,128)(2,1)S(1)}, bf16[688,128]{1,0:T(8,128)(2,1)S(1)}, u32[]{:S(2)}, u32[]{:S(2)}) collective-permute-start(bf16[688,128]{1,0:T(8,128)(2,1)S(1)} %get-tuple-element.35), channel_id=1, source_target_pairs={{0,16},{8,24},{16,0},{24,8},{1,17},{9,25},{17,1},{25,9},{2,18},{10... | collective-permute-start | bytes 528392 | tf_op jit(solution)/shard_map/ppermute | solution.py:517
  48.9 0.5 collective-permute-start.19
  49.4 5.0 %prep.1 = (bf16[4,4,4,256,256]{4,3,2,1,0:T(8,128)(2,1)S(1)}, bf16[4,4,4,256,256]{4,3,2,1,0:T(8,128)(2,1)S(1)}, bf16[4,4,256,256]{3,2,1,0:T(8,128)(2,1)S(1)}, f32[4,64,256]{2,1,0:T(8,128)S(1)}) custom-call(bf16[1024,256]{1,0:T(8,128)(2,1)S(1)} %get-tuple-element.24.query_ref, bf16[64,256]{1,0:T(8,128)(2,1)S(1)} %get-tuple-element.37.logit_ref, ...), custom_call_target="tpu_custom_call" | custom-call | flops 2000000000 | bytes 4000000 | tf_op jit(solution)/shard_map/prep/pallas_call | solution.py:635
  54.4 1.6 %collective-permute-done.15.refs_16_ = bf16[688,128]{1,0:T(8,128)(2,1)S(1)} collective-permute-done((bf16[688,128]{1,0:T(8,128)(2,1)S(1)}, bf16[688,128]{1,0:T(8,128)(2,1)S(1)}, u32[]{:S(2)}, u32[]{:S(2)}) %collective-permute-start.15) | collective-permute-done | bytes 176160 | tf_op jit(solution)/shard_map/ppermute | solution.py:517
  56.0 3.3 %collective-permute-done.18.refs_19_ = bf16[688,128]{1,0:T(8,128)(2,1)S(1)} collective-permute-done((bf16[688,128]{1,0:T(8,128)(2,1)S(1)}, bf16[688,128]{1,0:T(8,128)(2,1)S(1)}, u32[]{:S(2)}, u32[]{:S(2)}) %collective-permute-start.18) | collective-permute-done | bytes 176160 | tf_op jit(solution)/shard_map/ppermute | solution.py:517
  59.3 0.0 copy-start.5
  59.3 0.0 copy-start.6
  59.4 0.0 copy-start.7
  59.4 8.4 %attend.1.own_ref = bf16[1024,128]{1,0:T(8,128)(2,1)S(1)} custom-call(s32[16,8]{1,0:T(8,128)S(1)} %get-tuple-element.47.request_ref.refs_0_, s32[2]{0:T(128)S(1)} %pad_add_fusion.place_ref.refs_1_, s32[16,8]{1,0:T(8,128)S(1)} %get-tuple-element.46.asked_ref.refs_2_, bf16[1360,128]{1,0:T(8,128)(2,1)S(1)} %pad_maximum_fusion.refs_3_, ...), custom_call_target="tpu_custom_call" | custom-call | flops 2000000000 | bytes 4000000 | tf_op jit(solution)/shard_map/attend/pallas_call | solution.py:667
  67.7 0.1 collective-permute-start.20
  67.8 0.8 %own.1.pre_ref = f32[1024,256]{1,0:T(8,128)S(1)} custom-call(s32[1]{0:T(128)} %bitcast.head_ref, bf16[1024,256]{1,0:T(8,128)(2,1)S(1)} %get-tuple-element.24.query_ref, bf16[1024,128]{1,0:T(8,128)(2,1)S(1)} %attend.1.own_ref, bf16[256,256]{1,0:T(8,128)(2,1)S(1)} %copy-done.2, f32[1,256]{1,0:T(1,128)S(1)} %bitcast.25), custom_call_target="tpu_custom_call" | custom-call | tf_op jit(solution)/shard_map/own/pallas_call | solution.py:694
  68.6 0.7 %collective-permute-done.20.other_ref = bf16[1024,128]{1,0:T(8,128)(2,1)S(1)} collective-permute-done((bf16[1024,128]{1,0:T(8,128)(2,1)S(1)}, bf16[1024,128]{1,0:T(8,128)(2,1)S(1)}, u32[]{:S(2)}, u32[]{:S(2)}) %collective-permute-start.20) | collective-permute-done | bytes 262176 | tf_op jit(solution)/shard_map/ppermute | solution.py:690
  69.3 2.3 %norm.1 = bf16[1024,128]{1,0:T(8,128)(2,1)} custom-call(s32[1]{0:T(128)} %bitcast.head_ref, f32[1024,256]{1,0:T(8,128)S(1)} %own.1.pre_ref, bf16[1024,128]{1,0:T(8,128)(2,1)S(1)} %collective-permute-done.20.other_ref, bf16[256,256]{1,0:T(8,128)(2,1)S(1)} %copy-done.2, f32[1,128]{1,0:T(1,128)S(1)} %bitcast.26, f32[1,128]{1,0:T(1,128)S(1)} %bitcast.27), custom_call_target="tpu_custom_call" | custom-call | tf_op jit(solution)/shard_map/norm/pallas_call | solution.py:709
  (26 shorter events, 0.1 us)
Async XLA Ops:
  0.0 49.4 %copy-start.8 = (f32[64]{0:T(128)S(1)}, f32[64]{0:T(128)}, u32[]{:S(2)}) copy-start(f32[64]{0:T(128)} %param.21) | copy-start | bytes 772
  0.0 59.3 %copy-start.3 = (s32[4,1,4,8]{3,2,1,0:T(4,128)S(1)}, s32[4,1,4,8]{3,2,1,0:T(4,128)}, u32[]{:S(2)}) copy-start(s32[4,1,4,8]{3,2,1,0:T(4,128)} %refs_25_.1) | copy-start | bytes 1540
  1.1 19.2 %collective-permute-start.1 = (bf16[1360,128]{1,0:T(8,128)(2,1)S(1)}, bf16[1360,128]{1,0:T(8,128)(2,1)S(1)}, u32[]{:S(2)}, u32[]{:S(2)}) collective-permute-start(bf16[1360,128]{1,0:T(8,128)(2,1)S(1)} %pad_maximum_fusion.refs_3_), channel_id=1, source_target_pairs={{2,4},{4,2},{3,5},{5,3},{10,12},{12,10},{11,13},{13,11},{18,20},{2... | collective-permute-start | bytes 1044488 | tf_op jit(solution)/shard_map/ppermute | solution.py:472
  1.8 13.8 %collective-permute-start = (bf16[1360,128]{1,0:T(8,128)(2,1)S(1)}, bf16[1360,128]{1,0:T(8,128)(2,1)S(1)}, u32[]{:S(2)}, u32[]{:S(2)}) collective-permute-start(bf16[1360,128]{1,0:T(8,128)(2,1)S(1)} %pad_maximum_fusion.refs_3_), channel_id=1, source_target_pairs={{0,2},{2,0},{4,6},{6,4},{1,3},{3,1},{5,7},{7,5},{8,10},{10,8},{12,... | collective-permute-start | bytes 1044488 | tf_op jit(solution)/shard_map/ppermute | solution.py:472
  15.6 6.0 %collective-permute-start.3 = (bf16[1360,128]{1,0:T(8,128)(2,1)S(1)}, bf16[1360,128]{1,0:T(8,128)(2,1)S(1)}, u32[]{:S(2)}, u32[]{:S(2)}) collective-permute-start(bf16[1360,128]{1,0:T(8,128)(2,1)S(1)} %collective-permute-done.refs_3_.refs_4_), channel_id=1, source_target_pairs={{2,4},{4,2},{3,5},{5,3},{10,12},{12,10},{11,13},{13,11},{18,20},{2... | collective-permute-start | bytes 1044488 | tf_op jit(solution)/shard_map/ppermute | solution.py:472
  16.6 6.4 %collective-permute-start.5 = (s32[4,8]{1,0:T(4,128)S(1)}, s32[4,8]{1,0:T(4,128)S(1)}, u32[]{:S(2)}, u32[]{:S(2)}) collective-permute-start(s32[4,8]{1,0:T(4,128)S(1)} %copy.41), channel_id=1, source_target_pairs={{0,8},{8,0},{16,24},{24,16},{1,9},{9,1},{17,25},{25,17},{2,10},{10... | collective-permute-start | bytes 392 | tf_op jit(solution)/shard_map/ppermute | solution.py:492
  18.1 4.9 %collective-permute-start.6 = (s32[4,8]{1,0:T(4,128)S(1)}, s32[4,8]{1,0:T(4,128)S(1)}, u32[]{:S(2)}, u32[]{:S(2)}) collective-permute-start(s32[4,8]{1,0:T(4,128)S(1)} %copy.42), channel_id=1, source_target_pairs={{0,16},{8,24},{16,0},{24,8},{1,17},{9,25},{17,1},{25,9},{2,18},{10... | collective-permute-start | bytes 392 | tf_op jit(solution)/shard_map/ppermute | solution.py:492
  19.7 4.5 %collective-permute-start.7 = (s32[4,8]{1,0:T(4,128)S(1)}, s32[4,8]{1,0:T(4,128)S(1)}, u32[]{:S(2)}, u32[]{:S(2)}) collective-permute-start(s32[4,8]{1,0:T(4,128)S(1)} %copy.43), channel_id=1, source_target_pairs={{0,24},{8,16},{16,8},{24,0},{1,25},{9,17},{17,9},{25,1},{2,26},{10... | collective-permute-start | bytes 392 | tf_op jit(solution)/shard_map/ppermute | solution.py:492
  20.3 13.5 %collective-permute-start.2 = (bf16[1360,128]{1,0:T(8,128)(2,1)S(1)}, bf16[1360,128]{1,0:T(8,128)(2,1)S(1)}, u32[]{:S(2)}, u32[]{:S(2)}) collective-permute-start(bf16[1360,128]{1,0:T(8,128)(2,1)S(1)} %collective-permute-done.1.refs_3_.refs_5_), channel_id=1, source_target_pairs={{2,0},{4,6},{3,1},{5,7},{10,8},{12,14},{11,9},{13,15},{18,16},{20,... | collective-permute-start | bytes 1044488 | tf_op jit(solution)/shard_map/ppermute | solution.py:472
  21.6 16.8 %collective-permute-start.4 = (bf16[1360,128]{1,0:T(8,128)(2,1)S(1)}, bf16[1360,128]{1,0:T(8,128)(2,1)S(1)}, u32[]{:S(2)}, u32[]{:S(2)}) collective-permute-start(bf16[1360,128]{1,0:T(8,128)(2,1)S(1)} %collective-permute-done.3.refs_4_.refs_7_), channel_id=1, source_target_pairs={{2,0},{4,6},{3,1},{5,7},{10,8},{12,14},{11,9},{13,15},{18,16},{20,... | collective-permute-start | bytes 1044488 | tf_op jit(solution)/shard_map/ppermute | solution.py:472
  25.2 11.1 %collective-permute-start.8 = (bf16[688,128]{1,0:T(8,128)(2,1)S(1)}, bf16[688,128]{1,0:T(8,128)(2,1)S(1)}, u32[]{:S(2)}, u32[]{:S(2)}) collective-permute-start(bf16[688,128]{1,0:T(8,128)(2,1)S(1)} %get-tuple-element.25), channel_id=1, source_target_pairs={{0,8},{8,0},{16,24},{24,16},{1,9},{9,1},{17,25},{25,17},{2,10},{10... | collective-permute-start | bytes 528392 | tf_op jit(solution)/shard_map/ppermute | solution.py:517
  25.8 12.1 %collective-permute-start.9 = (bf16[688,128]{1,0:T(8,128)(2,1)S(1)}, bf16[688,128]{1,0:T(8,128)(2,1)S(1)}, u32[]{:S(2)}, u32[]{:S(2)}) collective-permute-start(bf16[688,128]{1,0:T(8,128)(2,1)S(1)} %get-tuple-element.26), channel_id=1, source_target_pairs={{0,16},{8,24},{16,0},{24,8},{1,17},{9,25},{17,1},{25,9},{2,18},{10... | collective-permute-start | bytes 528392 | tf_op jit(solution)/shard_map/ppermute | solution.py:517
  27.0 16.8 %collective-permute-start.10 = (bf16[688,128]{1,0:T(8,128)(2,1)S(1)}, bf16[688,128]{1,0:T(8,128)(2,1)S(1)}, u32[]{:S(2)}, u32[]{:S(2)}) collective-permute-start(bf16[688,128]{1,0:T(8,128)(2,1)S(1)} %get-tuple-element.27), channel_id=1, source_target_pairs={{0,24},{8,16},{16,8},{24,0},{1,25},{9,17},{17,9},{25,1},{2,26},{10... | collective-permute-start | bytes 528392 | tf_op jit(solution)/shard_map/ppermute | solution.py:517
  33.8 11.6 %collective-permute-start.11 = (bf16[688,128]{1,0:T(8,128)(2,1)S(1)}, bf16[688,128]{1,0:T(8,128)(2,1)S(1)}, u32[]{:S(2)}, u32[]{:S(2)}) collective-permute-start(bf16[688,128]{1,0:T(8,128)(2,1)S(1)} %get-tuple-element.28), channel_id=1, source_target_pairs={{0,8},{8,0},{16,24},{24,16},{1,9},{9,1},{17,25},{25,17},{2,10},{10... | collective-permute-start | bytes 528392 | tf_op jit(solution)/shard_map/ppermute | solution.py:517
  36.3 9.6 %collective-permute-start.12 = (bf16[688,128]{1,0:T(8,128)(2,1)S(1)}, bf16[688,128]{1,0:T(8,128)(2,1)S(1)}, u32[]{:S(2)}, u32[]{:S(2)}) collective-permute-start(bf16[688,128]{1,0:T(8,128)(2,1)S(1)} %get-tuple-element.29), channel_id=1, source_target_pairs={{0,16},{8,24},{16,0},{24,8},{1,17},{9,25},{17,1},{25,9},{2,18},{10... | collective-permute-start | bytes 528392 | tf_op jit(solution)/shard_map/ppermute | solution.py:517
  37.9 9.5 %collective-permute-start.13 = (bf16[688,128]{1,0:T(8,128)(2,1)S(1)}, bf16[688,128]{1,0:T(8,128)(2,1)S(1)}, u32[]{:S(2)}, u32[]{:S(2)}) collective-permute-start(bf16[688,128]{1,0:T(8,128)(2,1)S(1)} %get-tuple-element.30), channel_id=1, source_target_pairs={{0,24},{8,16},{16,8},{24,0},{1,25},{9,17},{17,9},{25,1},{2,26},{10... | collective-permute-start | bytes 528392 | tf_op jit(solution)/shard_map/ppermute | solution.py:517
  38.4 10.6 %collective-permute-start.14 = (bf16[688,128]{1,0:T(8,128)(2,1)S(1)}, bf16[688,128]{1,0:T(8,128)(2,1)S(1)}, u32[]{:S(2)}, u32[]{:S(2)}) collective-permute-start(bf16[688,128]{1,0:T(8,128)(2,1)S(1)} %get-tuple-element.31), channel_id=1, source_target_pairs={{0,8},{8,0},{16,24},{24,16},{1,9},{9,1},{17,25},{25,17},{2,10},{10... | collective-permute-start | bytes 528392 | tf_op jit(solution)/shard_map/ppermute | solution.py:517
  39.8 1.0 %copy-start = (bf16[64,16,256]{2,1,0:T(8,128)(2,1)S(1)}, bf16[64,16,256]{2,1,0:T(8,128)(2,1)}, u32[]{:S(2)}) copy-start(bf16[64,16,256]{2,1,0:T(8,128)(2,1)} %param.13) | copy-start | bytes 1572868
  40.9 1.0 %copy-start.1 = (s32[64,16,64]{2,1,0:T(8,128)S(1)}, s32[64,16,64]{2,1,0:T(8,128)}, u32[]{:S(2)}) copy-start(s32[64,16,64]{2,1,0:T(8,128)} %param.19) | copy-start | bytes 786436
  41.9 0.8 %copy-start.4 = (bf16[256,64]{0,1:T(8,128)(2,1)S(1)}, bf16[256,64]{0,1:T(8,128)(2,1)}, u32[]{:S(2)}) copy-start(bf16[256,64]{0,1:T(8,128)(2,1)} %param.20) | copy-start | bytes 98308
  43.8 12.1 %collective-permute-start.15 = (bf16[688,128]{1,0:T(8,128)(2,1)S(1)}, bf16[688,128]{1,0:T(8,128)(2,1)S(1)}, u32[]{:S(2)}, u32[]{:S(2)}) collective-permute-start(bf16[688,128]{1,0:T(8,128)(2,1)S(1)} %get-tuple-element.32), channel_id=1, source_target_pairs={{0,16},{8,24},{16,0},{24,8},{1,17},{9,25},{17,1},{25,9},{2,18},{10... | collective-permute-start | bytes 528392 | tf_op jit(solution)/shard_map/ppermute | solution.py:517
  45.4 10.6 %collective-permute-start.16 = (bf16[688,128]{1,0:T(8,128)(2,1)S(1)}, bf16[688,128]{1,0:T(8,128)(2,1)S(1)}, u32[]{:S(2)}, u32[]{:S(2)}) collective-permute-start(bf16[688,128]{1,0:T(8,128)(2,1)S(1)} %get-tuple-element.33), channel_id=1, source_target_pairs={{0,24},{8,16},{16,8},{24,0},{1,25},{9,17},{17,9},{25,1},{2,26},{10... | collective-permute-start | bytes 528392 | tf_op jit(solution)/shard_map/ppermute | solution.py:517
  45.9 10.1 %collective-permute-start.17 = (bf16[688,128]{1,0:T(8,128)(2,1)S(1)}, bf16[688,128]{1,0:T(8,128)(2,1)S(1)}, u32[]{:S(2)}, u32[]{:S(2)}) collective-permute-start(bf16[688,128]{1,0:T(8,128)(2,1)S(1)} %get-tuple-element.34), channel_id=1, source_target_pairs={{0,8},{8,0},{16,24},{24,16},{1,9},{9,1},{17,25},{25,17},{2,10},{10... | collective-permute-start | bytes 528392 | tf_op jit(solution)/shard_map/ppermute | solution.py:517
  47.4 11.9 %collective-permute-start.18 = (bf16[688,128]{1,0:T(8,128)(2,1)S(1)}, bf16[688,128]{1,0:T(8,128)(2,1)S(1)}, u32[]{:S(2)}, u32[]{:S(2)}) collective-permute-start(bf16[688,128]{1,0:T(8,128)(2,1)S(1)} %get-tuple-element.35), channel_id=1, source_target_pairs={{0,16},{8,24},{16,0},{24,8},{1,17},{9,25},{17,1},{25,9},{2,18},{10... | collective-permute-start | bytes 528392 | tf_op jit(solution)/shard_map/ppermute | solution.py:517
  48.9 10.4 %collective-permute-start.19 = (bf16[688,128]{1,0:T(8,128)(2,1)S(1)}, bf16[688,128]{1,0:T(8,128)(2,1)S(1)}, u32[]{:S(2)}, u32[]{:S(2)}) collective-permute-start(bf16[688,128]{1,0:T(8,128)(2,1)S(1)} %get-tuple-element.36), channel_id=1, source_target_pairs={{0,24},{8,16},{16,8},{24,0},{1,25},{9,17},{17,9},{25,1},{2,26},{10... | collective-permute-start | bytes 528392 | tf_op jit(solution)/shard_map/ppermute | solution.py:517
  59.3 8.5 %copy-start.2 = (bf16[256,256]{1,0:T(8,128)(2,1)S(1)}, bf16[256,256]{1,0:T(8,128)(2,1)}, u32[]{:S(2)}) copy-start(bf16[256,256]{1,0:T(8,128)(2,1)} %weight_ref.3) | copy-start | bytes 393220
  59.3 8.5 %copy-start.5 = (f32[256]{0:T(256)S(1)}, f32[256]{0:T(256)}, u32[]{:S(2)}) copy-start(f32[256]{0:T(256)} %param.23) | copy-start | bytes 3076
  59.3 10.0 %copy-start.6 = (f32[128]{0:T(128)S(1)}, f32[128]{0:T(128)}, u32[]{:S(2)}) copy-start(f32[128]{0:T(128)} %param.24) | copy-start | bytes 1540
  59.4 10.0 %copy-start.7 = (f32[128]{0:T(128)S(1)}, f32[128]{0:T(128)}, u32[]{:S(2)}) copy-start(f32[128]{0:T(128)} %param.25) | copy-start | bytes 1540
  67.7 1.6 %collective-permute-start.20 = (bf16[1024,128]{1,0:T(8,128)(2,1)S(1)}, bf16[1024,128]{1,0:T(8,128)(2,1)S(1)}, u32[]{:S(2)}, u32[]{:S(2)}) collective-permute-start(bf16[1024,128]{1,0:T(8,128)(2,1)S(1)} %attend.1.own_ref), channel_id=1, source_target_pairs={{0,1},{1,0},{2,3},{3,2},{4,5},{5,4},{6,7},{7,6},{8,9},{9,8},{10,11... | collective-permute-start | bytes 786440 | tf_op jit(solution)/shard_map/ppermute | solution.py:690

commit v8 on v7

--- a/solution.py
+++ b/solution.py
@@ -187,14 +187,14 @@
     return chosen
 
 
-def relay_select_kernel(dims, order, place_ref, request_ref, asked_ref, *refs):
+def relay_select_kernel(dims, order, table_ref, *refs):
     partners, candidates, capacity, sizes, blocks = dims
-    ids = refs[:partners]
-    sources = refs[partners : partners + candidates]
-    outs = refs[partners + candidates :]
+    sources = refs[:candidates]
+    outs = refs[candidates:]
     columns, numbers = order
-    column = pick(columns, place_ref[1])
-    which = pick(numbers, place_ref[1])
+    my_column = table_ref[0, 1]
+    column = pick(columns, my_column)
+    which = pick(numbers, my_column)
     for number, source in enumerate(sources):
 
         @pl.when(which == number)
@@ -205,7 +205,9 @@
                 for level in range(LEVELS - 1):
                     size = sizes[level]
                     for rank in range(capacity):
-                        index = jnp.maximum(ids[partner][column, level * capacity + rank], 0)
+                        index = jnp.maximum(
+                            table_ref[1 + partner * LINE + column, level * capacity + rank], 0
+                        )
                         outs[partner][base : base + size, :] = source[
                             pl.ds(pl.multiple_of(start + index * size, size), size), :
                         ]
@@ -247,15 +249,17 @@
         pltpu.make_async_copy(source, tile.at[request], sem).start()
 
 
-def gather_relay(dims, relay, request_ref, place_ref, asked_ref, near_refs, packs_refs, tiles, tile3):
-    _, capacity, sizes, _, _, _, _, blocks = dims
+def gather_relay(dims, relay, table_ref, near_refs, packs_refs, tiles, tile3):
+    peers, capacity, sizes, _, _, _, _, blocks = dims
     rows, columns, partner_of = relay
     small = tile3.shape[1]
-    my_row = place_ref[0]
-    my_column = place_ref[1]
+    my_row = table_ref[0, 0]
+    my_column = table_ref[0, 1]
+    requests = 1 + (rows - 1) * columns
+    asked = requests + peers
 
     def put(owner, level, rank, source, start):
-        request = request_ref[owner, level * capacity + rank]
+        request = table_ref[requests + owner, level * capacity + rank]
         size = sizes[level]
         tiles[level][jnp.maximum(request, 0)] = source[pl.ds(start, size), :]
 
@@ -274,7 +278,7 @@
             for level in range(LEVELS - 1):
                 size = sizes[level]
                 for rank in range(capacity):
-                    index = jnp.maximum(asked_ref[owner, level * capacity + rank], 0)
+                    index = jnp.maximum(table_ref[asked + owner, level * capacity + rank], 0)
                     put(owner, level, rank, source, pl.multiple_of(start + index * size, size))
                 start += blocks * size
             tile3[owner] = source[start : start + small, :]
@@ -400,9 +404,10 @@
 
 def norm_kernel(head_ref, pre_ref, other_ref, weight_ref, gain_ref, shift_ref, out_ref):
     own_head = head_ref[0]
-    channels = out_ref.shape[1]
+    pixels, channels = out_ref.shape
+    here = pl.ds(pl.multiple_of(pl.program_id(0) * pixels, pixels), pixels)
     rows = weight_ref[pl.ds(pl.multiple_of((1 - own_head) * channels, channels), channels), :]
-    pre = pre_ref[...] + jnp.dot(other_ref[...], rows, preferred_element_type=jnp.float32)
+    pre = pre_ref[here, :] + jnp.dot(other_ref[here, :], rows, preferred_element_type=jnp.float32)
     centered = pre - jnp.mean(pre, axis=1, keepdims=True)
     variance = jnp.mean(centered * centered, axis=1, keepdims=True)
     own = jnp.where(own_head == 0, centered[:, :channels], centered[:, channels:])
@@ -473,7 +478,6 @@
 
     move("first")
     move("cross")
-    place = jnp.stack([my_row, my_column]).astype(jnp.int32)
     owner, local, rank = tables(lists.reshape(1, blocks, LEVELS, per_block), grid)
     order = jnp.arange(blocks * per_block, dtype=jnp.int32)
     code = entries(owner, rank, jnp.arange(peers, dtype=jnp.int32), capacity, order * blocks + local)[0]
@@ -492,6 +496,10 @@
             lax.ppermute(mine, "row", [(row, partner_of(row, number)) for row in range(row_count)])
         )
 
+    width = asked.shape[1]
+    lane = jnp.arange(width)[None, :]
+    place = jnp.where(lane == 0, my_row, my_column).astype(jnp.int32)
+    table = jnp.concatenate([place, *ids, request, asked], axis=0)
     packs = []
     for slot, (buffers, columns) in enumerate(SLOTS):
         if slot == 1:
@@ -506,12 +514,11 @@
                 relay_select_kernel, (row_count - 1, len(names), capacity, sizes, blocks), (columns, numbers)
             ),
             out_shape=[jax.ShapeDtypeStruct((pack, channels), jnp.bfloat16)] * (row_count - 1),
-            in_specs=[pl.BlockSpec(memory_space=SMEM)] * (row_count + 2)
-            + [pl.BlockSpec(memory_space=VMEM)] * len(names),
+            in_specs=[pl.BlockSpec(memory_space=SMEM)] + [pl.BlockSpec(memory_space=VMEM)] * len(names),
             out_specs=[pl.BlockSpec(memory_space=VMEM)] * (row_count - 1),
             compiler_params=pltpu.CompilerParams(vmem_limit_bytes=SELECT_VMEM),
             cost_estimate=SELECT_COST,
-        )(place, request, asked, *ids, *[held[name] for name in names])
+        )(table, *[held[name] for name in names])
         for number in range(1, row_count):
             packs.append(
                 lax.ppermute(
@@ -520,18 +527,16 @@
             )
 
     near = [held[name] for name in NEAR]
-    sources = (request, place, asked, *near, *packs)
-    spaces = (SMEM, SMEM, SMEM) + (VMEM,) * (len(near) + len(packs))
+    sources = (table, *near, *packs)
+    spaces = (SMEM,) + (VMEM,) * (len(near) + len(packs))
 
     def gather(refs, tiles, tile3, sem):
         gather_relay(
             dims,
             (row_count, col_count, partner_of),
             refs[0],
-            refs[1],
-            refs[2],
-            refs[3 : 3 + len(near)],
-            refs[3 + len(near) :],
+            refs[1 : 1 + len(near)],
+            refs[1 + len(near) :],
             tiles,
             tile3,
         )
@@ -710,14 +715,7 @@
         norm_kernel,
         out_shape=jax.ShapeDtypeStruct((blocks * pixels, channels), jnp.bfloat16),
         grid=(blocks,),
-        in_specs=[
-            pl.BlockSpec(memory_space=SMEM),
-            wide_spec,
-            slim_spec,
-            matrix_spec,
-            pl.BlockSpec((1, channels), lambda i: (0, 0)),
-            pl.BlockSpec((1, channels), lambda i: (0, 0)),
-        ],
+        in_specs=[pl.BlockSpec(memory_space=SMEM)] + [whole] * 5,
         out_specs=slim_spec,
         compiler_params=pltpu.CompilerParams(vmem_limit_bytes=SELECT_VMEM),
         name="norm",

time: 72.7 us -> 73 us (level)
  the two profiles are of different devices: /device:TPU:0 before, /device:TPU:9 now
where the time goes in v8:
time: 73 us; the launch traced here: 72.6 us
  starting transfers between devices  26.5 us (36%)
  Pallas kernels  20.6 us (28%)
  waiting for transfers between devices  19.6 us (27%)
  local copies, waits for them, and re-layouts  3.91 us (5%)
  other arithmetic  1.71 us (2%)
    ppermute x12, starting transfers between devices, relay_tiles(): lax.ppermute(sent[number - 1], 'row', [(row, source_of(row, number)) for...  12.3 us
    ppermute x5, waiting for transfers between devices, move(): held[name] = lax.ppermute(held[source or 'own'], 'col', pairs)  10.9 us
    pallas_call x1, Pallas kernels, on_device(): pl.pallas_call(functools.partial(attend_kernel, dims, grid, gather, len(s...  8.46 us
    ppermute x12, waiting for transfers between devices, relay_tiles(): lax.ppermute(sent[number - 1], 'row', [(row, source_of(row, number)) for...  8.32 us
    ppermute x5, starting transfers between devices, move(): held[name] = lax.ppermute(held[source or 'own'], 'col', pairs)  7.94 us
    pallas_call x1, Pallas kernels, on_device(): pl.pallas_call(functools.partial(prep_kernel, dims), out_shape=[jax.Shape...  4.96 us
    pallas_call x4, Pallas kernels, relay_tiles(): pl.pallas_call(functools.partial(relay_select_kernel, (row_count - 1, len...  3.97 us
    ppermute x1, starting transfers between devices, on_device(): other = lax.ppermute(attn, 'head', [(0, 1), (1, 0)])  3.53 us
  transfers between devices with their start and end apart: 21, of which 7 were waited for; matrix products, arithmetic and copies ran while one was open for 2% of the time, Pallas kernels for 14%

profile of v8, /device:TPU:9, one launch (start us, length us, event | category | flops | bytes accessed | tf_op | source)
XLA Modules:
  0.0 72.6 jit_solution(2011457706881784207)
XLA Ops:
  0.0 1.1 %pad_maximum_fusion.refs_0_.refs_1_ = bf16[1360,128]{1,0:T(8,128)(2,1)S(1)} fusion(bf16[16,128]{1,0:T(8,128)(2,1)} %bitcast.31, bf16[64,128]{1,0:T(8,128)(2,1)} %bitcast.30, bf16[256,128]{1,0:T(8,128)(2,1)} %bitcast.28, bf16[1024,128]{1,0:T(8,128)(2,1)} %bitcast.27), kind=kLoop, calls=%fused_computation | loop fusion | flops 1392640 | bytes 696320 | tf_op jit(solution)/shard_map/concatenate | solution.py:473
  1.1 3.2 %collective-permute-start.4 = (bf16[1360,128]{1,0:T(8,128)(2,1)S(1)}, bf16[1360,128]{1,0:T(8,128)(2,1)S(1)}, u32[]{:S(2)}, u32[]{:S(2)}) collective-permute-start(bf16[1360,128]{1,0:T(8,128)(2,1)S(1)} %pad_maximum_fusion.refs_0_.refs_1_), channel_id=1, source_target_pairs={{2,4},{4,2},{3,5},{5,3},{10,12},{12,10},{11,13},{13,11},{18,20},{2... | collective-permute-start | bytes 1044488 | tf_op jit(solution)/shard_map/ppermute | solution.py:477
  4.3 0.1 collective-permute-start.3
  4.4 0.7 copy.32
  5.1 0.1 reshape.501
  5.2 0.2 convert_reduce_fusion
  5.5 0.2 select_reduce_fusion
  5.7 7.4 %collective-permute-done.3.refs_0_.refs_2_ = bf16[1360,128]{1,0:T(8,128)(2,1)S(1)} collective-permute-done((bf16[1360,128]{1,0:T(8,128)(2,1)S(1)}, bf16[1360,128]{1,0:T(8,128)(2,1)S(1)}, u32[]{:S(2)}, u32[]{:S(2)}) %collective-permute-start.3) | collective-permute-done | bytes 348192 | tf_op jit(solution)/shard_map/ppermute | solution.py:477
  13.1 2.1 %collective-permute-start.6 = (bf16[1360,128]{1,0:T(8,128)(2,1)S(1)}, bf16[1360,128]{1,0:T(8,128)(2,1)S(1)}, u32[]{:S(2)}, u32[]{:S(2)}) collective-permute-start(bf16[1360,128]{1,0:T(8,128)(2,1)S(1)} %collective-permute-done.3.refs_0_.refs_2_), channel_id=1, source_target_pairs={{2,4},{4,2},{3,5},{5,3},{10,12},{12,10},{11,13},{13,11},{18,20},{2... | collective-permute-start | bytes 1044488 | tf_op jit(solution)/shard_map/ppermute | solution.py:477
  15.2 0.1 sub.29
  15.3 0.1 select_reduce_fusion.1
  15.4 2.2 %collective-permute-start.2 = (s32[4,8]{0,1:T(8,128)S(1)}, s32[4,8]{0,1:T(8,128)S(1)}, u32[]{:S(2)}, u32[]{:S(2)}) collective-permute-start(s32[4,8]{0,1:T(8,128)S(1)} %get-tuple-element.43), channel_id=1, source_target_pairs={{0,24},{8,16},{16,8},{24,0},{1,25},{9,17},{17,9},{25,1},{2,26},{10... | collective-permute-start | bytes 392 | tf_op jit(solution)/shard_map/ppermute | solution.py:496
  17.6 0.2 collective-permute-start.1
  17.9 0.3 collective-permute-start
  18.1 0.0 collective-permute-done.4.refs_0_.refs_3_
  18.1 1.3 %collective-permute-start.5 = (bf16[1360,128]{1,0:T(8,128)(2,1)S(1)}, bf16[1360,128]{1,0:T(8,128)(2,1)S(1)}, u32[]{:S(2)}, u32[]{:S(2)}) collective-permute-start(bf16[1360,128]{1,0:T(8,128)(2,1)S(1)} %collective-permute-done.4.refs_0_.refs_3_), channel_id=1, source_target_pairs={{2,0},{4,6},{3,1},{5,7},{10,8},{12,14},{11,9},{13,15},{18,16},{20,... | collective-permute-start | bytes 1044488 | tf_op jit(solution)/shard_map/ppermute | solution.py:477
  19.4 3.4 %collective-permute-done.6.refs_1_.refs_5_ = bf16[1360,128]{1,0:T(8,128)(2,1)S(1)} collective-permute-done((bf16[1360,128]{1,0:T(8,128)(2,1)S(1)}, bf16[1360,128]{1,0:T(8,128)(2,1)S(1)}, u32[]{:S(2)}, u32[]{:S(2)}) %collective-permute-start.6) | collective-permute-done | bytes 348192 | tf_op jit(solution)/shard_map/ppermute | solution.py:477
  22.9 1.3 %collective-permute-start.7 = (bf16[1360,128]{1,0:T(8,128)(2,1)S(1)}, bf16[1360,128]{1,0:T(8,128)(2,1)S(1)}, u32[]{:S(2)}, u32[]{:S(2)}) collective-permute-start(bf16[1360,128]{1,0:T(8,128)(2,1)S(1)} %collective-permute-done.6.refs_1_.refs_5_), channel_id=1, source_target_pairs={{2,0},{4,6},{3,1},{5,7},{10,8},{12,14},{11,9},{13,15},{18,16},{20,... | collective-permute-start | bytes 1044488 | tf_op jit(solution)/shard_map/ppermute | solution.py:477
  24.2 0.0 collective-permute-done.2
  24.2 0.0 collective-permute-done.1
  24.3 0.0 collective-permute-done
  24.3 0.1 concatenate.6
  24.3 0.1 copy.37.table_ref.refs_0_
  24.4 1.0 %shard_map.127 = (bf16[688,128]{1,0:T(8,128)(2,1)S(1)}, bf16[688,128]{1,0:T(8,128)(2,1)S(1)}, bf16[688,128]{1,0:T(8,128)(2,1)S(1)}) custom-call(s32[45,8]{1,0:T(8,128)S(1)} %copy.37.table_ref.refs_0_, bf16[1360,128]{1,0:T(8,128)(2,1)S(1)} %pad_maximum_fusion.refs_0_.refs_1_), custom_call_target="tpu_custom_call" | custom-call | flops 500000000 | bytes 1000000 | tf_op jit(solution)/shard_map/pallas_call | solution.py:512
  25.4 1.3 %collective-permute-start.8 = (bf16[688,128]{1,0:T(8,128)(2,1)S(1)}, bf16[688,128]{1,0:T(8,128)(2,1)S(1)}, u32[]{:S(2)}, u32[]{:S(2)}) collective-permute-start(bf16[688,128]{1,0:T(8,128)(2,1)S(1)} %get-tuple-element.25), channel_id=1, source_target_pairs={{0,8},{8,0},{16,24},{24,16},{1,9},{9,1},{17,25},{25,17},{2,10},{10... | collective-permute-start | bytes 528392 | tf_op jit(solution)/shard_map/ppermute | solution.py:524
  26.7 1.2 %collective-permute-start.9 = (bf16[688,128]{1,0:T(8,128)(2,1)S(1)}, bf16[688,128]{1,0:T(8,128)(2,1)S(1)}, u32[]{:S(2)}, u32[]{:S(2)}) collective-permute-start(bf16[688,128]{1,0:T(8,128)(2,1)S(1)} %get-tuple-element.26), channel_id=1, source_target_pairs={{0,16},{8,24},{16,0},{24,8},{1,17},{9,25},{17,1},{25,9},{2,18},{10... | collective-permute-start | bytes 528392 | tf_op jit(solution)/shard_map/ppermute | solution.py:524
  28.0 0.2 collective-permute-start.10
  28.1 1.0 %shard_map.128 = (bf16[688,128]{1,0:T(8,128)(2,1)S(1)}, bf16[688,128]{1,0:T(8,128)(2,1)S(1)}, bf16[688,128]{1,0:T(8,128)(2,1)S(1)}) custom-call(s32[45,8]{1,0:T(8,128)S(1)} %copy.37.table_ref.refs_0_, bf16[1360,128]{1,0:T(8,128)(2,1)S(1)} %collective-permute-done.3.refs_0_.refs_2_), custom_call_target="tpu_custom_call" | custom-call | flops 500000000 | bytes 1000000 | tf_op jit(solution)/shard_map/pallas_call | solution.py:512
  29.1 0.0 collective-permute-done.5.refs_1_.refs_4_
  29.2 1.3 %collective-permute-start.11 = (bf16[688,128]{1,0:T(8,128)(2,1)S(1)}, bf16[688,128]{1,0:T(8,128)(2,1)S(1)}, u32[]{:S(2)}, u32[]{:S(2)}) collective-permute-start(bf16[688,128]{1,0:T(8,128)(2,1)S(1)} %get-tuple-element.28), channel_id=1, source_target_pairs={{0,8},{8,0},{16,24},{24,16},{1,9},{9,1},{17,25},{25,17},{2,10},{10... | collective-permute-start | bytes 528392 | tf_op jit(solution)/shard_map/ppermute | solution.py:524
  30.4 1.0 %shard_map.129 = (bf16[688,128]{1,0:T(8,128)(2,1)S(1)}, bf16[688,128]{1,0:T(8,128)(2,1)S(1)}, bf16[688,128]{1,0:T(8,128)(2,1)S(1)}) custom-call(s32[45,8]{1,0:T(8,128)S(1)} %copy.37.table_ref.refs_0_, bf16[1360,128]{1,0:T(8,128)(2,1)S(1)} %collective-permute-done.4.refs_0_.refs_3_, bf16[1360,128]{1,0:T(8,128)(2,1)S(1)} %collective-permute-done.5.refs_1_.refs_4_), custom_call_target="tpu_custom_call" | custom-call | flops 500000000 | bytes 1000000 | tf_op jit(solution)/shard_map/pallas_call | solution.py:512
  31.4 0.0 collective-permute-done.8.refs_7_
  31.4 1.3 %collective-permute-start.12 = (bf16[688,128]{1,0:T(8,128)(2,1)S(1)}, bf16[688,128]{1,0:T(8,128)(2,1)S(1)}, u32[]{:S(2)}, u32[]{:S(2)}) collective-permute-start(bf16[688,128]{1,0:T(8,128)(2,1)S(1)} %get-tuple-element.29), channel_id=1, source_target_pairs={{0,16},{8,24},{16,0},{24,8},{1,17},{9,25},{17,1},{25,9},{2,18},{10... | collective-permute-start | bytes 528392 | tf_op jit(solution)/shard_map/ppermute | solution.py:524
  32.8 0.0 collective-permute-done.9.refs_8_
  32.8 1.2 %collective-permute-start.13 = (bf16[688,128]{1,0:T(8,128)(2,1)S(1)}, bf16[688,128]{1,0:T(8,128)(2,1)S(1)}, u32[]{:S(2)}, u32[]{:S(2)}) collective-permute-start(bf16[688,128]{1,0:T(8,128)(2,1)S(1)} %get-tuple-element.30), channel_id=1, source_target_pairs={{0,24},{8,16},{16,8},{24,0},{1,25},{9,17},{17,9},{25,1},{2,26},{10... | collective-permute-start | bytes 528392 | tf_op jit(solution)/shard_map/ppermute | solution.py:524
  34.0 0.0 collective-permute-done.7.refs_0_.refs_6_
  34.0 1.2 %collective-permute-start.14 = (bf16[688,128]{1,0:T(8,128)(2,1)S(1)}, bf16[688,128]{1,0:T(8,128)(2,1)S(1)}, u32[]{:S(2)}, u32[]{:S(2)}) collective-permute-start(bf16[688,128]{1,0:T(8,128)(2,1)S(1)} %get-tuple-element.31), channel_id=1, source_target_pairs={{0,8},{8,0},{16,24},{24,16},{1,9},{9,1},{17,25},{25,17},{2,10},{10... | collective-permute-start | bytes 528392 | tf_op jit(solution)/shard_map/ppermute | solution.py:524
  35.2 1.0 %copy-done = bf16[64,16,256]{2,1,0:T(8,128)(2,1)S(1)} copy-done((bf16[64,16,256]{2,1,0:T(8,128)(2,1)S(1)}, bf16[64,16,256]{2,1,0:T(8,128)(2,1)}, u32[]{:S(2)}) %copy-start) | copy-done | bytes 524312
  36.3 1.0 %copy-done.1 = s32[64,16,64]{2,1,0:T(8,128)S(1)} copy-done((s32[64,16,64]{2,1,0:T(8,128)S(1)}, s32[64,16,64]{2,1,0:T(8,128)}, u32[]{:S(2)}) %copy-start.1) | copy-done | bytes 262168
  37.3 0.8 %copy-done.4 = bf16[256,64]{0,1:T(8,128)(2,1)S(1)} copy-done((bf16[256,64]{0,1:T(8,128)(2,1)S(1)}, bf16[256,64]{0,1:T(8,128)(2,1)}, u32[]{:S(2)}) %copy-start.4) | copy-done | bytes 32792
  38.1 0.1 load.1
  38.2 1.0 %shard_map.130 = (bf16[688,128]{1,0:T(8,128)(2,1)S(1)}, bf16[688,128]{1,0:T(8,128)(2,1)S(1)}, bf16[688,128]{1,0:T(8,128)(2,1)S(1)}) custom-call(s32[45,8]{1,0:T(8,128)S(1)} %copy.37.table_ref.refs_0_, bf16[1360,128]{1,0:T(8,128)(2,1)S(1)} %collective-permute-done.7.refs_0_.refs_6_, bf16[1360,128]{1,0:T(8,128)(2,1)S(1)} %collective-permute-done.6.refs_1_.refs_5_), custom_call_target="tpu_custom_call" | custom-call | flops 500000000 | bytes 1000000 | tf_op jit(solution)/shard_map/pallas_call | solution.py:512
  39.2 0.0 collective-permute-done.10.refs_9_
  39.2 0.3 collective-permute-start.15
  39.5 0.0 collective-permute-done.11.refs_10_
  39.5 1.2 %collective-permute-start.16 = (bf16[688,128]{1,0:T(8,128)(2,1)S(1)}, bf16[688,128]{1,0:T(8,128)(2,1)S(1)}, u32[]{:S(2)}, u32[]{:S(2)}) collective-permute-start(bf16[688,128]{1,0:T(8,128)(2,1)S(1)} %get-tuple-element.33), channel_id=1, source_target_pairs={{0,24},{8,16},{16,8},{24,0},{1,25},{9,17},{17,9},{25,1},{2,26},{10... | collective-permute-start | bytes 528392 | tf_op jit(solution)/shard_map/ppermute | solution.py:524
  40.7 0.0 collective-permute-done.12.refs_11_
  40.7 1.2 %collective-permute-start.17 = (bf16[688,128]{1,0:T(8,128)(2,1)S(1)}, bf16[688,128]{1,0:T(8,128)(2,1)S(1)}, u32[]{:S(2)}, u32[]{:S(2)}) collective-permute-start(bf16[688,128]{1,0:T(8,128)(2,1)S(1)} %get-tuple-element.34), channel_id=1, source_target_pairs={{0,8},{8,0},{16,24},{24,16},{1,9},{9,1},{17,25},{25,17},{2,10},{10... | collective-permute-start | bytes 528392 | tf_op jit(solution)/shard_map/ppermute | solution.py:524
  42.0 0.0 collective-permute-done.13.refs_12_
  42.0 0.7 collective-permute-start.18
  42.7 2.3 %collective-permute-done.14.refs_13_ = bf16[688,128]{1,0:T(8,128)(2,1)S(1)} collective-permute-done((bf16[688,128]{1,0:T(8,128)(2,1)S(1)}, bf16[688,128]{1,0:T(8,128)(2,1)S(1)}, u32[]{:S(2)}, u32[]{:S(2)}) %collective-permute-start.14) | collective-permute-done | bytes 176160 | tf_op jit(solution)/shard_map/ppermute | solution.py:524
  45.0 1.1 %collective-permute-start.19 = (bf16[688,128]{1,0:T(8,128)(2,1)S(1)}, bf16[688,128]{1,0:T(8,128)(2,1)S(1)}, u32[]{:S(2)}, u32[]{:S(2)}) collective-permute-start(bf16[688,128]{1,0:T(8,128)(2,1)S(1)} %get-tuple-element.36), channel_id=1, source_target_pairs={{0,24},{8,16},{16,8},{24,0},{1,25},{9,17},{17,9},{25,1},{2,26},{10... | collective-permute-start | bytes 528392 | tf_op jit(solution)/shard_map/ppermute | solution.py:524
  46.1 5.0 %prep.1 = (bf16[4,4,4,256,256]{4,3,2,1,0:T(8,128)(2,1)S(1)}, bf16[4,4,4,256,256]{4,3,2,1,0:T(8,128)(2,1)S(1)}, bf16[4,4,256,256]{3,2,1,0:T(8,128)(2,1)S(1)}, f32[4,64,256]{2,1,0:T(8,128)S(1)}) custom-call(bf16[1024,256]{1,0:T(8,128)(2,1)S(1)} %get-tuple-element.24.query_ref, bf16[64,256]{1,0:T(8,128)(2,1)S(1)} %get-tuple-element.37.logit_ref, ...), custom_call_target="tpu_custom_call" | custom-call | flops 2000000000 | bytes 4000000 | tf_op jit(solution)/shard_map/prep/pallas_call | solution.py:640
  51.1 0.0 collective-permute-done.15.refs_14_
  51.1 0.0 collective-permute-done.16.refs_15_
  51.1 1.5 %collective-permute-done.17.refs_16_ = bf16[688,128]{1,0:T(8,128)(2,1)S(1)} collective-permute-done((bf16[688,128]{1,0:T(8,128)(2,1)S(1)}, bf16[688,128]{1,0:T(8,128)(2,1)S(1)}, u32[]{:S(2)}, u32[]{:S(2)}) %collective-permute-start.17) | collective-permute-done | bytes 176160 | tf_op jit(solution)/shard_map/ppermute | solution.py:524
  52.6 3.0 %collective-permute-done.18.refs_17_ = bf16[688,128]{1,0:T(8,128)(2,1)S(1)} collective-permute-done((bf16[688,128]{1,0:T(8,128)(2,1)S(1)}, bf16[688,128]{1,0:T(8,128)(2,1)S(1)}, u32[]{:S(2)}, u32[]{:S(2)}) %collective-permute-start.18) | collective-permute-done | bytes 176160 | tf_op jit(solution)/shard_map/ppermute | solution.py:524
  55.6 1.5 %collective-permute-done.19.refs_18_ = bf16[688,128]{1,0:T(8,128)(2,1)S(1)} collective-permute-done((bf16[688,128]{1,0:T(8,128)(2,1)S(1)}, bf16[688,128]{1,0:T(8,128)(2,1)S(1)}, u32[]{:S(2)}, u32[]{:S(2)}) %collective-permute-start.19) | collective-permute-done | bytes 176160 | tf_op jit(solution)/shard_map/ppermute | solution.py:524
  57.1 0.0 copy-start.7
  57.1 8.5 %attend.1.own_ref = bf16[1024,128]{1,0:T(8,128)(2,1)S(1)} custom-call(s32[45,8]{1,0:T(8,128)S(1)} %copy.37.table_ref.refs_0_, bf16[1360,128]{1,0:T(8,128)(2,1)S(1)} %pad_maximum_fusion.refs_0_.refs_1_, bf16[1360,128]{1,0:T(8,128)(2,1)S(1)} %collective-permute-done.3.refs_0_.refs_2_, bf16[1360,128]{1,0:T(8,128)(2,1)S(1)} %collective-permute-done.4.refs_0_.refs_3_, ...), custom_call_target="tpu_custom_call" | custom-call | flops 2000000000 | bytes 4000000 | tf_op jit(solution)/shard_map/attend/pallas_call | solution.py:672
  65.6 3.5 %collective-permute-start.20 = (bf16[1024,128]{1,0:T(8,128)(2,1)S(1)}, bf16[1024,128]{1,0:T(8,128)(2,1)S(1)}, u32[]{:S(2)}, u32[]{:S(2)}) collective-permute-start(bf16[1024,128]{1,0:T(8,128)(2,1)S(1)} %attend.1.own_ref), channel_id=1, source_target_pairs={{0,1},{1,0},{2,3},{3,2},{4,5},{5,4},{6,7},{7,6},{8,9},{9,8},{10,11... | collective-permute-start | bytes 786440 | tf_op jit(solution)/shard_map/ppermute | solution.py:695
  69.1 0.7 %own.1.pre_ref = f32[1024,256]{1,0:T(8,128)S(1)} custom-call(s32[1]{0:T(128)} %bitcast.head_ref, bf16[1024,256]{1,0:T(8,128)(2,1)S(1)} %get-tuple-element.24.query_ref, bf16[1024,128]{1,0:T(8,128)(2,1)S(1)} %attend.1.own_ref, bf16[256,256]{1,0:T(8,128)(2,1)S(1)} %copy-done.2, f32[1,256]{1,0:T(1,128)S(1)} %bitcast.23), custom_call_target="tpu_custom_call" | custom-call | tf_op jit(solution)/shard_map/own/pallas_call | solution.py:699
  69.9 0.4 collective-permute-done.20.other_ref
  70.3 2.3 %norm.1 = bf16[1024,128]{1,0:T(8,128)(2,1)} custom-call(s32[1]{0:T(128)} %bitcast.head_ref, f32[1024,256]{1,0:T(8,128)S(1)} %own.1.pre_ref, bf16[1024,128]{1,0:T(8,128)(2,1)S(1)} %collective-permute-done.20.other_ref, bf16[256,256]{1,0:T(8,128)(2,1)S(1)} %copy-done.2, f32[1,128]{1,0:T(1,128)S(1)} %bitcast.24, f32[1,128]{1,0:T(1,128)S(1)} %bitcast.25), custom_call_target="tpu_custom_call" | custom-call | tf_op jit(solution)/shard_map/norm/pallas_call | solution.py:714
  (24 shorter events, 0.1 us)
Async XLA Ops:
  0.0 46.1 %copy-start.8 = (f32[64]{0:T(128)S(1)}, f32[64]{0:T(128)}, u32[]{:S(2)}) copy-start(f32[64]{0:T(128)} %param.21) | copy-start | bytes 772
  0.0 57.1 %copy-start.3 = (s32[4,1,4,8]{3,2,1,0:T(4,128)S(1)}, s32[4,1,4,8]{3,2,1,0:T(4,128)}, u32[]{:S(2)}) copy-start(s32[4,1,4,8]{3,2,1,0:T(4,128)} %refs_23_.1) | copy-start | bytes 1540
  1.1 17.1 %collective-permute-start.4 = (bf16[1360,128]{1,0:T(8,128)(2,1)S(1)}, bf16[1360,128]{1,0:T(8,128)(2,1)S(1)}, u32[]{:S(2)}, u32[]{:S(2)}) collective-permute-start(bf16[1360,128]{1,0:T(8,128)(2,1)S(1)} %pad_maximum_fusion.refs_0_.refs_1_), channel_id=1, source_target_pairs={{2,4},{4,2},{3,5},{5,3},{10,12},{12,10},{11,13},{13,11},{18,20},{2... | collective-permute-start | bytes 1044488 | tf_op jit(solution)/shard_map/ppermute | solution.py:477
  4.3 8.8 %collective-permute-start.3 = (bf16[1360,128]{1,0:T(8,128)(2,1)S(1)}, bf16[1360,128]{1,0:T(8,128)(2,1)S(1)}, u32[]{:S(2)}, u32[]{:S(2)}) collective-permute-start(bf16[1360,128]{1,0:T(8,128)(2,1)S(1)} %pad_maximum_fusion.refs_0_.refs_1_), channel_id=1, source_target_pairs={{0,2},{2,0},{4,6},{6,4},{1,3},{3,1},{5,7},{7,5},{8,10},{10,8},{12,... | collective-permute-start | bytes 1044488 | tf_op jit(solution)/shard_map/ppermute | solution.py:477
  13.1 9.8 %collective-permute-start.6 = (bf16[1360,128]{1,0:T(8,128)(2,1)S(1)}, bf16[1360,128]{1,0:T(8,128)(2,1)S(1)}, u32[]{:S(2)}, u32[]{:S(2)}) collective-permute-start(bf16[1360,128]{1,0:T(8,128)(2,1)S(1)} %collective-permute-done.3.refs_0_.refs_2_), channel_id=1, source_target_pairs={{2,4},{4,2},{3,5},{5,3},{10,12},{12,10},{11,13},{13,11},{18,20},{2... | collective-permute-start | bytes 1044488 | tf_op jit(solution)/shard_map/ppermute | solution.py:477
  15.4 8.8 %collective-permute-start.2 = (s32[4,8]{0,1:T(8,128)S(1)}, s32[4,8]{0,1:T(8,128)S(1)}, u32[]{:S(2)}, u32[]{:S(2)}) collective-permute-start(s32[4,8]{0,1:T(8,128)S(1)} %get-tuple-element.43), channel_id=1, source_target_pairs={{0,24},{8,16},{16,8},{24,0},{1,25},{9,17},{17,9},{25,1},{2,26},{10... | collective-permute-start | bytes 392 | tf_op jit(solution)/shard_map/ppermute | solution.py:496
  17.6 6.6 %collective-permute-start.1 = (s32[4,8]{0,1:T(8,128)S(1)}, s32[4,8]{0,1:T(8,128)S(1)}, u32[]{:S(2)}, u32[]{:S(2)}) collective-permute-start(s32[4,8]{0,1:T(8,128)S(1)} %get-tuple-element.44), channel_id=1, source_target_pairs={{0,16},{8,24},{16,0},{24,8},{1,17},{9,25},{17,1},{25,9},{2,18},{10... | collective-permute-start | bytes 392 | tf_op jit(solution)/shard_map/ppermute | solution.py:496
  17.9 6.4 %collective-permute-start = (s32[4,8]{0,1:T(8,128)S(1)}, s32[4,8]{0,1:T(8,128)S(1)}, u32[]{:S(2)}, u32[]{:S(2)}) collective-permute-start(s32[4,8]{0,1:T(8,128)S(1)} %get-tuple-element.45), channel_id=1, source_target_pairs={{0,8},{8,0},{16,24},{24,16},{1,9},{9,1},{17,25},{25,17},{2,10},{10... | collective-permute-start | bytes 392 | tf_op jit(solution)/shard_map/ppermute | solution.py:496
  18.1 11.0 %collective-permute-start.5 = (bf16[1360,128]{1,0:T(8,128)(2,1)S(1)}, bf16[1360,128]{1,0:T(8,128)(2,1)S(1)}, u32[]{:S(2)}, u32[]{:S(2)}) collective-permute-start(bf16[1360,128]{1,0:T(8,128)(2,1)S(1)} %collective-permute-done.4.refs_0_.refs_3_), channel_id=1, source_target_pairs={{2,0},{4,6},{3,1},{5,7},{10,8},{12,14},{11,9},{13,15},{18,16},{20,... | collective-permute-start | bytes 1044488 | tf_op jit(solution)/shard_map/ppermute | solution.py:477
  22.9 11.1 %collective-permute-start.7 = (bf16[1360,128]{1,0:T(8,128)(2,1)S(1)}, bf16[1360,128]{1,0:T(8,128)(2,1)S(1)}, u32[]{:S(2)}, u32[]{:S(2)}) collective-permute-start(bf16[1360,128]{1,0:T(8,128)(2,1)S(1)} %collective-permute-done.6.refs_1_.refs_5_), channel_id=1, source_target_pairs={{2,0},{4,6},{3,1},{5,7},{10,8},{12,14},{11,9},{13,15},{18,16},{20,... | collective-permute-start | bytes 1044488 | tf_op jit(solution)/shard_map/ppermute | solution.py:477
  25.4 6.0 %collective-permute-start.8 = (bf16[688,128]{1,0:T(8,128)(2,1)S(1)}, bf16[688,128]{1,0:T(8,128)(2,1)S(1)}, u32[]{:S(2)}, u32[]{:S(2)}) collective-permute-start(bf16[688,128]{1,0:T(8,128)(2,1)S(1)} %get-tuple-element.25), channel_id=1, source_target_pairs={{0,8},{8,0},{16,24},{24,16},{1,9},{9,1},{17,25},{25,17},{2,10},{10... | collective-permute-start | bytes 528392 | tf_op jit(solution)/shard_map/ppermute | solution.py:524
  26.7 6.0 %collective-permute-start.9 = (bf16[688,128]{1,0:T(8,128)(2,1)S(1)}, bf16[688,128]{1,0:T(8,128)(2,1)S(1)}, u32[]{:S(2)}, u32[]{:S(2)}) collective-permute-start(bf16[688,128]{1,0:T(8,128)(2,1)S(1)} %get-tuple-element.26), channel_id=1, source_target_pairs={{0,16},{8,24},{16,0},{24,8},{1,17},{9,25},{17,1},{25,9},{2,18},{10... | collective-permute-start | bytes 528392 | tf_op jit(solution)/shard_map/ppermute | solution.py:524
  28.0 11.3 %collective-permute-start.10 = (bf16[688,128]{1,0:T(8,128)(2,1)S(1)}, bf16[688,128]{1,0:T(8,128)(2,1)S(1)}, u32[]{:S(2)}, u32[]{:S(2)}) collective-permute-start(bf16[688,128]{1,0:T(8,128)(2,1)S(1)} %get-tuple-element.27), channel_id=1, source_target_pairs={{0,24},{8,16},{16,8},{24,0},{1,25},{9,17},{17,9},{25,1},{2,26},{10... | collective-permute-start | bytes 528392 | tf_op jit(solution)/shard_map/ppermute | solution.py:524
  29.2 10.3 %collective-permute-start.11 = (bf16[688,128]{1,0:T(8,128)(2,1)S(1)}, bf16[688,128]{1,0:T(8,128)(2,1)S(1)}, u32[]{:S(2)}, u32[]{:S(2)}) collective-permute-start(bf16[688,128]{1,0:T(8,128)(2,1)S(1)} %get-tuple-element.28), channel_id=1, source_target_pairs={{0,8},{8,0},{16,24},{24,16},{1,9},{9,1},{17,25},{25,17},{2,10},{10... | collective-permute-start | bytes 528392 | tf_op jit(solution)/shard_map/ppermute | solution.py:524
  31.4 9.3 %collective-permute-start.12 = (bf16[688,128]{1,0:T(8,128)(2,1)S(1)}, bf16[688,128]{1,0:T(8,128)(2,1)S(1)}, u32[]{:S(2)}, u32[]{:S(2)}) collective-permute-start(bf16[688,128]{1,0:T(8,128)(2,1)S(1)} %get-tuple-element.29), channel_id=1, source_target_pairs={{0,16},{8,24},{16,0},{24,8},{1,17},{9,25},{17,1},{25,9},{2,18},{10... | collective-permute-start | bytes 528392 | tf_op jit(solution)/shard_map/ppermute | solution.py:524
  32.8 9.2 %collective-permute-start.13 = (bf16[688,128]{1,0:T(8,128)(2,1)S(1)}, bf16[688,128]{1,0:T(8,128)(2,1)S(1)}, u32[]{:S(2)}, u32[]{:S(2)}) collective-permute-start(bf16[688,128]{1,0:T(8,128)(2,1)S(1)} %get-tuple-element.30), channel_id=1, source_target_pairs={{0,24},{8,16},{16,8},{24,0},{1,25},{9,17},{17,9},{25,1},{2,26},{10... | collective-permute-start | bytes 528392 | tf_op jit(solution)/shard_map/ppermute | solution.py:524
  34.0 11.0 %collective-permute-start.14 = (bf16[688,128]{1,0:T(8,128)(2,1)S(1)}, bf16[688,128]{1,0:T(8,128)(2,1)S(1)}, u32[]{:S(2)}, u32[]{:S(2)}) collective-permute-start(bf16[688,128]{1,0:T(8,128)(2,1)S(1)} %get-tuple-element.31), channel_id=1, source_target_pairs={{0,8},{8,0},{16,24},{24,16},{1,9},{9,1},{17,25},{25,17},{2,10},{10... | collective-permute-start | bytes 528392 | tf_op jit(solution)/shard_map/ppermute | solution.py:524
  35.2 1.0 %copy-start = (bf16[64,16,256]{2,1,0:T(8,128)(2,1)S(1)}, bf16[64,16,256]{2,1,0:T(8,128)(2,1)}, u32[]{:S(2)}) copy-start(bf16[64,16,256]{2,1,0:T(8,128)(2,1)} %param.13) | copy-start | bytes 1572868
  36.3 1.0 %copy-start.1 = (s32[64,16,64]{2,1,0:T(8,128)S(1)}, s32[64,16,64]{2,1,0:T(8,128)}, u32[]{:S(2)}) copy-start(s32[64,16,64]{2,1,0:T(8,128)} %param.19) | copy-start | bytes 786436
  37.3 0.8 %copy-start.4 = (bf16[256,64]{0,1:T(8,128)(2,1)S(1)}, bf16[256,64]{0,1:T(8,128)(2,1)}, u32[]{:S(2)}) copy-start(bf16[256,64]{0,1:T(8,128)(2,1)} %param.20) | copy-start | bytes 98308
  39.2 11.9 %collective-permute-start.15 = (bf16[688,128]{1,0:T(8,128)(2,1)S(1)}, bf16[688,128]{1,0:T(8,128)(2,1)S(1)}, u32[]{:S(2)}, u32[]{:S(2)}) collective-permute-start(bf16[688,128]{1,0:T(8,128)(2,1)S(1)} %get-tuple-element.32), channel_id=1, source_target_pairs={{0,16},{8,24},{16,0},{24,8},{1,17},{9,25},{17,1},{25,9},{2,18},{10... | collective-permute-start | bytes 528392 | tf_op jit(solution)/shard_map/ppermute | solution.py:524
  39.5 11.6 %collective-permute-start.16 = (bf16[688,128]{1,0:T(8,128)(2,1)S(1)}, bf16[688,128]{1,0:T(8,128)(2,1)S(1)}, u32[]{:S(2)}, u32[]{:S(2)}) collective-permute-start(bf16[688,128]{1,0:T(8,128)(2,1)S(1)} %get-tuple-element.33), channel_id=1, source_target_pairs={{0,24},{8,16},{16,8},{24,0},{1,25},{9,17},{17,9},{25,1},{2,26},{10... | collective-permute-start | bytes 528392 | tf_op jit(solution)/shard_map/ppermute | solution.py:524
  40.7 11.9 %collective-permute-start.17 = (bf16[688,128]{1,0:T(8,128)(2,1)S(1)}, bf16[688,128]{1,0:T(8,128)(2,1)S(1)}, u32[]{:S(2)}, u32[]{:S(2)}) collective-permute-start(bf16[688,128]{1,0:T(8,128)(2,1)S(1)} %get-tuple-element.34), channel_id=1, source_target_pairs={{0,8},{8,0},{16,24},{24,16},{1,9},{9,1},{17,25},{25,17},{2,10},{10... | collective-permute-start | bytes 528392 | tf_op jit(solution)/shard_map/ppermute | solution.py:524
  42.0 13.6 %collective-permute-start.18 = (bf16[688,128]{1,0:T(8,128)(2,1)S(1)}, bf16[688,128]{1,0:T(8,128)(2,1)S(1)}, u32[]{:S(2)}, u32[]{:S(2)}) collective-permute-start(bf16[688,128]{1,0:T(8,128)(2,1)S(1)} %get-tuple-element.35), channel_id=1, source_target_pairs={{0,16},{8,24},{16,0},{24,8},{1,17},{9,25},{17,1},{25,9},{2,18},{10... | collective-permute-start | bytes 528392 | tf_op jit(solution)/shard_map/ppermute | solution.py:524
  45.0 12.1 %collective-permute-start.19 = (bf16[688,128]{1,0:T(8,128)(2,1)S(1)}, bf16[688,128]{1,0:T(8,128)(2,1)S(1)}, u32[]{:S(2)}, u32[]{:S(2)}) collective-permute-start(bf16[688,128]{1,0:T(8,128)(2,1)S(1)} %get-tuple-element.36), channel_id=1, source_target_pairs={{0,24},{8,16},{16,8},{24,0},{1,25},{9,17},{17,9},{25,1},{2,26},{10... | collective-permute-start | bytes 528392 | tf_op jit(solution)/shard_map/ppermute | solution.py:524
  57.1 12.0 %copy-start.2 = (bf16[256,256]{1,0:T(8,128)(2,1)S(1)}, bf16[256,256]{1,0:T(8,128)(2,1)}, u32[]{:S(2)}) copy-start(bf16[256,256]{1,0:T(8,128)(2,1)} %weight_ref.3) | copy-start | bytes 393220
  57.1 12.0 %copy-start.5 = (f32[256]{0:T(256)S(1)}, f32[256]{0:T(256)}, u32[]{:S(2)}) copy-start(f32[256]{0:T(256)} %param.23) | copy-start | bytes 3076
  57.1 13.2 %copy-start.6 = (f32[128]{0:T(128)S(1)}, f32[128]{0:T(128)}, u32[]{:S(2)}) copy-start(f32[128]{0:T(128)} %param.24) | copy-start | bytes 1540
  57.1 13.2 %copy-start.7 = (f32[128]{0:T(128)S(1)}, f32[128]{0:T(128)}, u32[]{:S(2)}) copy-start(f32[128]{0:T(128)} %param.25) | copy-start | bytes 1540
  65.6 4.7 %collective-permute-start.20 = (bf16[1024,128]{1,0:T(8,128)(2,1)S(1)}, bf16[1024,128]{1,0:T(8,128)(2,1)S(1)}, u32[]{:S(2)}, u32[]{:S(2)}) collective-permute-start(bf16[1024,128]{1,0:T(8,128)(2,1)S(1)} %attend.1.own_ref), channel_id=1, source_target_pairs={{0,1},{1,0},{2,3},{3,2},{4,5},{5,4},{6,7},{7,6},{8,9},{9,8},{10,11... | collective-permute-start | bytes 786440 | tf_op jit(solution)/shard_map/ppermute | solution.py:695

commit v9 on v8

--- a/solution.py
+++ b/solution.py
@@ -14,7 +14,7 @@
 SELECT_VMEM = 4 * 1024 * 1024
 PREP_VMEM = 8 * 1024 * 1024
 ATTEND_VMEM = 12 * 1024 * 1024
-GROUPS = (2, 4)
+GROUPS = (2, 2)
 
 
 def to_blocks(source, tile_rows, tile_cols, tile_side):
@@ -93,14 +93,16 @@
             for point in range(POINTS):
                 hot_ref[point, :rows, :] = hot_of(head, level, point, rows)
                 across = hat(
-                    col_ref[line_of(head, level, point), :], iota((side, pixels), 0).astype(jnp.float32)
+                    col_ref[line_of(head, level, point), :], (iota((16, pixels), 0) % side).astype(jnp.float32)
                 )
                 for index in range(0, rows, step):
-                    stack = [hot_ref[point, row : row + 1, :] * across for row in range(index, index + step)]
+                    stack = [
+                        jnp.broadcast_to(hot_ref[point, row : row + 1, :], (side, pixels))
+                        for row in range(index, index + step)
+                    ]
                     piece = stack[0] if step == 1 else jnp.concatenate(stack, axis=0)
-                    weight[0, head, point, index * side : (index + step) * side, :] = piece.astype(
-                        jnp.bfloat16
-                    )
+                    piece = (piece * across).astype(jnp.bfloat16)
+                    weight[0, head, point, index * side : (index + step) * side, :] = piece
         for level in (2, 3):
             side = sides[level]
             size = sizes[level]
@@ -330,10 +332,13 @@
     for request in range(blocks * per_block):
         block, entry = divmod(request, per_block)
         tile = lists_ref[block // tile_cols, block % tile_cols, LEVELS - 1, entry]
-        tile_row = tile // grid_cols
-        tile_col = tile % grid_cols
-        owner = tile_row // tile_rows * col_count + tile_col // tile_cols
-        first = owner * small + (tile_row % tile_rows * tile_cols + tile_col % tile_cols) * size3
+        tile_row = lax.div(tile, grid_cols)
+        tile_col = tile - tile_row * grid_cols
+        high = lax.div(tile_row, tile_rows)
+        wide_col = lax.div(tile_col, tile_cols)
+        owner = high * col_count + wide_col
+        place = (tile_row - high * tile_rows) * tile_cols + tile_col - wide_col * tile_cols
+        first = owner * small + place * size3
         target = target + jnp.where(lane // size3 == request, first, 0)
     chosen = (iota((peers * small, wide), 0) == target).astype(jnp.bfloat16)
     picked = lax.dot_general(flat, chosen, (((0,), (0,)), ((), ())), preferred_element_type=jnp.float32)
@@ -416,9 +421,9 @@
 
 def tables(lists, grid):
     tile_rows, tile_cols, grid_cols, col_count, _ = grid
-    count, blocks, level_count, per_block = lists.shape
+    _, blocks, _, per_block = lists.shape
     requests = blocks * per_block
-    wanted = lists.transpose(0, 2, 1, 3).reshape(count, level_count, requests)
+    wanted = jnp.concatenate([lists[:, block] for block in range(blocks)], axis=2)
     grid_row = wanted // grid_cols
     grid_col = wanted % grid_cols
     owner = grid_row // tile_rows * col_count + grid_col // tile_cols

time: 73 us -> 72.8 us (level)
  waiting for transfers between devices: 19.6 us -> 22.3 us
  local copies, waits for them, and re-layouts: 3.91 us -> 2.74 us
  starting transfers between devices: 26.5 us -> 25.5 us
    ppermute x12, waiting for transfers between devices: 8.32 us -> 11.1 us  [relay_tiles(): lax.ppermute(sent[number - 1], 'row', [(row, source_of(row, number)) for...]
    unnamed x18 -> x24, local copies, waits for them, and re-layouts: 2.86 us -> 1.75 us
    ppermute x12, starting transfers between devices: 12.3 us -> 11.3 us  [relay_tiles(): lax.ppermute(sent[number - 1], 'row', [(row, source_of(row, number)) for...]
    concatenate x0 -> x1, local copies, waits for them, and re-layouts: none -> 0.74 us  [tables(): jnp.concatenate([lists[:, block] for block in range(blocks)], axis=2)]
  transfers between devices with their start and end apart: 21 -> 21, of which waited for: 7 -> 9; matrix products, arithmetic and copies ran while one was open for 2% -> 2% of each run, Pallas kernels for 14% -> 13%
where the time goes in v9:
time: 72.8 us; the launch traced here: 72.6 us
  starting transfers between devices  25.5 us (35%)
  waiting for transfers between devices  22.3 us (31%)
  Pallas kernels  19.9 us (27%)
  local copies, waits for them, and re-layouts  2.74 us (4%)
  other arithmetic  1.86 us (3%)
    ppermute x12, starting transfers between devices, relay_tiles(): lax.ppermute(sent[number - 1], 'row', [(row, source_of(row, number)) for...  11.3 us
    ppermute x12, waiting for transfers between devices, relay_tiles(): lax.ppermute(sent[number - 1], 'row', [(row, source_of(row, number)) for...  11.1 us
    ppermute x5, waiting for transfers between devices, move(): held[name] = lax.ppermute(held[source or 'own'], 'col', pairs)  10.8 us
    pallas_call x1, Pallas kernels, on_device(): pl.pallas_call(functools.partial(attend_kernel, dims, grid, gather, len(s...  8.37 us
    ppermute x5, starting transfers between devices, move(): held[name] = lax.ppermute(held[source or 'own'], 'col', pairs)  7.94 us
    pallas_call x1, Pallas kernels, on_device(): pl.pallas_call(functools.partial(prep_kernel, dims), out_shape=[jax.Shape...  4.35 us
    pallas_call x4, Pallas kernels, relay_tiles(): pl.pallas_call(functools.partial(relay_select_kernel, (row_count - 1, len...  3.97 us
    ppermute x1, starting transfers between devices, on_device(): other = lax.ppermute(attn, 'head', [(0, 1), (1, 0)])  3.53 us
  transfers between devices with their start and end apart: 21, of which 9 were waited for; matrix products, arithmetic and copies ran while one was open for 2% of the time, Pallas kernels for 13%

profile of v9, /device:TPU:9, one launch (start us, length us, event | category | flops | bytes accessed | tf_op | source)
XLA Modules:
  0.0 72.6 jit_solution(17162876721267988926)
XLA Ops:
  0.0 1.1 %pad_maximum_fusion.refs_0_.refs_1_ = bf16[1360,128]{1,0:T(8,128)(2,1)S(1)} fusion(bf16[16,128]{1,0:T(8,128)(2,1)} %bitcast.37, bf16[64,128]{1,0:T(8,128)(2,1)} %bitcast.36, bf16[256,128]{1,0:T(8,128)(2,1)} %bitcast.34, bf16[1024,128]{1,0:T(8,128)(2,1)} %bitcast.33), kind=kLoop, calls=%fused_computation | loop fusion | flops 1392640 | bytes 696320 | tf_op jit(solution)/shard_map/concatenate | solution.py:478
  1.1 3.2 %collective-permute-start.4 = (bf16[1360,128]{1,0:T(8,128)(2,1)S(1)}, bf16[1360,128]{1,0:T(8,128)(2,1)S(1)}, u32[]{:S(2)}, u32[]{:S(2)}) collective-permute-start(bf16[1360,128]{1,0:T(8,128)(2,1)S(1)} %pad_maximum_fusion.refs_0_.refs_1_), channel_id=1, source_target_pairs={{2,4},{4,2},{3,5},{5,3},{10,12},{12,10},{11,13},{13,11},{18,20},{2... | collective-permute-start | bytes 1044488 | tf_op jit(solution)/shard_map/ppermute | solution.py:482
  4.4 0.1 collective-permute-start.3
  4.5 0.7 %slice_bitcast_fusion.3 = (s32[4,8]{1,0:T(4,128)S(1)}, s32[4,8]{1,0:T(4,128)S(1)}, s32[4,8]{1,0:T(4,128)S(1)}, s32[4,8]{1,0:T(4,128)S(1)}) fusion(s32[1,4,4,8]{3,2,1,0:T(4,128)} %bitcast.27), kind=kLoop, calls=%fused_computation.43 | loop fusion | bytes 1024 | tf_op jit(solution)/shard_map/concatenate | solution.py:426
  5.2 0.1 fusion.8
  5.3 0.2 convert_reduce_fusion
  5.6 0.2 select_reduce_fusion
  5.8 7.4 %collective-permute-done.3.refs_0_.refs_2_ = bf16[1360,128]{1,0:T(8,128)(2,1)S(1)} collective-permute-done((bf16[1360,128]{1,0:T(8,128)(2,1)S(1)}, bf16[1360,128]{1,0:T(8,128)(2,1)S(1)}, u32[]{:S(2)}, u32[]{:S(2)}) %collective-permute-start.3) | collective-permute-done | bytes 348192 | tf_op jit(solution)/shard_map/ppermute | solution.py:482
  13.2 2.1 %collective-permute-start.6 = (bf16[1360,128]{1,0:T(8,128)(2,1)S(1)}, bf16[1360,128]{1,0:T(8,128)(2,1)S(1)}, u32[]{:S(2)}, u32[]{:S(2)}) collective-permute-start(bf16[1360,128]{1,0:T(8,128)(2,1)S(1)} %collective-permute-done.3.refs_0_.refs_2_), channel_id=1, source_target_pairs={{2,4},{4,2},{3,5},{5,3},{10,12},{12,10},{11,13},{13,11},{18,20},{2... | collective-permute-start | bytes 1044488 | tf_op jit(solution)/shard_map/ppermute | solution.py:482
  15.3 0.1 sub.29
  15.4 0.1 select_reduce_fusion.1
  15.5 2.2 %collective-permute-start.2 = (s32[4,8]{0,1:T(8,128)S(1)}, s32[4,8]{0,1:T(8,128)S(1)}, u32[]{:S(2)}, u32[]{:S(2)}) collective-permute-start(s32[4,8]{0,1:T(8,128)S(1)} %get-tuple-element.43), channel_id=1, source_target_pairs={{0,24},{8,16},{16,8},{24,0},{1,25},{9,17},{17,9},{25,1},{2,26},{10... | collective-permute-start | bytes 392 | tf_op jit(solution)/shard_map/ppermute | solution.py:501
  17.7 0.2 collective-permute-start.1
  17.9 0.3 collective-permute-start
  18.2 0.0 collective-permute-done.4.refs_0_.refs_3_
  18.2 1.3 %collective-permute-start.5 = (bf16[1360,128]{1,0:T(8,128)(2,1)S(1)}, bf16[1360,128]{1,0:T(8,128)(2,1)S(1)}, u32[]{:S(2)}, u32[]{:S(2)}) collective-permute-start(bf16[1360,128]{1,0:T(8,128)(2,1)S(1)} %collective-permute-done.4.refs_0_.refs_3_), channel_id=1, source_target_pairs={{2,0},{4,6},{3,1},{5,7},{10,8},{12,14},{11,9},{13,15},{18,16},{20,... | collective-permute-start | bytes 1044488 | tf_op jit(solution)/shard_map/ppermute | solution.py:482
  19.5 3.4 %collective-permute-done.6.refs_1_.refs_5_ = bf16[1360,128]{1,0:T(8,128)(2,1)S(1)} collective-permute-done((bf16[1360,128]{1,0:T(8,128)(2,1)S(1)}, bf16[1360,128]{1,0:T(8,128)(2,1)S(1)}, u32[]{:S(2)}, u32[]{:S(2)}) %collective-permute-start.6) | collective-permute-done | bytes 348192 | tf_op jit(solution)/shard_map/ppermute | solution.py:482
  23.0 1.3 %collective-permute-start.7 = (bf16[1360,128]{1,0:T(8,128)(2,1)S(1)}, bf16[1360,128]{1,0:T(8,128)(2,1)S(1)}, u32[]{:S(2)}, u32[]{:S(2)}) collective-permute-start(bf16[1360,128]{1,0:T(8,128)(2,1)S(1)} %collective-permute-done.6.refs_1_.refs_5_), channel_id=1, source_target_pairs={{2,0},{4,6},{3,1},{5,7},{10,8},{12,14},{11,9},{13,15},{18,16},{20,... | collective-permute-start | bytes 1044488 | tf_op jit(solution)/shard_map/ppermute | solution.py:482
  24.3 0.0 collective-permute-done.2
  24.3 0.0 collective-permute-done.1
  24.3 0.0 collective-permute-done
  24.3 0.1 concatenate.157
  24.4 0.1 copy.33.table_ref.refs_0_
  24.5 1.0 %shard_map.127 = (bf16[688,128]{1,0:T(8,128)(2,1)S(1)}, bf16[688,128]{1,0:T(8,128)(2,1)S(1)}, bf16[688,128]{1,0:T(8,128)(2,1)S(1)}) custom-call(s32[45,8]{1,0:T(8,128)S(1)} %copy.33.table_ref.refs_0_, bf16[1360,128]{1,0:T(8,128)(2,1)S(1)} %pad_maximum_fusion.refs_0_.refs_1_), custom_call_target="tpu_custom_call" | custom-call | flops 500000000 | bytes 1000000 | tf_op jit(solution)/shard_map/pallas_call | solution.py:517
  25.5 1.3 %collective-permute-start.8 = (bf16[688,128]{1,0:T(8,128)(2,1)S(1)}, bf16[688,128]{1,0:T(8,128)(2,1)S(1)}, u32[]{:S(2)}, u32[]{:S(2)}) collective-permute-start(bf16[688,128]{1,0:T(8,128)(2,1)S(1)} %get-tuple-element.25), channel_id=1, source_target_pairs={{0,8},{8,0},{16,24},{24,16},{1,9},{9,1},{17,25},{25,17},{2,10},{10... | collective-permute-start | bytes 528392 | tf_op jit(solution)/shard_map/ppermute | solution.py:529
  26.8 1.2 %collective-permute-start.9 = (bf16[688,128]{1,0:T(8,128)(2,1)S(1)}, bf16[688,128]{1,0:T(8,128)(2,1)S(1)}, u32[]{:S(2)}, u32[]{:S(2)}) collective-permute-start(bf16[688,128]{1,0:T(8,128)(2,1)S(1)} %get-tuple-element.26), channel_id=1, source_target_pairs={{0,16},{8,24},{16,0},{24,8},{1,17},{9,25},{17,1},{25,9},{2,18},{10... | collective-permute-start | bytes 528392 | tf_op jit(solution)/shard_map/ppermute | solution.py:529
  28.0 0.2 collective-permute-start.10
  28.2 1.0 %shard_map.128 = (bf16[688,128]{1,0:T(8,128)(2,1)S(1)}, bf16[688,128]{1,0:T(8,128)(2,1)S(1)}, bf16[688,128]{1,0:T(8,128)(2,1)S(1)}) custom-call(s32[45,8]{1,0:T(8,128)S(1)} %copy.33.table_ref.refs_0_, bf16[1360,128]{1,0:T(8,128)(2,1)S(1)} %collective-permute-done.3.refs_0_.refs_2_), custom_call_target="tpu_custom_call" | custom-call | flops 500000000 | bytes 1000000 | tf_op jit(solution)/shard_map/pallas_call | solution.py:517
  29.2 0.0 collective-permute-done.5.refs_1_.refs_4_
  29.2 1.3 %collective-permute-start.11 = (bf16[688,128]{1,0:T(8,128)(2,1)S(1)}, bf16[688,128]{1,0:T(8,128)(2,1)S(1)}, u32[]{:S(2)}, u32[]{:S(2)}) collective-permute-start(bf16[688,128]{1,0:T(8,128)(2,1)S(1)} %get-tuple-element.28), channel_id=1, source_target_pairs={{0,8},{8,0},{16,24},{24,16},{1,9},{9,1},{17,25},{25,17},{2,10},{10... | collective-permute-start | bytes 528392 | tf_op jit(solution)/shard_map/ppermute | solution.py:529
  30.5 1.0 %shard_map.129 = (bf16[688,128]{1,0:T(8,128)(2,1)S(1)}, bf16[688,128]{1,0:T(8,128)(2,1)S(1)}, bf16[688,128]{1,0:T(8,128)(2,1)S(1)}) custom-call(s32[45,8]{1,0:T(8,128)S(1)} %copy.33.table_ref.refs_0_, bf16[1360,128]{1,0:T(8,128)(2,1)S(1)} %collective-permute-done.4.refs_0_.refs_3_, bf16[1360,128]{1,0:T(8,128)(2,1)S(1)} %collective-permute-done.5.refs_1_.refs_4_), custom_call_target="tpu_custom_call" | custom-call | flops 500000000 | bytes 1000000 | tf_op jit(solution)/shard_map/pallas_call | solution.py:517
  31.5 0.0 collective-permute-done.8.refs_7_
  31.5 1.3 %collective-permute-start.12 = (bf16[688,128]{1,0:T(8,128)(2,1)S(1)}, bf16[688,128]{1,0:T(8,128)(2,1)S(1)}, u32[]{:S(2)}, u32[]{:S(2)}) collective-permute-start(bf16[688,128]{1,0:T(8,128)(2,1)S(1)} %get-tuple-element.29), channel_id=1, source_target_pairs={{0,16},{8,24},{16,0},{24,8},{1,17},{9,25},{17,1},{25,9},{2,18},{10... | collective-permute-start | bytes 528392 | tf_op jit(solution)/shard_map/ppermute | solution.py:529
  32.8 0.0 collective-permute-done.9.refs_8_
  32.8 1.2 %collective-permute-start.13 = (bf16[688,128]{1,0:T(8,128)(2,1)S(1)}, bf16[688,128]{1,0:T(8,128)(2,1)S(1)}, u32[]{:S(2)}, u32[]{:S(2)}) collective-permute-start(bf16[688,128]{1,0:T(8,128)(2,1)S(1)} %get-tuple-element.30), channel_id=1, source_target_pairs={{0,24},{8,16},{16,8},{24,0},{1,25},{9,17},{17,9},{25,1},{2,26},{10... | collective-permute-start | bytes 528392 | tf_op jit(solution)/shard_map/ppermute | solution.py:529
  34.0 0.0 collective-permute-done.7.refs_0_.refs_6_
  34.0 0.7 %copy-done.3 = bf16[1360,128]{1,0:T(8,128)(2,1)} copy-done((bf16[1360,128]{1,0:T(8,128)(2,1)}, bf16[1360,128]{1,0:T(8,128)(2,1)S(1)}, u32[]{:S(2)}) %copy-start.3) | copy-done | bytes 348184
  34.8 1.2 %collective-permute-start.14 = (bf16[688,128]{1,0:T(8,128)(2,1)S(1)}, bf16[688,128]{1,0:T(8,128)(2,1)S(1)}, u32[]{:S(2)}, u32[]{:S(2)}) collective-permute-start(bf16[688,128]{1,0:T(8,128)(2,1)S(1)} %get-tuple-element.31), channel_id=1, source_target_pairs={{0,8},{8,0},{16,24},{24,16},{1,9},{9,1},{17,25},{25,17},{2,10},{10... | collective-permute-start | bytes 528392 | tf_op jit(solution)/shard_map/ppermute | solution.py:529
  36.0 0.1 load.1
  36.2 1.0 %copy-done.4 = bf16[1360,128]{1,0:T(8,128)(2,1)S(1)} copy-done((bf16[1360,128]{1,0:T(8,128)(2,1)S(1)}, bf16[1360,128]{1,0:T(8,128)(2,1)}, u32[]{:S(2)}) %copy-start.4) | copy-done | bytes 348184
  37.2 1.0 %shard_map.130 = (bf16[688,128]{1,0:T(8,128)(2,1)S(1)}, bf16[688,128]{1,0:T(8,128)(2,1)S(1)}, bf16[688,128]{1,0:T(8,128)(2,1)S(1)}) custom-call(s32[45,8]{1,0:T(8,128)S(1)} %copy.33.table_ref.refs_0_, bf16[1360,128]{1,0:T(8,128)(2,1)S(1)} %copy-done.4, bf16[1360,128]{1,0:T(8,128)(2,1)S(1)} %collective-permute-done.6.refs_1_.refs_5_), custom_call_target="tpu_custom_call" | custom-call | flops 500000000 | bytes 1000000 | tf_op jit(solution)/shard_map/pallas_call | solution.py:517
  38.2 0.0 collective-permute-done.10.refs_9_
  38.2 0.3 collective-permute-start.15
  38.4 0.0 collective-permute-done.11.refs_10_
  38.4 1.2 %collective-permute-start.16 = (bf16[688,128]{1,0:T(8,128)(2,1)S(1)}, bf16[688,128]{1,0:T(8,128)(2,1)S(1)}, u32[]{:S(2)}, u32[]{:S(2)}) collective-permute-start(bf16[688,128]{1,0:T(8,128)(2,1)S(1)} %get-tuple-element.33), channel_id=1, source_target_pairs={{0,24},{8,16},{16,8},{24,0},{1,25},{9,17},{17,9},{25,1},{2,26},{10... | collective-permute-start | bytes 528392 | tf_op jit(solution)/shard_map/ppermute | solution.py:529
  39.7 1.1 %collective-permute-done.12.refs_11_ = bf16[688,128]{1,0:T(8,128)(2,1)S(1)} collective-permute-done((bf16[688,128]{1,0:T(8,128)(2,1)S(1)}, bf16[688,128]{1,0:T(8,128)(2,1)S(1)}, u32[]{:S(2)}, u32[]{:S(2)}) %collective-permute-start.12) | collective-permute-done | bytes 176160 | tf_op jit(solution)/shard_map/ppermute | solution.py:529
  40.7 0.2 collective-permute-start.17
  40.9 1.1 %collective-permute-done.13.refs_12_ = bf16[688,128]{1,0:T(8,128)(2,1)S(1)} collective-permute-done((bf16[688,128]{1,0:T(8,128)(2,1)S(1)}, bf16[688,128]{1,0:T(8,128)(2,1)S(1)}, u32[]{:S(2)}, u32[]{:S(2)}) %collective-permute-start.13) | collective-permute-done | bytes 176160 | tf_op jit(solution)/shard_map/ppermute | solution.py:529
  42.0 0.8 %collective-permute-start.18 = (bf16[688,128]{1,0:T(8,128)(2,1)S(1)}, bf16[688,128]{1,0:T(8,128)(2,1)S(1)}, u32[]{:S(2)}, u32[]{:S(2)}) collective-permute-start(bf16[688,128]{1,0:T(8,128)(2,1)S(1)} %get-tuple-element.35), channel_id=1, source_target_pairs={{0,16},{8,24},{16,0},{24,8},{1,17},{9,25},{17,1},{25,9},{2,18},{10... | collective-permute-start | bytes 528392 | tf_op jit(solution)/shard_map/ppermute | solution.py:529
  42.7 2.3 %collective-permute-done.14.refs_13_ = bf16[688,128]{1,0:T(8,128)(2,1)S(1)} collective-permute-done((bf16[688,128]{1,0:T(8,128)(2,1)S(1)}, bf16[688,128]{1,0:T(8,128)(2,1)S(1)}, u32[]{:S(2)}, u32[]{:S(2)}) %collective-permute-start.14) | collective-permute-done | bytes 176160 | tf_op jit(solution)/shard_map/ppermute | solution.py:529
  45.1 1.1 %collective-permute-start.19 = (bf16[688,128]{1,0:T(8,128)(2,1)S(1)}, bf16[688,128]{1,0:T(8,128)(2,1)S(1)}, u32[]{:S(2)}, u32[]{:S(2)}) collective-permute-start(bf16[688,128]{1,0:T(8,128)(2,1)S(1)} %get-tuple-element.36), channel_id=1, source_target_pairs={{0,24},{8,16},{16,8},{24,0},{1,25},{9,17},{17,9},{25,1},{2,26},{10... | collective-permute-start | bytes 528392 | tf_op jit(solution)/shard_map/ppermute | solution.py:529
  46.2 4.4 %prep.1 = (bf16[4,4,4,256,256]{4,3,2,1,0:T(8,128)(2,1)S(1)}, bf16[4,4,4,128,256]{4,3,2,1,0:T(8,128)(2,1)S(1)}, bf16[4,4,256,256]{3,2,1,0:T(8,128)(2,1)S(1)}, f32[4,64,256]{2,1,0:T(8,128)S(1)}) custom-call(bf16[1024,256]{1,0:T(8,128)(2,1)S(1)} %get-tuple-element.24.query_ref, bf16[64,256]{1,0:T(8,128)(2,1)S(1)} %get-tuple-element.37.logit_ref, ...), custom_call_target="tpu_custom_call" | custom-call | flops 2000000000 | bytes 4000000 | tf_op jit(solution)/shard_map/prep/pallas_call | solution.py:645
  50.6 0.0 collective-permute-done.15.refs_14_
  50.6 0.0 collective-permute-done.16.refs_15_
  50.6 2.1 %collective-permute-done.17.refs_16_ = bf16[688,128]{1,0:T(8,128)(2,1)S(1)} collective-permute-done((bf16[688,128]{1,0:T(8,128)(2,1)S(1)}, bf16[688,128]{1,0:T(8,128)(2,1)S(1)}, u32[]{:S(2)}, u32[]{:S(2)}) %collective-permute-start.17) | collective-permute-done | bytes 176160 | tf_op jit(solution)/shard_map/ppermute | solution.py:529
  52.7 3.0 %collective-permute-done.18.refs_17_ = bf16[688,128]{1,0:T(8,128)(2,1)S(1)} collective-permute-done((bf16[688,128]{1,0:T(8,128)(2,1)S(1)}, bf16[688,128]{1,0:T(8,128)(2,1)S(1)}, u32[]{:S(2)}, u32[]{:S(2)}) %collective-permute-start.18) | collective-permute-done | bytes 176160 | tf_op jit(solution)/shard_map/ppermute | solution.py:529
  55.6 1.5 %collective-permute-done.19.refs_18_ = bf16[688,128]{1,0:T(8,128)(2,1)S(1)} collective-permute-done((bf16[688,128]{1,0:T(8,128)(2,1)S(1)}, bf16[688,128]{1,0:T(8,128)(2,1)S(1)}, u32[]{:S(2)}, u32[]{:S(2)}) %collective-permute-start.19) | collective-permute-done | bytes 176160 | tf_op jit(solution)/shard_map/ppermute | solution.py:529
  57.2 0.0 copy-start.9
  57.2 0.0 copy-start.10
  57.2 8.4 %attend.1.own_ref = bf16[1024,128]{1,0:T(8,128)(2,1)S(1)} custom-call(s32[45,8]{1,0:T(8,128)S(1)} %copy.33.table_ref.refs_0_, bf16[1360,128]{1,0:T(8,128)(2,1)S(1)} %pad_maximum_fusion.refs_0_.refs_1_, bf16[1360,128]{1,0:T(8,128)(2,1)S(1)} %collective-permute-done.3.refs_0_.refs_2_, bf16[1360,128]{1,0:T(8,128)(2,1)S(1)} %collective-permute-done.4.refs_0_.refs_3_, ...), custom_call_target="tpu_custom_call" | custom-call | flops 2000000000 | bytes 4000000 | tf_op jit(solution)/shard_map/attend/pallas_call | solution.py:677
  65.6 3.5 %collective-permute-start.20 = (bf16[1024,128]{1,0:T(8,128)(2,1)S(1)}, bf16[1024,128]{1,0:T(8,128)(2,1)S(1)}, u32[]{:S(2)}, u32[]{:S(2)}) collective-permute-start(bf16[1024,128]{1,0:T(8,128)(2,1)S(1)} %attend.1.own_ref), channel_id=1, source_target_pairs={{0,1},{1,0},{2,3},{3,2},{4,5},{5,4},{6,7},{7,6},{8,9},{9,8},{10,11... | collective-permute-start | bytes 786440 | tf_op jit(solution)/shard_map/ppermute | solution.py:700
  69.1 0.7 %own.1.pre_ref = f32[1024,256]{1,0:T(8,128)S(1)} custom-call(s32[1]{0:T(128)} %bitcast.head_ref, bf16[1024,256]{1,0:T(8,128)(2,1)S(1)} %get-tuple-element.24.query_ref, bf16[1024,128]{1,0:T(8,128)(2,1)S(1)} %attend.1.own_ref, bf16[256,256]{1,0:T(8,128)(2,1)S(1)} %copy-done.2, f32[1,256]{1,0:T(1,128)S(1)} %bitcast.29), custom_call_target="tpu_custom_call" | custom-call | tf_op jit(solution)/shard_map/own/pallas_call | solution.py:704
  69.8 0.4 collective-permute-done.20.other_ref
  70.3 2.3 %norm.1 = bf16[1024,128]{1,0:T(8,128)(2,1)} custom-call(s32[1]{0:T(128)} %bitcast.head_ref, f32[1024,256]{1,0:T(8,128)S(1)} %own.1.pre_ref, bf16[1024,128]{1,0:T(8,128)(2,1)S(1)} %collective-permute-done.20.other_ref, bf16[256,256]{1,0:T(8,128)(2,1)S(1)} %copy-done.2, f32[1,128]{1,0:T(1,128)S(1)} %bitcast.30, f32[1,128]{1,0:T(1,128)S(1)} %bitcast.31), custom_call_target="tpu_custom_call" | custom-call | tf_op jit(solution)/shard_map/norm/pallas_call | solution.py:719
  (30 shorter events, 0.1 us)
Async XLA Ops:
  0.0 36.0 %copy-start.7 = (bf16[256,64]{0,1:T(8,128)(2,1)S(1)}, bf16[256,64]{0,1:T(8,128)(2,1)}, u32[]{:S(2)}) copy-start(bf16[256,64]{0,1:T(8,128)(2,1)} %param.20) | copy-start | bytes 98308
  0.0 36.0 %copy-start.1 = (s32[64,16,64]{2,1,0:T(8,128)S(1)}, s32[64,16,64]{2,1,0:T(8,128)}, u32[]{:S(2)}) copy-start(s32[64,16,64]{2,1,0:T(8,128)} %param.19) | copy-start | bytes 786436
  0.0 36.0 %copy-start = (bf16[64,16,256]{2,1,0:T(8,128)(2,1)S(1)}, bf16[64,16,256]{2,1,0:T(8,128)(2,1)}, u32[]{:S(2)}) copy-start(bf16[64,16,256]{2,1,0:T(8,128)(2,1)} %param.13) | copy-start | bytes 1572868
  1.1 17.1 %collective-permute-start.4 = (bf16[1360,128]{1,0:T(8,128)(2,1)S(1)}, bf16[1360,128]{1,0:T(8,128)(2,1)S(1)}, u32[]{:S(2)}, u32[]{:S(2)}) collective-permute-start(bf16[1360,128]{1,0:T(8,128)(2,1)S(1)} %pad_maximum_fusion.refs_0_.refs_1_), channel_id=1, source_target_pairs={{2,4},{4,2},{3,5},{5,3},{10,12},{12,10},{11,13},{13,11},{18,20},{2... | collective-permute-start | bytes 1044488 | tf_op jit(solution)/shard_map/ppermute | solution.py:482
  4.4 8.8 %collective-permute-start.3 = (bf16[1360,128]{1,0:T(8,128)(2,1)S(1)}, bf16[1360,128]{1,0:T(8,128)(2,1)S(1)}, u32[]{:S(2)}, u32[]{:S(2)}) collective-permute-start(bf16[1360,128]{1,0:T(8,128)(2,1)S(1)} %pad_maximum_fusion.refs_0_.refs_1_), channel_id=1, source_target_pairs={{0,2},{2,0},{4,6},{6,4},{1,3},{3,1},{5,7},{7,5},{8,10},{10,8},{12,... | collective-permute-start | bytes 1044488 | tf_op jit(solution)/shard_map/ppermute | solution.py:482
  13.2 9.8 %collective-permute-start.6 = (bf16[1360,128]{1,0:T(8,128)(2,1)S(1)}, bf16[1360,128]{1,0:T(8,128)(2,1)S(1)}, u32[]{:S(2)}, u32[]{:S(2)}) collective-permute-start(bf16[1360,128]{1,0:T(8,128)(2,1)S(1)} %collective-permute-done.3.refs_0_.refs_2_), channel_id=1, source_target_pairs={{2,4},{4,2},{3,5},{5,3},{10,12},{12,10},{11,13},{13,11},{18,20},{2... | collective-permute-start | bytes 1044488 | tf_op jit(solution)/shard_map/ppermute | solution.py:482
  15.5 8.8 %collective-permute-start.2 = (s32[4,8]{0,1:T(8,128)S(1)}, s32[4,8]{0,1:T(8,128)S(1)}, u32[]{:S(2)}, u32[]{:S(2)}) collective-permute-start(s32[4,8]{0,1:T(8,128)S(1)} %get-tuple-element.43), channel_id=1, source_target_pairs={{0,24},{8,16},{16,8},{24,0},{1,25},{9,17},{17,9},{25,1},{2,26},{10... | collective-permute-start | bytes 392 | tf_op jit(solution)/shard_map/ppermute | solution.py:501
  17.7 6.6 %collective-permute-start.1 = (s32[4,8]{0,1:T(8,128)S(1)}, s32[4,8]{0,1:T(8,128)S(1)}, u32[]{:S(2)}, u32[]{:S(2)}) collective-permute-start(s32[4,8]{0,1:T(8,128)S(1)} %get-tuple-element.44), channel_id=1, source_target_pairs={{0,16},{8,24},{16,0},{24,8},{1,17},{9,25},{17,1},{25,9},{2,18},{10... | collective-permute-start | bytes 392 | tf_op jit(solution)/shard_map/ppermute | solution.py:501
  17.9 6.4 %collective-permute-start = (s32[4,8]{0,1:T(8,128)S(1)}, s32[4,8]{0,1:T(8,128)S(1)}, u32[]{:S(2)}, u32[]{:S(2)}) collective-permute-start(s32[4,8]{0,1:T(8,128)S(1)} %get-tuple-element.45), channel_id=1, source_target_pairs={{0,8},{8,0},{16,24},{24,16},{1,9},{9,1},{17,25},{25,17},{2,10},{10... | collective-permute-start | bytes 392 | tf_op jit(solution)/shard_map/ppermute | solution.py:501
  18.2 11.0 %collective-permute-start.5 = (bf16[1360,128]{1,0:T(8,128)(2,1)S(1)}, bf16[1360,128]{1,0:T(8,128)(2,1)S(1)}, u32[]{:S(2)}, u32[]{:S(2)}) collective-permute-start(bf16[1360,128]{1,0:T(8,128)(2,1)S(1)} %collective-permute-done.4.refs_0_.refs_3_), channel_id=1, source_target_pairs={{2,0},{4,6},{3,1},{5,7},{10,8},{12,14},{11,9},{13,15},{18,16},{20,... | collective-permute-start | bytes 1044488 | tf_op jit(solution)/shard_map/ppermute | solution.py:482
  23.0 11.1 %collective-permute-start.7 = (bf16[1360,128]{1,0:T(8,128)(2,1)S(1)}, bf16[1360,128]{1,0:T(8,128)(2,1)S(1)}, u32[]{:S(2)}, u32[]{:S(2)}) collective-permute-start(bf16[1360,128]{1,0:T(8,128)(2,1)S(1)} %collective-permute-done.6.refs_1_.refs_5_), channel_id=1, source_target_pairs={{2,0},{4,6},{3,1},{5,7},{10,8},{12,14},{11,9},{13,15},{18,16},{20,... | collective-permute-start | bytes 1044488 | tf_op jit(solution)/shard_map/ppermute | solution.py:482
  24.5 21.7 %copy-start.11 = (f32[64]{0:T(128)S(1)}, f32[64]{0:T(128)}, u32[]{:S(2)}) copy-start(f32[64]{0:T(128)} %param.21) | copy-start | bytes 772
  25.5 6.0 %collective-permute-start.8 = (bf16[688,128]{1,0:T(8,128)(2,1)S(1)}, bf16[688,128]{1,0:T(8,128)(2,1)S(1)}, u32[]{:S(2)}, u32[]{:S(2)}) collective-permute-start(bf16[688,128]{1,0:T(8,128)(2,1)S(1)} %get-tuple-element.25), channel_id=1, source_target_pairs={{0,8},{8,0},{16,24},{24,16},{1,9},{9,1},{17,25},{25,17},{2,10},{10... | collective-permute-start | bytes 528392 | tf_op jit(solution)/shard_map/ppermute | solution.py:529
  26.8 6.0 %collective-permute-start.9 = (bf16[688,128]{1,0:T(8,128)(2,1)S(1)}, bf16[688,128]{1,0:T(8,128)(2,1)S(1)}, u32[]{:S(2)}, u32[]{:S(2)}) collective-permute-start(bf16[688,128]{1,0:T(8,128)(2,1)S(1)} %get-tuple-element.26), channel_id=1, source_target_pairs={{0,16},{8,24},{16,0},{24,8},{1,17},{9,25},{17,1},{25,9},{2,18},{10... | collective-permute-start | bytes 528392 | tf_op jit(solution)/shard_map/ppermute | solution.py:529
  28.0 10.2 %collective-permute-start.10 = (bf16[688,128]{1,0:T(8,128)(2,1)S(1)}, bf16[688,128]{1,0:T(8,128)(2,1)S(1)}, u32[]{:S(2)}, u32[]{:S(2)}) collective-permute-start(bf16[688,128]{1,0:T(8,128)(2,1)S(1)} %get-tuple-element.27), channel_id=1, source_target_pairs={{0,24},{8,16},{16,8},{24,0},{1,25},{9,17},{17,9},{25,1},{2,26},{10... | collective-permute-start | bytes 528392 | tf_op jit(solution)/shard_map/ppermute | solution.py:529
  29.2 9.2 %collective-permute-start.11 = (bf16[688,128]{1,0:T(8,128)(2,1)S(1)}, bf16[688,128]{1,0:T(8,128)(2,1)S(1)}, u32[]{:S(2)}, u32[]{:S(2)}) collective-permute-start(bf16[688,128]{1,0:T(8,128)(2,1)S(1)} %get-tuple-element.28), channel_id=1, source_target_pairs={{0,8},{8,0},{16,24},{24,16},{1,9},{9,1},{17,25},{25,17},{2,10},{10... | collective-permute-start | bytes 528392 | tf_op jit(solution)/shard_map/ppermute | solution.py:529
  31.5 9.2 %collective-permute-start.12 = (bf16[688,128]{1,0:T(8,128)(2,1)S(1)}, bf16[688,128]{1,0:T(8,128)(2,1)S(1)}, u32[]{:S(2)}, u32[]{:S(2)}) collective-permute-start(bf16[688,128]{1,0:T(8,128)(2,1)S(1)} %get-tuple-element.29), channel_id=1, source_target_pairs={{0,16},{8,24},{16,0},{24,8},{1,17},{9,25},{17,1},{25,9},{2,18},{10... | collective-permute-start | bytes 528392 | tf_op jit(solution)/shard_map/ppermute | solution.py:529
  32.8 9.1 %collective-permute-start.13 = (bf16[688,128]{1,0:T(8,128)(2,1)S(1)}, bf16[688,128]{1,0:T(8,128)(2,1)S(1)}, u32[]{:S(2)}, u32[]{:S(2)}) collective-permute-start(bf16[688,128]{1,0:T(8,128)(2,1)S(1)} %get-tuple-element.30), channel_id=1, source_target_pairs={{0,24},{8,16},{16,8},{24,0},{1,25},{9,17},{17,9},{25,1},{2,26},{10... | collective-permute-start | bytes 528392 | tf_op jit(solution)/shard_map/ppermute | solution.py:529
  34.0 0.7 %copy-start.3 = (bf16[1360,128]{1,0:T(8,128)(2,1)}, bf16[1360,128]{1,0:T(8,128)(2,1)S(1)}, u32[]{:S(2)}) copy-start(bf16[1360,128]{1,0:T(8,128)(2,1)S(1)} %collective-permute-done.7.refs_0_.refs_6_) | copy-start | bytes 1044484
  34.8 10.3 %collective-permute-start.14 = (bf16[688,128]{1,0:T(8,128)(2,1)S(1)}, bf16[688,128]{1,0:T(8,128)(2,1)S(1)}, u32[]{:S(2)}, u32[]{:S(2)}) collective-permute-start(bf16[688,128]{1,0:T(8,128)(2,1)S(1)} %get-tuple-element.31), channel_id=1, source_target_pairs={{0,8},{8,0},{16,24},{24,16},{1,9},{9,1},{17,25},{25,17},{2,10},{10... | collective-permute-start | bytes 528392 | tf_op jit(solution)/shard_map/ppermute | solution.py:529
  36.2 1.0 %copy-start.4 = (bf16[1360,128]{1,0:T(8,128)(2,1)S(1)}, bf16[1360,128]{1,0:T(8,128)(2,1)}, u32[]{:S(2)}) copy-start(bf16[1360,128]{1,0:T(8,128)(2,1)} %copy-done.3) | copy-start | bytes 1044484
  37.2 20.0 %copy-start.5 = (bf16[1360,128]{1,0:T(8,128)(2,1)S(1)}, bf16[1360,128]{1,0:T(8,128)(2,1)}, u32[]{:S(2)}) copy-start(bf16[1360,128]{1,0:T(8,128)(2,1)} %copy-done.3) | copy-start | bytes 1044484
  37.2 20.0 %copy-start.6 = (s32[4,1,4,8]{3,2,1,0:T(4,128)S(1)}, s32[4,1,4,8]{3,2,1,0:T(4,128)}, u32[]{:S(2)}) copy-start(s32[4,1,4,8]{3,2,1,0:T(4,128)} %refs_23_.1) | copy-start | bytes 1540
  38.2 12.4 %collective-permute-start.15 = (bf16[688,128]{1,0:T(8,128)(2,1)S(1)}, bf16[688,128]{1,0:T(8,128)(2,1)S(1)}, u32[]{:S(2)}, u32[]{:S(2)}) collective-permute-start(bf16[688,128]{1,0:T(8,128)(2,1)S(1)} %get-tuple-element.32), channel_id=1, source_target_pairs={{0,16},{8,24},{16,0},{24,8},{1,17},{9,25},{17,1},{25,9},{2,18},{10... | collective-permute-start | bytes 528392 | tf_op jit(solution)/shard_map/ppermute | solution.py:529
  38.4 12.1 %collective-permute-start.16 = (bf16[688,128]{1,0:T(8,128)(2,1)S(1)}, bf16[688,128]{1,0:T(8,128)(2,1)S(1)}, u32[]{:S(2)}, u32[]{:S(2)}) collective-permute-start(bf16[688,128]{1,0:T(8,128)(2,1)S(1)} %get-tuple-element.33), channel_id=1, source_target_pairs={{0,24},{8,16},{16,8},{24,0},{1,25},{9,17},{17,9},{25,1},{2,26},{10... | collective-permute-start | bytes 528392 | tf_op jit(solution)/shard_map/ppermute | solution.py:529
  40.7 11.9 %collective-permute-start.17 = (bf16[688,128]{1,0:T(8,128)(2,1)S(1)}, bf16[688,128]{1,0:T(8,128)(2,1)S(1)}, u32[]{:S(2)}, u32[]{:S(2)}) collective-permute-start(bf16[688,128]{1,0:T(8,128)(2,1)S(1)} %get-tuple-element.34), channel_id=1, source_target_pairs={{0,8},{8,0},{16,24},{24,16},{1,9},{9,1},{17,25},{25,17},{2,10},{10... | collective-permute-start | bytes 528392 | tf_op jit(solution)/shard_map/ppermute | solution.py:529
  42.0 13.7 %collective-permute-start.18 = (bf16[688,128]{1,0:T(8,128)(2,1)S(1)}, bf16[688,128]{1,0:T(8,128)(2,1)S(1)}, u32[]{:S(2)}, u32[]{:S(2)}) collective-permute-start(bf16[688,128]{1,0:T(8,128)(2,1)S(1)} %get-tuple-element.35), channel_id=1, source_target_pairs={{0,16},{8,24},{16,0},{24,8},{1,17},{9,25},{17,1},{25,9},{2,18},{10... | collective-permute-start | bytes 528392 | tf_op jit(solution)/shard_map/ppermute | solution.py:529
  45.1 12.1 %collective-permute-start.19 = (bf16[688,128]{1,0:T(8,128)(2,1)S(1)}, bf16[688,128]{1,0:T(8,128)(2,1)S(1)}, u32[]{:S(2)}, u32[]{:S(2)}) collective-permute-start(bf16[688,128]{1,0:T(8,128)(2,1)S(1)} %get-tuple-element.36), channel_id=1, source_target_pairs={{0,24},{8,16},{16,8},{24,0},{1,25},{9,17},{17,9},{25,1},{2,26},{10... | collective-permute-start | bytes 528392 | tf_op jit(solution)/shard_map/ppermute | solution.py:529
  57.2 11.9 %copy-start.2 = (bf16[256,256]{1,0:T(8,128)(2,1)S(1)}, bf16[256,256]{1,0:T(8,128)(2,1)}, u32[]{:S(2)}) copy-start(bf16[256,256]{1,0:T(8,128)(2,1)} %weight_ref.3) | copy-start | bytes 393220
  57.2 11.9 %copy-start.8 = (f32[256]{0:T(256)S(1)}, f32[256]{0:T(256)}, u32[]{:S(2)}) copy-start(f32[256]{0:T(256)} %param.23) | copy-start | bytes 3076
  57.2 13.1 %copy-start.9 = (f32[128]{0:T(128)S(1)}, f32[128]{0:T(128)}, u32[]{:S(2)}) copy-start(f32[128]{0:T(128)} %param.24) | copy-start | bytes 1540
  57.2 13.1 %copy-start.10 = (f32[128]{0:T(128)S(1)}, f32[128]{0:T(128)}, u32[]{:S(2)}) copy-start(f32[128]{0:T(128)} %param.25) | copy-start | bytes 1540
  65.6 4.7 %collective-permute-start.20 = (bf16[1024,128]{1,0:T(8,128)(2,1)S(1)}, bf16[1024,128]{1,0:T(8,128)(2,1)S(1)}, u32[]{:S(2)}, u32[]{:S(2)}) collective-permute-start(bf16[1024,128]{1,0:T(8,128)(2,1)S(1)} %attend.1.own_ref), channel_id=1, source_target_pairs={{0,1},{1,0},{2,3},{3,2},{4,5},{5,4},{6,7},{7,6},{8,9},{9,8},{10,11... | collective-permute-start | bytes 786440 | tf_op jit(solution)/shard_map/ppermute | solution.py:700

commit v10 on v9

--- a/solution.py
+++ b/solution.py
@@ -312,6 +312,7 @@
         left0,
         left1,
         left2,
+        turn_ref,
         sem,
     ) = refs[count:]
     peers, capacity, sizes, sides, per_block, heads, head_dim, blocks = dims
@@ -322,7 +323,9 @@
     side0, side1 = sides[0], sides[1]
 
     gather(sources, (tile0, tile1, tile2), tile3, sem)
-    left0[...] = jnp.zeros_like(left0)
+    left0[:, side0 // GROUPS[0] * head_dim :, :] = jnp.zeros(
+        (heads, head_dim, left0.shape[2]), jnp.bfloat16
+    )
     flat = tile3[...].reshape(peers * small, channels)
     size3 = sizes[3]
     wide = blocks * per_block * size3
@@ -375,26 +378,26 @@
                 ]
         left2[:, :base2] = tile2[mine].reshape(per_block * sizes[2], channels).T
 
-        for head in range(heads):
-            total = jnp.dot(
-                left2[head * head_dim : (head + 1) * head_dim, :],
-                weight2[block, head],
-                preferred_element_type=jnp.float32,
-            )
+        def per_head(head, carry):
+            rows = pl.ds(head * head_dim, head_dim)
+            total = jnp.dot(left2[rows, :], weight2[block, head], preferred_element_type=jnp.float32)
             for level in range(2):
                 left = (left0, left1)[level]
                 weight = (weight0, weight1)[level]
                 for point in range(POINTS):
                     row = (head * LEVELS + level) * POINTS + point
                     product = jnp.dot(left[head], weight[block, head, point], preferred_element_type=jnp.float32)
-                    down = down_ref[block, row : row + 1, :]
+                    down = down_ref[block, pl.ds(row, 1), :]
                     for offset in range(sides[level] // GROUPS[level] + 1):
                         total = total + product[offset * head_dim : (offset + 1) * head_dim, :] * hat(
                             down, float(offset)
                         )
-            out_ref[
-                pl.ds(pl.multiple_of(block * pixels, pixels), pixels), head * head_dim : (head + 1) * head_dim
-            ] = total.T.astype(jnp.bfloat16)
+            turn_ref[rows, :] = total
+            return carry
+
+        for head in range(heads):
+            per_head(head, 0)
+        out_ref[pl.ds(pl.multiple_of(block * pixels, pixels), pixels), :] = turn_ref[...].T.astype(jnp.bfloat16)
         return carry
 
     lax.fori_loop(0, blocks, one, 0)
@@ -689,6 +692,7 @@
             VMEM((heads, (sides[0] // GROUPS[0] + 1) * head_dim, depth0), jnp.bfloat16),
             VMEM((heads, (sides[1] // GROUPS[1] + 1) * head_dim, depth1), jnp.bfloat16),
             VMEM((channels, depth2), jnp.bfloat16),
+            VMEM((channels, pixels), jnp.float32),
             pltpu.SemaphoreType.DMA((LEVELS,)),
         ],
         compiler_params=pltpu.CompilerParams(vmem_limit_bytes=ATTEND_VMEM),

time: 72.8 us -> 72.3 us (level)
  no operation moved by 1% of the time
where the time goes in v10:
time: 72.3 us; the launch traced here: 72.1 us
  starting transfers between devices  25.5 us (35%)
  waiting for transfers between devices  22.3 us (31%)
  Pallas kernels  19.4 us (27%)
  local copies, waits for them, and re-layouts  2.74 us (4%)
  other arithmetic  1.86 us (3%)
    ppermute x12, starting transfers between devices, relay_tiles(): lax.ppermute(sent[number - 1], 'row', [(row, source_of(row, number)) for...  11.3 us
    ppermute x12, waiting for transfers between devices, relay_tiles(): lax.ppermute(sent[number - 1], 'row', [(row, source_of(row, number)) for...  11.1 us
    ppermute x5, waiting for transfers between devices, move(): held[name] = lax.ppermute(held[source or 'own'], 'col', pairs)  10.8 us
    ppermute x5, starting transfers between devices, move(): held[name] = lax.ppermute(held[source or 'own'], 'col', pairs)  7.94 us
    pallas_call x1, Pallas kernels, on_device(): pl.pallas_call(functools.partial(attend_kernel, dims, grid, gather, len(s...  7.86 us
    pallas_call x1, Pallas kernels, on_device(): pl.pallas_call(functools.partial(prep_kernel, dims), out_shape=[jax.Shape...  4.35 us
    pallas_call x4, Pallas kernels, relay_tiles(): pl.pallas_call(functools.partial(relay_select_kernel, (row_count - 1, len...  3.97 us
    ppermute x1, starting transfers between devices, on_device(): other = lax.ppermute(attn, 'head', [(0, 1), (1, 0)])  3.53 us
  transfers between devices with their start and end apart: 21, of which 9 were waited for; matrix products, arithmetic and copies ran while one was open for 2% of the time, Pallas kernels for 13%

profile of v10, /device:TPU:9, one launch (start us, length us, event | category | flops | bytes accessed | tf_op | source)
XLA Modules:
  0.0 72.1 jit_solution(5077572523689399410)
XLA Ops:
  0.0 1.1 %pad_maximum_fusion.refs_0_.refs_1_ = bf16[1360,128]{1,0:T(8,128)(2,1)S(1)} fusion(bf16[16,128]{1,0:T(8,128)(2,1)} %bitcast.37, bf16[64,128]{1,0:T(8,128)(2,1)} %bitcast.36, bf16[256,128]{1,0:T(8,128)(2,1)} %bitcast.34, bf16[1024,128]{1,0:T(8,128)(2,1)} %bitcast.33), kind=kLoop, calls=%fused_computation | loop fusion | flops 1392640 | bytes 696320 | tf_op jit(solution)/shard_map/concatenate | solution.py:481
  1.1 3.2 %collective-permute-start.4 = (bf16[1360,128]{1,0:T(8,128)(2,1)S(1)}, bf16[1360,128]{1,0:T(8,128)(2,1)S(1)}, u32[]{:S(2)}, u32[]{:S(2)}) collective-permute-start(bf16[1360,128]{1,0:T(8,128)(2,1)S(1)} %pad_maximum_fusion.refs_0_.refs_1_), channel_id=1, source_target_pairs={{2,4},{4,2},{3,5},{5,3},{10,12},{12,10},{11,13},{13,11},{18,20},{2... | collective-permute-start | bytes 1044488 | tf_op jit(solution)/shard_map/ppermute | solution.py:485
  4.4 0.1 collective-permute-start.3
  4.5 0.7 %slice_bitcast_fusion.3 = (s32[4,8]{1,0:T(4,128)S(1)}, s32[4,8]{1,0:T(4,128)S(1)}, s32[4,8]{1,0:T(4,128)S(1)}, s32[4,8]{1,0:T(4,128)S(1)}) fusion(s32[1,4,4,8]{3,2,1,0:T(4,128)} %bitcast.27), kind=kLoop, calls=%fused_computation.43 | loop fusion | bytes 1024 | tf_op jit(solution)/shard_map/concatenate | solution.py:429
  5.2 0.1 fusion.8
  5.3 0.2 convert_reduce_fusion
  5.6 0.2 select_reduce_fusion
  5.8 7.4 %collective-permute-done.3.refs_0_.refs_2_ = bf16[1360,128]{1,0:T(8,128)(2,1)S(1)} collective-permute-done((bf16[1360,128]{1,0:T(8,128)(2,1)S(1)}, bf16[1360,128]{1,0:T(8,128)(2,1)S(1)}, u32[]{:S(2)}, u32[]{:S(2)}) %collective-permute-start.3) | collective-permute-done | bytes 348192 | tf_op jit(solution)/shard_map/ppermute | solution.py:485
  13.2 2.1 %collective-permute-start.6 = (bf16[1360,128]{1,0:T(8,128)(2,1)S(1)}, bf16[1360,128]{1,0:T(8,128)(2,1)S(1)}, u32[]{:S(2)}, u32[]{:S(2)}) collective-permute-start(bf16[1360,128]{1,0:T(8,128)(2,1)S(1)} %collective-permute-done.3.refs_0_.refs_2_), channel_id=1, source_target_pairs={{2,4},{4,2},{3,5},{5,3},{10,12},{12,10},{11,13},{13,11},{18,20},{2... | collective-permute-start | bytes 1044488 | tf_op jit(solution)/shard_map/ppermute | solution.py:485
  15.3 0.1 sub.29
  15.4 0.1 select_reduce_fusion.1
  15.5 2.2 %collective-permute-start.2 = (s32[4,8]{0,1:T(8,128)S(1)}, s32[4,8]{0,1:T(8,128)S(1)}, u32[]{:S(2)}, u32[]{:S(2)}) collective-permute-start(s32[4,8]{0,1:T(8,128)S(1)} %get-tuple-element.43), channel_id=1, source_target_pairs={{0,24},{8,16},{16,8},{24,0},{1,25},{9,17},{17,9},{25,1},{2,26},{10... | collective-permute-start | bytes 392 | tf_op jit(solution)/shard_map/ppermute | solution.py:504
  17.7 0.2 collective-permute-start.1
  17.9 0.3 collective-permute-start
  18.2 0.0 collective-permute-done.4.refs_0_.refs_3_
  18.2 1.3 %collective-permute-start.5 = (bf16[1360,128]{1,0:T(8,128)(2,1)S(1)}, bf16[1360,128]{1,0:T(8,128)(2,1)S(1)}, u32[]{:S(2)}, u32[]{:S(2)}) collective-permute-start(bf16[1360,128]{1,0:T(8,128)(2,1)S(1)} %collective-permute-done.4.refs_0_.refs_3_), channel_id=1, source_target_pairs={{2,0},{4,6},{3,1},{5,7},{10,8},{12,14},{11,9},{13,15},{18,16},{20,... | collective-permute-start | bytes 1044488 | tf_op jit(solution)/shard_map/ppermute | solution.py:485
  19.5 3.4 %collective-permute-done.6.refs_1_.refs_5_ = bf16[1360,128]{1,0:T(8,128)(2,1)S(1)} collective-permute-done((bf16[1360,128]{1,0:T(8,128)(2,1)S(1)}, bf16[1360,128]{1,0:T(8,128)(2,1)S(1)}, u32[]{:S(2)}, u32[]{:S(2)}) %collective-permute-start.6) | collective-permute-done | bytes 348192 | tf_op jit(solution)/shard_map/ppermute | solution.py:485
  23.0 1.3 %collective-permute-start.7 = (bf16[1360,128]{1,0:T(8,128)(2,1)S(1)}, bf16[1360,128]{1,0:T(8,128)(2,1)S(1)}, u32[]{:S(2)}, u32[]{:S(2)}) collective-permute-start(bf16[1360,128]{1,0:T(8,128)(2,1)S(1)} %collective-permute-done.6.refs_1_.refs_5_), channel_id=1, source_target_pairs={{2,0},{4,6},{3,1},{5,7},{10,8},{12,14},{11,9},{13,15},{18,16},{20,... | collective-permute-start | bytes 1044488 | tf_op jit(solution)/shard_map/ppermute | solution.py:485
  24.3 0.0 collective-permute-done.2
  24.3 0.0 collective-permute-done.1
  24.3 0.0 collective-permute-done
  24.3 0.1 concatenate.157
  24.4 0.1 copy.33.table_ref.refs_0_
  24.5 1.0 %shard_map.127 = (bf16[688,128]{1,0:T(8,128)(2,1)S(1)}, bf16[688,128]{1,0:T(8,128)(2,1)S(1)}, bf16[688,128]{1,0:T(8,128)(2,1)S(1)}) custom-call(s32[45,8]{1,0:T(8,128)S(1)} %copy.33.table_ref.refs_0_, bf16[1360,128]{1,0:T(8,128)(2,1)S(1)} %pad_maximum_fusion.refs_0_.refs_1_), custom_call_target="tpu_custom_call" | custom-call | flops 500000000 | bytes 1000000 | tf_op jit(solution)/shard_map/pallas_call | solution.py:520
  25.5 1.3 %collective-permute-start.8 = (bf16[688,128]{1,0:T(8,128)(2,1)S(1)}, bf16[688,128]{1,0:T(8,128)(2,1)S(1)}, u32[]{:S(2)}, u32[]{:S(2)}) collective-permute-start(bf16[688,128]{1,0:T(8,128)(2,1)S(1)} %get-tuple-element.25), channel_id=1, source_target_pairs={{0,8},{8,0},{16,24},{24,16},{1,9},{9,1},{17,25},{25,17},{2,10},{10... | collective-permute-start | bytes 528392 | tf_op jit(solution)/shard_map/ppermute | solution.py:532
  26.8 1.2 %collective-permute-start.9 = (bf16[688,128]{1,0:T(8,128)(2,1)S(1)}, bf16[688,128]{1,0:T(8,128)(2,1)S(1)}, u32[]{:S(2)}, u32[]{:S(2)}) collective-permute-start(bf16[688,128]{1,0:T(8,128)(2,1)S(1)} %get-tuple-element.26), channel_id=1, source_target_pairs={{0,16},{8,24},{16,0},{24,8},{1,17},{9,25},{17,1},{25,9},{2,18},{10... | collective-permute-start | bytes 528392 | tf_op jit(solution)/shard_map/ppermute | solution.py:532
  28.0 0.2 collective-permute-start.10
  28.2 1.0 %shard_map.128 = (bf16[688,128]{1,0:T(8,128)(2,1)S(1)}, bf16[688,128]{1,0:T(8,128)(2,1)S(1)}, bf16[688,128]{1,0:T(8,128)(2,1)S(1)}) custom-call(s32[45,8]{1,0:T(8,128)S(1)} %copy.33.table_ref.refs_0_, bf16[1360,128]{1,0:T(8,128)(2,1)S(1)} %collective-permute-done.3.refs_0_.refs_2_), custom_call_target="tpu_custom_call" | custom-call | flops 500000000 | bytes 1000000 | tf_op jit(solution)/shard_map/pallas_call | solution.py:520
  29.2 0.0 collective-permute-done.5.refs_1_.refs_4_
  29.2 1.3 %collective-permute-start.11 = (bf16[688,128]{1,0:T(8,128)(2,1)S(1)}, bf16[688,128]{1,0:T(8,128)(2,1)S(1)}, u32[]{:S(2)}, u32[]{:S(2)}) collective-permute-start(bf16[688,128]{1,0:T(8,128)(2,1)S(1)} %get-tuple-element.28), channel_id=1, source_target_pairs={{0,8},{8,0},{16,24},{24,16},{1,9},{9,1},{17,25},{25,17},{2,10},{10... | collective-permute-start | bytes 528392 | tf_op jit(solution)/shard_map/ppermute | solution.py:532
  30.5 1.0 %shard_map.129 = (bf16[688,128]{1,0:T(8,128)(2,1)S(1)}, bf16[688,128]{1,0:T(8,128)(2,1)S(1)}, bf16[688,128]{1,0:T(8,128)(2,1)S(1)}) custom-call(s32[45,8]{1,0:T(8,128)S(1)} %copy.33.table_ref.refs_0_, bf16[1360,128]{1,0:T(8,128)(2,1)S(1)} %collective-permute-done.4.refs_0_.refs_3_, bf16[1360,128]{1,0:T(8,128)(2,1)S(1)} %collective-permute-done.5.refs_1_.refs_4_), custom_call_target="tpu_custom_call" | custom-call | flops 500000000 | bytes 1000000 | tf_op jit(solution)/shard_map/pallas_call | solution.py:520
  31.5 0.0 collective-permute-done.8.refs_7_
  31.5 1.3 %collective-permute-start.12 = (bf16[688,128]{1,0:T(8,128)(2,1)S(1)}, bf16[688,128]{1,0:T(8,128)(2,1)S(1)}, u32[]{:S(2)}, u32[]{:S(2)}) collective-permute-start(bf16[688,128]{1,0:T(8,128)(2,1)S(1)} %get-tuple-element.29), channel_id=1, source_target_pairs={{0,16},{8,24},{16,0},{24,8},{1,17},{9,25},{17,1},{25,9},{2,18},{10... | collective-permute-start | bytes 528392 | tf_op jit(solution)/shard_map/ppermute | solution.py:532
  32.8 0.0 collective-permute-done.9.refs_8_
  32.8 1.2 %collective-permute-start.13 = (bf16[688,128]{1,0:T(8,128)(2,1)S(1)}, bf16[688,128]{1,0:T(8,128)(2,1)S(1)}, u32[]{:S(2)}, u32[]{:S(2)}) collective-permute-start(bf16[688,128]{1,0:T(8,128)(2,1)S(1)} %get-tuple-element.30), channel_id=1, source_target_pairs={{0,24},{8,16},{16,8},{24,0},{1,25},{9,17},{17,9},{25,1},{2,26},{10... | collective-permute-start | bytes 528392 | tf_op jit(solution)/shard_map/ppermute | solution.py:532
  34.0 0.0 collective-permute-done.7.refs_0_.refs_6_
  34.0 0.7 %copy-done.3 = bf16[1360,128]{1,0:T(8,128)(2,1)} copy-done((bf16[1360,128]{1,0:T(8,128)(2,1)}, bf16[1360,128]{1,0:T(8,128)(2,1)S(1)}, u32[]{:S(2)}) %copy-start.3) | copy-done | bytes 348184
  34.8 1.2 %collective-permute-start.14 = (bf16[688,128]{1,0:T(8,128)(2,1)S(1)}, bf16[688,128]{1,0:T(8,128)(2,1)S(1)}, u32[]{:S(2)}, u32[]{:S(2)}) collective-permute-start(bf16[688,128]{1,0:T(8,128)(2,1)S(1)} %get-tuple-element.31), channel_id=1, source_target_pairs={{0,8},{8,0},{16,24},{24,16},{1,9},{9,1},{17,25},{25,17},{2,10},{10... | collective-permute-start | bytes 528392 | tf_op jit(solution)/shard_map/ppermute | solution.py:532
  36.0 0.1 load.1
  36.2 1.0 %copy-done.4 = bf16[1360,128]{1,0:T(8,128)(2,1)S(1)} copy-done((bf16[1360,128]{1,0:T(8,128)(2,1)S(1)}, bf16[1360,128]{1,0:T(8,128)(2,1)}, u32[]{:S(2)}) %copy-start.4) | copy-done | bytes 348184
  37.2 1.0 %shard_map.130 = (bf16[688,128]{1,0:T(8,128)(2,1)S(1)}, bf16[688,128]{1,0:T(8,128)(2,1)S(1)}, bf16[688,128]{1,0:T(8,128)(2,1)S(1)}) custom-call(s32[45,8]{1,0:T(8,128)S(1)} %copy.33.table_ref.refs_0_, bf16[1360,128]{1,0:T(8,128)(2,1)S(1)} %copy-done.4, bf16[1360,128]{1,0:T(8,128)(2,1)S(1)} %collective-permute-done.6.refs_1_.refs_5_), custom_call_target="tpu_custom_call" | custom-call | flops 500000000 | bytes 1000000 | tf_op jit(solution)/shard_map/pallas_call | solution.py:520
  38.2 0.0 collective-permute-done.10.refs_9_
  38.2 0.3 collective-permute-start.15
  38.4 0.0 collective-permute-done.11.refs_10_
  38.4 1.2 %collective-permute-start.16 = (bf16[688,128]{1,0:T(8,128)(2,1)S(1)}, bf16[688,128]{1,0:T(8,128)(2,1)S(1)}, u32[]{:S(2)}, u32[]{:S(2)}) collective-permute-start(bf16[688,128]{1,0:T(8,128)(2,1)S(1)} %get-tuple-element.33), channel_id=1, source_target_pairs={{0,24},{8,16},{16,8},{24,0},{1,25},{9,17},{17,9},{25,1},{2,26},{10... | collective-permute-start | bytes 528392 | tf_op jit(solution)/shard_map/ppermute | solution.py:532
  39.7 1.1 %collective-permute-done.12.refs_11_ = bf16[688,128]{1,0:T(8,128)(2,1)S(1)} collective-permute-done((bf16[688,128]{1,0:T(8,128)(2,1)S(1)}, bf16[688,128]{1,0:T(8,128)(2,1)S(1)}, u32[]{:S(2)}, u32[]{:S(2)}) %collective-permute-start.12) | collective-permute-done | bytes 176160 | tf_op jit(solution)/shard_map/ppermute | solution.py:532
  40.7 0.2 collective-permute-start.17
  40.9 1.1 %collective-permute-done.13.refs_12_ = bf16[688,128]{1,0:T(8,128)(2,1)S(1)} collective-permute-done((bf16[688,128]{1,0:T(8,128)(2,1)S(1)}, bf16[688,128]{1,0:T(8,128)(2,1)S(1)}, u32[]{:S(2)}, u32[]{:S(2)}) %collective-permute-start.13) | collective-permute-done | bytes 176160 | tf_op jit(solution)/shard_map/ppermute | solution.py:532
  42.0 0.8 %collective-permute-start.18 = (bf16[688,128]{1,0:T(8,128)(2,1)S(1)}, bf16[688,128]{1,0:T(8,128)(2,1)S(1)}, u32[]{:S(2)}, u32[]{:S(2)}) collective-permute-start(bf16[688,128]{1,0:T(8,128)(2,1)S(1)} %get-tuple-element.35), channel_id=1, source_target_pairs={{0,16},{8,24},{16,0},{24,8},{1,17},{9,25},{17,1},{25,9},{2,18},{10... | collective-permute-start | bytes 528392 | tf_op jit(solution)/shard_map/ppermute | solution.py:532
  42.7 2.3 %collective-permute-done.14.refs_13_ = bf16[688,128]{1,0:T(8,128)(2,1)S(1)} collective-permute-done((bf16[688,128]{1,0:T(8,128)(2,1)S(1)}, bf16[688,128]{1,0:T(8,128)(2,1)S(1)}, u32[]{:S(2)}, u32[]{:S(2)}) %collective-permute-start.14) | collective-permute-done | bytes 176160 | tf_op jit(solution)/shard_map/ppermute | solution.py:532
  45.1 1.1 %collective-permute-start.19 = (bf16[688,128]{1,0:T(8,128)(2,1)S(1)}, bf16[688,128]{1,0:T(8,128)(2,1)S(1)}, u32[]{:S(2)}, u32[]{:S(2)}) collective-permute-start(bf16[688,128]{1,0:T(8,128)(2,1)S(1)} %get-tuple-element.36), channel_id=1, source_target_pairs={{0,24},{8,16},{16,8},{24,0},{1,25},{9,17},{17,9},{25,1},{2,26},{10... | collective-permute-start | bytes 528392 | tf_op jit(solution)/shard_map/ppermute | solution.py:532
  46.2 4.4 %prep.1 = (bf16[4,4,4,256,256]{4,3,2,1,0:T(8,128)(2,1)S(1)}, bf16[4,4,4,128,256]{4,3,2,1,0:T(8,128)(2,1)S(1)}, bf16[4,4,256,256]{3,2,1,0:T(8,128)(2,1)S(1)}, f32[4,64,256]{2,1,0:T(8,128)S(1)}) custom-call(bf16[1024,256]{1,0:T(8,128)(2,1)S(1)} %get-tuple-element.24.query_ref, bf16[64,256]{1,0:T(8,128)(2,1)S(1)} %get-tuple-element.37.logit_ref, ...), custom_call_target="tpu_custom_call" | custom-call | flops 2000000000 | bytes 4000000 | tf_op jit(solution)/shard_map/prep/pallas_call | solution.py:648
  50.6 0.0 collective-permute-done.15.refs_14_
  50.6 0.0 collective-permute-done.16.refs_15_
  50.6 2.1 %collective-permute-done.17.refs_16_ = bf16[688,128]{1,0:T(8,128)(2,1)S(1)} collective-permute-done((bf16[688,128]{1,0:T(8,128)(2,1)S(1)}, bf16[688,128]{1,0:T(8,128)(2,1)S(1)}, u32[]{:S(2)}, u32[]{:S(2)}) %collective-permute-start.17) | collective-permute-done | bytes 176160 | tf_op jit(solution)/shard_map/ppermute | solution.py:532
  52.7 3.0 %collective-permute-done.18.refs_17_ = bf16[688,128]{1,0:T(8,128)(2,1)S(1)} collective-permute-done((bf16[688,128]{1,0:T(8,128)(2,1)S(1)}, bf16[688,128]{1,0:T(8,128)(2,1)S(1)}, u32[]{:S(2)}, u32[]{:S(2)}) %collective-permute-start.18) | collective-permute-done | bytes 176160 | tf_op jit(solution)/shard_map/ppermute | solution.py:532
  55.6 1.5 %collective-permute-done.19.refs_18_ = bf16[688,128]{1,0:T(8,128)(2,1)S(1)} collective-permute-done((bf16[688,128]{1,0:T(8,128)(2,1)S(1)}, bf16[688,128]{1,0:T(8,128)(2,1)S(1)}, u32[]{:S(2)}, u32[]{:S(2)}) %collective-permute-start.19) | collective-permute-done | bytes 176160 | tf_op jit(solution)/shard_map/ppermute | solution.py:532
  57.2 0.0 copy-start.9
  57.2 0.0 copy-start.10
  57.2 7.9 %attend.1.own_ref = bf16[1024,128]{1,0:T(8,128)(2,1)S(1)} custom-call(s32[45,8]{1,0:T(8,128)S(1)} %copy.33.table_ref.refs_0_, bf16[1360,128]{1,0:T(8,128)(2,1)S(1)} %pad_maximum_fusion.refs_0_.refs_1_, bf16[1360,128]{1,0:T(8,128)(2,1)S(1)} %collective-permute-done.3.refs_0_.refs_2_, bf16[1360,128]{1,0:T(8,128)(2,1)S(1)} %collective-permute-done.4.refs_0_.refs_3_, ...), custom_call_target="tpu_custom_call" | custom-call | flops 2000000000 | bytes 4000000 | tf_op jit(solution)/shard_map/attend/pallas_call | solution.py:680
  65.1 3.5 %collective-permute-start.20 = (bf16[1024,128]{1,0:T(8,128)(2,1)S(1)}, bf16[1024,128]{1,0:T(8,128)(2,1)S(1)}, u32[]{:S(2)}, u32[]{:S(2)}) collective-permute-start(bf16[1024,128]{1,0:T(8,128)(2,1)S(1)} %attend.1.own_ref), channel_id=1, source_target_pairs={{0,1},{1,0},{2,3},{3,2},{4,5},{5,4},{6,7},{7,6},{8,9},{9,8},{10,11... | collective-permute-start | bytes 786440 | tf_op jit(solution)/shard_map/ppermute | solution.py:704
  68.6 0.7 %own.1.pre_ref = f32[1024,256]{1,0:T(8,128)S(1)} custom-call(s32[1]{0:T(128)} %bitcast.head_ref, bf16[1024,256]{1,0:T(8,128)(2,1)S(1)} %get-tuple-element.24.query_ref, bf16[1024,128]{1,0:T(8,128)(2,1)S(1)} %attend.1.own_ref, bf16[256,256]{1,0:T(8,128)(2,1)S(1)} %copy-done.2, f32[1,256]{1,0:T(1,128)S(1)} %bitcast.29), custom_call_target="tpu_custom_call" | custom-call | tf_op jit(solution)/shard_map/own/pallas_call | solution.py:708
  69.3 0.4 collective-permute-done.20.other_ref
  69.8 2.3 %norm.1 = bf16[1024,128]{1,0:T(8,128)(2,1)} custom-call(s32[1]{0:T(128)} %bitcast.head_ref, f32[1024,256]{1,0:T(8,128)S(1)} %own.1.pre_ref, bf16[1024,128]{1,0:T(8,128)(2,1)S(1)} %collective-permute-done.20.other_ref, bf16[256,256]{1,0:T(8,128)(2,1)S(1)} %copy-done.2, f32[1,128]{1,0:T(1,128)S(1)} %bitcast.30, f32[1,128]{1,0:T(1,128)S(1)} %bitcast.31), custom_call_target="tpu_custom_call" | custom-call | tf_op jit(solution)/shard_map/norm/pallas_call | solution.py:723
  (30 shorter events, 0.1 us)
Async XLA Ops:
  0.0 36.0 %copy-start.7 = (bf16[256,64]{0,1:T(8,128)(2,1)S(1)}, bf16[256,64]{0,1:T(8,128)(2,1)}, u32[]{:S(2)}) copy-start(bf16[256,64]{0,1:T(8,128)(2,1)} %param.20) | copy-start | bytes 98308
  0.0 36.0 %copy-start.1 = (s32[64,16,64]{2,1,0:T(8,128)S(1)}, s32[64,16,64]{2,1,0:T(8,128)}, u32[]{:S(2)}) copy-start(s32[64,16,64]{2,1,0:T(8,128)} %param.19) | copy-start | bytes 786436
  0.0 36.0 %copy-start = (bf16[64,16,256]{2,1,0:T(8,128)(2,1)S(1)}, bf16[64,16,256]{2,1,0:T(8,128)(2,1)}, u32[]{:S(2)}) copy-start(bf16[64,16,256]{2,1,0:T(8,128)(2,1)} %param.13) | copy-start | bytes 1572868
  1.1 17.1 %collective-permute-start.4 = (bf16[1360,128]{1,0:T(8,128)(2,1)S(1)}, bf16[1360,128]{1,0:T(8,128)(2,1)S(1)}, u32[]{:S(2)}, u32[]{:S(2)}) collective-permute-start(bf16[1360,128]{1,0:T(8,128)(2,1)S(1)} %pad_maximum_fusion.refs_0_.refs_1_), channel_id=1, source_target_pairs={{2,4},{4,2},{3,5},{5,3},{10,12},{12,10},{11,13},{13,11},{18,20},{2... | collective-permute-start | bytes 1044488 | tf_op jit(solution)/shard_map/ppermute | solution.py:485
  4.4 8.8 %collective-permute-start.3 = (bf16[1360,128]{1,0:T(8,128)(2,1)S(1)}, bf16[1360,128]{1,0:T(8,128)(2,1)S(1)}, u32[]{:S(2)}, u32[]{:S(2)}) collective-permute-start(bf16[1360,128]{1,0:T(8,128)(2,1)S(1)} %pad_maximum_fusion.refs_0_.refs_1_), channel_id=1, source_target_pairs={{0,2},{2,0},{4,6},{6,4},{1,3},{3,1},{5,7},{7,5},{8,10},{10,8},{12,... | collective-permute-start | bytes 1044488 | tf_op jit(solution)/shard_map/ppermute | solution.py:485
  13.2 9.8 %collective-permute-start.6 = (bf16[1360,128]{1,0:T(8,128)(2,1)S(1)}, bf16[1360,128]{1,0:T(8,128)(2,1)S(1)}, u32[]{:S(2)}, u32[]{:S(2)}) collective-permute-start(bf16[1360,128]{1,0:T(8,128)(2,1)S(1)} %collective-permute-done.3.refs_0_.refs_2_), channel_id=1, source_target_pairs={{2,4},{4,2},{3,5},{5,3},{10,12},{12,10},{11,13},{13,11},{18,20},{2... | collective-permute-start | bytes 1044488 | tf_op jit(solution)/shard_map/ppermute | solution.py:485
  15.5 8.8 %collective-permute-start.2 = (s32[4,8]{0,1:T(8,128)S(1)}, s32[4,8]{0,1:T(8,128)S(1)}, u32[]{:S(2)}, u32[]{:S(2)}) collective-permute-start(s32[4,8]{0,1:T(8,128)S(1)} %get-tuple-element.43), channel_id=1, source_target_pairs={{0,24},{8,16},{16,8},{24,0},{1,25},{9,17},{17,9},{25,1},{2,26},{10... | collective-permute-start | bytes 392 | tf_op jit(solution)/shard_map/ppermute | solution.py:504
  17.7 6.6 %collective-permute-start.1 = (s32[4,8]{0,1:T(8,128)S(1)}, s32[4,8]{0,1:T(8,128)S(1)}, u32[]{:S(2)}, u32[]{:S(2)}) collective-permute-start(s32[4,8]{0,1:T(8,128)S(1)} %get-tuple-element.44), channel_id=1, source_target_pairs={{0,16},{8,24},{16,0},{24,8},{1,17},{9,25},{17,1},{25,9},{2,18},{10... | collective-permute-start | bytes 392 | tf_op jit(solution)/shard_map/ppermute | solution.py:504
  17.9 6.4 %collective-permute-start = (s32[4,8]{0,1:T(8,128)S(1)}, s32[4,8]{0,1:T(8,128)S(1)}, u32[]{:S(2)}, u32[]{:S(2)}) collective-permute-start(s32[4,8]{0,1:T(8,128)S(1)} %get-tuple-element.45), channel_id=1, source_target_pairs={{0,8},{8,0},{16,24},{24,16},{1,9},{9,1},{17,25},{25,17},{2,10},{10... | collective-permute-start | bytes 392 | tf_op jit(solution)/shard_map/ppermute | solution.py:504
  18.2 11.0 %collective-permute-start.5 = (bf16[1360,128]{1,0:T(8,128)(2,1)S(1)}, bf16[1360,128]{1,0:T(8,128)(2,1)S(1)}, u32[]{:S(2)}, u32[]{:S(2)}) collective-permute-start(bf16[1360,128]{1,0:T(8,128)(2,1)S(1)} %collective-permute-done.4.refs_0_.refs_3_), channel_id=1, source_target_pairs={{2,0},{4,6},{3,1},{5,7},{10,8},{12,14},{11,9},{13,15},{18,16},{20,... | collective-permute-start | bytes 1044488 | tf_op jit(solution)/shard_map/ppermute | solution.py:485
  23.0 11.1 %collective-permute-start.7 = (bf16[1360,128]{1,0:T(8,128)(2,1)S(1)}, bf16[1360,128]{1,0:T(8,128)(2,1)S(1)}, u32[]{:S(2)}, u32[]{:S(2)}) collective-permute-start(bf16[1360,128]{1,0:T(8,128)(2,1)S(1)} %collective-permute-done.6.refs_1_.refs_5_), channel_id=1, source_target_pairs={{2,0},{4,6},{3,1},{5,7},{10,8},{12,14},{11,9},{13,15},{18,16},{20,... | collective-permute-start | bytes 1044488 | tf_op jit(solution)/shard_map/ppermute | solution.py:485
  24.5 21.7 %copy-start.11 = (f32[64]{0:T(128)S(1)}, f32[64]{0:T(128)}, u32[]{:S(2)}) copy-start(f32[64]{0:T(128)} %param.21) | copy-start | bytes 772
  25.5 6.0 %collective-permute-start.8 = (bf16[688,128]{1,0:T(8,128)(2,1)S(1)}, bf16[688,128]{1,0:T(8,128)(2,1)S(1)}, u32[]{:S(2)}, u32[]{:S(2)}) collective-permute-start(bf16[688,128]{1,0:T(8,128)(2,1)S(1)} %get-tuple-element.25), channel_id=1, source_target_pairs={{0,8},{8,0},{16,24},{24,16},{1,9},{9,1},{17,25},{25,17},{2,10},{10... | collective-permute-start | bytes 528392 | tf_op jit(solution)/shard_map/ppermute | solution.py:532
  26.8 6.0 %collective-permute-start.9 = (bf16[688,128]{1,0:T(8,128)(2,1)S(1)}, bf16[688,128]{1,0:T(8,128)(2,1)S(1)}, u32[]{:S(2)}, u32[]{:S(2)}) collective-permute-start(bf16[688,128]{1,0:T(8,128)(2,1)S(1)} %get-tuple-element.26), channel_id=1, source_target_pairs={{0,16},{8,24},{16,0},{24,8},{1,17},{9,25},{17,1},{25,9},{2,18},{10... | collective-permute-start | bytes 528392 | tf_op jit(solution)/shard_map/ppermute | solution.py:532
  28.0 10.2 %collective-permute-start.10 = (bf16[688,128]{1,0:T(8,128)(2,1)S(1)}, bf16[688,128]{1,0:T(8,128)(2,1)S(1)}, u32[]{:S(2)}, u32[]{:S(2)}) collective-permute-start(bf16[688,128]{1,0:T(8,128)(2,1)S(1)} %get-tuple-element.27), channel_id=1, source_target_pairs={{0,24},{8,16},{16,8},{24,0},{1,25},{9,17},{17,9},{25,1},{2,26},{10... | collective-permute-start | bytes 528392 | tf_op jit(solution)/shard_map/ppermute | solution.py:532
  29.2 9.2 %collective-permute-start.11 = (bf16[688,128]{1,0:T(8,128)(2,1)S(1)}, bf16[688,128]{1,0:T(8,128)(2,1)S(1)}, u32[]{:S(2)}, u32[]{:S(2)}) collective-permute-start(bf16[688,128]{1,0:T(8,128)(2,1)S(1)} %get-tuple-element.28), channel_id=1, source_target_pairs={{0,8},{8,0},{16,24},{24,16},{1,9},{9,1},{17,25},{25,17},{2,10},{10... | collective-permute-start | bytes 528392 | tf_op jit(solution)/shard_map/ppermute | solution.py:532
  31.5 9.2 %collective-permute-start.12 = (bf16[688,128]{1,0:T(8,128)(2,1)S(1)}, bf16[688,128]{1,0:T(8,128)(2,1)S(1)}, u32[]{:S(2)}, u32[]{:S(2)}) collective-permute-start(bf16[688,128]{1,0:T(8,128)(2,1)S(1)} %get-tuple-element.29), channel_id=1, source_target_pairs={{0,16},{8,24},{16,0},{24,8},{1,17},{9,25},{17,1},{25,9},{2,18},{10... | collective-permute-start | bytes 528392 | tf_op jit(solution)/shard_map/ppermute | solution.py:532
  32.8 9.1 %collective-permute-start.13 = (bf16[688,128]{1,0:T(8,128)(2,1)S(1)}, bf16[688,128]{1,0:T(8,128)(2,1)S(1)}, u32[]{:S(2)}, u32[]{:S(2)}) collective-permute-start(bf16[688,128]{1,0:T(8,128)(2,1)S(1)} %get-tuple-element.30), channel_id=1, source_target_pairs={{0,24},{8,16},{16,8},{24,0},{1,25},{9,17},{17,9},{25,1},{2,26},{10... | collective-permute-start | bytes 528392 | tf_op jit(solution)/shard_map/ppermute | solution.py:532
  34.0 0.7 %copy-start.3 = (bf16[1360,128]{1,0:T(8,128)(2,1)}, bf16[1360,128]{1,0:T(8,128)(2,1)S(1)}, u32[]{:S(2)}) copy-start(bf16[1360,128]{1,0:T(8,128)(2,1)S(1)} %collective-permute-done.7.refs_0_.refs_6_) | copy-start | bytes 1044484
  34.8 10.3 %collective-permute-start.14 = (bf16[688,128]{1,0:T(8,128)(2,1)S(1)}, bf16[688,128]{1,0:T(8,128)(2,1)S(1)}, u32[]{:S(2)}, u32[]{:S(2)}) collective-permute-start(bf16[688,128]{1,0:T(8,128)(2,1)S(1)} %get-tuple-element.31), channel_id=1, source_target_pairs={{0,8},{8,0},{16,24},{24,16},{1,9},{9,1},{17,25},{25,17},{2,10},{10... | collective-permute-start | bytes 528392 | tf_op jit(solution)/shard_map/ppermute | solution.py:532
  36.2 1.0 %copy-start.4 = (bf16[1360,128]{1,0:T(8,128)(2,1)S(1)}, bf16[1360,128]{1,0:T(8,128)(2,1)}, u32[]{:S(2)}) copy-start(bf16[1360,128]{1,0:T(8,128)(2,1)} %copy-done.3) | copy-start | bytes 1044484
  37.2 20.0 %copy-start.5 = (bf16[1360,128]{1,0:T(8,128)(2,1)S(1)}, bf16[1360,128]{1,0:T(8,128)(2,1)}, u32[]{:S(2)}) copy-start(bf16[1360,128]{1,0:T(8,128)(2,1)} %copy-done.3) | copy-start | bytes 1044484
  37.2 20.0 %copy-start.6 = (s32[4,1,4,8]{3,2,1,0:T(4,128)S(1)}, s32[4,1,4,8]{3,2,1,0:T(4,128)}, u32[]{:S(2)}) copy-start(s32[4,1,4,8]{3,2,1,0:T(4,128)} %refs_23_.1) | copy-start | bytes 1540
  38.2 12.4 %collective-permute-start.15 = (bf16[688,128]{1,0:T(8,128)(2,1)S(1)}, bf16[688,128]{1,0:T(8,128)(2,1)S(1)}, u32[]{:S(2)}, u32[]{:S(2)}) collective-permute-start(bf16[688,128]{1,0:T(8,128)(2,1)S(1)} %get-tuple-element.32), channel_id=1, source_target_pairs={{0,16},{8,24},{16,0},{24,8},{1,17},{9,25},{17,1},{25,9},{2,18},{10... | collective-permute-start | bytes 528392 | tf_op jit(solution)/shard_map/ppermute | solution.py:532
  38.4 12.1 %collective-permute-start.16 = (bf16[688,128]{1,0:T(8,128)(2,1)S(1)}, bf16[688,128]{1,0:T(8,128)(2,1)S(1)}, u32[]{:S(2)}, u32[]{:S(2)}) collective-permute-start(bf16[688,128]{1,0:T(8,128)(2,1)S(1)} %get-tuple-element.33), channel_id=1, source_target_pairs={{0,24},{8,16},{16,8},{24,0},{1,25},{9,17},{17,9},{25,1},{2,26},{10... | collective-permute-start | bytes 528392 | tf_op jit(solution)/shard_map/ppermute | solution.py:532
  40.7 11.9 %collective-permute-start.17 = (bf16[688,128]{1,0:T(8,128)(2,1)S(1)}, bf16[688,128]{1,0:T(8,128)(2,1)S(1)}, u32[]{:S(2)}, u32[]{:S(2)}) collective-permute-start(bf16[688,128]{1,0:T(8,128)(2,1)S(1)} %get-tuple-element.34), channel_id=1, source_target_pairs={{0,8},{8,0},{16,24},{24,16},{1,9},{9,1},{17,25},{25,17},{2,10},{10... | collective-permute-start | bytes 528392 | tf_op jit(solution)/shard_map/ppermute | solution.py:532
  42.0 13.7 %collective-permute-start.18 = (bf16[688,128]{1,0:T(8,128)(2,1)S(1)}, bf16[688,128]{1,0:T(8,128)(2,1)S(1)}, u32[]{:S(2)}, u32[]{:S(2)}) collective-permute-start(bf16[688,128]{1,0:T(8,128)(2,1)S(1)} %get-tuple-element.35), channel_id=1, source_target_pairs={{0,16},{8,24},{16,0},{24,8},{1,17},{9,25},{17,1},{25,9},{2,18},{10... | collective-permute-start | bytes 528392 | tf_op jit(solution)/shard_map/ppermute | solution.py:532
  45.1 12.1 %collective-permute-start.19 = (bf16[688,128]{1,0:T(8,128)(2,1)S(1)}, bf16[688,128]{1,0:T(8,128)(2,1)S(1)}, u32[]{:S(2)}, u32[]{:S(2)}) collective-permute-start(bf16[688,128]{1,0:T(8,128)(2,1)S(1)} %get-tuple-element.36), channel_id=1, source_target_pairs={{0,24},{8,16},{16,8},{24,0},{1,25},{9,17},{17,9},{25,1},{2,26},{10... | collective-permute-start | bytes 528392 | tf_op jit(solution)/shard_map/ppermute | solution.py:532
  57.2 11.4 %copy-start.2 = (bf16[256,256]{1,0:T(8,128)(2,1)S(1)}, bf16[256,256]{1,0:T(8,128)(2,1)}, u32[]{:S(2)}) copy-start(bf16[256,256]{1,0:T(8,128)(2,1)} %weight_ref.3) | copy-start | bytes 393220
  57.2 11.4 %copy-start.8 = (f32[256]{0:T(256)S(1)}, f32[256]{0:T(256)}, u32[]{:S(2)}) copy-start(f32[256]{0:T(256)} %param.23) | copy-start | bytes 3076
  57.2 12.6 %copy-start.9 = (f32[128]{0:T(128)S(1)}, f32[128]{0:T(128)}, u32[]{:S(2)}) copy-start(f32[128]{0:T(128)} %param.24) | copy-start | bytes 1540
  57.2 12.6 %copy-start.10 = (f32[128]{0:T(128)S(1)}, f32[128]{0:T(128)}, u32[]{:S(2)}) copy-start(f32[128]{0:T(128)} %param.25) | copy-start | bytes 1540
  65.1 4.7 %collective-permute-start.20 = (bf16[1024,128]{1,0:T(8,128)(2,1)S(1)}, bf16[1024,128]{1,0:T(8,128)(2,1)S(1)}, u32[]{:S(2)}, u32[]{:S(2)}) collective-permute-start(bf16[1024,128]{1,0:T(8,128)(2,1)S(1)} %attend.1.own_ref), channel_id=1, source_target_pairs={{0,1},{1,0},{2,3},{3,2},{4,5},{5,4},{6,7},{7,6},{8,9},{9,8},{10,11... | collective-permute-start | bytes 786440 | tf_op jit(solution)/shard_map/ppermute | solution.py:704

commit v11 on v10

--- a/solution.py
+++ b/solution.py
@@ -720,12 +720,13 @@
         compiler_params=pltpu.CompilerParams(vmem_limit_bytes=SELECT_VMEM),
         name="own",
     )(own_head, queries_blocked, attn, output_weight, output_bias.reshape(1, width_all))
+    merged = 2 if blocks % 2 == 0 else 1
     updated = pl.pallas_call(
         norm_kernel,
         out_shape=jax.ShapeDtypeStruct((blocks * pixels, channels), jnp.bfloat16),
-        grid=(blocks,),
+        grid=(blocks // merged,),
         in_specs=[pl.BlockSpec(memory_space=SMEM)] + [whole] * 5,
-        out_specs=slim_spec,
+        out_specs=pl.BlockSpec((merged * pixels, channels), lambda i: (i, 0)),
         compiler_params=pltpu.CompilerParams(vmem_limit_bytes=SELECT_VMEM),
         name="norm",
     )(

time: 72.3 us -> 71.5 us (0.989)
  Pallas kernels: 19.4 us -> 18.5 us
    pallas_call x1, Pallas kernels: 2.32 us -> 1.45 us  [on_device(): pl.pallas_call(norm_kernel, out_shape=jax.ShapeDtypeStruct((blocks * pixe...]
where the time goes in v11:
time: 71.5 us; the launch traced here: 71.2 us
  starting transfers between devices  25.5 us (36%)
  waiting for transfers between devices  22.3 us (31%)
  Pallas kernels  18.5 us (26%)
  local copies, waits for them, and re-layouts  2.74 us (4%)
  other arithmetic  1.86 us (3%)
    ppermute x12, starting transfers between devices, relay_tiles(): lax.ppermute(sent[number - 1], 'row', [(row, source_of(row, number)) for...  11.3 us
    ppermute x12, waiting for transfers between devices, relay_tiles(): lax.ppermute(sent[number - 1], 'row', [(row, source_of(row, number)) for...  11.1 us
    ppermute x5, waiting for transfers between devices, move(): held[name] = lax.ppermute(held[source or 'own'], 'col', pairs)  10.8 us
    ppermute x5, starting transfers between devices, move(): held[name] = lax.ppermute(held[source or 'own'], 'col', pairs)  7.94 us
    pallas_call x1, Pallas kernels, on_device(): pl.pallas_call(functools.partial(attend_kernel, dims, grid, gather, len(s...  7.86 us
    pallas_call x1, Pallas kernels, on_device(): pl.pallas_call(functools.partial(prep_kernel, dims), out_shape=[jax.Shape...  4.35 us
    pallas_call x4, Pallas kernels, relay_tiles(): pl.pallas_call(functools.partial(relay_select_kernel, (row_count - 1, len...  3.97 us
    ppermute x1, starting transfers between devices, on_device(): other = lax.ppermute(attn, 'head', [(0, 1), (1, 0)])  3.53 us
  transfers between devices with their start and end apart: 21, of which 9 were waited for; matrix products, arithmetic and copies ran while one was open for 2% of the time, Pallas kernels for 13%

profile of v11, /device:TPU:9, one launch (start us, length us, event | category | flops | bytes accessed | tf_op | source)
XLA Modules:
  0.0 71.2 jit_solution(870691976421553137)
XLA Ops:
  0.0 1.1 %pad_maximum_fusion.refs_0_.refs_1_ = bf16[1360,128]{1,0:T(8,128)(2,1)S(1)} fusion(bf16[16,128]{1,0:T(8,128)(2,1)} %bitcast.37, bf16[64,128]{1,0:T(8,128)(2,1)} %bitcast.36, bf16[256,128]{1,0:T(8,128)(2,1)} %bitcast.34, bf16[1024,128]{1,0:T(8,128)(2,1)} %bitcast.33), kind=kLoop, calls=%fused_computation | loop fusion | flops 1392640 | bytes 696320 | tf_op jit(solution)/shard_map/concatenate | solution.py:481
  1.1 3.2 %collective-permute-start.4 = (bf16[1360,128]{1,0:T(8,128)(2,1)S(1)}, bf16[1360,128]{1,0:T(8,128)(2,1)S(1)}, u32[]{:S(2)}, u32[]{:S(2)}) collective-permute-start(bf16[1360,128]{1,0:T(8,128)(2,1)S(1)} %pad_maximum_fusion.refs_0_.refs_1_), channel_id=1, source_target_pairs={{2,4},{4,2},{3,5},{5,3},{10,12},{12,10},{11,13},{13,11},{18,20},{2... | collective-permute-start | bytes 1044488 | tf_op jit(solution)/shard_map/ppermute | solution.py:485
  4.4 0.1 collective-permute-start.3
  4.5 0.7 %slice_bitcast_fusion.3 = (s32[4,8]{1,0:T(4,128)S(1)}, s32[4,8]{1,0:T(4,128)S(1)}, s32[4,8]{1,0:T(4,128)S(1)}, s32[4,8]{1,0:T(4,128)S(1)}) fusion(s32[1,4,4,8]{3,2,1,0:T(4,128)} %bitcast.27), kind=kLoop, calls=%fused_computation.43 | loop fusion | bytes 1024 | tf_op jit(solution)/shard_map/concatenate | solution.py:429
  5.2 0.1 fusion.8
  5.3 0.2 convert_reduce_fusion
  5.6 0.2 select_reduce_fusion
  5.8 7.4 %collective-permute-done.3.refs_0_.refs_2_ = bf16[1360,128]{1,0:T(8,128)(2,1)S(1)} collective-permute-done((bf16[1360,128]{1,0:T(8,128)(2,1)S(1)}, bf16[1360,128]{1,0:T(8,128)(2,1)S(1)}, u32[]{:S(2)}, u32[]{:S(2)}) %collective-permute-start.3) | collective-permute-done | bytes 348192 | tf_op jit(solution)/shard_map/ppermute | solution.py:485
  13.2 2.1 %collective-permute-start.6 = (bf16[1360,128]{1,0:T(8,128)(2,1)S(1)}, bf16[1360,128]{1,0:T(8,128)(2,1)S(1)}, u32[]{:S(2)}, u32[]{:S(2)}) collective-permute-start(bf16[1360,128]{1,0:T(8,128)(2,1)S(1)} %collective-permute-done.3.refs_0_.refs_2_), channel_id=1, source_target_pairs={{2,4},{4,2},{3,5},{5,3},{10,12},{12,10},{11,13},{13,11},{18,20},{2... | collective-permute-start | bytes 1044488 | tf_op jit(solution)/shard_map/ppermute | solution.py:485
  15.3 0.1 sub.29
  15.4 0.1 select_reduce_fusion.1
  15.5 2.2 %collective-permute-start.2 = (s32[4,8]{0,1:T(8,128)S(1)}, s32[4,8]{0,1:T(8,128)S(1)}, u32[]{:S(2)}, u32[]{:S(2)}) collective-permute-start(s32[4,8]{0,1:T(8,128)S(1)} %get-tuple-element.43), channel_id=1, source_target_pairs={{0,24},{8,16},{16,8},{24,0},{1,25},{9,17},{17,9},{25,1},{2,26},{10... | collective-permute-start | bytes 392 | tf_op jit(solution)/shard_map/ppermute | solution.py:504
  17.7 0.2 collective-permute-start.1
  17.9 0.3 collective-permute-start
  18.2 0.0 collective-permute-done.4.refs_0_.refs_3_
  18.2 1.3 %collective-permute-start.5 = (bf16[1360,128]{1,0:T(8,128)(2,1)S(1)}, bf16[1360,128]{1,0:T(8,128)(2,1)S(1)}, u32[]{:S(2)}, u32[]{:S(2)}) collective-permute-start(bf16[1360,128]{1,0:T(8,128)(2,1)S(1)} %collective-permute-done.4.refs_0_.refs_3_), channel_id=1, source_target_pairs={{2,0},{4,6},{3,1},{5,7},{10,8},{12,14},{11,9},{13,15},{18,16},{20,... | collective-permute-start | bytes 1044488 | tf_op jit(solution)/shard_map/ppermute | solution.py:485
  19.5 3.4 %collective-permute-done.6.refs_1_.refs_5_ = bf16[1360,128]{1,0:T(8,128)(2,1)S(1)} collective-permute-done((bf16[1360,128]{1,0:T(8,128)(2,1)S(1)}, bf16[1360,128]{1,0:T(8,128)(2,1)S(1)}, u32[]{:S(2)}, u32[]{:S(2)}) %collective-permute-start.6) | collective-permute-done | bytes 348192 | tf_op jit(solution)/shard_map/ppermute | solution.py:485
  23.0 1.3 %collective-permute-start.7 = (bf16[1360,128]{1,0:T(8,128)(2,1)S(1)}, bf16[1360,128]{1,0:T(8,128)(2,1)S(1)}, u32[]{:S(2)}, u32[]{:S(2)}) collective-permute-start(bf16[1360,128]{1,0:T(8,128)(2,1)S(1)} %collective-permute-done.6.refs_1_.refs_5_), channel_id=1, source_target_pairs={{2,0},{4,6},{3,1},{5,7},{10,8},{12,14},{11,9},{13,15},{18,16},{20,... | collective-permute-start | bytes 1044488 | tf_op jit(solution)/shard_map/ppermute | solution.py:485
  24.3 0.0 collective-permute-done.2
  24.3 0.0 collective-permute-done.1
  24.3 0.0 collective-permute-done
  24.3 0.1 concatenate.157
  24.4 0.1 copy.33.table_ref.refs_0_
  24.5 1.0 %shard_map.127 = (bf16[688,128]{1,0:T(8,128)(2,1)S(1)}, bf16[688,128]{1,0:T(8,128)(2,1)S(1)}, bf16[688,128]{1,0:T(8,128)(2,1)S(1)}) custom-call(s32[45,8]{1,0:T(8,128)S(1)} %copy.33.table_ref.refs_0_, bf16[1360,128]{1,0:T(8,128)(2,1)S(1)} %pad_maximum_fusion.refs_0_.refs_1_), custom_call_target="tpu_custom_call" | custom-call | flops 500000000 | bytes 1000000 | tf_op jit(solution)/shard_map/pallas_call | solution.py:520
  25.5 1.3 %collective-permute-start.8 = (bf16[688,128]{1,0:T(8,128)(2,1)S(1)}, bf16[688,128]{1,0:T(8,128)(2,1)S(1)}, u32[]{:S(2)}, u32[]{:S(2)}) collective-permute-start(bf16[688,128]{1,0:T(8,128)(2,1)S(1)} %get-tuple-element.25), channel_id=1, source_target_pairs={{0,8},{8,0},{16,24},{24,16},{1,9},{9,1},{17,25},{25,17},{2,10},{10... | collective-permute-start | bytes 528392 | tf_op jit(solution)/shard_map/ppermute | solution.py:532
  26.8 1.2 %collective-permute-start.9 = (bf16[688,128]{1,0:T(8,128)(2,1)S(1)}, bf16[688,128]{1,0:T(8,128)(2,1)S(1)}, u32[]{:S(2)}, u32[]{:S(2)}) collective-permute-start(bf16[688,128]{1,0:T(8,128)(2,1)S(1)} %get-tuple-element.26), channel_id=1, source_target_pairs={{0,16},{8,24},{16,0},{24,8},{1,17},{9,25},{17,1},{25,9},{2,18},{10... | collective-permute-start | bytes 528392 | tf_op jit(solution)/shard_map/ppermute | solution.py:532
  28.0 0.2 collective-permute-start.10
  28.2 1.0 %shard_map.128 = (bf16[688,128]{1,0:T(8,128)(2,1)S(1)}, bf16[688,128]{1,0:T(8,128)(2,1)S(1)}, bf16[688,128]{1,0:T(8,128)(2,1)S(1)}) custom-call(s32[45,8]{1,0:T(8,128)S(1)} %copy.33.table_ref.refs_0_, bf16[1360,128]{1,0:T(8,128)(2,1)S(1)} %collective-permute-done.3.refs_0_.refs_2_), custom_call_target="tpu_custom_call" | custom-call | flops 500000000 | bytes 1000000 | tf_op jit(solution)/shard_map/pallas_call | solution.py:520
  29.2 0.0 collective-permute-done.5.refs_1_.refs_4_
  29.2 1.3 %collective-permute-start.11 = (bf16[688,128]{1,0:T(8,128)(2,1)S(1)}, bf16[688,128]{1,0:T(8,128)(2,1)S(1)}, u32[]{:S(2)}, u32[]{:S(2)}) collective-permute-start(bf16[688,128]{1,0:T(8,128)(2,1)S(1)} %get-tuple-element.28), channel_id=1, source_target_pairs={{0,8},{8,0},{16,24},{24,16},{1,9},{9,1},{17,25},{25,17},{2,10},{10... | collective-permute-start | bytes 528392 | tf_op jit(solution)/shard_map/ppermute | solution.py:532
  30.5 1.0 %shard_map.129 = (bf16[688,128]{1,0:T(8,128)(2,1)S(1)}, bf16[688,128]{1,0:T(8,128)(2,1)S(1)}, bf16[688,128]{1,0:T(8,128)(2,1)S(1)}) custom-call(s32[45,8]{1,0:T(8,128)S(1)} %copy.33.table_ref.refs_0_, bf16[1360,128]{1,0:T(8,128)(2,1)S(1)} %collective-permute-done.4.refs_0_.refs_3_, bf16[1360,128]{1,0:T(8,128)(2,1)S(1)} %collective-permute-done.5.refs_1_.refs_4_), custom_call_target="tpu_custom_call" | custom-call | flops 500000000 | bytes 1000000 | tf_op jit(solution)/shard_map/pallas_call | solution.py:520
  31.5 0.0 collective-permute-done.8.refs_7_
  31.5 1.3 %collective-permute-start.12 = (bf16[688,128]{1,0:T(8,128)(2,1)S(1)}, bf16[688,128]{1,0:T(8,128)(2,1)S(1)}, u32[]{:S(2)}, u32[]{:S(2)}) collective-permute-start(bf16[688,128]{1,0:T(8,128)(2,1)S(1)} %get-tuple-element.29), channel_id=1, source_target_pairs={{0,16},{8,24},{16,0},{24,8},{1,17},{9,25},{17,1},{25,9},{2,18},{10... | collective-permute-start | bytes 528392 | tf_op jit(solution)/shard_map/ppermute | solution.py:532
  32.8 0.0 collective-permute-done.9.refs_8_
  32.8 1.2 %collective-permute-start.13 = (bf16[688,128]{1,0:T(8,128)(2,1)S(1)}, bf16[688,128]{1,0:T(8,128)(2,1)S(1)}, u32[]{:S(2)}, u32[]{:S(2)}) collective-permute-start(bf16[688,128]{1,0:T(8,128)(2,1)S(1)} %get-tuple-element.30), channel_id=1, source_target_pairs={{0,24},{8,16},{16,8},{24,0},{1,25},{9,17},{17,9},{25,1},{2,26},{10... | collective-permute-start | bytes 528392 | tf_op jit(solution)/shard_map/ppermute | solution.py:532
  34.0 0.0 collective-permute-done.7.refs_0_.refs_6_
  34.0 0.7 %copy-done.3 = bf16[1360,128]{1,0:T(8,128)(2,1)} copy-done((bf16[1360,128]{1,0:T(8,128)(2,1)}, bf16[1360,128]{1,0:T(8,128)(2,1)S(1)}, u32[]{:S(2)}) %copy-start.3) | copy-done | bytes 348184
  34.8 1.2 %collective-permute-start.14 = (bf16[688,128]{1,0:T(8,128)(2,1)S(1)}, bf16[688,128]{1,0:T(8,128)(2,1)S(1)}, u32[]{:S(2)}, u32[]{:S(2)}) collective-permute-start(bf16[688,128]{1,0:T(8,128)(2,1)S(1)} %get-tuple-element.31), channel_id=1, source_target_pairs={{0,8},{8,0},{16,24},{24,16},{1,9},{9,1},{17,25},{25,17},{2,10},{10... | collective-permute-start | bytes 528392 | tf_op jit(solution)/shard_map/ppermute | solution.py:532
  36.0 0.1 load.1
  36.2 1.0 %copy-done.4 = bf16[1360,128]{1,0:T(8,128)(2,1)S(1)} copy-done((bf16[1360,128]{1,0:T(8,128)(2,1)S(1)}, bf16[1360,128]{1,0:T(8,128)(2,1)}, u32[]{:S(2)}) %copy-start.4) | copy-done | bytes 348184
  37.2 1.0 %shard_map.130 = (bf16[688,128]{1,0:T(8,128)(2,1)S(1)}, bf16[688,128]{1,0:T(8,128)(2,1)S(1)}, bf16[688,128]{1,0:T(8,128)(2,1)S(1)}) custom-call(s32[45,8]{1,0:T(8,128)S(1)} %copy.33.table_ref.refs_0_, bf16[1360,128]{1,0:T(8,128)(2,1)S(1)} %copy-done.4, bf16[1360,128]{1,0:T(8,128)(2,1)S(1)} %collective-permute-done.6.refs_1_.refs_5_), custom_call_target="tpu_custom_call" | custom-call | flops 500000000 | bytes 1000000 | tf_op jit(solution)/shard_map/pallas_call | solution.py:520
  38.2 0.0 collective-permute-done.10.refs_9_
  38.2 0.3 collective-permute-start.15
  38.4 0.0 collective-permute-done.11.refs_10_
  38.4 1.2 %collective-permute-start.16 = (bf16[688,128]{1,0:T(8,128)(2,1)S(1)}, bf16[688,128]{1,0:T(8,128)(2,1)S(1)}, u32[]{:S(2)}, u32[]{:S(2)}) collective-permute-start(bf16[688,128]{1,0:T(8,128)(2,1)S(1)} %get-tuple-element.33), channel_id=1, source_target_pairs={{0,24},{8,16},{16,8},{24,0},{1,25},{9,17},{17,9},{25,1},{2,26},{10... | collective-permute-start | bytes 528392 | tf_op jit(solution)/shard_map/ppermute | solution.py:532
  39.7 1.1 %collective-permute-done.12.refs_11_ = bf16[688,128]{1,0:T(8,128)(2,1)S(1)} collective-permute-done((bf16[688,128]{1,0:T(8,128)(2,1)S(1)}, bf16[688,128]{1,0:T(8,128)(2,1)S(1)}, u32[]{:S(2)}, u32[]{:S(2)}) %collective-permute-start.12) | collective-permute-done | bytes 176160 | tf_op jit(solution)/shard_map/ppermute | solution.py:532
  40.7 0.2 collective-permute-start.17
  40.9 1.1 %collective-permute-done.13.refs_12_ = bf16[688,128]{1,0:T(8,128)(2,1)S(1)} collective-permute-done((bf16[688,128]{1,0:T(8,128)(2,1)S(1)}, bf16[688,128]{1,0:T(8,128)(2,1)S(1)}, u32[]{:S(2)}, u32[]{:S(2)}) %collective-permute-start.13) | collective-permute-done | bytes 176160 | tf_op jit(solution)/shard_map/ppermute | solution.py:532
  42.0 0.8 %collective-permute-start.18 = (bf16[688,128]{1,0:T(8,128)(2,1)S(1)}, bf16[688,128]{1,0:T(8,128)(2,1)S(1)}, u32[]{:S(2)}, u32[]{:S(2)}) collective-permute-start(bf16[688,128]{1,0:T(8,128)(2,1)S(1)} %get-tuple-element.35), channel_id=1, source_target_pairs={{0,16},{8,24},{16,0},{24,8},{1,17},{9,25},{17,1},{25,9},{2,18},{10... | collective-permute-start | bytes 528392 | tf_op jit(solution)/shard_map/ppermute | solution.py:532
  42.7 2.3 %collective-permute-done.14.refs_13_ = bf16[688,128]{1,0:T(8,128)(2,1)S(1)} collective-permute-done((bf16[688,128]{1,0:T(8,128)(2,1)S(1)}, bf16[688,128]{1,0:T(8,128)(2,1)S(1)}, u32[]{:S(2)}, u32[]{:S(2)}) %collective-permute-start.14) | collective-permute-done | bytes 176160 | tf_op jit(solution)/shard_map/ppermute | solution.py:532
  45.1 1.1 %collective-permute-start.19 = (bf16[688,128]{1,0:T(8,128)(2,1)S(1)}, bf16[688,128]{1,0:T(8,128)(2,1)S(1)}, u32[]{:S(2)}, u32[]{:S(2)}) collective-permute-start(bf16[688,128]{1,0:T(8,128)(2,1)S(1)} %get-tuple-element.36), channel_id=1, source_target_pairs={{0,24},{8,16},{16,8},{24,0},{1,25},{9,17},{17,9},{25,1},{2,26},{10... | collective-permute-start | bytes 528392 | tf_op jit(solution)/shard_map/ppermute | solution.py:532
  46.2 4.4 %prep.1 = (bf16[4,4,4,256,256]{4,3,2,1,0:T(8,128)(2,1)S(1)}, bf16[4,4,4,128,256]{4,3,2,1,0:T(8,128)(2,1)S(1)}, bf16[4,4,256,256]{3,2,1,0:T(8,128)(2,1)S(1)}, f32[4,64,256]{2,1,0:T(8,128)S(1)}) custom-call(bf16[1024,256]{1,0:T(8,128)(2,1)S(1)} %get-tuple-element.24.query_ref, bf16[64,256]{1,0:T(8,128)(2,1)S(1)} %get-tuple-element.37.logit_ref, ...), custom_call_target="tpu_custom_call" | custom-call | flops 2000000000 | bytes 4000000 | tf_op jit(solution)/shard_map/prep/pallas_call | solution.py:648
  50.6 0.0 collective-permute-done.15.refs_14_
  50.6 0.0 collective-permute-done.16.refs_15_
  50.6 2.1 %collective-permute-done.17.refs_16_ = bf16[688,128]{1,0:T(8,128)(2,1)S(1)} collective-permute-done((bf16[688,128]{1,0:T(8,128)(2,1)S(1)}, bf16[688,128]{1,0:T(8,128)(2,1)S(1)}, u32[]{:S(2)}, u32[]{:S(2)}) %collective-permute-start.17) | collective-permute-done | bytes 176160 | tf_op jit(solution)/shard_map/ppermute | solution.py:532
  52.7 3.0 %collective-permute-done.18.refs_17_ = bf16[688,128]{1,0:T(8,128)(2,1)S(1)} collective-permute-done((bf16[688,128]{1,0:T(8,128)(2,1)S(1)}, bf16[688,128]{1,0:T(8,128)(2,1)S(1)}, u32[]{:S(2)}, u32[]{:S(2)}) %collective-permute-start.18) | collective-permute-done | bytes 176160 | tf_op jit(solution)/shard_map/ppermute | solution.py:532
  55.6 1.5 %collective-permute-done.19.refs_18_ = bf16[688,128]{1,0:T(8,128)(2,1)S(1)} collective-permute-done((bf16[688,128]{1,0:T(8,128)(2,1)S(1)}, bf16[688,128]{1,0:T(8,128)(2,1)S(1)}, u32[]{:S(2)}, u32[]{:S(2)}) %collective-permute-start.19) | collective-permute-done | bytes 176160 | tf_op jit(solution)/shard_map/ppermute | solution.py:532
  57.2 0.0 copy-start.9
  57.2 0.0 copy-start.10
  57.2 7.9 %attend.1.own_ref = bf16[1024,128]{1,0:T(8,128)(2,1)S(1)} custom-call(s32[45,8]{1,0:T(8,128)S(1)} %copy.33.table_ref.refs_0_, bf16[1360,128]{1,0:T(8,128)(2,1)S(1)} %pad_maximum_fusion.refs_0_.refs_1_, bf16[1360,128]{1,0:T(8,128)(2,1)S(1)} %collective-permute-done.3.refs_0_.refs_2_, bf16[1360,128]{1,0:T(8,128)(2,1)S(1)} %collective-permute-done.4.refs_0_.refs_3_, ...), custom_call_target="tpu_custom_call" | custom-call | flops 2000000000 | bytes 4000000 | tf_op jit(solution)/shard_map/attend/pallas_call | solution.py:680
  65.1 3.5 %collective-permute-start.20 = (bf16[1024,128]{1,0:T(8,128)(2,1)S(1)}, bf16[1024,128]{1,0:T(8,128)(2,1)S(1)}, u32[]{:S(2)}, u32[]{:S(2)}) collective-permute-start(bf16[1024,128]{1,0:T(8,128)(2,1)S(1)} %attend.1.own_ref), channel_id=1, source_target_pairs={{0,1},{1,0},{2,3},{3,2},{4,5},{5,4},{6,7},{7,6},{8,9},{9,8},{10,11... | collective-permute-start | bytes 786440 | tf_op jit(solution)/shard_map/ppermute | solution.py:704
  68.6 0.7 %own.1.pre_ref = f32[1024,256]{1,0:T(8,128)S(1)} custom-call(s32[1]{0:T(128)} %bitcast.head_ref, bf16[1024,256]{1,0:T(8,128)(2,1)S(1)} %get-tuple-element.24.query_ref, bf16[1024,128]{1,0:T(8,128)(2,1)S(1)} %attend.1.own_ref, bf16[256,256]{1,0:T(8,128)(2,1)S(1)} %copy-done.2, f32[1,256]{1,0:T(1,128)S(1)} %bitcast.29), custom_call_target="tpu_custom_call" | custom-call | tf_op jit(solution)/shard_map/own/pallas_call | solution.py:708
  69.3 0.4 collective-permute-done.20.other_ref
  69.8 1.5 %norm.1 = bf16[1024,128]{1,0:T(8,128)(2,1)} custom-call(s32[1]{0:T(128)} %bitcast.head_ref, f32[1024,256]{1,0:T(8,128)S(1)} %own.1.pre_ref, bf16[1024,128]{1,0:T(8,128)(2,1)S(1)} %collective-permute-done.20.other_ref, bf16[256,256]{1,0:T(8,128)(2,1)S(1)} %copy-done.2, f32[1,128]{1,0:T(1,128)S(1)} %bitcast.30, f32[1,128]{1,0:T(1,128)S(1)} %bitcast.31), custom_call_target="tpu_custom_call" | custom-call | tf_op jit(solution)/shard_map/norm/pallas_call | solution.py:724
  (30 shorter events, 0.1 us)
Async XLA Ops:
  0.0 36.0 %copy-start.7 = (bf16[256,64]{0,1:T(8,128)(2,1)S(1)}, bf16[256,64]{0,1:T(8,128)(2,1)}, u32[]{:S(2)}) copy-start(bf16[256,64]{0,1:T(8,128)(2,1)} %param.20) | copy-start | bytes 98308
  0.0 36.0 %copy-start.1 = (s32[64,16,64]{2,1,0:T(8,128)S(1)}, s32[64,16,64]{2,1,0:T(8,128)}, u32[]{:S(2)}) copy-start(s32[64,16,64]{2,1,0:T(8,128)} %param.19) | copy-start | bytes 786436
  0.0 36.0 %copy-start = (bf16[64,16,256]{2,1,0:T(8,128)(2,1)S(1)}, bf16[64,16,256]{2,1,0:T(8,128)(2,1)}, u32[]{:S(2)}) copy-start(bf16[64,16,256]{2,1,0:T(8,128)(2,1)} %param.13) | copy-start | bytes 1572868
  1.1 17.1 %collective-permute-start.4 = (bf16[1360,128]{1,0:T(8,128)(2,1)S(1)}, bf16[1360,128]{1,0:T(8,128)(2,1)S(1)}, u32[]{:S(2)}, u32[]{:S(2)}) collective-permute-start(bf16[1360,128]{1,0:T(8,128)(2,1)S(1)} %pad_maximum_fusion.refs_0_.refs_1_), channel_id=1, source_target_pairs={{2,4},{4,2},{3,5},{5,3},{10,12},{12,10},{11,13},{13,11},{18,20},{2... | collective-permute-start | bytes 1044488 | tf_op jit(solution)/shard_map/ppermute | solution.py:485
  4.4 8.8 %collective-permute-start.3 = (bf16[1360,128]{1,0:T(8,128)(2,1)S(1)}, bf16[1360,128]{1,0:T(8,128)(2,1)S(1)}, u32[]{:S(2)}, u32[]{:S(2)}) collective-permute-start(bf16[1360,128]{1,0:T(8,128)(2,1)S(1)} %pad_maximum_fusion.refs_0_.refs_1_), channel_id=1, source_target_pairs={{0,2},{2,0},{4,6},{6,4},{1,3},{3,1},{5,7},{7,5},{8,10},{10,8},{12,... | collective-permute-start | bytes 1044488 | tf_op jit(solution)/shard_map/ppermute | solution.py:485
  13.2 9.8 %collective-permute-start.6 = (bf16[1360,128]{1,0:T(8,128)(2,1)S(1)}, bf16[1360,128]{1,0:T(8,128)(2,1)S(1)}, u32[]{:S(2)}, u32[]{:S(2)}) collective-permute-start(bf16[1360,128]{1,0:T(8,128)(2,1)S(1)} %collective-permute-done.3.refs_0_.refs_2_), channel_id=1, source_target_pairs={{2,4},{4,2},{3,5},{5,3},{10,12},{12,10},{11,13},{13,11},{18,20},{2... | collective-permute-start | bytes 1044488 | tf_op jit(solution)/shard_map/ppermute | solution.py:485
  15.5 8.8 %collective-permute-start.2 = (s32[4,8]{0,1:T(8,128)S(1)}, s32[4,8]{0,1:T(8,128)S(1)}, u32[]{:S(2)}, u32[]{:S(2)}) collective-permute-start(s32[4,8]{0,1:T(8,128)S(1)} %get-tuple-element.43), channel_id=1, source_target_pairs={{0,24},{8,16},{16,8},{24,0},{1,25},{9,17},{17,9},{25,1},{2,26},{10... | collective-permute-start | bytes 392 | tf_op jit(solution)/shard_map/ppermute | solution.py:504
  17.7 6.6 %collective-permute-start.1 = (s32[4,8]{0,1:T(8,128)S(1)}, s32[4,8]{0,1:T(8,128)S(1)}, u32[]{:S(2)}, u32[]{:S(2)}) collective-permute-start(s32[4,8]{0,1:T(8,128)S(1)} %get-tuple-element.44), channel_id=1, source_target_pairs={{0,16},{8,24},{16,0},{24,8},{1,17},{9,25},{17,1},{25,9},{2,18},{10... | collective-permute-start | bytes 392 | tf_op jit(solution)/shard_map/ppermute | solution.py:504
  17.9 6.4 %collective-permute-start = (s32[4,8]{0,1:T(8,128)S(1)}, s32[4,8]{0,1:T(8,128)S(1)}, u32[]{:S(2)}, u32[]{:S(2)}) collective-permute-start(s32[4,8]{0,1:T(8,128)S(1)} %get-tuple-element.45), channel_id=1, source_target_pairs={{0,8},{8,0},{16,24},{24,16},{1,9},{9,1},{17,25},{25,17},{2,10},{10... | collective-permute-start | bytes 392 | tf_op jit(solution)/shard_map/ppermute | solution.py:504
  18.2 11.0 %collective-permute-start.5 = (bf16[1360,128]{1,0:T(8,128)(2,1)S(1)}, bf16[1360,128]{1,0:T(8,128)(2,1)S(1)}, u32[]{:S(2)}, u32[]{:S(2)}) collective-permute-start(bf16[1360,128]{1,0:T(8,128)(2,1)S(1)} %collective-permute-done.4.refs_0_.refs_3_), channel_id=1, source_target_pairs={{2,0},{4,6},{3,1},{5,7},{10,8},{12,14},{11,9},{13,15},{18,16},{20,... | collective-permute-start | bytes 1044488 | tf_op jit(solution)/shard_map/ppermute | solution.py:485
  23.0 11.1 %collective-permute-start.7 = (bf16[1360,128]{1,0:T(8,128)(2,1)S(1)}, bf16[1360,128]{1,0:T(8,128)(2,1)S(1)}, u32[]{:S(2)}, u32[]{:S(2)}) collective-permute-start(bf16[1360,128]{1,0:T(8,128)(2,1)S(1)} %collective-permute-done.6.refs_1_.refs_5_), channel_id=1, source_target_pairs={{2,0},{4,6},{3,1},{5,7},{10,8},{12,14},{11,9},{13,15},{18,16},{20,... | collective-permute-start | bytes 1044488 | tf_op jit(solution)/shard_map/ppermute | solution.py:485
  24.5 21.7 %copy-start.11 = (f32[64]{0:T(128)S(1)}, f32[64]{0:T(128)}, u32[]{:S(2)}) copy-start(f32[64]{0:T(128)} %param.21) | copy-start | bytes 772
  25.5 6.0 %collective-permute-start.8 = (bf16[688,128]{1,0:T(8,128)(2,1)S(1)}, bf16[688,128]{1,0:T(8,128)(2,1)S(1)}, u32[]{:S(2)}, u32[]{:S(2)}) collective-permute-start(bf16[688,128]{1,0:T(8,128)(2,1)S(1)} %get-tuple-element.25), channel_id=1, source_target_pairs={{0,8},{8,0},{16,24},{24,16},{1,9},{9,1},{17,25},{25,17},{2,10},{10... | collective-permute-start | bytes 528392 | tf_op jit(solution)/shard_map/ppermute | solution.py:532
  26.8 6.0 %collective-permute-start.9 = (bf16[688,128]{1,0:T(8,128)(2,1)S(1)}, bf16[688,128]{1,0:T(8,128)(2,1)S(1)}, u32[]{:S(2)}, u32[]{:S(2)}) collective-permute-start(bf16[688,128]{1,0:T(8,128)(2,1)S(1)} %get-tuple-element.26), channel_id=1, source_target_pairs={{0,16},{8,24},{16,0},{24,8},{1,17},{9,25},{17,1},{25,9},{2,18},{10... | collective-permute-start | bytes 528392 | tf_op jit(solution)/shard_map/ppermute | solution.py:532
  28.0 10.2 %collective-permute-start.10 = (bf16[688,128]{1,0:T(8,128)(2,1)S(1)}, bf16[688,128]{1,0:T(8,128)(2,1)S(1)}, u32[]{:S(2)}, u32[]{:S(2)}) collective-permute-start(bf16[688,128]{1,0:T(8,128)(2,1)S(1)} %get-tuple-element.27), channel_id=1, source_target_pairs={{0,24},{8,16},{16,8},{24,0},{1,25},{9,17},{17,9},{25,1},{2,26},{10... | collective-permute-start | bytes 528392 | tf_op jit(solution)/shard_map/ppermute | solution.py:532
  29.2 9.2 %collective-permute-start.11 = (bf16[688,128]{1,0:T(8,128)(2,1)S(1)}, bf16[688,128]{1,0:T(8,128)(2,1)S(1)}, u32[]{:S(2)}, u32[]{:S(2)}) collective-permute-start(bf16[688,128]{1,0:T(8,128)(2,1)S(1)} %get-tuple-element.28), channel_id=1, source_target_pairs={{0,8},{8,0},{16,24},{24,16},{1,9},{9,1},{17,25},{25,17},{2,10},{10... | collective-permute-start | bytes 528392 | tf_op jit(solution)/shard_map/ppermute | solution.py:532
  31.5 9.2 %collective-permute-start.12 = (bf16[688,128]{1,0:T(8,128)(2,1)S(1)}, bf16[688,128]{1,0:T(8,128)(2,1)S(1)}, u32[]{:S(2)}, u32[]{:S(2)}) collective-permute-start(bf16[688,128]{1,0:T(8,128)(2,1)S(1)} %get-tuple-element.29), channel_id=1, source_target_pairs={{0,16},{8,24},{16,0},{24,8},{1,17},{9,25},{17,1},{25,9},{2,18},{10... | collective-permute-start | bytes 528392 | tf_op jit(solution)/shard_map/ppermute | solution.py:532
  32.8 9.1 %collective-permute-start.13 = (bf16[688,128]{1,0:T(8,128)(2,1)S(1)}, bf16[688,128]{1,0:T(8,128)(2,1)S(1)}, u32[]{:S(2)}, u32[]{:S(2)}) collective-permute-start(bf16[688,128]{1,0:T(8,128)(2,1)S(1)} %get-tuple-element.30), channel_id=1, source_target_pairs={{0,24},{8,16},{16,8},{24,0},{1,25},{9,17},{17,9},{25,1},{2,26},{10... | collective-permute-start | bytes 528392 | tf_op jit(solution)/shard_map/ppermute | solution.py:532
  34.0 0.7 %copy-start.3 = (bf16[1360,128]{1,0:T(8,128)(2,1)}, bf16[1360,128]{1,0:T(8,128)(2,1)S(1)}, u32[]{:S(2)}) copy-start(bf16[1360,128]{1,0:T(8,128)(2,1)S(1)} %collective-permute-done.7.refs_0_.refs_6_) | copy-start | bytes 1044484
  34.8 10.3 %collective-permute-start.14 = (bf16[688,128]{1,0:T(8,128)(2,1)S(1)}, bf16[688,128]{1,0:T(8,128)(2,1)S(1)}, u32[]{:S(2)}, u32[]{:S(2)}) collective-permute-start(bf16[688,128]{1,0:T(8,128)(2,1)S(1)} %get-tuple-element.31), channel_id=1, source_target_pairs={{0,8},{8,0},{16,24},{24,16},{1,9},{9,1},{17,25},{25,17},{2,10},{10... | collective-permute-start | bytes 528392 | tf_op jit(solution)/shard_map/ppermute | solution.py:532
  36.2 1.0 %copy-start.4 = (bf16[1360,128]{1,0:T(8,128)(2,1)S(1)}, bf16[1360,128]{1,0:T(8,128)(2,1)}, u32[]{:S(2)}) copy-start(bf16[1360,128]{1,0:T(8,128)(2,1)} %copy-done.3) | copy-start | bytes 1044484
  37.2 20.0 %copy-start.5 = (bf16[1360,128]{1,0:T(8,128)(2,1)S(1)}, bf16[1360,128]{1,0:T(8,128)(2,1)}, u32[]{:S(2)}) copy-start(bf16[1360,128]{1,0:T(8,128)(2,1)} %copy-done.3) | copy-start | bytes 1044484
  37.2 20.0 %copy-start.6 = (s32[4,1,4,8]{3,2,1,0:T(4,128)S(1)}, s32[4,1,4,8]{3,2,1,0:T(4,128)}, u32[]{:S(2)}) copy-start(s32[4,1,4,8]{3,2,1,0:T(4,128)} %refs_23_.1) | copy-start | bytes 1540
  38.2 12.4 %collective-permute-start.15 = (bf16[688,128]{1,0:T(8,128)(2,1)S(1)}, bf16[688,128]{1,0:T(8,128)(2,1)S(1)}, u32[]{:S(2)}, u32[]{:S(2)}) collective-permute-start(bf16[688,128]{1,0:T(8,128)(2,1)S(1)} %get-tuple-element.32), channel_id=1, source_target_pairs={{0,16},{8,24},{16,0},{24,8},{1,17},{9,25},{17,1},{25,9},{2,18},{10... | collective-permute-start | bytes 528392 | tf_op jit(solution)/shard_map/ppermute | solution.py:532
  38.4 12.1 %collective-permute-start.16 = (bf16[688,128]{1,0:T(8,128)(2,1)S(1)}, bf16[688,128]{1,0:T(8,128)(2,1)S(1)}, u32[]{:S(2)}, u32[]{:S(2)}) collective-permute-start(bf16[688,128]{1,0:T(8,128)(2,1)S(1)} %get-tuple-element.33), channel_id=1, source_target_pairs={{0,24},{8,16},{16,8},{24,0},{1,25},{9,17},{17,9},{25,1},{2,26},{10... | collective-permute-start | bytes 528392 | tf_op jit(solution)/shard_map/ppermute | solution.py:532
  40.7 11.9 %collective-permute-start.17 = (bf16[688,128]{1,0:T(8,128)(2,1)S(1)}, bf16[688,128]{1,0:T(8,128)(2,1)S(1)}, u32[]{:S(2)}, u32[]{:S(2)}) collective-permute-start(bf16[688,128]{1,0:T(8,128)(2,1)S(1)} %get-tuple-element.34), channel_id=1, source_target_pairs={{0,8},{8,0},{16,24},{24,16},{1,9},{9,1},{17,25},{25,17},{2,10},{10... | collective-permute-start | bytes 528392 | tf_op jit(solution)/shard_map/ppermute | solution.py:532
  42.0 13.7 %collective-permute-start.18 = (bf16[688,128]{1,0:T(8,128)(2,1)S(1)}, bf16[688,128]{1,0:T(8,128)(2,1)S(1)}, u32[]{:S(2)}, u32[]{:S(2)}) collective-permute-start(bf16[688,128]{1,0:T(8,128)(2,1)S(1)} %get-tuple-element.35), channel_id=1, source_target_pairs={{0,16},{8,24},{16,0},{24,8},{1,17},{9,25},{17,1},{25,9},{2,18},{10... | collective-permute-start | bytes 528392 | tf_op jit(solution)/shard_map/ppermute | solution.py:532
  45.1 12.1 %collective-permute-start.19 = (bf16[688,128]{1,0:T(8,128)(2,1)S(1)}, bf16[688,128]{1,0:T(8,128)(2,1)S(1)}, u32[]{:S(2)}, u32[]{:S(2)}) collective-permute-start(bf16[688,128]{1,0:T(8,128)(2,1)S(1)} %get-tuple-element.36), channel_id=1, source_target_pairs={{0,24},{8,16},{16,8},{24,0},{1,25},{9,17},{17,9},{25,1},{2,26},{10... | collective-permute-start | bytes 528392 | tf_op jit(solution)/shard_map/ppermute | solution.py:532
  57.2 11.4 %copy-start.2 = (bf16[256,256]{1,0:T(8,128)(2,1)S(1)}, bf16[256,256]{1,0:T(8,128)(2,1)}, u32[]{:S(2)}) copy-start(bf16[256,256]{1,0:T(8,128)(2,1)} %weight_ref.3) | copy-start | bytes 393220
  57.2 11.4 %copy-start.8 = (f32[256]{0:T(256)S(1)}, f32[256]{0:T(256)}, u32[]{:S(2)}) copy-start(f32[256]{0:T(256)} %param.23) | copy-start | bytes 3076
  57.2 12.6 %copy-start.9 = (f32[128]{0:T(128)S(1)}, f32[128]{0:T(128)}, u32[]{:S(2)}) copy-start(f32[128]{0:T(128)} %param.24) | copy-start | bytes 1540
  57.2 12.6 %copy-start.10 = (f32[128]{0:T(128)S(1)}, f32[128]{0:T(128)}, u32[]{:S(2)}) copy-start(f32[128]{0:T(128)} %param.25) | copy-start | bytes 1540
  65.1 4.7 %collective-permute-start.20 = (bf16[1024,128]{1,0:T(8,128)(2,1)S(1)}, bf16[1024,128]{1,0:T(8,128)(2,1)S(1)}, u32[]{:S(2)}, u32[]{:S(2)}) collective-permute-start(bf16[1024,128]{1,0:T(8,128)(2,1)S(1)} %attend.1.own_ref), channel_id=1, source_target_pairs={{0,1},{1,0},{2,3},{3,2},{4,5},{5,4},{6,7},{7,6},{8,9},{9,8},{10,11... | collective-permute-start | bytes 786440 | tf_op jit(solution)/shard_map/ppermute | solution.py:704
